TPU v7x, 32 devices: a whole 2x2x4 slice. The times are simulated.
32 devices in a mesh: shard: 8 (over z, core), context: 2 (over x), tensor: 2 (over y).
Axes of the slice: x: 2, y: 2, z: 4, core: 2. Of those that a mesh axis runs over, the one named last changes fastest.
Arguments:
- inputs: bfloat16 [32, 1024, 768], P('shard', 'context'), may hold values from -6 to 6
- out_grad: bfloat16 [32, 1024, 768], P('shard', 'context'), may hold values from -6 to 6
- picture_starts: int32 [32, 2], P('shard'), may hold values from 0 to 768, as said below
- segment_offsets: int32 [12, 5], P('tensor'), may hold values from 0 to 1023
- dilation_offsets: int32 [12, 5], P('tensor'), may hold values from 0 to 11
- norm_gains: bfloat16 [2, 768], P(None, 'shard'), may hold values from 0.5 to 1.5
- w_qkv: bfloat16 [3, 768, 768], P(None, 'shard', 'tensor'), may hold values from -0.21875 to 0.21875
- head_biases: bfloat16 [2, 12, 64], P(None, 'tensor', 'shard'), may hold values from -3 to 3
- head_gain: bfloat16 [12, 64], P('tensor', 'shard'), may hold values from 0.5 to 1.5
- w_out: bfloat16 [768, 768], P('tensor', 'shard'), may hold values from -0.21875 to 0.21875
- out_biases: bfloat16 [2, 768], P(None, 'shard'), may hold values from -3 to 3
- w_up: bfloat16 [768, 3072], P('shard', 'tensor'), may hold values from -0.21875 to 0.21875
- unit_bias: bfloat16 [48, 64], P('tensor', 'shard'), may hold values from -3 to 3
- unit_gain: bfloat16 [48, 64], P('tensor', 'shard'), may hold values from 0.5 to 1.5
- w_down: bfloat16 [3072, 768], P('tensor', 'shard'), may hold values from -0.109375 to 0.109375
Outputs:
- layer_out: bfloat16 [32, 1024, 768], P('shard', 'context')
- input_grad: bfloat16 [32, 1024, 768], P('shard', 'context')
- norm_gains_grad: float32 [2, 768], P(None, 'shard')
- w_qkv_grad: float32 [3, 768, 768], P(None, 'shard', 'tensor')
- head_biases_grad: float32 [2, 12, 64], P(None, 'tensor', 'shard')
- head_gain_grad: float32 [12, 64], P('tensor', 'shard')
- w_out_grad: float32 [768, 768], P('tensor', 'shard')
- out_biases_grad: float32 [2, 768], P(None, 'shard')
- w_up_grad: float32 [768, 3072], P('shard', 'tensor')
- unit_bias_grad: float32 [48, 64], P('tensor', 'shard')
- unit_gain_grad: float32 [48, 64], P('tensor', 'shard')
- w_down_grad: float32 [3072, 768], P('tensor', 'shard')
Inputs may be any that keep to these rules, and one draw needn't show every extreme that they name: `picture_starts`: in every sequence, piece k (k = 0 to 1) covers 256 positions from its start, which lies between k * 512 and that plus 1024 // 2 - 256, on a multiple of 32; pieces never intersect. `segment_offsets`: used modulo each pattern's segment span. `dilation_offsets`: used modulo each pattern's dilation.
All inputs are finite; a program needn't handle non-finite values.
Results may differ from a plain program's by a relative error of at most 0.018.
Values may be sent and summed in bfloat16 or wider, within the bound.
A program may use at most 320 MiB of HBM per device.

v0:
```python
from functools import partial

import jax
import jax.numpy as jnp
from jax import lax
from jax.sharding import PartitionSpec as P

HD = 64
FF = 3072
PIECE = 256
MICRO = 4


epsilon = 1e-05
span_parts = (1, 2, 4, 6, 8)
dilation_rates = (1, 2, 4, 6, 12)


def pattern_total(query_position, key_position, segmented_offsets, dilated_offsets, token_length):
    tallied_total = jnp.zeros(
        (segmented_offsets.shape[0], query_position.shape[0], key_position.shape[0]), jnp.float32
    )
    for item_number in range(len(span_parts)):
        segmented_span = token_length * span_parts[item_number] // 8
        dilated_stride = dilation_rates[item_number]
        seg_shift = (segmented_offsets[:, item_number] % segmented_span)[:, None, None]
        dilated_phase = (dilated_offsets[:, item_number] % dilated_stride)[:, None, None]
        query_lookup = query_position[None, :, None] + seg_shift
        key_lookup = key_position[None, None, :] + seg_shift
        merged_heads = (
            (query_lookup // segmented_span == key_lookup // segmented_span)
            & (query_lookup % dilated_stride == dilated_phase)
            & (key_lookup % dilated_stride == dilated_phase)
        )
        tallied_total = tallied_total + merged_heads.astype(jnp.float32)
    return tallied_total


def picture_index(starts, token_positions):
    marked = jnp.zeros((starts.shape[0], token_positions.shape[0]), jnp.int32)
    for piece_number in range(starts.shape[1]):
        begin_at = starts[:, piece_number][:, None]
        inside = (token_positions[None, :] >= begin_at) & (
            token_positions[None, :] < begin_at + PIECE
        )
        marked = marked + (piece_number + 1) * inside.astype(jnp.int32)
    return marked


def allowed_keys(query_pic, key_pic, query_position, key_position):
    causal_ok = key_position[None, None, :] <= query_position[None, :, None]
    same_piece = (query_pic[:, :, None] == key_pic[:, None, :]) & (query_pic[:, :, None] > 0)
    return (causal_ok | same_piece).astype(jnp.float32)


def outer_sum(left_rows, right_rows):
    return lax.dot_general(
        left_rows, right_rows, (((0,), (0,)), ((), ())), preferred_element_type=jnp.float32
    )


def back_dot(left_rows, weight_rows):
    return lax.dot_general(
        left_rows, weight_rows, (((1,), (1,)), ((), ())), preferred_element_type=jnp.float32
    )


def norm_rows(values, scale_row):
    mean_row = jnp.mean(values, -1, keepdims=True)
    centered = values - mean_row
    inv_std = lax.rsqrt(jnp.mean(centered * centered, -1, keepdims=True) + epsilon)
    normed = centered * inv_std
    return (normed, inv_std, normed * scale_row)


def norm_back(normed, inv_std, scale_row, grad_rows):
    scaled = grad_rows * scale_row
    mean_plain = jnp.mean(scaled, -1, keepdims=True)
    mean_cross = jnp.mean(scaled * normed, -1, keepdims=True)
    return (inv_std * (scaled - mean_plain - normed * mean_cross), jnp.sum(grad_rows * normed, 0))


def width_sums(sum_plain, sum_square):
    return lax.psum((sum_plain, sum_square), "tensor")


def row_sums(partial_rows):
    return lax.psum(partial_rows, "tensor")


def split_norm(values, scale_row, full_width):
    sum_plain, sum_square = width_sums(jnp.sum(values, -1), jnp.sum(values * values, -1))
    mean_row = (sum_plain / full_width)[:, None]
    inv_std = lax.rsqrt(sum_square[:, None] / full_width - mean_row * mean_row + epsilon)
    normed = (values - mean_row) * inv_std
    return (normed, inv_std, normed * scale_row)


def split_back(normed, inv_std, scale_row, grad_rows, full_width):
    scaled = grad_rows * scale_row
    sum_plain, sum_cross = width_sums(jnp.sum(scaled, -1), jnp.sum(scaled * normed, -1))
    shifted = (
        scaled - (sum_plain / full_width)[:, None] - normed * (sum_cross / full_width)[:, None]
    )
    return (inv_std * shifted, jnp.sum(grad_rows * normed, 0))


def probabilities(query_heads, key_heads, mask_table):
    raw_scores = jnp.einsum(
        "sqhd,skhd->shqk", query_heads, key_heads, preferred_element_type=jnp.float32
    ) * HD ** (-0.5)
    masked = jnp.where(mask_table > 0, raw_scores, -1000000000.0)
    row_top = jnp.max(masked, -1, keepdims=True)
    exponent = mask_table * jnp.exp(masked - row_top)
    row_total = jnp.sum(exponent, -1, keepdims=True)
    return (exponent / row_total, row_top, row_total)


def gather_per_batch(shards):
    return (
        lax.all_gather(shards[0], "shard", axis=1, tiled=True),
        lax.all_gather(shards[1], "shard", axis=1, tiled=True),
        lax.all_gather(shards[2], "shard", axis=0, tiled=True),
        lax.all_gather(shards[3], "shard", axis=1, tiled=True),
        lax.all_gather(shards[4], "shard", axis=1, tiled=True),
        lax.all_gather(shards[5], "shard", axis=1, tiled=True),
        lax.all_gather(shards[6], "shard", axis=2, tiled=True),
        lax.all_gather(shards[7], "shard", axis=1, tiled=True),
        lax.all_gather(shards[8], "shard", axis=1, tiled=True),
        lax.all_gather(shards[9], "shard", axis=1, tiled=True),
    )


def forward_pass(block_in, starts, tallied_total, gathered, query_position, key_position):
    (
        w_qkv,
        w_out,
        w_up,
        w_down,
        norm_gains,
        out_biases,
        head_biases,
        head_gain,
        unit_bias,
        unit_gain,
    ) = gathered
    seq_count, local_len, model_width = block_in.shape
    seq_len = key_position.shape[0]
    row_count = seq_count * local_len
    flattened_input = block_in.reshape(row_count, model_width).astype(jnp.float32)
    gain_rows = norm_gains.astype(jnp.float32)
    bias_rows = out_biases.astype(jnp.float32)
    first_normed, first_inv, first_out = norm_rows(flattened_input, gain_rows[0])
    attn_in = first_out.astype(jnp.bfloat16)
    projected = jnp.einsum("rd,jde->jre", attn_in, w_qkv, preferred_element_type=jnp.float32)
    head_bias = head_biases.reshape(2, -1).astype(jnp.float32)
    head_width = head_bias.shape[1]
    head_local = head_width // HD
    query_matrix = (projected[0] + head_bias[0]).astype(jnp.bfloat16)
    keys_local = projected[1].astype(jnp.bfloat16).reshape(seq_count, local_len, head_width)
    values_local = (
        (projected[2] + head_bias[1]).astype(jnp.bfloat16).reshape(seq_count, local_len, head_width)
    )
    key_all, value_all = (
        lax.all_gather(keys_local, "context", axis=1, tiled=True),
        lax.all_gather(values_local, "context", axis=1, tiled=True),
    )
    query_pic = picture_index(starts, query_position)
    key_pic = picture_index(starts, key_position)
    mask_table = (
        allowed_keys(query_pic, key_pic, query_position, key_position)[:, None]
        * tallied_total[None]
    )
    query_heads = query_matrix.reshape(seq_count, local_len, head_local, HD)
    weights_soft = probabilities(
        query_heads, key_all.reshape(seq_count, seq_len, head_local, HD), mask_table
    )[0]
    attended = jnp.einsum(
        "shqk,skhd->sqhd",
        weights_soft.astype(jnp.bfloat16),
        value_all.reshape(seq_count, seq_len, head_local, HD),
        preferred_element_type=jnp.float32,
    ).reshape(row_count, head_width)
    sub_normed, sub_inv, sub_out = split_norm(
        attended, head_gain.reshape(-1).astype(jnp.float32), model_width
    )
    sub_in = sub_out.astype(jnp.bfloat16)
    middle = flattened_input + (
        row_sums(jnp.dot(sub_in, w_out, preferred_element_type=jnp.float32)) + bias_rows[0]
    )
    second_normed, second_inv, second_out = norm_rows(middle, gain_rows[1])
    ffn_in = second_out.astype(jnp.bfloat16)
    hidden = jnp.dot(ffn_in, w_up, preferred_element_type=jnp.float32) + unit_bias.reshape(
        -1
    ).astype(jnp.float32)
    activated = jax.nn.gelu(hidden, approximate=True)
    unit_normed, unit_inv, unit_out = split_norm(
        activated, unit_gain.reshape(-1).astype(jnp.float32), FF
    )
    ffn_mid = unit_out.astype(jnp.bfloat16)
    layer_out = (
        middle
        + (row_sums(jnp.dot(ffn_mid, w_down, preferred_element_type=jnp.float32)) + bias_rows[1])
    ).astype(jnp.bfloat16)
    kept_state = (
        attn_in,
        first_normed,
        first_inv,
        query_heads,
        keys_local,
        values_local,
        key_all,
        value_all,
        mask_table,
        sub_normed,
        sub_inv,
        sub_in,
        second_normed,
        second_inv,
        ffn_in,
        hidden,
        unit_normed,
        unit_inv,
        ffn_mid,
    )
    return (kept_state, layer_out.reshape(seq_count, local_len, model_width))


def backward_pass(kept_state, block_grad, gathered):
    (
        w_qkv,
        w_out,
        w_up,
        w_down,
        norm_gains,
        out_biases,
        head_biases,
        head_gain,
        unit_bias,
        unit_gain,
    ) = gathered
    (
        attn_in,
        first_normed,
        first_inv,
        query_heads,
        keys_local,
        values_local,
        key_matrix,
        value_matrix,
        mask_table,
        sub_normed,
        sub_inv,
        sub_in,
        second_normed,
        second_inv,
        ffn_in,
        hidden,
        unit_normed,
        unit_inv,
        ffn_mid,
    ) = kept_state
    seq_count, local_len, model_width = block_grad.shape
    row_count = seq_count * local_len
    gain_rows = norm_gains.astype(jnp.float32)
    grad_low = block_grad.reshape(row_count, model_width)
    grad_full = grad_low.astype(jnp.float32)
    down_grad = outer_sum(ffn_mid, grad_low)
    last_bias_grad = jnp.sum(grad_full, 0)
    unit_grad = back_dot(grad_low, w_down)
    activated_grad, unit_gain_grad = split_back(
        unit_normed, unit_inv, unit_gain.reshape(-1).astype(jnp.float32), unit_grad, FF
    )
    gelu_value, gelu_pull = jax.vjp(partial(jax.nn.gelu, approximate=True), hidden)
    hidden_low = gelu_pull(activated_grad)[0].astype(jnp.bfloat16)
    up_grad = outer_sum(ffn_in, hidden_low)
    unit_bias_grad = jnp.sum(hidden_low, 0, dtype=jnp.float32)
    ffn_in_grad = row_sums(back_dot(hidden_low, w_up))
    middle_part, second_gain_grad = norm_back(second_normed, second_inv, gain_rows[1], ffn_in_grad)
    middle_grad = grad_full + middle_part
    middle_low = middle_grad.astype(jnp.bfloat16)
    out_weight_grad = outer_sum(sub_in, middle_low)
    first_bias_grad = jnp.sum(middle_low, 0, dtype=jnp.float32)
    sub_grad = back_dot(middle_low, w_out)
    attended_grad, head_gain_grad = split_back(
        sub_normed, sub_inv, head_gain.reshape(-1).astype(jnp.float32), sub_grad, model_width
    )
    attended_low = attended_grad.astype(jnp.bfloat16)
    key_all, value_all = (
        lax.all_gather(keys_local, "context", axis=1, tiled=True),
        lax.all_gather(values_local, "context", axis=1, tiled=True),
    )
    seq_len = key_all.shape[1]
    head_local = query_heads.shape[2]
    key_heads = key_all.reshape(seq_count, seq_len, head_local, HD)
    value_heads = value_all.reshape(seq_count, seq_len, head_local, HD)
    weights_soft, row_top, row_total = probabilities(query_heads, key_heads, mask_table)
    grad_heads = attended_low.reshape(seq_count, local_len, head_local, HD)
    soft_grad = jnp.einsum(
        "sqhd,skhd->shqk", grad_heads, value_heads, preferred_element_type=jnp.float32
    )
    inner_sum = jnp.sum(weights_soft * soft_grad, -1, keepdims=True)
    score_low = (weights_soft * (soft_grad - inner_sum)).astype(jnp.bfloat16)
    root_scale = HD ** (-0.5)
    query_low = (
        (
            jnp.einsum("shqk,skhd->sqhd", score_low, key_heads, preferred_element_type=jnp.float32)
            * root_scale
        )
        .astype(jnp.bfloat16)
        .reshape(row_count, -1)
    )
    key_part = (
        jnp.einsum("shqk,sqhd->skhd", score_low, query_heads, preferred_element_type=jnp.float32)
        * root_scale
    )
    value_part = jnp.einsum(
        "shqk,sqhd->skhd",
        weights_soft.astype(jnp.bfloat16),
        grad_heads,
        preferred_element_type=jnp.float32,
    )
    key_total, value_total = (
        lax.psum_scatter(
            key_part.reshape(seq_count, seq_len, -1).astype(jnp.bfloat16),
            "context",
            scatter_dimension=1,
            tiled=True,
        ).astype(jnp.float32),
        lax.psum_scatter(
            value_part.reshape(seq_count, seq_len, -1).astype(jnp.bfloat16),
            "context",
            scatter_dimension=1,
            tiled=True,
        ).astype(jnp.float32),
    )
    key_low = key_total.astype(jnp.bfloat16).reshape(row_count, -1)
    value_low = value_total.astype(jnp.bfloat16).reshape(row_count, -1)
    stacked = jnp.stack([query_low, key_low, value_low])
    qkv_grad = jnp.einsum("rd,jre->jde", attn_in, stacked, preferred_element_type=jnp.float32)
    head_bias_grad = jnp.stack(
        [jnp.sum(query_low, 0, dtype=jnp.float32), jnp.sum(value_low, 0, dtype=jnp.float32)]
    )
    attn_in_grad = row_sums(
        jnp.einsum("jre,jde->rd", stacked, w_qkv, preferred_element_type=jnp.float32)
    )
    input_part, first_gain_grad = norm_back(first_normed, first_inv, gain_rows[0], attn_in_grad)
    input_low = (middle_grad + input_part).astype(jnp.bfloat16)
    grad_terms = (
        qkv_grad,
        out_weight_grad,
        up_grad,
        down_grad,
        jnp.stack([first_gain_grad, second_gain_grad]),
        jnp.stack([first_bias_grad, last_bias_grad]),
        head_bias_grad,
        head_gain_grad,
        unit_bias_grad,
        unit_gain_grad,
    )
    return (grad_terms, input_low.reshape(seq_count, local_len, model_width))


def local(
    inputs,
    out_grad,
    picture_starts,
    segment_offsets,
    dilation_offsets,
    norm_gains,
    w_qkv,
    head_biases,
    head_gain,
    w_out,
    out_biases,
    w_up,
    unit_bias,
    unit_gain,
    w_down,
):
    local_seqs, local_len, model_width = inputs.shape
    batch_seqs = local_seqs // MICRO
    seq_len = local_len * lax.axis_size("context")
    query_position = lax.axis_index("context") * local_len + jnp.arange(local_len, dtype=jnp.int32)
    key_position = jnp.arange(seq_len, dtype=jnp.int32)
    tallied_total = pattern_total(
        query_position, key_position, segment_offsets, dilation_offsets, seq_len
    )
    shards = (
        w_qkv,
        w_out,
        w_up,
        w_down,
        norm_gains,
        out_biases,
        head_biases,
        head_gain,
        unit_bias,
        unit_gain,
    )
    head_width = w_qkv.shape[2]
    unit_width = w_up.shape[1]
    totals = (
        jnp.zeros((3, model_width, head_width), jnp.float32),
        jnp.zeros((head_width, model_width), jnp.float32),
        jnp.zeros((model_width, unit_width), jnp.float32),
        jnp.zeros((unit_width, model_width), jnp.float32),
        jnp.zeros((2, model_width), jnp.float32),
        jnp.zeros((2, model_width), jnp.float32),
        jnp.zeros((2, head_width), jnp.float32),
        jnp.zeros((head_width,), jnp.float32),
        jnp.zeros((unit_width,), jnp.float32),
        jnp.zeros((unit_width,), jnp.float32),
    )
    output_blocks = []
    grad_blocks = []
    for micro_index in range(MICRO):
        gathered = gather_per_batch(shards)
        lower_seq = micro_index * batch_seqs
        block_in = inputs[lower_seq : lower_seq + batch_seqs]
        block_grad = out_grad[lower_seq : lower_seq + batch_seqs]
        starts = picture_starts[lower_seq : lower_seq + batch_seqs]
        kept_state, layer_block = forward_pass(
            block_in, starts, tallied_total, gathered, query_position, key_position
        )
        grad_terms, input_block = backward_pass(kept_state, block_grad, gathered)
        totals = tuple((current + addend for current, addend in zip(totals, grad_terms)))
        output_blocks.append(layer_block)
        grad_blocks.append(input_block)
    head_local = head_width // HD
    unit_rows = unit_width // HD
    shaped = (
        totals[0],
        totals[1],
        totals[2],
        totals[3],
        totals[4],
        totals[5],
        totals[6].reshape(2, head_local, HD),
        totals[7].reshape(head_local, HD),
        totals[8].reshape(unit_rows, HD),
        totals[9].reshape(unit_rows, HD),
    )
    shares = (
        lax.psum_scatter(
            shaped[0].astype(jnp.bfloat16), "shard", scatter_dimension=1, tiled=True
        ).astype(jnp.float32),
        lax.psum_scatter(
            shaped[1].astype(jnp.bfloat16), "shard", scatter_dimension=1, tiled=True
        ).astype(jnp.float32),
        lax.psum_scatter(
            shaped[2].astype(jnp.bfloat16), "shard", scatter_dimension=0, tiled=True
        ).astype(jnp.float32),
        lax.psum_scatter(
            shaped[3].astype(jnp.bfloat16), "shard", scatter_dimension=1, tiled=True
        ).astype(jnp.float32),
        lax.psum_scatter(
            shaped[4].astype(jnp.bfloat16), "shard", scatter_dimension=1, tiled=True
        ).astype(jnp.float32),
        lax.psum_scatter(
            shaped[5].astype(jnp.bfloat16), "shard", scatter_dimension=1, tiled=True
        ).astype(jnp.float32),
        lax.psum_scatter(
            shaped[6].astype(jnp.bfloat16), "shard", scatter_dimension=2, tiled=True
        ).astype(jnp.float32),
        lax.psum_scatter(
            shaped[7].astype(jnp.bfloat16), "shard", scatter_dimension=1, tiled=True
        ).astype(jnp.float32),
        lax.psum_scatter(
            shaped[8].astype(jnp.bfloat16), "shard", scatter_dimension=1, tiled=True
        ).astype(jnp.float32),
        lax.psum_scatter(
            shaped[9].astype(jnp.bfloat16), "shard", scatter_dimension=1, tiled=True
        ).astype(jnp.float32),
    )
    reduced = (
        lax.psum(shares[0].astype(jnp.bfloat16), "context").astype(jnp.float32),
        lax.psum(shares[1].astype(jnp.bfloat16), "context").astype(jnp.float32),
        lax.psum(shares[2].astype(jnp.bfloat16), "context").astype(jnp.float32),
        lax.psum(shares[3].astype(jnp.bfloat16), "context").astype(jnp.float32),
        lax.psum(shares[4].astype(jnp.bfloat16), "context").astype(jnp.float32),
        lax.psum(shares[5].astype(jnp.bfloat16), "context").astype(jnp.float32),
        lax.psum(shares[6].astype(jnp.bfloat16), "context").astype(jnp.float32),
        lax.psum(shares[7].astype(jnp.bfloat16), "context").astype(jnp.float32),
        lax.psum(shares[8].astype(jnp.bfloat16), "context").astype(jnp.float32),
        lax.psum(shares[9].astype(jnp.bfloat16), "context").astype(jnp.float32),
    )
    layer_out = jnp.concatenate(output_blocks, 0)
    input_grad = jnp.concatenate(grad_blocks, 0)
    return (
        layer_out,
        input_grad,
        reduced[4],
        reduced[0],
        reduced[6],
        reduced[7],
        reduced[1],
        reduced[5],
        reduced[2],
        reduced[8],
        reduced[9],
        reduced[3],
    )


def solution(mesh):
    placed = (
        P("shard", "context", None),
        P("shard", "context", None),
        P("shard", None),
        P("tensor", None),
        P("tensor", None),
        P(None, "shard"),
        P(None, "shard", "tensor"),
        P(None, "tensor", "shard"),
        P("tensor", "shard"),
        P("tensor", "shard"),
        P(None, "shard"),
        P("shard", "tensor"),
        P("tensor", "shard"),
        P("tensor", "shard"),
        P("tensor", "shard"),
    )
    return jax.shard_map(
        local,
        mesh=mesh,
        in_specs=placed,
        out_specs=(
            P("shard", "context", None),
            P("shard", "context", None),
            P(None, "shard"),
            P(None, "shard", "tensor"),
            P(None, "tensor", "shard"),
            P("tensor", "shard"),
            P("tensor", "shard"),
            P(None, "shard"),
            P("shard", "tensor"),
            P("tensor", "shard"),
            P("tensor", "shard"),
            P("tensor", "shard"),
        ),
        check_vma=False,
    )
```

profile of v0, /device:TPU:0, one launch (start us, length us, event | category | flops | bytes accessed | tf_op | source)
XLA Modules:
  0.0 1726.6 jit_solution(13538409955858462024)
XLA Ops:
  28.6 13.6 all-gather
  45.6 14.1 all_gather.38
  60.8 12.8 all_gather.41
  77.4 16.0 all_gather.42
  102.4 12.1 all_gather.51
  114.6 11.8 all_gather.50
  126.5 34.4 %fusion.386 = (f32[6,512]{1,0:T(8,128)S(1)}, f32[6,512,1024]{2,1,0:T(8,128)}) fusion(f32[512,1024]{1,0:T(8,128)} %get-tuple-element.329, bf16[1024,6,64]{0,2,1:T(8,128)(2,1)} %bitcast.562, pred[6,1024]{1,0:T(8,128)(4,1)S(1)} %copy-done.252, pred[6,512]{1,0:T(8,128)(4,1)S(1)} %get-tuple-element.342, s32[6,1024]{1,0:T(8,128)S(1)} %add_select_fusion.1, ...), kind=kOutput, calls=%fused_computation.764 | convolution fusion | flops 566625280 | bytes 16487936 | tf_op jit(solution)/shard_map/sub | solution.py:114
  160.9 7.9 fusion.186
  181.2 8.9 all-gather.1
  190.2 12.8 all_gather.45
  203.2 12.9 all_gather.46
  216.9 12.9 all-reduce.26.cloned.1.call-done
  233.0 29.9 %all-gather.8.cloned.1.call-done = bf16[768,1536]{1,0:T(8,128)(2,1)} async-done(((bf16[96,1536]{1,0:T(8,128)(2,1)}), bf16[768,1536]{1,0:T(8,128)(2,1)}) %all-gather.8.cloned.1.call-update) | async-done | bytes 2359312 | tf_op jit(solution)/shard_map/all_gather | solution.py:123
  273.8 21.4 %all-gather.10.cloned.1.call-done = bf16[1536,768]{0,1:T(8,128)(2,1)} async-done(((bf16[1536,96]{0,1:T(8,128)(2,1)}), bf16[1536,768]{0,1:T(8,128)(2,1)}) %all-gather.10.cloned.1.call-update) | async-done | bytes 2359312 | tf_op jit(solution)/shard_map/all_gather | solution.py:124
  295.2 7.4 multiply_reduce_fusion.5
  317.8 50.9 %all-reduce.28.cloned.1.call-done = f32[512,768]{1,0:T(8,128)} async-done(((f32[512,768]{1,0:T(8,128)}), f32[512,768]{1,0:T(8,128)}) %all-reduce.28.cloned.1.call-update) | async-done | bytes 1572880 | tf_op jit(solution)/shard_map/psum | solution.py:88
  383.4 10.5 multiply_reduce_fusion.1
  425.0 19.8 %reduce-scatter.35.cloned.1.call-done = bf16[1,512,384]{2,1,0:T(8,128)(2,1)} async-done(((bf16[1,1024,384]{2,1,0:T(8,128)(2,1)}), bf16[1,512,384]{2,1,0:T(8,128)(2,1)}) %reduce-scatter.35.cloned.1.call-update) | async-done | bytes 393232 | tf_op jit(solution)/shard_map/reduce_scatter | solution.py:330
  449.2 51.5 %all-reduce.30.cloned.1.call-done = f32[512,768]{1,0:T(8,128)} async-done(((f32[512,768]{1,0:T(8,128)}), f32[512,768]{1,0:T(8,128)}) %all-reduce.30.cloned.1.call-update) | async-done | bytes 1572880 | tf_op jit(solution)/shard_map/psum | solution.py:88
  511.9 11.5 all_gather.49
  523.4 10.9 all_gather.48
  534.7 32.7 %fusion.389 = (f32[6,512]{1,0:T(8,128)S(1)}, f32[6,512,1024]{2,1,0:T(8,128)}) fusion(f32[512,1024]{1,0:T(8,128)} %get-tuple-element.330, bf16[512,6,64]{0,2,1:T(8,128)(2,1)S(1)} %get-tuple-element.302, bf16[1024,6,64]{0,2,1:T(8,128)(2,1)S(1)} %bitcast.558, pred[6,1024]{1,0:T(8,128)(4,1)S(1)} %copy-done.253, pred[6,512]{1,0:T(8,128)(4,1)S(1)} %copy-done.259, ...), kind=kOutput, calls=%fused_computation.767 | convolution fusion | flops 566232064 | bytes 16093184 | tf_op jit(solution)/shard_map/sub | solution.py:114
  574.1 9.7 all_gather.40
  583.8 9.0 all_gather.39
  593.0 32.8 %fusion.388 = (f32[6,512]{1,0:T(8,128)S(1)}, f32[6,512,1024]{2,1,0:T(8,128)}) fusion(f32[512,1024]{1,0:T(8,128)} %get-tuple-element.331, bf16[512,6,64]{0,2,1:T(8,128)(2,1)S(1)} %get-tuple-element.303, bf16[1024,6,64]{0,2,1:T(8,128)(2,1)S(1)} %bitcast.556, pred[6,1024]{1,0:T(8,128)(4,1)S(1)} %copy-done.254, pred[6,512]{1,0:T(8,128)(4,1)S(1)} %copy-done.260, ...), kind=kOutput, calls=%fused_computation.766 | convolution fusion | flops 566232064 | bytes 16093184 | tf_op jit(solution)/shard_map/sub | solution.py:114
  632.5 10.1 all_gather.53
  642.6 8.8 all_gather.52
  651.4 32.5 %fusion.387 = (f32[6,512]{1,0:T(8,128)S(1)}, f32[6,512,1024]{2,1,0:T(8,128)}) fusion(f32[512,1024]{1,0:T(8,128)} %get-tuple-element.328, bf16[512,6,64]{0,2,1:T(8,128)(2,1)S(1)} %get-tuple-element.301, bf16[1024,6,64]{0,2,1:T(8,128)(2,1)S(1)} %bitcast.560, pred[6,1024]{1,0:T(8,128)(4,1)S(1)} %copy-done.254, pred[6,512]{1,0:T(8,128)(4,1)S(1)} %copy-done.260, ...), kind=kOutput, calls=%fused_computation.765 | convolution fusion | flops 566232064 | bytes 16093184 | tf_op jit(solution)/shard_map/sub | solution.py:114
  690.1 7.7 all-reduce.7
  713.1 110.5 %all-reduce.36.cloned.1.call-done = (f32[512,768]{1,0:T(8,128)}, f32[512,768]{1,0:T(8,128)}, f32[512,768]{1,0:T(8,128)}) async-done(((f32[512,768]{1,0:T(8,128)}, f32[512,768]{1,0:T(8,128)}, f32[512,768]{1,0:T(8,128)}), (f32[512,768]{1,0:T(8,128)}, f32[512,768]{1,0:T(8,128)}, f32[512,768]{1,0:T(8,128)})) %all-reduce.36.cloned.1.call-update) | async-done | bytes 4718608 | tf_op jit(solution)/shard_map/psum | solution.py:88
  848.2 13.0 multiply_reduce_fusion.4
  861.2 8.5 all-reduce.5
  869.8 15.6 convert_reduce_fusion
  898.5 114.2 %all-reduce.34.cloned.1.call-done = (f32[512,768]{1,0:T(8,128)}, f32[512,768]{1,0:T(8,128)}, f32[512,768]{1,0:T(8,128)}) async-done(((f32[512,768]{1,0:T(8,128)}, f32[512,768]{1,0:T(8,128)}, f32[512,768]{1,0:T(8,128)}), (f32[512,768]{1,0:T(8,128)}, f32[512,768]{1,0:T(8,128)}, f32[512,768]{1,0:T(8,128)})) %all-reduce.34.cloned.1.call-update) | async-done | bytes 4718608 | tf_op jit(solution)/shard_map/psum | solution.py:88
  1029.9 7.1 all-reduce.4
  1041.0 10.3 multiply_reduce_fusion.2
  1068.3 9.4 multiply_reduce_fusion.3
  1077.7 9.3 multiply_convert_fusion.3
  1101.6 9.5 multiply_reduce_fusion
  1111.2 9.5 multiply_convert_fusion
  1164.3 18.8 %reduce-scatter.39.cloned.1.call-done = bf16[1,512,384]{2,1,0:T(8,128)(2,1)} async-done(((bf16[1,1024,384]{2,1,0:T(8,128)(2,1)}), bf16[1,512,384]{2,1,0:T(8,128)(2,1)}) %reduce-scatter.39.cloned.1.call-update) | async-done | bytes 393232 | tf_op jit(solution)/shard_map/reduce_scatter | solution.py:330
  1253.5 17.5 %reduce-scatter.45.cloned.1.call-done = bf16[1536,96]{0,1:T(8,128)(2,1)} async-done(((bf16[1536,768]{0,1:T(8,128)(2,1)}), bf16[1536,96]{0,1:T(8,128)(2,1)}) %reduce-scatter.45.cloned.1.call-update) | async-done | bytes 294928 | tf_op jit(solution)/shard_map/reduce_scatter | solution.py:454
  1271.0 38.3 %reduce-scatter.43.cloned.1.call-done = bf16[96,1536]{1,0:T(8,128)(2,1)} async-done(((bf16[768,1536]{1,0:T(8,128)(2,1)}), bf16[96,1536]{1,0:T(8,128)(2,1)}) %reduce-scatter.43.cloned.1.call-update) | async-done | bytes 294928 | tf_op jit(solution)/shard_map/reduce_scatter | solution.py:451
  1309.3 32.9 %reduce-scatter.41.cloned.1.call-done = bf16[384,96]{0,1:T(8,128)(2,1)} async-done(((bf16[384,768]{0,1:T(8,128)(2,1)}), bf16[384,96]{0,1:T(8,128)(2,1)}) %reduce-scatter.41.cloned.1.call-update) | async-done | bytes 73744 | tf_op jit(solution)/shard_map/reduce_scatter | solution.py:448
  1383.0 27.0 %all-reduce.15 = (bf16[2,6,64]{2,1,0:T(8,128)(2,1)S(1)}, bf16[24,64]{1,0:T(8,128)(2,1)S(1)}, bf16[24,64]{1,0:T(8,128)(2,1)S(1)}, bf16[6,64]{1,0:T(8,128)(2,1)S(1)}) all-reduce(bf16[2,6,64]{2,1,0:T(8,128)(2,1)S(1)} %fusion.272, ...), channel_id=12, replica_groups=mesh['shard'=8,'context'=2,'tensor'=2] {'shard'}, use_global_device_ids=true, to_apply=%region_152.153.clone | all-reduce | flops 4224 | bytes 16896
  1419.4 251.4 %all-reduce.32.cloned.1.call-done = (f32[512,768]{1,0:T(8,128)}, f32[512,768]{1,0:T(8,128)}, f32[512,768]{1,0:T(8,128)}, f32[512,768]{1,0:T(8,128)}, f32[512,768...) async-done(((f32[512,768]{1,0:T(8,128)}, f32[512,768]{1,0:T(8,128)}, f32[512,768]{1,0:T(8,128)}, f32[512,768]{1,0:T(8,128)}, f32[512,768]{1,0:T(8,128)}, ...) | async-done | bytes 11010064 | tf_op jit(solution)/shard_map/psum | solution.py:88
  1689.5 17.0 reduce-scatter.47.cloned.1.call-done
  1707.3 8.3 all-reduce.16
  (915 shorter events, 446.7 us)
Async XLA Ops:
  7.2 53.5 %copy-start.272 = (bf16[6,8]{1,0:T(8,128)(2,1)S(1)}, bf16[6,8]{1,0:T(8,128)(2,1)}, u32[]{:S(2)}) copy-start(bf16[6,8]{1,0:T(8,128)(2,1)} %param.23) | copy-start | bytes 292
  7.2 70.2 %copy-start.109 = (bf16[384,96]{0,1:T(8,128)(2,1)S(1)}, bf16[384,96]{0,1:T(8,128)(2,1)}, u32[]{:S(2)}) copy-start(bf16[384,96]{0,1:T(8,128)(2,1)} %param.24) | copy-start | bytes 221188
  7.2 91.3 %all-gather.6.cloned.1.call-start = ((), (), s32[]{:S(2)}) async-start(), calls=%async_computation.14 | async-start | bytes 1990656 | tf_op jit(solution)/shard_map/all_gather | solution.py:121
  8.0 221.9 %all-reduce.26.cloned.1.call-start = ((), (), s32[]{:S(2)}) async-start(), calls=%async_computation.17 | async-start | bytes 3145728 | tf_op jit(solution)/shard_map/psum | solution.py:88
  73.8 308.0 %copy-start.105 = (f32[384]{0:T(512)}, f32[384]{0:T(512)S(1)}, u32[]{:S(2)}) copy-start(f32[384]{0:T(512)S(1)} %reshape.2714) | copy-start | bytes 4612
  73.8 298.2 %copy-start.90 = (f32[768]{0:T(1024)}, f32[768]{0:T(1024)S(1)}, u32[]{:S(2)}) copy-start(f32[768]{0:T(1024)S(1)} %get-tuple-element.157) | copy-start | bytes 9220
  73.8 434.9 %copy-start.100 = (f32[768]{0:T(1024)}, f32[768]{0:T(1024)S(1)}, u32[]{:S(2)}) copy-start(f32[768]{0:T(1024)S(1)} %get-tuple-element.158) | copy-start | bytes 9220
  175.0 199.6 %copy-start.146 = (f32[512]{0:T(512)}, f32[512]{0:T(512)S(1)}, u32[]{:S(2)}) copy-start(f32[512]{0:T(512)S(1)} %get-tuple-element.334) | copy-start | bytes 6148
  175.0 199.6 %copy-start.147 = (f32[512]{0:T(512)}, f32[512]{0:T(512)S(1)}, u32[]{:S(2)}) copy-start(f32[512]{0:T(512)S(1)} %get-tuple-element.335) | copy-start | bytes 6148
  179.8 83.1 %all-gather.8.cloned.1.call-start = ((), (), s32[]{:S(2)}) async-start(), calls=%async_computation.15 | async-start | bytes 2654208 | tf_op jit(solution)/shard_map/all_gather | solution.py:123
  180.6 114.6 %all-gather.10.cloned.1.call-start = ((), (), s32[]{:S(2)}) async-start(), calls=%async_computation.16 | async-start | bytes 2654208 | tf_op jit(solution)/shard_map/all_gather | solution.py:124
  181.1 187.6 %all-reduce.28.cloned.1.call-start = ((), (), s32[]{:S(2)}) async-start(), calls=%async_computation.22 | async-start | bytes 3145728 | tf_op jit(solution)/shard_map/psum | solution.py:88
  203.2 65.7 %copy-start.242 = (f32[1536]{0:T(1024)}, f32[1536]{0:T(1024)S(1)}, u32[]{:S(2)}) copy-start(f32[1536]{0:T(1024)S(1)} %reshape.2715) | copy-start | bytes 18436
  216.3 91.2 %copy-start.102 = (f32[1536]{0:T(1024)}, f32[1536]{0:T(1024)S(1)}, u32[]{:S(2)}) copy-start(f32[1536]{0:T(1024)S(1)} %reshape.2716) | copy-start | bytes 18436
  231.6 140.5 %copy-start.107 = (f32[512]{0:T(512)}, f32[512]{0:T(512)S(1)}, u32[]{:S(2)}) copy-start(f32[512]{0:T(512)S(1)} %broadcast_multiply_fusion.39) | copy-start | bytes 6148
  233.0 139.0 %copy-start.115 = (f32[512]{0:T(512)}, f32[512]{0:T(512)S(1)}, u32[]{:S(2)}) copy-start(f32[512]{0:T(512)S(1)} %add_rsqrt_fusion.5) | copy-start | bytes 6148
  317.8 107.2 %reduce-scatter.33.cloned.1.call-start = ((), (), s32[]{:S(2)}) async-start(), calls=%async_computation.23 | async-start | bytes 1179648 | tf_op jit(solution)/shard_map/reduce_scatter | solution.py:324
  407.4 37.5 %reduce-scatter.35.cloned.1.call-start = ((), (), s32[]{:S(2)}) async-start(), calls=%async_computation.24 | async-start | bytes 1179648 | tf_op jit(solution)/shard_map/reduce_scatter | solution.py:330
  416.2 84.5 %all-reduce.30.cloned.1.call-start = ((), (), s32[]{:S(2)}) async-start(), calls=%async_computation.25 | async-start | bytes 3145728 | tf_op jit(solution)/shard_map/psum | solution.py:88
  423.0 77.8 %copy-start.131 = (f32[512]{0:T(512)S(1)}, f32[512]{0:T(512)}, u32[]{:S(2)}) copy-start(f32[512]{0:T(512)} %copy-done.130) | copy-start | bytes 6148
  423.0 77.8 %copy-start.172 = (f32[512]{0:T(512)S(1)}, f32[512]{0:T(512)}, u32[]{:S(2)}) copy-start(f32[512]{0:T(512)} %copy-done.171) | copy-start | bytes 6148
  449.1 374.6 %all-reduce.36.cloned.1.call-start = ((), (), s32[]{:S(2)}) async-start(), calls=%async_computation.36 | async-start | bytes 9437184 | tf_op jit(solution)/shard_map/psum | solution.py:88
  449.1 56.3 %copy-start.159 = (f32[512]{0:T(512)}, f32[512]{0:T(512)S(1)}, u32[]{:S(2)}) copy-start(f32[512]{0:T(512)S(1)} %broadcast_multiply_fusion.44) | copy-start | bytes 6148
  449.2 56.5 %copy-start.162 = (f32[512]{0:T(512)}, f32[512]{0:T(512)S(1)}, u32[]{:S(2)}) copy-start(f32[512]{0:T(512)S(1)} %get-tuple-element.394) | copy-start | bytes 6148
  449.2 59.5 %copy-start.126 = (f32[512]{0:T(512)}, f32[512]{0:T(512)S(1)}, u32[]{:S(2)}) copy-start(f32[512]{0:T(512)S(1)} %get-tuple-element.393) | copy-start | bytes 6148
  534.5 58.4 %copy-start.76 = (bf16[512,6,64]{0,2,1:T(8,128)(2,1)}, bf16[512,6,64]{0,2,1:T(8,128)(2,1)S(1)}, u32[]{:S(2)}) copy-start(bf16[512,6,64]{0,2,1:T(8,128)(2,1)S(1)} %get-tuple-element.303) | copy-start | bytes 1179652
  534.5 116.9 %copy-start.74 = (bf16[512,6,64]{0,2,1:T(8,128)(2,1)}, bf16[512,6,64]{0,2,1:T(8,128)(2,1)S(1)}, u32[]{:S(2)}) copy-start(bf16[512,6,64]{0,2,1:T(8,128)(2,1)S(1)} %get-tuple-element.301) | copy-start | bytes 1179652
  573.9 124.0 %copy-start.36 = (f32[6,64,512]{2,1,0:T(8,128)}, f32[6,64,512]{2,1,0:T(8,128)S(1)}, u32[]{:S(2)}) copy-start(f32[6,64,512]{2,1,0:T(8,128)S(1)} %get-tuple-element.371) | copy-start | bytes 2359300
  632.4 65.5 %copy-start.38 = (f32[6,64,512]{2,1,0:T(8,128)}, f32[6,64,512]{2,1,0:T(8,128)S(1)}, u32[]{:S(2)}) copy-start(f32[6,64,512]{2,1,0:T(8,128)S(1)} %get-tuple-element.367) | copy-start | bytes 2359300
  703.7 309.0 %all-reduce.34.cloned.1.call-start = ((), (), s32[]{:S(2)}) async-start(), calls=%async_computation.35 | async-start | bytes 9437184 | tf_op jit(solution)/shard_map/psum | solution.py:88
  708.6 115.0 %copy-start.1 = (bf16[4,512,768]{2,1,0:T(8,128)(2,1)S(1)}, bf16[4,512,768]{2,1,0:T(8,128)(2,1)}, u32[]{:S(2)}) copy-start(bf16[4,512,768]{2,1,0:T(8,128)(2,1)} %param.15) | copy-start | bytes 9437188
  708.6 115.0 %copy-start.129 = (f32[768]{0:T(1024)S(1)}, f32[768]{0:T(1024)}, u32[]{:S(2)}) copy-start(f32[768]{0:T(1024)} %copy-done.128) | copy-start | bytes 9220
  827.1 194.2 %copy-start.110 = (f32[512]{0:T(512)}, f32[512]{0:T(512)S(1)}, u32[]{:S(2)}) copy-start(f32[512]{0:T(512)S(1)} %broadcast_multiply_fusion.42) | copy-start | bytes 6148
  893.2 262.4 %reduce-scatter.29.cloned.1.call-start = ((), (), s32[]{:S(2)}) async-start(), calls=%async_computation.20 | async-start | bytes 1179648 | tf_op jit(solution)/shard_map/reduce_scatter | solution.py:324
  1041.0 60.7 %copy-start.99 = (bf16[512,384]{0,1:T(8,128)(2,1)}, bf16[512,384]{0,1:T(8,128)(2,1)S(1)}, u32[]{:S(2)}) copy-start(bf16[512,384]{0,1:T(8,128)(2,1)S(1)} %get-tuple-element.305) | copy-start | bytes 1179652
  1065.9 89.7 %reduce-scatter.31.cloned.1.call-start = ((), (), s32[]{:S(2)}) async-start(), calls=%async_computation.21 | async-start | bytes 1179648 | tf_op jit(solution)/shard_map/reduce_scatter | solution.py:330
  1077.7 82.3 %reduce-scatter.25.cloned.1.call-start = ((), (), s32[]{:S(2)}) async-start(), calls=%async_computation.18 | async-start | bytes 1179648 | tf_op jit(solution)/shard_map/reduce_scatter | solution.py:324
  1101.6 58.4 %reduce-scatter.27.cloned.1.call-start = ((), (), s32[]{:S(2)}) async-start(), calls=%async_computation.19 | async-start | bytes 1179648 | tf_op jit(solution)/shard_map/reduce_scatter | solution.py:330
  1111.1 53.2 %reduce-scatter.37.cloned.1.call-start = ((), (), s32[]{:S(2)}) async-start(), calls=%async_computation.26 | async-start | bytes 1179648 | tf_op jit(solution)/shard_map/reduce_scatter | solution.py:324
  1125.9 57.2 %reduce-scatter.39.cloned.1.call-start = ((), (), s32[]{:S(2)}) async-start(), calls=%async_computation.27 | async-start | bytes 1179648 | tf_op jit(solution)/shard_map/reduce_scatter | solution.py:330
  1142.2 109.4 %reduce-scatter.49.cloned.1.call-start = ((), (), s32[]{:S(2)}) async-start(), calls=%async_computation.32 | async-start | bytes 1990656
  1198.5 72.5 %reduce-scatter.45.cloned.1.call-start = ((), (), s32[]{:S(2)}) async-start(), calls=%async_computation.30 | async-start | bytes 2654208 | tf_op jit(solution)/shard_map/reduce_scatter | solution.py:454
  1211.3 98.0 %reduce-scatter.43.cloned.1.call-start = ((), (), s32[]{:S(2)}) async-start(), calls=%async_computation.29 | async-start | bytes 2654208 | tf_op jit(solution)/shard_map/reduce_scatter | solution.py:451
  1222.6 119.5 %reduce-scatter.41.cloned.1.call-start = ((), (), s32[]{:S(2)}) async-start(), calls=%async_computation.28 | async-start | bytes 663552 | tf_op jit(solution)/shard_map/reduce_scatter | solution.py:448
  1234.1 139.3 %reduce-scatter.51.cloned.1.call-start = ((), (), s32[]{:S(2)}) async-start(), calls=%async_computation.33 | async-start | bytes 221184
  1245.4 166.9 %all-reduce.38.cloned.1.call-start = ((), (), s32[]{:S(2)}) async-start(), calls=%async_computation.37 | async-start | bytes 1916928 | tf_op jit(solution)/shard_map/psum | solution.py:477
  1342.2 328.7 %all-reduce.32.cloned.1.call-start = ((), (), s32[]{:S(2)}) async-start(), calls=%async_computation.34 | async-start | bytes 22020096 | tf_op jit(solution)/shard_map/psum | solution.py:88
  1351.5 355.0 %reduce-scatter.47.cloned.1.call-start = ((), (), s32[]{:S(2)}) async-start(), calls=%async_computation.31 | async-start | bytes 221184
  (267 other events, 3167.0 us)
Sparse Core Ops, SparseCore 0:
  9.6 29.1 all-gather.5
  180.0 49.8 all-reduce.25
  231.5 31.4 all-gather.7
  264.5 30.6 all-gather.9
  317.9 50.7 all-reduce.27
  407.5 17.5 reduce-scatter.32
  427.3 17.4 reduce-scatter.34
  449.2 51.5 all-reduce.29
  703.8 119.8 all-reduce.35
  893.3 119.2 all-reduce.33
  1066.1 18.7 reduce-scatter.28
  1086.9 17.4 reduce-scatter.30
  1106.7 17.4 reduce-scatter.24
  1126.3 17.4 reduce-scatter.26
  1146.0 17.4 reduce-scatter.36
  1165.6 17.4 reduce-scatter.38
  1198.6 35.2 reduce-scatter.48
  1236.1 34.8 reduce-scatter.44
  1273.3 35.9 reduce-scatter.42
  1312.0 30.1 reduce-scatter.40
  1344.4 28.9 reduce-scatter.50
  1375.9 36.3 all-reduce.37
  1416.0 254.7 all-reduce.31
  1675.8 30.6 reduce-scatter.46
where the time goes:
time: 1730 us
  waiting for transfers between devices  794 us (46%)
  matrix products  413 us (24%)
  blocking collectives  260 us (15%)
  other arithmetic  149 us (9%)
  local copies, waits for them, and re-layouts  83.4 us (5%)
  between operations  24.5 us (1%)
    psum x6, waiting for transfers between devices, row_sums(): return lax.psum(partial_rows, 'tensor')  591 us
    sub x4, matrix products, probabilities(): exponent = mask_table * jnp.exp(masked - row_top)  132 us
    psum x8, blocking collectives, width_sums(): return lax.psum((sum_plain, sum_square), 'tensor')  50 us
    dot_general x12, matrix products, back_dot(): lax.dot_general(left_rows, weight_rows, (((1,), (1,)), ((), ())), preferr...  45.3 us
    all_gather x4, blocking collectives, forward_pass(): lax.all_gather(keys_local, 'context', axis=1, tiled=True)  43.5 us
    unnamed x601, local copies, waits for them, and re-layouts  41.2 us
    all_gather x4, blocking collectives, forward_pass(): lax.all_gather(values_local, 'context', axis=1, tiled=True)  40.4 us
    dot_general x4, matrix products, backward_pass(): jnp.einsum('sqhd,skhd->shqk', grad_heads, value_heads, preferred_element_...  39.7 us
  transfers between devices with their start and end apart: 24, of which 17 were waited for; matrix products, arithmetic and copies ran while one was open for 16% of the time, Pallas kernels for 0%

commit v1 on v0

v1 whole, which is shorter than its diff:
```python
from functools import partial

import jax
import jax.numpy as jnp
from jax import lax
from jax.sharding import PartitionSpec as P

HD = 64
FF = 3072
PIECE = 256


epsilon = 1e-05
span_parts = (1, 2, 4, 6, 8)
dilation_rates = (1, 2, 4, 6, 12)


def pattern_total(query_position, key_position, segmented_offsets, dilated_offsets, token_length):
    tallied_total = jnp.zeros(
        (segmented_offsets.shape[0], query_position.shape[0], key_position.shape[0]), jnp.float32
    )
    for item_number in range(len(span_parts)):
        segmented_span = token_length * span_parts[item_number] // 8
        dilated_stride = dilation_rates[item_number]
        seg_shift = (segmented_offsets[:, item_number] % segmented_span)[:, None, None]
        dilated_phase = (dilated_offsets[:, item_number] % dilated_stride)[:, None, None]
        query_lookup = query_position[None, :, None] + seg_shift
        key_lookup = key_position[None, None, :] + seg_shift
        merged_heads = (
            (query_lookup // segmented_span == key_lookup // segmented_span)
            & (query_lookup % dilated_stride == dilated_phase)
            & (key_lookup % dilated_stride == dilated_phase)
        )
        tallied_total = tallied_total + merged_heads.astype(jnp.float32)
    return tallied_total


def picture_index(starts, token_positions):
    marked = jnp.zeros((starts.shape[0], token_positions.shape[0]), jnp.int32)
    for piece_number in range(starts.shape[1]):
        begin_at = starts[:, piece_number][:, None]
        inside = (token_positions[None, :] >= begin_at) & (
            token_positions[None, :] < begin_at + PIECE
        )
        marked = marked + (piece_number + 1) * inside.astype(jnp.int32)
    return marked


def allowed_keys(query_pic, key_pic, query_position, key_position):
    causal_ok = key_position[None, None, :] <= query_position[None, :, None]
    same_piece = (query_pic[:, :, None] == key_pic[:, None, :]) & (query_pic[:, :, None] > 0)
    return (causal_ok | same_piece).astype(jnp.float32)


def outer_sum(left_rows, right_rows):
    return lax.dot_general(
        left_rows, right_rows, (((0,), (0,)), ((), ())), preferred_element_type=jnp.float32
    )


def back_dot(left_rows, weight_rows):
    return lax.dot_general(
        left_rows, weight_rows, (((1,), (1,)), ((), ())), preferred_element_type=jnp.float32
    )


def norm_rows(values, scale_row):
    mean_row = jnp.mean(values, -1, keepdims=True)
    centered = values - mean_row
    inv_std = lax.rsqrt(jnp.mean(centered * centered, -1, keepdims=True) + epsilon)
    normed = centered * inv_std
    return (normed, inv_std, normed * scale_row)


def norm_back(normed, inv_std, scale_row, grad_rows):
    scaled = grad_rows * scale_row
    mean_plain = jnp.mean(scaled, -1, keepdims=True)
    mean_cross = jnp.mean(scaled * normed, -1, keepdims=True)
    return (inv_std * (scaled - mean_plain - normed * mean_cross), jnp.sum(grad_rows * normed, 0))


def probabilities(query_heads, key_heads, mask_table):
    raw_scores = jnp.einsum(
        "sqhd,skhd->shqk", query_heads, key_heads, preferred_element_type=jnp.float32
    ) * HD ** (-0.5)
    masked = jnp.where(mask_table > 0, raw_scores, -1000000000.0)
    row_top = jnp.max(masked, -1, keepdims=True)
    exponent = mask_table * jnp.exp(masked - row_top)
    row_total = jnp.sum(exponent, -1, keepdims=True)
    return (exponent / row_total, row_top, row_total)


def gather_weight(local_block, shard_dim, tensor_dim):
    ns = lax.axis_size("shard")
    nt = lax.axis_size("tensor")
    stacked = lax.all_gather(local_block, ("shard", "tensor"), axis=0, tiled=False)
    stacked = stacked.reshape((ns, nt) + local_block.shape)
    rank = local_block.ndim
    order = []
    for dim in range(rank):
        if dim == shard_dim:
            order.append(0)
        if dim == tensor_dim:
            order.append(1)
        order.append(dim + 2)
    moved = stacked.transpose(order)
    full_shape = list(local_block.shape)
    full_shape[shard_dim] *= ns
    full_shape[tensor_dim] *= nt
    return moved.reshape(full_shape)


def scatter_weight(full_grad, shard_dim, tensor_dim):
    ns = lax.axis_size("shard")
    nt = lax.axis_size("tensor")
    rank = full_grad.ndim
    split_shape = []
    positions = {}
    for dim in range(rank):
        size = full_grad.shape[dim]
        if dim == shard_dim:
            positions["s"] = len(split_shape)
            split_shape += [ns, size // ns]
        elif dim == tensor_dim:
            positions["t"] = len(split_shape)
            split_shape += [nt, size // nt]
        else:
            split_shape.append(size)
    pieces = full_grad.astype(jnp.bfloat16).reshape(split_shape)
    rest = [d for d in range(len(split_shape)) if d not in (positions["s"], positions["t"])]
    pieces = pieces.transpose([positions["s"], positions["t"]] + rest)
    pieces = pieces.reshape((ns * nt,) + pieces.shape[2:])
    share = lax.psum_scatter(pieces, ("shard", "tensor"), scatter_dimension=0, tiled=False)
    return lax.psum(share, "context").astype(jnp.float32)


def block_of(full, dims_axes):
    starts = [0] * full.ndim
    sizes = list(full.shape)
    for dim, axis in dims_axes:
        count = lax.axis_size(axis)
        sizes[dim] = full.shape[dim] // count
        starts[dim] = lax.axis_index(axis) * sizes[dim]
    return lax.dynamic_slice(full, starts, sizes)


def forward_pass(block_in, starts, tallied_total, weights, query_position, key_position):
    w_qkv, w_out, w_up, w_down, norm_gains, out_biases, head_biases, head_gain, unit_bias, unit_gain = weights
    seq_count, local_len, model_width = block_in.shape
    seq_len = key_position.shape[0]
    row_count = seq_count * local_len
    heads = model_width // HD
    flattened_input = block_in.reshape(row_count, model_width).astype(jnp.float32)
    first_normed, first_inv, first_out = norm_rows(flattened_input, norm_gains[0])
    attn_in = first_out.astype(jnp.bfloat16)
    projected = jnp.einsum("rd,jde->jre", attn_in, w_qkv, preferred_element_type=jnp.float32)
    query_matrix = (projected[0] + head_biases[0]).astype(jnp.bfloat16)
    keys_local = projected[1].astype(jnp.bfloat16).reshape(seq_count, local_len, model_width)
    values_local = (projected[2] + head_biases[1]).astype(jnp.bfloat16).reshape(
        seq_count, local_len, model_width
    )
    key_all = lax.all_gather(keys_local, "context", axis=1, tiled=True)
    value_all = lax.all_gather(values_local, "context", axis=1, tiled=True)
    query_pic = picture_index(starts, query_position)
    key_pic = picture_index(starts, key_position)
    mask_table = (
        allowed_keys(query_pic, key_pic, query_position, key_position)[:, None] * tallied_total[None]
    )
    query_heads = query_matrix.reshape(seq_count, local_len, heads, HD)
    key_heads = key_all.reshape(seq_count, seq_len, heads, HD)
    value_heads = value_all.reshape(seq_count, seq_len, heads, HD)
    weights_soft = probabilities(query_heads, key_heads, mask_table)[0]
    attended = jnp.einsum(
        "shqk,skhd->sqhd",
        weights_soft.astype(jnp.bfloat16),
        value_heads,
        preferred_element_type=jnp.float32,
    ).reshape(row_count, model_width)
    sub_normed, sub_inv, sub_out = norm_rows(attended, head_gain)
    sub_in = sub_out.astype(jnp.bfloat16)
    middle = flattened_input + (
        jnp.dot(sub_in, w_out, preferred_element_type=jnp.float32) + out_biases[0]
    )
    second_normed, second_inv, second_out = norm_rows(middle, norm_gains[1])
    ffn_in = second_out.astype(jnp.bfloat16)
    hidden = jnp.dot(ffn_in, w_up, preferred_element_type=jnp.float32) + unit_bias
    activated = jax.nn.gelu(hidden, approximate=True)
    unit_normed, unit_inv, unit_out = norm_rows(activated, unit_gain)
    ffn_mid = unit_out.astype(jnp.bfloat16)
    layer_out = (
        middle + (jnp.dot(ffn_mid, w_down, preferred_element_type=jnp.float32) + out_biases[1])
    ).astype(jnp.bfloat16)
    kept_state = (
        attn_in,
        first_normed,
        first_inv,
        query_heads,
        key_heads,
        value_heads,
        mask_table,
        sub_normed,
        sub_inv,
        sub_in,
        second_normed,
        second_inv,
        ffn_in,
        hidden,
        unit_normed,
        unit_inv,
        ffn_mid,
    )
    return (kept_state, layer_out.reshape(seq_count, local_len, model_width))


def backward_pass(kept_state, block_grad, weights):
    w_qkv, w_out, w_up, w_down, norm_gains, out_biases, head_biases, head_gain, unit_bias, unit_gain = weights
    (
        attn_in,
        first_normed,
        first_inv,
        query_heads,
        key_heads,
        value_heads,
        mask_table,
        sub_normed,
        sub_inv,
        sub_in,
        second_normed,
        second_inv,
        ffn_in,
        hidden,
        unit_normed,
        unit_inv,
        ffn_mid,
    ) = kept_state
    seq_count, local_len, model_width = block_grad.shape
    row_count = seq_count * local_len
    seq_len = key_heads.shape[1]
    grad_low = block_grad.reshape(row_count, model_width)
    grad_full = grad_low.astype(jnp.float32)
    down_grad = outer_sum(ffn_mid, grad_low)
    last_bias_grad = jnp.sum(grad_full, 0)
    unit_grad = back_dot(grad_low, w_down)
    activated_grad, unit_gain_grad = norm_back(unit_normed, unit_inv, unit_gain, unit_grad)
    gelu_value, gelu_pull = jax.vjp(partial(jax.nn.gelu, approximate=True), hidden)
    hidden_low = gelu_pull(activated_grad)[0].astype(jnp.bfloat16)
    up_grad = outer_sum(ffn_in, hidden_low)
    unit_bias_grad = jnp.sum(hidden_low, 0, dtype=jnp.float32)
    ffn_in_grad = back_dot(hidden_low, w_up)
    middle_part, second_gain_grad = norm_back(second_normed, second_inv, norm_gains[1], ffn_in_grad)
    middle_grad = grad_full + middle_part
    middle_low = middle_grad.astype(jnp.bfloat16)
    out_weight_grad = outer_sum(sub_in, middle_low)
    first_bias_grad = jnp.sum(middle_low, 0, dtype=jnp.float32)
    sub_grad = back_dot(middle_low, w_out)
    attended_grad, head_gain_grad = norm_back(sub_normed, sub_inv, head_gain, sub_grad)
    attended_low = attended_grad.astype(jnp.bfloat16)
    heads = query_heads.shape[2]
    weights_soft, row_top, row_total = probabilities(query_heads, key_heads, mask_table)
    grad_heads = attended_low.reshape(seq_count, local_len, heads, HD)
    soft_grad = jnp.einsum(
        "sqhd,skhd->shqk", grad_heads, value_heads, preferred_element_type=jnp.float32
    )
    inner_sum = jnp.sum(weights_soft * soft_grad, -1, keepdims=True)
    score_low = (weights_soft * (soft_grad - inner_sum)).astype(jnp.bfloat16)
    root_scale = HD ** (-0.5)
    query_low = (
        (
            jnp.einsum("shqk,skhd->sqhd", score_low, key_heads, preferred_element_type=jnp.float32)
            * root_scale
        )
        .astype(jnp.bfloat16)
        .reshape(row_count, -1)
    )
    key_part = (
        jnp.einsum("shqk,sqhd->skhd", score_low, query_heads, preferred_element_type=jnp.float32)
        * root_scale
    )
    value_part = jnp.einsum(
        "shqk,sqhd->skhd",
        weights_soft.astype(jnp.bfloat16),
        grad_heads,
        preferred_element_type=jnp.float32,
    )
    key_low = lax.psum_scatter(
        key_part.reshape(seq_count, seq_len, -1).astype(jnp.bfloat16),
        "context",
        scatter_dimension=1,
        tiled=True,
    ).reshape(row_count, -1)
    value_low = lax.psum_scatter(
        value_part.reshape(seq_count, seq_len, -1).astype(jnp.bfloat16),
        "context",
        scatter_dimension=1,
        tiled=True,
    ).reshape(row_count, -1)
    stacked = jnp.stack([query_low, key_low, value_low])
    qkv_grad = jnp.einsum("rd,jre->jde", attn_in, stacked, preferred_element_type=jnp.float32)
    head_bias_grad = jnp.stack(
        [jnp.sum(query_low, 0, dtype=jnp.float32), jnp.sum(value_low, 0, dtype=jnp.float32)]
    )
    attn_in_grad = jnp.einsum("jre,jde->rd", stacked, w_qkv, preferred_element_type=jnp.float32)
    input_part, first_gain_grad = norm_back(first_normed, first_inv, norm_gains[0], attn_in_grad)
    input_low = (middle_grad + input_part).astype(jnp.bfloat16)
    big_terms = (qkv_grad, out_weight_grad, up_grad, down_grad)
    small_terms = (
        jnp.stack([first_gain_grad, second_gain_grad]),
        head_bias_grad,
        head_gain_grad,
        jnp.stack([first_bias_grad, last_bias_grad]),
        unit_bias_grad,
        unit_gain_grad,
    )
    return (big_terms, small_terms, input_low.reshape(seq_count, local_len, model_width))


def local(
    inputs,
    out_grad,
    picture_starts,
    segment_offsets,
    dilation_offsets,
    norm_gains,
    w_qkv,
    head_biases,
    head_gain,
    w_out,
    out_biases,
    w_up,
    unit_bias,
    unit_gain,
    w_down,
):
    local_seqs, local_len, model_width = inputs.shape
    tensor_count = lax.axis_size("tensor")
    mine = local_seqs // tensor_count
    first_seq = lax.axis_index("tensor") * mine
    block_in = lax.dynamic_slice_in_dim(inputs, first_seq, mine, 0)
    block_grad = lax.dynamic_slice_in_dim(out_grad, first_seq, mine, 0)
    starts = lax.dynamic_slice_in_dim(picture_starts, first_seq, mine, 0)
    seq_len = local_len * lax.axis_size("context")
    query_position = lax.axis_index("context") * local_len + jnp.arange(local_len, dtype=jnp.int32)
    key_position = jnp.arange(seq_len, dtype=jnp.int32)
    all_segments = lax.all_gather(segment_offsets, "tensor", axis=0, tiled=True)
    all_dilations = lax.all_gather(dilation_offsets, "tensor", axis=0, tiled=True)
    tallied_total = pattern_total(
        query_position, key_position, all_segments, all_dilations, seq_len
    )
    f32 = jnp.float32
    weights = (
        gather_weight(w_qkv, 1, 2),
        gather_weight(w_out, 1, 0),
        gather_weight(w_up, 0, 1),
        gather_weight(w_down, 1, 0),
        lax.all_gather(norm_gains, "shard", axis=1, tiled=True).astype(f32),
        lax.all_gather(out_biases, "shard", axis=1, tiled=True).astype(f32),
        gather_weight(head_biases, 2, 1).reshape(2, model_width).astype(f32),
        gather_weight(head_gain, 1, 0).reshape(model_width).astype(f32),
        gather_weight(unit_bias, 1, 0).reshape(-1).astype(f32),
        gather_weight(unit_gain, 1, 0).reshape(-1).astype(f32),
    )
    kept_state, layer_block = forward_pass(
        block_in, starts, tallied_total, weights, query_position, key_position
    )
    layer_out = lax.all_gather(layer_block, "tensor", axis=0, tiled=True)
    big_terms, small_terms, input_block = backward_pass(kept_state, block_grad, weights)
    input_grad = lax.all_gather(input_block, "tensor", axis=0, tiled=True)
    qkv_grad, out_weight_grad, up_grad, down_grad = big_terms
    down_share = scatter_weight(down_grad, 1, 0)
    up_share = scatter_weight(up_grad, 0, 1)
    out_share = scatter_weight(out_weight_grad, 1, 0)
    qkv_share = scatter_weight(qkv_grad, 1, 2)
    packed = jnp.concatenate([term.reshape(-1) for term in small_terms])
    packed = lax.psum(packed, ("shard", "context", "tensor"))
    unpacked = []
    offset = 0
    for term in small_terms:
        unpacked.append(packed[offset : offset + term.size].reshape(term.shape))
        offset += term.size
    gains_full, head_bias_full, head_gain_full, out_bias_full, unit_bias_full, unit_gain_full = unpacked
    heads = model_width // HD
    unit_rows = unit_bias_full.shape[0] // HD
    gains_share = block_of(gains_full, ((1, "shard"),))
    head_bias_share = block_of(head_bias_full.reshape(2, heads, HD), ((1, "tensor"), (2, "shard")))
    head_gain_share = block_of(head_gain_full.reshape(heads, HD), ((0, "tensor"), (1, "shard")))
    out_bias_share = block_of(out_bias_full, ((1, "shard"),))
    unit_bias_share = block_of(unit_bias_full.reshape(unit_rows, HD), ((0, "tensor"), (1, "shard")))
    unit_gain_share = block_of(unit_gain_full.reshape(unit_rows, HD), ((0, "tensor"), (1, "shard")))
    return (
        layer_out,
        input_grad,
        gains_share,
        qkv_share,
        head_bias_share,
        head_gain_share,
        out_share,
        out_bias_share,
        up_share,
        unit_bias_share,
        unit_gain_share,
        down_share,
    )


def solution(mesh):
    placed = (
        P("shard", "context", None),
        P("shard", "context", None),
        P("shard", None),
        P("tensor", None),
        P("tensor", None),
        P(None, "shard"),
        P(None, "shard", "tensor"),
        P(None, "tensor", "shard"),
        P("tensor", "shard"),
        P("tensor", "shard"),
        P(None, "shard"),
        P("shard", "tensor"),
        P("tensor", "shard"),
        P("tensor", "shard"),
        P("tensor", "shard"),
    )
    return jax.shard_map(
        local,
        mesh=mesh,
        in_specs=placed,
        out_specs=(
            P("shard", "context", None),
            P("shard", "context", None),
            P(None, "shard"),
            P(None, "shard", "tensor"),
            P(None, "tensor", "shard"),
            P("tensor", "shard"),
            P("tensor", "shard"),
            P(None, "shard"),
            P("shard", "tensor"),
            P("tensor", "shard"),
            P("tensor", "shard"),
            P("tensor", "shard"),
        ),
        check_vma=False,
    )
```

time: 1730 us -> 1040 us (0.60)
  waiting for transfers between devices: 794 us -> 272 us
  matrix products: 413 us -> 243 us
  local copies, waits for them, and re-layouts: 83.4 us -> 178 us
  blocking collectives: 260 us -> 193 us
  other arithmetic: 149 us -> 130 us
    psum x7 -> x1, waiting for transfers between devices: 594 us -> 38.9 us  [scatter_weight(): return lax.psum(share, 'context').astype(jnp.float32)]
    reduce_scatter x3 -> x4, waiting for transfers between devices: 88.6 us -> 229 us  [scatter_weight(): lax.psum_scatter(pieces, ('shard', 'tensor'), scatter_dimension=0, tiled=...]
    sub x4 -> x1, matrix products: 132 us -> 48 us  [probabilities(): exponent = mask_table * jnp.exp(masked - row_top)]
    reshape x0 -> x18, local copies, waits for them, and re-layouts: none -> 69.7 us  [the longest x6 33 us: gather_weight(): stacked = stacked.reshape((ns, nt) + local_block.shape)]
    all_gather x3 -> x8, waiting for transfers between devices: 51.4 us -> 1.41 us  [the longest x1 1.38 us: local(): input_grad = lax.all_gather(input_block, 'tensor', axis=0, tiled=True)]
    reduce_scatter x4 -> x1, waiting for transfers between devices: 38.6 us -> 0.01 us  [backward_pass(): lax.psum_scatter(value_part.reshape(seq_count, seq_len, -1).astype(jnp.bf...]
    dot_general x16 -> x4, matrix products: 74.1 us -> 38.5 us  [the longest x1 19 us: forward_pass(): jnp.einsum('shqk,skhd->sqhd', weights_soft.astype(jnp.bfloat16), value_he...]
    unnamed x1 -> x0, blocking collectives: 27 us -> none
  transfers between devices with their start and end apart: 24 -> 15, of which waited for: 17 -> 6; matrix products, arithmetic and copies ran while one was open for 16% -> 37% of each run, Pallas kernels for 0% -> 0%
where the time goes in v1:
time: 1040 us; the launch traced here: 1030 us
  waiting for transfers between devices  272 us (26%)
  matrix products  243 us (23%)
  blocking collectives  193 us (19%)
  local copies, waits for them, and re-layouts  178 us (17%)
  other arithmetic  130 us (12%)
  between operations  15.6 us (2%)
    reduce_scatter x4, waiting for transfers between devices, scatter_weight(): lax.psum_scatter(pieces, ('shard', 'tensor'), scatter_dimension=0, tiled=...  229 us
    all_gather x4, blocking collectives, gather_weight(): lax.all_gather(local_block, ('shard', 'tensor'), axis=0, tiled=False)  125 us
    sub x1, matrix products, probabilities(): exponent = mask_table * jnp.exp(masked - row_top)  48 us
    convert_element_type x1, other arithmetic, backward_pass(): score_low = (weights_soft * (soft_grad - inner_sum)).astype(jnp.bfloat16)  41.2 us
    psum x1, blocking collectives, local(): packed = lax.psum(packed, ('shard', 'context', 'tensor'))  40.8 us
    psum x1, waiting for transfers between devices, scatter_weight(): return lax.psum(share, 'context').astype(jnp.float32)  38.9 us
    dot_general x1, matrix products, backward_pass(): jnp.einsum('sqhd,skhd->shqk', grad_heads, value_heads, preferred_element_...  33.1 us
    reshape x6, local copies, waits for them, and re-layouts, gather_weight(): stacked = stacked.reshape((ns, nt) + local_block.shape)  33 us
  transfers between devices with their start and end apart: 15, of which 6 were waited for; matrix products, arithmetic and copies ran while one was open for 37% of the time, Pallas kernels for 0%

profile of v1, /device:TPU:0, one launch (start us, length us, event | category | flops | bytes accessed | tf_op | source)
XLA Modules:
  0.0 1032.9 jit_solution(14236429053673769433)
XLA Ops:
  10.1 34.5 %all-gather.11 = bf16[16,6,8]{2,1,0:T(8,128)(2,1)S(1)} all-gather(bf16[1,6,8]{2,1,0:T(8,128)(2,1)} %bitcast.306), channel_id=4, replica_groups=mesh['shard'=8,'context'=2,'tensor'=2] {'shard','tensor'}, dimensions={0}, use_global_device_ids=true | all-gather | bytes 1632 | tf_op jit(solution)/shard_map/all_gather | solution.py:96
  45.9 8.6 all-gather.8
  55.3 10.5 %all-gather.12 = bf16[8,96,2]{1,2,0:T(2,128)(2,1)S(1)} all-gather(bf16[1,96,2]{1,2,0:T(2,128)(2,1)} %bitcast.310), channel_id=1, replica_groups=mesh['shard'=8,'context'=2,'tensor'=2] {'shard'}, dimensions={0}, use_global_device_ids=true | all-gather | bytes 3456 | tf_op jit(solution)/shard_map/all_gather | solution.py:356
  65.9 4.5 all-gather.9
  70.5 4.5 all-gather.10
  75.2 29.0 %all-gather.1 = bf16[32,6,8]{2,1,0:T(8,128)(2,1)S(1)} all-gather(bf16[2,6,8]{2,1,0:T(8,128)(2,1)S(1)} %copy.151), channel_id=3, replica_groups=mesh['shard'=8,'context'=2,'tensor'=2] {'shard','tensor'}, dimensions={0}, use_global_device_ids=true | all-gather | bytes 3264 | tf_op jit(solution)/shard_map/all_gather | solution.py:96
  104.4 31.5 %all-gather.14 = bf16[16,24,8]{1,2,0:T(8,128)(2,1)S(1)} all-gather(bf16[1,24,8]{1,2,0:T(8,128)(2,1)} %bitcast.307), channel_id=8, replica_groups=mesh['shard'=8,'context'=2,'tensor'=2] {'shard','tensor'}, dimensions={0}, use_global_device_ids=true | all-gather | bytes 6528 | tf_op jit(solution)/shard_map/all_gather | solution.py:96
  136.8 29.6 %all-gather.13 = bf16[16,24,8]{1,2,0:T(8,128)(2,1)S(1)} all-gather(bf16[1,24,8]{1,2,0:T(8,128)(2,1)} %bitcast.308), channel_id=7, replica_groups=mesh['shard'=8,'context'=2,'tensor'=2] {'shard','tensor'}, dimensions={0}, use_global_device_ids=true | all-gather | bytes 6528 | tf_op jit(solution)/shard_map/all_gather | solution.py:96
  189.5 5.5 copy.213
  195.0 4.0 reshape.1920
  199.1 6.3 convolution_bitcast_fusion
  211.0 25.5 %convert_add_fusion = f32[12,512,1024]{2,1,0:T(8,128)} fusion(s32[12,1024]{1,0:T(8,128)S(1)} %copy-done.28, s32[12,512]{1,0:T(8,128)S(1)} %copy-done.34, s32[12,1024]{1,0:T(8,128)S(1)} %copy-done.27, s32[12,512]{1,0:T(8,128)S(1)} %copy-done.33, s32[12,1024]{1,0:T(8,128)S(1)} %copy-done.26, s32[12,512]{1,0:T(8,128)S(1)} %copy-done.31, ...), kind=kLoop, calls=%fused_computation.12 | loop fusion | flops 138412032 | bytes 25608192 | tf_op jit(solution)/shard_map/add | solution.py:34
  240.6 5.9 fusion.149
  256.0 9.3 copy.163
  265.4 6.1 copy.188
  271.5 7.7 reshape.1927
  279.2 7.8 copy.166
  286.9 5.7 copy.189
  295.8 48.0 %fusion.153 = (f32[2,12,512]{2,1,0:T(8,128)S(1)}, f32[2,12,512,1024]{3,2,1,0:T(8,128)}) fusion(f32[12,512,1024]{2,1,0:T(8,128)} %convert_add_fusion, f32[2,512,1024]{2,1,0:T(8,128)} %or_convert_fusion, bf16[2,1024,12,64]{1,3,2,0:T(8,128)(2,1)S(1)} %bitcast.237, f32[2,512,12,64]{1,0,3,2:T(2,128)} %squeeze.36, f32[12,64]{1,0:T(8,128)S(1)} %add.702), kind=kOutput, calls=%fused_computation.344 | convolution fusion | flops 1712849920 | bytes 86035456 | tf_op jit(solution)/shard_map/sub | solution.py:88
  347.0 19.0 %fusion.154 = (f32[2,512]{1,0:T(2,128)S(1)}, f32[2,512,12,64]{1,3,2,0:T(8,128)S(1)}) fusion(bf16[2,1024,12,64]{1,3,2,0:T(8,128)(2,1)S(1)} %bitcast.270, f32[2,12,512,1024]{3,2,1,0:T(8,128)} %get-tuple-element.130, f32[2,12,512]{2,1,0:T(8,128)S(1)} %get-tuple-element.129), kind=kOutput, calls=%fused_computation.345 | convolution fusion | flops 1636563968 | bytes 56676352 | tf_op jit(solution)/shard_map/shqk,skhd->sqhd/dot_general | solution.py:173
  375.1 7.7 fusion.146
  382.8 5.6 multiply_reduce_fusion.3
  388.4 15.8 %multiply_reduce_fusion.1 = (f32[3072]{0:T(1024)}, f32[1024]{0:T(1024)S(1)}, f32[1024]{0:T(1024)S(1)}, f32[1024,3072]{1,0:T(8,128)}) fusion(f32[1024]{0:T(1024)S(1)} %add_rsqrt_fusion, f32[1024]{0:T(1024)S(1)} %broadcast_multiply_fusion.2, f32[1024,3072]{1,0:T(8,128)S(1)} %get-tuple-element.136, f32[3072]{0:T(1024)S(1)} %copy-done.35, ...), kind=kOutput, calls=%fused_computation.23 | convolution fusion | flops 4885310464 | bytes 31510528 | tf_op jit(solution)/shard_map/dot_general | solution.py:62
  404.2 19.7 %convert_reduce_fusion = (f32[3072]{0:T(1024)}, bf16[1024,3072]{1,0:T(8,128)(2,1)}, bf16[1024,3072]{1,0:T(8,128)(2,1)}) fusion(f32[1024]{0:T(1024)S(1)} %broadcast_multiply_fusion, f32[1024]{0:T(1024)S(1)} %broadcast_multiply_fusion.2, f32[1024,3072]{1,0:T(8,128)S(1)} %get-tuple-element.136, f32[3072]{0:T(1024)S(1)} %copy-done.35, ...), kind=kLoop, calls=%fused_computation.24 | loop fusion | flops 103805952 | bytes 37801984 | tf_op jit(solution)/shard_map/reduce_sum | solution.py:248
  423.9 9.9 multiply_reduce_fusion.6
  441.9 19.6 %fusion.38 = bf16[2,12,64,1024]{3,2,1,0:T(8,128)(2,1)} fusion(bf16[2,512,12,64]{1,0,3,2:T(2,128)(2,1)} %reshape.1932, f32[2,12,512,1024]{3,2,1,0:T(8,128)} %get-tuple-element.130, f32[2,12,512]{2,1,0:T(8,128)S(1)} %get-tuple-element.129), kind=kOutput, calls=%fused_computation.92 | convolution fusion | flops 1637351424 | bytes 55099392 | tf_op jit(solution)/shard_map/shqk,sqhd->skhd/dot_general | solution.py:279
  461.5 33.1 %multiply_reduce_fusion = (f32[2,12,512]{2,1,0:T(8,128)S(1)}, f32[2,12,512,1024]{3,2,1,0:T(8,128)}) fusion(f32[2,12,512,1024]{3,2,1,0:T(8,128)} %get-tuple-element.130, f32[2,12,512]{2,1,0:T(8,128)S(1)} %get-tuple-element.129, bf16[2,1024,12,64]{1,3,2,0:T(8,128)(2,1)S(1)} %bitcast.271, bf16[2,512,12,64]{1,0,3,2:T(2,128)(2,1)} %reshape.1932), kind=kOutput, calls=%fused_computation.4 | convolution fusion | flops 1648349184 | bytes 105480192 | tf_op jit(solution)/shard_map/sqhd,skhd->shqk/dot_general | solution.py:261
  494.7 41.2 %multiply_convert_fusion = bf16[2,12,512,1024]{3,2,1,0:T(8,128)(2,1)} fusion(f32[2,12,512,1024]{3,2,1,0:T(8,128)} %get-tuple-element.141, f32[2,12,512]{2,1,0:T(8,128)S(1)} %get-tuple-element.140, f32[2,12,512,1024]{3,2,1,0:T(8,128)} %get-tuple-element.130, f32[2,12,512]{2,1,0:T(8,128)S(1)} %get-tuple-element.129), kind=kLoop, calls=%fused_computation.3 | loop fusion | flops 50331648 | bytes 125927424 | tf_op jit(solution)/shard_map/convert_element_type | solution.py:265
  535.8 14.5 %multiply_convert_fusion.2 = bf16[2,12,64,1024]{3,2,1,0:T(8,128)(2,1)} fusion(bf16[2,12,512,1024]{3,2,1,0:T(8,128)(2,1)} %multiply_convert_fusion, f32[2,512,12,64]{1,0,3,2:T(2,128)S(1)} %copy-done.10, f32[12,64]{1,0:T(8,128)S(1)} %copy-done.37), kind=kOutput, calls=%fused_computation.35 | convolution fusion | flops 1615331328 | bytes 31460352 | tf_op jit(solution)/shard_map/shqk,sqhd->skhd/dot_general | solution.py:276
  551.0 10.2 add_convert_fusion
  561.3 4.4 fusion.50
  574.5 10.3 convolution_convert_fusion.1
  584.7 11.6 %reshape.1942 = bf16[8,96,2,1536]{3,2,1,0:T(2,128)(2,1)} reshape(bf16[768,3072]{1,0:T(8,128)(2,1)} %convolution_convert_fusion.1) | data formatting | bytes 9437184 | tf_op jit(solution)/shard_map/reshape | solution.py:129
  596.4 5.5 copy.179
  603.4 10.2 convolution_convert_fusion
  613.6 6.6 copy.180
  620.2 11.6 %reshape.1946 = bf16[2,1536,8,96]{1,0,3,2:T(2,128)(2,1)} reshape(bf16[3072,768]{0,1:T(8,128)(2,1)} %copy.180) | data formatting | bytes 9437184 | tf_op jit(solution)/shard_map/reshape | solution.py:129
  631.9 5.5 copy.181
  639.2 14.1 %convert_reduce_fusion.5 = (f32[12,64]{1,0:T(8,128)S(1)}, bf16[2,512,12,64]{1,3,2,0:T(8,128)(2,1)}) fusion(bf16[2,1024,12,64]{1,3,2,0:T(8,128)(2,1)S(1)} %bitcast.238, bf16[2,12,512,1024]{3,2,1,0:T(8,128)(2,1)} %multiply_convert_fusion), kind=kOutput, calls=%fused_computation.74 | convolution fusion | flops 1613757696 | bytes 29887488 | tf_op jit(solution)/shard_map/shqk,skhd->sqhd/dot_general | solution.py:269
  664.6 9.7 fusion.20
  674.3 5.6 convert_bitcast_fusion
  679.9 4.3 copy.175
  687.3 4.5 copy.176
  700.6 78.5 %reduce-scatter.15.cloned.1.call-done = bf16[1,96,1536]{2,1,0:T(8,128)(2,1)} async-done(((bf16[16,96,1536]{2,1,0:T(8,128)(2,1)}), bf16[1,96,1536]{2,1,0:T(8,128)(2,1)}) %reduce-scatter.15.cloned.1.call-update) | async-done | bytes 294928 | tf_op jit(solution)/shard_map/reduce_scatter | solution.py:133
  779.1 78.5 %reduce-scatter.17.cloned.1.call-done = bf16[1,1536,96]{1,2,0:T(8,128)(2,1)} async-done(((bf16[16,1536,96]{1,2,0:T(8,128)(2,1)}), bf16[1,1536,96]{1,2,0:T(8,128)(2,1)}) %reduce-scatter.17.cloned.1.call-update) | async-done | bytes 294928 | tf_op jit(solution)/shard_map/reduce_scatter | solution.py:133
  857.6 71.2 %reduce-scatter.11.cloned.1.call-done = bf16[1,3,96,384]{3,2,1,0:T(8,128)(2,1)} async-done(((bf16[16,3,96,384]{3,2,1,0:T(8,128)(2,1)}), bf16[1,3,96,384]{3,2,1,0:T(8,128)(2,1)}) %reduce-scatter.11.cloned.1.call-update) | async-done | bytes 221200 | tf_op jit(solution)/shard_map/reduce_scatter | solution.py:133
  928.8 40.8 %psum.35 = f32[11520]{0:T(1024)S(1)} all-reduce(f32[11520]{0:T(1024)S(1)} %constant_dynamic-update-slice_fusion), channel_id=1, replica_groups=mesh['shard'=8,'context'=2,'tensor'=2] {'shard','context','tensor'}, use_global_device_ids=true, to_apply=%region_30.31 | all-reduce | flops 11520 | bytes 92160 | tf_op jit(solution)/shard_map/psum | solution.py:374
  975.4 38.9 %all-reduce.3.cloned.1.call-done = (bf16[3,96,384]{2,1,0:T(8,128)(2,1)}, bf16[384,96]{0,1:T(8,128)(2,1)}, bf16[96,1536]{1,0:T(8,128)(2,1)}, bf16[1536,96]{0,1:T(8,128)(2,1)}) async-done(((bf16[3,96,384]{2,1,0:T(8,128)(2,1)}, bf16[384,96]{0,1:T(8,128)(2,1)}, bf16[96,1536]{1,0:T(8,128)(2,1)}, bf16[1536,96]{0,1:T(8,128)(2,1)}), (bf16[3,96,384]{2,1,0:T(8,128)(2,1)}, bf16[384,96]{0,1:T(8,128)(2,1)}, ...) | async-done | bytes 884752 | tf_op jit(solution)/shard_map/psum | solution.py:134
  (340 shorter events, 124.9 us)
Async XLA Ops:
  7.2 160.0 %copy-start = (s32[4,2]{0,1:T(2,128)S(1)}, s32[4,2]{0,1:T(2,128)}, u32[]{:S(2)}) copy-start(s32[4,2]{0,1:T(2,128)} %param.17) | copy-start | bytes 100
  7.2 164.0 %copy-start.8 = (bf16[4,512,768]{2,1,0:T(8,128)(2,1)S(1)}, bf16[4,512,768]{2,1,0:T(8,128)(2,1)}, u32[]{:S(2)}) copy-start(bf16[4,512,768]{2,1,0:T(8,128)(2,1)} %param.15) | copy-start | bytes 9437188
  7.2 182.3 %all-gather.32.cloned.1.call-start = ((), (), s32[]{:S(2)}) async-start(), calls=%async_computation.16 | async-start | bytes 3760128 | tf_op jit(solution)/shard_map/all_gather | solution.py:96
  7.9 228.6 %all-gather.34.cloned.1.call-start = ((), (), s32[]{:S(2)}) async-start(), calls=%async_computation.17 | async-start | bytes 1253376 | tf_op jit(solution)/shard_map/all_gather | solution.py:96
  8.7 247.3 %all-gather.36.cloned.1.call-start = ((), (), s32[]{:S(2)}) async-start(), calls=%async_computation.18 | async-start | bytes 5013504 | tf_op jit(solution)/shard_map/all_gather | solution.py:96
  9.4 262.1 %all-gather.38.cloned.1.call-start = ((), (), s32[]{:S(2)}) async-start(), calls=%async_computation.19 | async-start | bytes 5013504 | tf_op jit(solution)/shard_map/all_gather | solution.py:96
  10.0 282.6 %all-gather.26.cloned.1.call-start = ((), (), s32[]{:S(2)}) async-start(), calls=%async_computation.7 | async-start | bytes 4718592 | tf_op jit(solution)/shard_map/all_gather | solution.py:162
  104.3 191.6 %copy-start.36 = (f32[12,64]{1,0:T(8,128)}, f32[12,64]{1,0:T(8,128)S(1)}, u32[]{:S(2)}) copy-start(f32[12,64]{1,0:T(8,128)S(1)} %add.702) | copy-start | bytes 9220
  167.9 17.5 %copy-start.50 = (f32[768]{0:T(1024)}, f32[768]{0:T(1024)S(1)}, u32[]{:S(2)}) copy-start(f32[768]{0:T(1024)S(1)} %get-tuple-element.75) | copy-start | bytes 9220
  210.5 133.3 %all-gather.24.cloned.1.call-start = ((), (), s32[]{:S(2)}) async-start(), calls=%async_computation.6 | async-start | bytes 4718592 | tf_op jit(solution)/shard_map/all_gather | solution.py:163
  255.9 403.3 %reduce-scatter.9.cloned.1.call-start = ((), (), s32[]{:S(2)}) async-start(), calls=%async_computation.10 | async-start | bytes 4718592 | tf_op jit(solution)/shard_map/reduce_scatter | solution.py:291
  295.8 48.0 %copy-start.6 = (bf16[2,1024,768]{1,2,0:T(8,128)(2,1)}, bf16[2,1024,768]{1,2,0:T(8,128)(2,1)S(1)}, u32[]{:S(2)}) copy-start(bf16[2,1024,768]{1,2,0:T(8,128)(2,1)S(1)} %copy.158) | copy-start | bytes 9437188
  347.0 19.1 %copy-start.19 = (bf16[2,1024,768]{1,2,0:T(8,128)(2,1)}, bf16[2,1024,768]{1,2,0:T(8,128)(2,1)S(1)}, u32[]{:S(2)}) copy-start(bf16[2,1024,768]{1,2,0:T(8,128)(2,1)S(1)} %copy.153) | copy-start | bytes 9437188
  366.1 72.5 %copy-start.44 = (f32[1,4,2,128]{3,1,2,0:T(4,128)}, f32[1,4,2,128]{3,1,2,0:T(4,128)S(1)}, u32[]{:S(2)}) copy-start(f32[1,4,2,128]{3,1,2,0:T(4,128)S(1)} %copy.193) | copy-start | bytes 12292
  368.9 69.7 %copy-start.46 = (f32[1,4,2,128]{3,1,2,0:T(4,128)}, f32[1,4,2,128]{3,1,2,0:T(4,128)S(1)}, u32[]{:S(2)}) copy-start(f32[1,4,2,128]{3,1,2,0:T(4,128)S(1)} %copy.191) | copy-start | bytes 12292
  369.7 68.9 %copy-start.2 = (f32[96,8,2,512]{3,1,2,0:T(8,128)}, f32[96,8,2,512]{3,1,2,0:T(8,128)S(1)}, u32[]{:S(2)}) copy-start(f32[96,8,2,512]{3,1,2,0:T(8,128)S(1)} %copy.192) | copy-start | bytes 9437188
  374.2 59.6 %copy-start.11 = (f32[1024,768]{1,0:T(8,128)}, f32[1024,768]{1,0:T(8,128)S(1)}, u32[]{:S(2)}) copy-start(f32[1024,768]{1,0:T(8,128)S(1)} %get-tuple-element.134) | copy-start | bytes 9437188
  374.2 59.5 %copy-start.52 = (f32[1024]{0:T(1024)}, f32[1024]{0:T(1024)S(1)}, u32[]{:S(2)}) copy-start(f32[1024]{0:T(1024)S(1)} %broadcast_multiply_fusion.9) | copy-start | bytes 12292
  374.8 59.0 %copy-start.64 = (f32[1024]{0:T(1024)}, f32[1024]{0:T(1024)S(1)}, u32[]{:S(2)}) copy-start(f32[1024]{0:T(1024)S(1)} %add_rsqrt_fusion.1) | copy-start | bytes 12292
  382.8 5.6 copy-start.14
  382.8 5.6 copy-start.42
  441.9 19.6 %copy-start.20 = (bf16[2,1024,768]{1,2,0:T(8,128)(2,1)S(1)}, bf16[2,1024,768]{1,2,0:T(8,128)(2,1)}, u32[]{:S(2)}) copy-start(bf16[2,1024,768]{1,2,0:T(8,128)(2,1)} %copy-done.19) | copy-start | bytes 9437188
  494.6 167.3 %reduce-scatter.7.cloned.1.call-start = ((), (), s32[]{:S(2)}) async-start(), calls=%async_computation.9 | async-start | bytes 4718592 | tf_op jit(solution)/shard_map/reduce_scatter | solution.py:285
  494.7 41.2 %copy-start.10 = (f32[2,512,12,64]{1,0,3,2:T(2,128)S(1)}, f32[2,512,12,64]{1,0,3,2:T(2,128)}, u32[]{:S(2)}) copy-start(f32[2,512,12,64]{1,0,3,2:T(2,128)} %squeeze.36) | copy-start | bytes 9437188
  494.7 41.2 %copy-start.37 = (f32[12,64]{1,0:T(8,128)S(1)}, f32[12,64]{1,0:T(8,128)}, u32[]{:S(2)}) copy-start(f32[12,64]{1,0:T(8,128)} %copy-done.36) | copy-start | bytes 9220
  550.4 147.5 %all-gather.28.cloned.1.call-start = ((), (), s32[]{:S(2)}) async-start(), calls=%async_computation.8 | async-start | bytes 4718592 | tf_op jit(solution)/shard_map/all_gather | solution.py:365
  551.0 10.3 copy-start.3
  551.0 10.3 copy-start.45
  551.0 10.3 copy-start.47
  551.0 10.3 copy-start.49
  561.2 139.3 %reduce-scatter.13.cloned.1.call-start = ((), (), s32[]{:S(2)}) async-start(), calls=%async_computation.13 | async-start | bytes 1253376 | tf_op jit(solution)/shard_map/reduce_scatter | solution.py:133
  568.2 6.3 copy-start.12
  568.2 6.3 copy-start.53
  568.2 6.3 copy-start.60
  568.2 6.3 copy-start.65
  574.4 204.7 %reduce-scatter.15.cloned.1.call-start = ((), (), s32[]{:S(2)}) async-start(), calls=%async_computation.14 | async-start | bytes 5013504 | tf_op jit(solution)/shard_map/reduce_scatter | solution.py:133
  601.9 255.6 %reduce-scatter.17.cloned.1.call-start = ((), (), s32[]{:S(2)}) async-start(), calls=%async_computation.15 | async-start | bytes 5013504 | tf_op jit(solution)/shard_map/reduce_scatter | solution.py:133
  637.4 291.4 %reduce-scatter.11.cloned.1.call-start = ((), (), s32[]{:S(2)}) async-start(), calls=%async_computation.12 | async-start | bytes 3760128 | tf_op jit(solution)/shard_map/reduce_scatter | solution.py:133
  639.2 25.3 %copy-start.66 = (f32[1,4,2,128]{3,1,2,0:T(4,128)}, f32[1,4,2,128]{3,1,2,0:T(4,128)S(1)}, u32[]{:S(2)}) copy-start(f32[1,4,2,128]{3,1,2,0:T(4,128)S(1)} %copy.190) | copy-start | bytes 12292
  659.2 5.3 copy-start.9
  659.2 5.3 copy-start.51
  664.5 9.8 copy-start.21
  664.6 9.8 copy-start.22
  664.6 9.8 copy-start.23
  691.8 283.6 %all-gather.30.cloned.1.call-start = ((), (), s32[]{:S(2)}) async-start(), calls=%async_computation.11 | async-start | bytes 4718592 | tf_op jit(solution)/shard_map/all_gather | solution.py:367
  697.6 231.2 %copy-start.70 = (f32[3072]{0:T(1024)S(1)}, f32[3072]{0:T(1024)}, u32[]{:S(2)}) copy-start(f32[3072]{0:T(1024)} %get-tuple-element.60) | copy-start | bytes 36868
  697.6 316.7 %all-reduce.3.cloned.1.call-start = ((), (), s32[]{:S(2)}) async-start(), calls=%async_computation.20 | async-start | bytes 1769472 | tf_op jit(solution)/shard_map/psum | solution.py:134
  697.9 323.4 %copy-start.17 = (bf16[4,512,768]{2,1,0:T(8,128)(2,1)S(1)}, bf16[4,512,768]{2,1,0:T(8,128)(2,1)}, u32[]{:S(2)}) copy-start(bf16[4,512,768]{2,1,0:T(8,128)(2,1)} %all-gather.28.cloned.1.call-done) | copy-start | bytes 9437188
  (46 other events, 92.2 us)
Sparse Core Ops, SparseCore 0:
  10.3 49.9 all-gather.31
  62.3 35.7 all-gather.33
  100.5 52.9 all-gather.35
  155.6 51.6 all-gather.37
  210.7 43.5 all-gather.25
  256.1 44.4 all-gather.23
  494.7 41.9 reduce-scatter.8
  550.5 41.8 reduce-scatter.6
  594.0 44.9 all-gather.27
  642.4 58.1 reduce-scatter.12
  704.4 74.5 reduce-scatter.14
  782.8 74.7 reduce-scatter.16
  861.4 67.2 reduce-scatter.10
  930.7 44.6 all-gather.29
  977.8 36.4 all-reduce.2

commit v2 on v1

--- a/solution.py
+++ b/solution.py
@@ -90,24 +90,77 @@
     return (exponent / row_total, row_top, row_total)
 
 
-def gather_weight(local_block, shard_dim, tensor_dim):
-    ns = lax.axis_size("shard")
-    nt = lax.axis_size("tensor")
-    stacked = lax.all_gather(local_block, ("shard", "tensor"), axis=0, tiled=False)
-    stacked = stacked.reshape((ns, nt) + local_block.shape)
-    rank = local_block.ndim
+def assemble(stacked, shard_dim, tensor_dim):
+    ns, nt = stacked.shape[0], stacked.shape[1]
+    if shard_dim is None:
+        stacked = stacked[:1]
+    if tensor_dim is None:
+        stacked = stacked[:, :1]
+    local_shape = stacked.shape[2:]
     order = []
-    for dim in range(rank):
+    for dim in range(len(local_shape)):
         if dim == shard_dim:
             order.append(0)
         if dim == tensor_dim:
             order.append(1)
         order.append(dim + 2)
+    if shard_dim is None:
+        order = [0] + order
+    if tensor_dim is None:
+        order = [1] + order
     moved = stacked.transpose(order)
-    full_shape = list(local_block.shape)
-    full_shape[shard_dim] *= ns
-    full_shape[tensor_dim] *= nt
+    full_shape = list(local_shape)
+    if shard_dim is not None:
+        full_shape[shard_dim] *= ns
+    if tensor_dim is not None:
+        full_shape[tensor_dim] *= nt
     return moved.reshape(full_shape)
+
+
+def gather_weight(local_block, shard_dim, tensor_dim):
+    ns = lax.axis_size("shard")
+    nt = lax.axis_size("tensor")
+    stacked = lax.all_gather(local_block, ("shard", "tensor"), axis=0, tiled=False)
+    return assemble(stacked.reshape((ns, nt) + local_block.shape), shard_dim, tensor_dim)
+
+
+def gather_packed(blocks):
+    ns = lax.axis_size("shard")
+    nt = lax.axis_size("tensor")
+    flat = jnp.concatenate([block.reshape(-1) for block, _, _ in blocks])
+    padded = -flat.size % 2048
+    flat = jnp.pad(flat, (0, padded)).reshape(-1, 128)
+    stacked = lax.all_gather(flat, ("shard", "tensor"), axis=0, tiled=False).reshape(ns, nt, -1)
+    pieces = []
+    offset = 0
+    for block, shard_dim, tensor_dim in blocks:
+        part = stacked[:, :, offset : offset + block.size].reshape((ns, nt) + block.shape)
+        pieces.append(assemble(part, shard_dim, tensor_dim))
+        offset += block.size
+    return pieces
+
+
+def pair_gather(block, axis_name, dim):
+    if lax.axis_size(axis_name) != 2:
+        return lax.all_gather(block, axis_name, axis=dim, tiled=True)
+    other = lax.ppermute(block, axis_name, perm=[(0, 1), (1, 0)])
+    first = lax.axis_index(axis_name) == 0
+    return jnp.where(
+        first, jnp.concatenate([block, other], dim), jnp.concatenate([other, block], dim)
+    )
+
+
+def pair_reduce(full, axis_name, dim):
+    if lax.axis_size(axis_name) != 2:
+        return lax.psum_scatter(
+            full.astype(jnp.bfloat16), axis_name, scatter_dimension=dim, tiled=True
+        ).astype(jnp.float32)
+    half = full.shape[dim] // 2
+    me = lax.axis_index(axis_name)
+    kept = lax.dynamic_slice_in_dim(full, me * half, half, dim)
+    sent = lax.dynamic_slice_in_dim(full, (1 - me) * half, half, dim).astype(jnp.bfloat16)
+    received = lax.ppermute(sent, axis_name, perm=[(0, 1), (1, 0)])
+    return kept + received.astype(jnp.float32)
 
 
 def scatter_weight(full_grad, shard_dim, tensor_dim):
@@ -159,8 +212,8 @@
     values_local = (projected[2] + head_biases[1]).astype(jnp.bfloat16).reshape(
         seq_count, local_len, model_width
     )
-    key_all = lax.all_gather(keys_local, "context", axis=1, tiled=True)
-    value_all = lax.all_gather(values_local, "context", axis=1, tiled=True)
+    key_all = pair_gather(keys_local, "context", 1)
+    value_all = pair_gather(values_local, "context", 1)
     query_pic = picture_index(starts, query_position)
     key_pic = picture_index(starts, key_position)
     mask_table = (
@@ -282,18 +335,16 @@
         grad_heads,
         preferred_element_type=jnp.float32,
     )
-    key_low = lax.psum_scatter(
-        key_part.reshape(seq_count, seq_len, -1).astype(jnp.bfloat16),
-        "context",
-        scatter_dimension=1,
-        tiled=True,
-    ).reshape(row_count, -1)
-    value_low = lax.psum_scatter(
-        value_part.reshape(seq_count, seq_len, -1).astype(jnp.bfloat16),
-        "context",
-        scatter_dimension=1,
-        tiled=True,
-    ).reshape(row_count, -1)
+    key_low = (
+        pair_reduce(key_part.reshape(seq_count, seq_len, -1), "context", 1)
+        .astype(jnp.bfloat16)
+        .reshape(row_count, -1)
+    )
+    value_low = (
+        pair_reduce(value_part.reshape(seq_count, seq_len, -1), "context", 1)
+        .astype(jnp.bfloat16)
+        .reshape(row_count, -1)
+    )
     stacked = jnp.stack([query_low, key_low, value_low])
     qkv_grad = jnp.einsum("rd,jre->jde", attn_in, stacked, preferred_element_type=jnp.float32)
     head_bias_grad = jnp.stack(
@@ -341,30 +392,60 @@
     seq_len = local_len * lax.axis_size("context")
     query_position = lax.axis_index("context") * local_len + jnp.arange(local_len, dtype=jnp.int32)
     key_position = jnp.arange(seq_len, dtype=jnp.int32)
-    all_segments = lax.all_gather(segment_offsets, "tensor", axis=0, tiled=True)
-    all_dilations = lax.all_gather(dilation_offsets, "tensor", axis=0, tiled=True)
+    spans = jnp.array([seq_len * part // 8 for part in span_parts], jnp.int32)
+    rates = jnp.array(dilation_rates, jnp.int32)
+    segment_kept = segment_offsets % spans
+    dilation_kept = dilation_offsets % rates
+    offset_digits = jnp.concatenate(
+        [segment_kept // 32, segment_kept % 32, dilation_kept], 1
+    ).astype(jnp.bfloat16)
+    f32 = jnp.float32
+    (
+        w_qkv_full,
+        gains_full,
+        out_bias_full,
+        head_bias_full,
+        head_gain_full,
+        unit_bias_full,
+        unit_gain_full,
+        digits_full,
+    ) = gather_packed(
+        (
+            (w_qkv, 1, 2),
+            (norm_gains, 1, None),
+            (out_biases, 1, None),
+            (head_biases, 2, 1),
+            (head_gain, 1, 0),
+            (unit_bias, 1, 0),
+            (unit_gain, 1, 0),
+            (offset_digits, None, 0),
+        )
+    )
+    patterns = len(span_parts)
+    digits_full = digits_full.astype(jnp.int32)
+    all_segments = digits_full[:, :patterns] * 32 + digits_full[:, patterns : 2 * patterns]
+    all_dilations = digits_full[:, 2 * patterns :]
     tallied_total = pattern_total(
         query_position, key_position, all_segments, all_dilations, seq_len
     )
-    f32 = jnp.float32
     weights = (
-        gather_weight(w_qkv, 1, 2),
+        w_qkv_full,
         gather_weight(w_out, 1, 0),
         gather_weight(w_up, 0, 1),
         gather_weight(w_down, 1, 0),
-        lax.all_gather(norm_gains, "shard", axis=1, tiled=True).astype(f32),
-        lax.all_gather(out_biases, "shard", axis=1, tiled=True).astype(f32),
-        gather_weight(head_biases, 2, 1).reshape(2, model_width).astype(f32),
-        gather_weight(head_gain, 1, 0).reshape(model_width).astype(f32),
-        gather_weight(unit_bias, 1, 0).reshape(-1).astype(f32),
-        gather_weight(unit_gain, 1, 0).reshape(-1).astype(f32),
+        gains_full.astype(f32),
+        out_bias_full.astype(f32),
+        head_bias_full.reshape(2, model_width).astype(f32),
+        head_gain_full.reshape(model_width).astype(f32),
+        unit_bias_full.reshape(-1).astype(f32),
+        unit_gain_full.reshape(-1).astype(f32),
     )
     kept_state, layer_block = forward_pass(
         block_in, starts, tallied_total, weights, query_position, key_position
     )
-    layer_out = lax.all_gather(layer_block, "tensor", axis=0, tiled=True)
+    layer_out = pair_gather(layer_block, "tensor", 0)
     big_terms, small_terms, input_block = backward_pass(kept_state, block_grad, weights)
-    input_grad = lax.all_gather(input_block, "tensor", axis=0, tiled=True)
+    input_grad = pair_gather(input_block, "tensor", 0)
     qkv_grad, out_weight_grad, up_grad, down_grad = big_terms
     down_share = scatter_weight(down_grad, 1, 0)
     up_share = scatter_weight(up_grad, 0, 1)

time: 1040 us -> 899 us (0.86)
  waiting for transfers between devices: 272 us -> 150 us
  blocking collectives: 193 us -> 109 us
  local copies, waits for them, and re-layouts: 178 us -> 227 us
  other arithmetic: 130 us -> 148 us
    reduce_scatter x4, waiting for transfers between devices: 229 us -> 46.6 us  [scatter_weight(): lax.psum_scatter(pieces, ('shard', 'tensor'), scatter_dimension=0, tiled=...]
    all_gather x8 -> x0, blocking collectives: 153 us -> none  [the longest x4 125 us: gather_weight(): lax.all_gather(local_block, ('shard', 'tensor'), axis=0, tiled=False)]
    psum x1, blocking collectives: 40.8 us -> 109 us  [local(): packed = lax.psum(packed, ('shard', 'context', 'tensor'))]
    all_gather x4 -> x1, waiting for transfers between devices: 1.38 us -> 43.6 us  [gather_packed(): lax.all_gather(flat, ('shard', 'tensor'), axis=0, tiled=False)]
    convert_element_type x10 -> x20, local copies, waits for them, and re-layouts: 3.22 us -> 25.1 us  [the longest x3 11.9 us: forward_pass(): projected[1].astype(jnp.bfloat16).reshape(seq_count, local_len, model_width)]
    reshape x7 -> x17, local copies, waits for them, and re-layouts: 37 us -> 57.1 us  [the longest x5 29.4 us: gather_weight(): stacked.reshape((ns, nt) + local_block.shape)]
    ppermute x0 -> x6, waiting for transfers between devices: none -> 15.9 us  [the longest x2 11.3 us: pair_reduce(): received = lax.ppermute(sent, axis_name, perm=[(0, 1), (1, 0)])]
    all_gather x4 -> x3, waiting for transfers between devices: 0.02 us -> 14.1 us  [gather_weight(): lax.all_gather(local_block, ('shard', 'tensor'), axis=0, tiled=False)]
  transfers between devices with their start and end apart: 15 -> 15, of which waited for: 6 -> 6; matrix products, arithmetic and copies ran while one was open for 37% -> 50% of each run, Pallas kernels for 0% -> 0%
where the time goes in v2:
time: 899 us; the launch traced here: 893 us
  matrix products  238 us (26%)
  local copies, waits for them, and re-layouts  227 us (25%)
  waiting for transfers between devices  150 us (17%)
  other arithmetic  148 us (16%)
  blocking collectives  109 us (12%)
  between operations  15.3 us (2%)
    psum x1, blocking collectives, local(): packed = lax.psum(packed, ('shard', 'context', 'tensor'))  109 us
    sub x1, matrix products, probabilities(): exponent = mask_table * jnp.exp(masked - row_top)  49.2 us
    reduce_scatter x4, waiting for transfers between devices, scatter_weight(): lax.psum_scatter(pieces, ('shard', 'tensor'), scatter_dimension=0, tiled=...  46.6 us
    all_gather x1, waiting for transfers between devices, gather_packed(): lax.all_gather(flat, ('shard', 'tensor'), axis=0, tiled=False)  43.6 us
    convert_element_type x1, other arithmetic, backward_pass(): score_low = (weights_soft * (soft_grad - inner_sum)).astype(jnp.bfloat16)  41 us
    dot_general x1, matrix products, backward_pass(): jnp.einsum('sqhd,skhd->shqk', grad_heads, value_heads, preferred_element_...  32.3 us
    reshape x5, local copies, waits for them, and re-layouts, gather_weight(): stacked.reshape((ns, nt) + local_block.shape)  29.4 us
    dot_general x3, matrix products, back_dot(): lax.dot_general(left_rows, weight_rows, (((1,), (1,)), ((), ())), preferr...  28.8 us
  transfers between devices with their start and end apart: 15, of which 6 were waited for; matrix products, arithmetic and copies ran while one was open for 50% of the time, Pallas kernels for 0%

profile of v2, /device:TPU:0, one launch (start us, length us, event | category | flops | bytes accessed | tf_op | source)
XLA Modules:
  0.0 892.9 jit_solution(6100905170781371759)
XLA Ops:
  35.9 14.1 %all-gather.10.cloned.1.call-done = bf16[6144,96]{0,1:T(8,128)(2,1)} async-done(((bf16[384,96]{0,1:T(8,128)(2,1)}), bf16[6144,96]{0,1:T(8,128)(2,1)}) %all-gather.10.cloned.1.call-update) | async-done | bytes 1179664 | tf_op jit(solution)/shard_map/all_gather | solution.py:123
  56.1 43.6 %all-gather.8.cloned.1.call-done = bf16[16,880,128]{2,1,0:T(8,128)(2,1)} async-done(((bf16[1,880,128]{2,1,0:T(8,128)(2,1)}), bf16[16,880,128]{2,1,0:T(8,128)(2,1)}) %all-gather.8.cloned.1.call-update) | async-done | bytes 3604496 | tf_op jit(solution)/shard_map/all_gather | solution.py:133
  99.7 6.7 reshape.1994
  114.1 6.3 slice.232
  127.9 7.4 reshape.2046
  135.3 7.3 copy.172
  142.6 9.1 %reshape.1996 = bf16[3,768,768]{2,1,0:T(8,128)(2,1)} reshape(bf16[3,8,96,2,384]{4,3,2,1,0:T(2,128)(2,1)} %copy.172) | data formatting | bytes 7077888 | tf_op jit(solution)/shard_map/reshape | solution.py:117
  153.1 6.0 convolution_bitcast_fusion
  181.5 4.6 squeeze.39
  186.1 4.1 copy.182
  197.3 25.7 %convert_add_fusion = f32[12,512,1024]{2,1,0:T(8,128)} fusion(s32[12,1024]{1,0:T(8,128)S(1)} %add_select_fusion.1, s32[12,512]{1,0:T(8,128)S(1)} %copy-done.34, s32[12,1024]{1,0:T(8,128)S(1)} %add_select_fusion.3, s32[12,512]{1,0:T(8,128)S(1)} %copy-done.33, s32[12,1024]{1,0:T(8,128)S(1)} %add_select_fusion.5, s32[12,512]{1,0:T(8,128)S(1)} %copy-done.31, ...), kind=kLoop, calls=%fused_computation.12 | loop fusion | flops 138412032 | bytes 25608192 | tf_op jit(solution)/shard_map/add | solution.py:34
  223.0 4.6 collective-permute-done.1
  229.1 49.2 %fusion.162 = (f32[2,12,512]{2,1,0:T(8,128)S(1)}, f32[2,12,512,1024]{3,2,1,0:T(8,128)}) fusion(f32[12,512,1024]{2,1,0:T(8,128)} %convert_add_fusion, f32[2,512,1024]{2,1,0:T(8,128)} %or_convert_fusion, bf16[2,512,12,64]{1,3,2,0:T(8,128)(2,1)} %bitcast.230, bf16[2,512,12,64]{1,3,2,0:T(8,128)(2,1)} %copy.182, pred[]{:T(512)S(6)} %eq.264, ...), kind=kOutput, calls=%fused_computation.387 | convolution fusion | flops 1727005696 | bytes 86035456 | tf_op jit(solution)/shard_map/sub | solution.py:88
  281.1 20.6 %fusion.163 = (f32[2,512]{1,0:T(2,128)S(1)}, f32[2,512,12,64]{1,3,2,0:T(8,128)S(1)}) fusion(f32[2,12,512,1024]{3,2,1,0:T(8,128)} %get-tuple-element.139, f32[2,12,512]{2,1,0:T(8,128)S(1)} %get-tuple-element.138, bf16[2,512,12,64]{1,3,2,0:T(8,128)(2,1)} %bitcast.232, bf16[2,512,12,64]{1,3,2,0:T(8,128)(2,1)} %fusion.37, pred[]{:T(512)S(6)} %eq.264), kind=kOutput, calls=%fused_computation.388 | convolution fusion | flops 1650719744 | bytes 56676352 | tf_op jit(solution)/shard_map/shqk,skhd->sqhd/dot_general | solution.py:226
  312.8 9.6 %copy.188 = bf16[8,2,96,1536]{3,1,2,0:T(2,128)(2,1)} copy(bf16[8,2,96,1536]{3,2,1,0:T(8,128)(2,1)} %bitcast.220) | data formatting | bytes 9437184 | tf_op jit(solution)/shard_map/reshape | solution.py:124
  322.4 5.7 copy.223
  328.1 7.3 reshape.2003
  335.4 7.7 copy.193
  343.1 5.9 copy.224
  349.0 7.4 fusion.154
  356.5 5.8 multiply_reduce_fusion.3
  362.3 15.8 %multiply_reduce_fusion.1 = (f32[3072]{0:T(1024)}, f32[1024]{0:T(1024)S(1)}, f32[1024]{0:T(1024)S(1)}, f32[1024,3072]{1,0:T(8,128)}) fusion(f32[1024]{0:T(1024)S(1)} %add_rsqrt_fusion, f32[1024]{0:T(1024)S(1)} %broadcast_multiply_fusion.3, f32[1024,3072]{1,0:T(8,128)S(1)} %get-tuple-element.145, f32[3072]{0:T(1024)S(1)} %copy-done.35, ...), kind=kOutput, calls=%fused_computation.23 | convolution fusion | flops 4885310464 | bytes 31510528 | tf_op jit(solution)/shard_map/dot_general | solution.py:62
  378.0 19.3 %convert_reduce_fusion = (f32[3072]{0:T(1024)}, bf16[1024,3072]{1,0:T(8,128)(2,1)}, bf16[1024,3072]{1,0:T(8,128)(2,1)}) fusion(f32[1024]{0:T(1024)S(1)} %broadcast_multiply_fusion.1, f32[1024]{0:T(1024)S(1)} %broadcast_multiply_fusion.3, f32[1024,3072]{1,0:T(8,128)S(1)} %get-tuple-element.145, f32[3072]{0:T(1024)S(1)} %copy-done.35, ...), kind=kLoop, calls=%fused_computation.24 | loop fusion | flops 103805952 | bytes 37801984 | tf_op jit(solution)/shard_map/reduce_sum | solution.py:301
  397.3 10.3 %multiply_reduce_fusion.6 = (f32[768]{0:T(1024)}, f32[1024]{0:T(1024)S(1)}, f32[1024]{0:T(1024)S(1)}, f32[1024,768]{1,0:T(8,128)S(1)}) fusion(f32[1024,768]{1,0:T(8,128)S(1)} %copy-done.13, f32[1024]{0:T(1024)S(1)} %add_rsqrt_fusion.1, f32[1024]{0:T(1024)S(1)} %broadcast_multiply_fusion.10, f32[768]{0:T(1024)S(1)} %copy-done.61, ...), kind=kOutput, calls=%fused_computation.79 | convolution fusion | flops 4838126592 | bytes 17324032 | tf_op jit(solution)/shard_map/dot_general | solution.py:62
  420.1 19.8 %fusion.14 = f32[2,12,64,1024]{3,2,1,0:T(8,128)} fusion(bf16[2,512,12,64]{1,0,3,2:T(2,128)(2,1)S(1)} %reshape.2008, f32[2,12,512,1024]{3,2,1,0:T(8,128)} %get-tuple-element.139, f32[2,12,512]{2,1,0:T(8,128)S(1)} %get-tuple-element.138), kind=kOutput, calls=%fused_computation.28 | convolution fusion | flops 1635778560 | bytes 58245120 | tf_op jit(solution)/shard_map/shqk,sqhd->skhd/dot_general | solution.py:332
  439.9 32.3 %multiply_reduce_fusion = (f32[2,12,512]{2,1,0:T(8,128)S(1)}, f32[2,12,512,1024]{3,2,1,0:T(8,128)}) fusion(f32[2,12,512,1024]{3,2,1,0:T(8,128)} %get-tuple-element.139, f32[2,12,512]{2,1,0:T(8,128)S(1)} %get-tuple-element.138, bf16[2,512,12,64]{1,3,2,0:T(8,128)(2,1)S(1)} %bitcast.233, bf16[2,512,12,64]{1,3,2,0:T(8,128)(2,1)} %fusion.37, pred[]{:T(512)S(6)} %eq.264, ...), kind=kOutput, calls=%fused_computation.4 | convolution fusion | flops 1662504960 | bytes 105480192 | tf_op jit(solution)/shard_map/sqhd,skhd->shqk/dot_general | solution.py:314
  480.3 41.0 %multiply_convert_fusion = bf16[2,12,512,1024]{3,2,1,0:T(8,128)(2,1)} fusion(f32[2,12,512,1024]{3,2,1,0:T(8,128)} %get-tuple-element.150, f32[2,12,512]{2,1,0:T(8,128)S(1)} %get-tuple-element.149, f32[2,12,512,1024]{3,2,1,0:T(8,128)} %get-tuple-element.139, f32[2,12,512]{2,1,0:T(8,128)S(1)} %get-tuple-element.138), kind=kLoop, calls=%fused_computation.3 | loop fusion | flops 50331648 | bytes 125927424 | tf_op jit(solution)/shard_map/convert_element_type | solution.py:318
  521.4 10.6 %broadcast_multiply_fusion = f32[2,12,64,1024]{3,2,1,0:T(8,128)S(1)} fusion(bf16[2,12,512,1024]{3,2,1,0:T(8,128)(2,1)} %multiply_convert_fusion, f32[2,512,12,64]{1,0,3,2:T(2,128)S(1)} %copy-done.10, f32[12,64]{1,0:T(8,128)S(1)} %copy-done.37), kind=kOutput, calls=%fused_computation.84 | convolution fusion | flops 1613758464 | bytes 34606080 | tf_op jit(solution)/shard_map/shqk,sqhd->skhd/dot_general | solution.py:329
  536.2 12.8 %convert_reduce_fusion.5 = (f32[12,64]{1,0:T(8,128)}, bf16[2,512,12,64]{1,3,2,0:T(8,128)(2,1)S(1)}) fusion(bf16[2,12,512,1024]{3,2,1,0:T(8,128)(2,1)} %multiply_convert_fusion, bf16[2,512,12,64]{1,3,2,0:T(8,128)(2,1)S(1)} %bitcast.231, bf16[2,512,12,64]{1,3,2,0:T(8,128)(2,1)S(1)} %copy-done.22, pred[]{:T(512)S(6)} %eq.264), kind=kOutput, calls=%fused_computation.78 | convolution fusion | flops 1627913472 | bytes 29887488 | tf_op jit(solution)/shard_map/shqk,skhd->sqhd/dot_general | solution.py:322
  557.7 11.3 %collective-permute-done.3 = bf16[2,512,768]{1,2,0:T(8,128)(2,1)} collective-permute-done((bf16[2,512,768]{1,2,0:T(8,128)(2,1)}, bf16[2,512,768]{1,2,0:T(8,128)(2,1)}, u32[]{:S(2)}, u32[]{:S(2)}) %collective-permute-start.3) | collective-permute-done | bytes 1572896 | tf_op jit(solution)/shard_map/ppermute | solution.py:162
  569.0 4.1 add_convert_fusion.1
  575.9 9.7 %fusion.20 = (f32[768]{0:T(1024)}, f32[1024]{0:T(1024)}, f32[1024]{0:T(1024)}, bf16[1024,768]{1,0:T(8,128)(2,1)S(1)}, f32[1024,768,1]{1,0,2:T(8,128)}) fusion(f32[1024]{0:T(1024)S(1)} %bitcast.254, f32[1024]{0:T(1024)S(1)} %bitcast.256, bf16[4,512,768]{2,1,0:T(8,128)(2,1)S(1)} %copy-done.8, s32[]{:T(128)S(6)} %select_n.328, f32[768]{0:T(1024)S(1)} %copy-done.46, ...), kind=kOutput, calls=%fused_computation.49 | convolution fusion | flops 3637245184 | bytes 14571524 | tf_op jit(solution)/shard_map/jre,jde->rd/dot_general | solution.py:353
  585.6 5.7 convert_bitcast_fusion
  591.3 4.3 copy.203
  598.7 4.4 copy.204
  605.0 10.2 %convolution_convert_fusion.1 = bf16[768,3072]{1,0:T(8,128)(2,1)} fusion(bf16[1024,3072]{1,0:T(8,128)(2,1)} %get-tuple-element.91, f32[1024,768]{1,0:T(8,128)S(1)} %copy-done.14, f32[768]{0:T(1024)S(1)} %copy-done.62, f32[1024]{0:T(1024)S(1)} %copy-done.65, f32[1024]{0:T(1024)S(1)} %copy-done.48), kind=kOutput, calls=%fused_computation.37 | convolution fusion | flops 4837343232 | bytes 14167040 | tf_op jit(solution)/shard_map/dot_general | solution.py:56
  615.1 11.7 %reshape.2020 = bf16[8,96,2,1536]{3,2,1,0:T(2,128)(2,1)} reshape(bf16[768,3072]{1,0:T(8,128)(2,1)} %convolution_convert_fusion.1) | data formatting | bytes 9437184 | tf_op jit(solution)/shard_map/reshape | solution.py:182
  626.8 5.7 copy.207
  633.9 10.0 %convolution_convert_fusion = bf16[3072,768]{1,0:T(8,128)(2,1)} fusion(bf16[1024,3072]{1,0:T(8,128)(2,1)} %get-tuple-element.100, bf16[1024,768]{1,0:T(8,128)(2,1)S(1)} %bitcast.214), kind=kOutput, calls=%fused_computation.36 | convolution fusion | flops 4834197504 | bytes 12582912 | tf_op jit(solution)/shard_map/dot_general | solution.py:56
  644.0 6.6 copy.208
  650.6 11.6 %reshape.2024 = bf16[2,1536,8,96]{1,0,3,2:T(2,128)(2,1)} reshape(bf16[3072,768]{0,1:T(8,128)(2,1)} %copy.208) | data formatting | bytes 9437184 | tf_op jit(solution)/shard_map/reshape | solution.py:182
  662.2 5.5 copy.209
  668.7 10.2 %add_convert_fusion.2 = bf16[1024,768]{1,0:T(8,128)(2,1)} fusion(f32[1024,768]{1,0:T(8,128)} %copy-done.12, bf16[1024,3072]{1,0:T(8,128)(2,1)} %get-tuple-element.100, bf16[3072,768]{0,1:T(8,128)(2,1)} %bitcast.222, f32[768]{0:T(1024)S(1)} %add.756), kind=kOutput, calls=%fused_computation.91 | convolution fusion | flops 4834197504 | bytes 15731712 | tf_op jit(solution)/shard_map/dot_general | solution.py:244
  679.0 4.1 fusion.34
  685.3 108.7 %psum.35 = f32[11520]{0:T(1024)S(1)} all-reduce(f32[11520]{0:T(1024)S(1)} %constant_dynamic-update-slice_fusion), channel_id=1, replica_groups=mesh['shard'=8,'context'=2,'tensor'=2] {'shard','context','tensor'}, use_global_device_ids=true, to_apply=%region_28.30 | all-reduce | flops 11520 | bytes 92160 | tf_op jit(solution)/shard_map/psum | solution.py:455
  794.2 46.6 %reduce-scatter.11.cloned.1.call-done = bf16[1,1536,96]{1,2,0:T(8,128)(2,1)} async-done(((bf16[16,1536,96]{1,2,0:T(8,128)(2,1)}), bf16[1,1536,96]{1,2,0:T(8,128)(2,1)}) %reduce-scatter.11.cloned.1.call-update) | async-done | bytes 294928 | tf_op jit(solution)/shard_map/reduce_scatter | solution.py:186
  845.2 4.4 maximum_select_fusion.2
  851.5 27.7 %all-reduce.4.cloned.1.call-done = (bf16[3,96,384]{2,1,0:T(8,128)(2,1)}, bf16[384,96]{0,1:T(8,128)(2,1)}, bf16[96,1536]{1,0:T(8,128)(2,1)}, bf16[1536,96]{0,1:T(8,128)(2,1)}) async-done(((bf16[3,96,384]{2,1,0:T(8,128)(2,1)}, bf16[384,96]{0,1:T(8,128)(2,1)}, bf16[96,1536]{1,0:T(8,128)(2,1)}, bf16[1536,96]{0,1:T(8,128)(2,1)}), (bf16[3,96,384]{2,1,0:T(8,128)(2,1)}, bf16[384,96]{0,1:T(8,128)(2,1)}, ...) | async-done | bytes 884752 | tf_op jit(solution)/shard_map/psum | solution.py:187
  (372 shorter events, 154.9 us)
Async XLA Ops:
  7.2 15.2 %copy-start = (s32[4,2]{0,1:T(2,128)S(1)}, s32[4,2]{0,1:T(2,128)}, u32[]{:S(2)}) copy-start(s32[4,2]{0,1:T(2,128)} %param.21) | copy-start | bytes 100
  7.2 19.2 %copy-start.7 = (bf16[4,512,768]{2,1,0:T(8,128)(2,1)S(1)}, bf16[4,512,768]{2,1,0:T(8,128)(2,1)}, u32[]{:S(2)}) copy-start(bf16[4,512,768]{2,1,0:T(8,128)(2,1)} %param.19) | copy-start | bytes 9437188
  7.2 42.8 %all-gather.10.cloned.1.call-start = ((), (), s32[]{:S(2)}) async-start(), calls=%async_computation.9 | async-start | bytes 1253376 | tf_op jit(solution)/shard_map/all_gather | solution.py:123
  7.9 91.7 %all-gather.8.cloned.1.call-start = ((), (), s32[]{:S(2)}) async-start(), calls=%async_computation.4 | async-start | bytes 3829760 | tf_op jit(solution)/shard_map/all_gather | solution.py:133
  21.0 291.8 %all-gather.12.cloned.1.call-start = ((), (), s32[]{:S(2)}) async-start(), calls=%async_computation.10 | async-start | bytes 5013504 | tf_op jit(solution)/shard_map/all_gather | solution.py:123
  21.7 306.4 %all-gather.14.cloned.1.call-start = ((), (), s32[]{:S(2)}) async-start(), calls=%async_computation.11 | async-start | bytes 5013504 | tf_op jit(solution)/shard_map/all_gather | solution.py:123
  22.3 771.9 %reduce-scatter.7.cloned.1.call-start = ((), (), s32[]{:S(2)}) async-start(), calls=%async_computation.6 | async-start | bytes 1253376 | tf_op jit(solution)/shard_map/reduce_scatter | solution.py:186
  108.9 13.2 %copy-start.69 = (s32[12]{0:T(128)}, s32[12]{0:T(128)S(1)}, u32[]{:S(2)}) copy-start(s32[12]{0:T(128)S(1)} %get-tuple-element.163) | copy-start | bytes 148
  108.9 13.1 %copy-start.70 = (s32[12]{0:T(128)}, s32[12]{0:T(128)S(1)}, u32[]{:S(2)}) copy-start(s32[12]{0:T(128)S(1)} %get-tuple-element.159) | copy-start | bytes 148
  108.9 12.9 %copy-start.71 = (s32[12]{0:T(128)}, s32[12]{0:T(128)S(1)}, u32[]{:S(2)}) copy-start(s32[12]{0:T(128)S(1)} %get-tuple-element.161) | copy-start | bytes 148
  109.0 12.8 %copy-start.72 = (s32[12]{0:T(128)}, s32[12]{0:T(128)S(1)}, u32[]{:S(2)}) copy-start(s32[12]{0:T(128)S(1)} %get-tuple-element.157) | copy-start | bytes 148
  114.0 8.2 slice-start
  142.6 9.1 %copy-start.56 = (bf16[8,2,192]{2,1,0:T(2,128)(2,1)S(1)}, bf16[8,2,192]{2,1,0:T(2,128)(2,1)}, u32[]{:S(2)}) copy-start(bf16[8,2,192]{2,1,0:T(2,128)(2,1)} %get-tuple-element.104) | copy-start | bytes 18436
  142.6 9.2 %copy-start.55 = (bf16[8,2,192]{2,1,0:T(2,128)(2,1)S(1)}, bf16[8,2,192]{2,1,0:T(2,128)(2,1)}, u32[]{:S(2)}) copy-start(bf16[8,2,192]{2,1,0:T(2,128)(2,1)} %get-tuple-element.106) | copy-start | bytes 18436
  152.6 6.6 copy-start.45
  178.9 50.2 %copy-start.36 = (f32[12,64]{1,0:T(8,128)}, f32[12,64]{1,0:T(8,128)S(1)}, u32[]{:S(2)}) copy-start(f32[12,64]{1,0:T(8,128)S(1)} %add.742) | copy-start | bytes 9220
  181.5 10.2 %copy-start.68 = (f32[768]{0:T(1024)S(1)}, f32[768]{0:T(1024)}, u32[]{:S(2)}) copy-start(f32[768]{0:T(1024)} %add.683) | copy-start | bytes 9220
  186.1 43.1 %copy-start.9 = (f32[2,512,12,64]{1,0,3,2:T(2,128)}, f32[2,512,12,64]{1,0,3,2:T(2,128)S(1)}, u32[]{:S(2)}) copy-start(f32[2,512,12,64]{1,0,3,2:T(2,128)S(1)} %squeeze.39) | copy-start | bytes 9437188
  190.2 37.5 %collective-permute-start.1 = (bf16[2,512,768]{1,0,2:T(2,128)(2,1)}, bf16[2,512,768]{1,0,2:T(2,128)(2,1)S(1)}, u32[]{:S(2)}, u32[]{:S(2)}) collective-permute-start(bf16[2,512,768]{1,0,2:T(2,128)(2,1)} %convert_element_type.328), channel_id=1, source_target_pairs={{0,2},{2,0},{1,3},{3,1},{4,6},{6,4},{5,7},{7,5},{8,10},{10,8},{9,1... | collective-permute-start | bytes 4718600 | tf_op jit(solution)/shard_map/ppermute | solution.py:146
  194.9 83.4 %collective-permute-start = (bf16[2,512,768]{1,0,2:T(2,128)(2,1)}, bf16[2,512,768]{1,0,2:T(2,128)(2,1)}, u32[]{:S(2)}, u32[]{:S(2)}) collective-permute-start(bf16[2,512,768]{1,0,2:T(2,128)(2,1)} %add_convert_fusion.3), channel_id=1, source_target_pairs={{0,2},{2,0},{1,3},{3,1},{4,6},{6,4},{5,7},{7,5},{8,10},{10,8},{9,1... | collective-permute-start | bytes 4718600 | tf_op jit(solution)/shard_map/ppermute | solution.py:146
  310.6 97.0 %copy-start.47 = (f32[1024]{0:T(1024)}, f32[1024]{0:T(1024)S(1)}, u32[]{:S(2)}) copy-start(f32[1024]{0:T(1024)S(1)} %broadcast_multiply_fusion.10) | copy-start | bytes 12292
  312.8 94.8 %copy-start.64 = (f32[1024]{0:T(1024)}, f32[1024]{0:T(1024)S(1)}, u32[]{:S(2)}) copy-start(f32[1024]{0:T(1024)S(1)} %add_rsqrt_fusion.1) | copy-start | bytes 12292
  420.1 19.8 %copy-start.24 = (bf16[2,512,768]{1,2,0:T(8,128)(2,1)S(1)}, bf16[2,512,768]{1,2,0:T(8,128)(2,1)}, u32[]{:S(2)}) copy-start(bf16[2,512,768]{1,2,0:T(8,128)(2,1)} %copy.178) | copy-start | bytes 4718596
  475.5 318.7 %reduce-scatter.5.cloned.1.call-start = ((), (), s32[]{:S(2)}) async-start(), calls=%async_computation.5 | async-start | bytes 3760128 | tf_op jit(solution)/shard_map/reduce_scatter | solution.py:186
  478.8 74.5 %collective-permute-start.4 = (bf16[2,512,768]{1,2,0:T(8,128)(2,1)}, bf16[2,512,768]{1,2,0:T(8,128)(2,1)}, u32[]{:S(2)}, u32[]{:S(2)}) collective-permute-start(bf16[2,512,768]{1,2,0:T(8,128)(2,1)} %dynamic-slice_convert_fusion), channel_id=1, source_target_pairs={{0,2},{2,0},{1,3},{3,1},{4,6},{6,4},{5,7},{7,5},{8,10},{10,8},{9,1... | collective-permute-start | bytes 4718600 | tf_op jit(solution)/shard_map/ppermute | solution.py:162
  480.3 41.0 %copy-start.10 = (f32[2,512,12,64]{1,0,3,2:T(2,128)S(1)}, f32[2,512,12,64]{1,0,3,2:T(2,128)}, u32[]{:S(2)}) copy-start(f32[2,512,12,64]{1,0,3,2:T(2,128)} %copy-done.9) | copy-start | bytes 9437188
  480.3 41.0 %copy-start.37 = (f32[12,64]{1,0:T(8,128)S(1)}, f32[12,64]{1,0:T(8,128)}, u32[]{:S(2)}) copy-start(f32[12,64]{1,0:T(8,128)} %copy-done.36) | copy-start | bytes 9220
  532.0 17.0 %copy-start.6 = (f32[2,12,64,1024]{3,2,1,0:T(8,128)}, f32[2,12,64,1024]{3,2,1,0:T(8,128)S(1)}, u32[]{:S(2)}) copy-start(f32[2,12,64,1024]{3,2,1,0:T(8,128)S(1)} %broadcast_multiply_fusion) | copy-start | bytes 18874372
  533.5 35.5 %collective-permute-start.3 = (bf16[2,512,768]{1,2,0:T(8,128)(2,1)}, bf16[2,512,768]{1,2,0:T(8,128)(2,1)}, u32[]{:S(2)}, u32[]{:S(2)}) collective-permute-start(bf16[2,512,768]{1,2,0:T(8,128)(2,1)} %dynamic-slice_convert_fusion.1), channel_id=1, source_target_pairs={{0,2},{2,0},{1,3},{3,1},{4,6},{6,4},{5,7},{7,5},{8,10},{10,8},{9,1... | collective-permute-start | bytes 4718600 | tf_op jit(solution)/shard_map/ppermute | solution.py:162
  569.0 6.8 copy-start.59
  569.0 6.8 copy-start.60
  575.8 9.8 %copy-start.25 = (bf16[1,1024,768]{2,1,0:T(8,128)(2,1)S(1)}, bf16[1,1024,768]{2,1,0:T(8,128)(2,1)}, u32[]{:S(2)}) copy-start(bf16[1,1024,768]{2,1,0:T(8,128)(2,1)} %copy.201) | copy-start | bytes 4718596
  575.8 9.8 %copy-start.26 = (bf16[2,512,768]{2,1,0:T(8,128)(2,1)S(1)}, bf16[2,512,768]{2,1,0:T(8,128)(2,1)}, u32[]{:S(2)}) copy-start(bf16[2,512,768]{2,1,0:T(8,128)(2,1)} %copy.200) | copy-start | bytes 4718596
  575.9 9.8 %copy-start.27 = (bf16[2,512,768]{2,1,0:T(8,128)(2,1)S(1)}, bf16[2,512,768]{2,1,0:T(8,128)(2,1)}, u32[]{:S(2)}) copy-start(bf16[2,512,768]{2,1,0:T(8,128)(2,1)} %copy.198) | copy-start | bytes 4718596
  603.1 191.1 %reduce-scatter.9.cloned.1.call-start = ((), (), s32[]{:S(2)}) async-start(), calls=%async_computation.7 | async-start | bytes 5013504 | tf_op jit(solution)/shard_map/reduce_scatter | solution.py:186
  632.6 208.2 %reduce-scatter.11.cloned.1.call-start = ((), (), s32[]{:S(2)}) async-start(), calls=%async_computation.8 | async-start | bytes 5013504 | tf_op jit(solution)/shard_map/reduce_scatter | solution.py:186
  667.8 211.3 %all-reduce.4.cloned.1.call-start = ((), (), s32[]{:S(2)}) async-start(), calls=%async_computation.12 | async-start | bytes 1769472 | tf_op jit(solution)/shard_map/psum | solution.py:187
  668.6 10.2 %copy-start.74 = (f32[12,64]{1,0:T(8,128)S(1)}, f32[12,64]{1,0:T(8,128)}, u32[]{:S(2)}) copy-start(f32[12,64]{1,0:T(8,128)} %get-tuple-element.152) | copy-start | bytes 9220
  668.6 10.3 %copy-start.76 = (f32[768]{0:T(1024)S(1)}, f32[768]{0:T(1024)}, u32[]{:S(2)}) copy-start(f32[768]{0:T(1024)} %get-tuple-element.66) | copy-start | bytes 9220
  668.6 10.3 %copy-start.78 = (f32[1024]{0:T(1024)S(1)}, f32[1024]{0:T(1024)}, u32[]{:S(2)}) copy-start(f32[1024]{0:T(1024)} %get-tuple-element.67) | copy-start | bytes 12292
  668.6 10.4 %copy-start.77 = (f32[1024]{0:T(1024)S(1)}, f32[1024]{0:T(1024)}, u32[]{:S(2)}) copy-start(f32[1024]{0:T(1024)} %get-tuple-element.71) | copy-start | bytes 12292
  668.6 10.4 %copy-start.5 = (f32[1024,768]{1,0:T(8,128)S(1)}, f32[1024,768]{1,0:T(8,128)}, u32[]{:S(2)}) copy-start(f32[1024,768]{1,0:T(8,128)} %copy-done.4) | copy-start | bytes 9437188
  678.8 166.4 %collective-permute-start.2 = (bf16[2,512,768]{2,1,0:T(8,128)(2,1)}, bf16[2,512,768]{2,1,0:T(8,128)(2,1)}, u32[]{:S(2)}, u32[]{:S(2)}) collective-permute-start(bf16[2,512,768]{2,1,0:T(8,128)(2,1)} %bitcast.24), channel_id=1, source_target_pairs={{0,1},{1,0},{2,3},{3,2},{4,5},{5,4},{6,7},{7,6},{8,9},{9,8},{10,11... | collective-permute-start | bytes 4718600 | tf_op jit(solution)/shard_map/ppermute | solution.py:146
  679.0 6.2 copy-start.63
  679.0 6.3 copy-start.43
  679.0 6.3 copy-start.73
  683.2 166.4 %collective-permute-start.5 = (bf16[2,512,768]{2,1,0:T(8,128)(2,1)}, bf16[2,512,768]{2,1,0:T(8,128)(2,1)S(1)}, u32[]{:S(2)}, u32[]{:S(2)}) collective-permute-start(bf16[2,512,768]{2,1,0:T(8,128)(2,1)} %bitcast.216), channel_id=1, source_target_pairs={{0,1},{1,0},{2,3},{3,2},{4,5},{5,4},{6,7},{7,6},{8,9},{9,8},{10,11... | collective-permute-start | bytes 4718600 | tf_op jit(solution)/shard_map/ppermute | solution.py:146
  845.2 40.9 %copy-start.1 = (s32[4,2]{0,1:T(2,128)S(1)}, s32[4,2]{0,1:T(2,128)}, u32[]{:S(2)}) copy-start(s32[4,2]{0,1:T(2,128)} %param.21) | copy-start | bytes 100
  (47 other events, 139.3 us)
Sparse Core Ops, SparseCore 0:
  10.1 39.8 all-gather.9
  52.8 46.8 all-gather.7
  102.0 51.8 all-gather.11
  156.0 51.6 all-gather.13
  475.6 56.6 reduce-scatter.6
  603.2 65.3 reduce-scatter.4
  672.4 90.3 reduce-scatter.8
  766.7 74.0 reduce-scatter.10
  843.3 35.7 all-reduce.3

commit v3 on v2

--- a/solution.py
+++ b/solution.py
@@ -163,14 +163,19 @@
     return kept + received.astype(jnp.float32)
 
 
-def scatter_weight(full_grad, shard_dim, tensor_dim):
+def pair_sum(share, axis_name):
+    if lax.axis_size(axis_name) != 2:
+        return lax.psum(share, axis_name).astype(jnp.float32)
+    received = lax.ppermute(share, axis_name, perm=[(0, 1), (1, 0)])
+    return share.astype(jnp.float32) + received.astype(jnp.float32)
+
+
+def disassemble(full, shard_dim, tensor_dim):
     ns = lax.axis_size("shard")
     nt = lax.axis_size("tensor")
-    rank = full_grad.ndim
     split_shape = []
     positions = {}
-    for dim in range(rank):
-        size = full_grad.shape[dim]
+    for dim, size in enumerate(full.shape):
         if dim == shard_dim:
             positions["s"] = len(split_shape)
             split_shape += [ns, size // ns]
@@ -179,22 +184,48 @@
             split_shape += [nt, size // nt]
         else:
             split_shape.append(size)
-    pieces = full_grad.astype(jnp.bfloat16).reshape(split_shape)
-    rest = [d for d in range(len(split_shape)) if d not in (positions["s"], positions["t"])]
-    pieces = pieces.transpose([positions["s"], positions["t"]] + rest)
-    pieces = pieces.reshape((ns * nt,) + pieces.shape[2:])
-    share = lax.psum_scatter(pieces, ("shard", "tensor"), scatter_dimension=0, tiled=False)
-    return lax.psum(share, "context").astype(jnp.float32)
-
-
-def block_of(full, dims_axes):
-    starts = [0] * full.ndim
-    sizes = list(full.shape)
-    for dim, axis in dims_axes:
-        count = lax.axis_size(axis)
-        sizes[dim] = full.shape[dim] // count
-        starts[dim] = lax.axis_index(axis) * sizes[dim]
-    return lax.dynamic_slice(full, starts, sizes)
+    pieces = full.reshape(split_shape)
+    lead = [positions[key] for key in ("s", "t") if key in positions]
+    rest = [d for d in range(len(split_shape)) if d not in lead]
+    pieces = pieces.transpose(lead + rest)
+    if "s" not in positions:
+        pieces = jnp.broadcast_to(pieces[None], (ns,) + pieces.shape)
+    if "t" not in positions:
+        pieces = jnp.broadcast_to(pieces[:, None], (ns, nt) + pieces.shape[1:])
+    return pieces.reshape(ns * nt, -1)
+
+
+def pack_rows(terms):
+    rows = jnp.concatenate(
+        [disassemble(full.astype(jnp.bfloat16), shard_dim, tensor_dim) for full, shard_dim, tensor_dim in terms],
+        1,
+    )
+    width = rows.shape[1]
+    return jnp.pad(rows, ((0, 0), (0, -width % 1024))).reshape(rows.shape[0], -1, 128)
+
+
+def scatter_rows(rows):
+    return lax.psum_scatter(rows, ("shard", "tensor"), scatter_dimension=0, tiled=False)
+
+
+def unpack_share(share, terms):
+    total = pair_sum(share, "context").reshape(-1)
+    pieces = []
+    offset = 0
+    ns = lax.axis_size("shard")
+    nt = lax.axis_size("tensor")
+    for full, shard_dim, tensor_dim in terms:
+        local_shape = list(full.shape)
+        if shard_dim is not None:
+            local_shape[shard_dim] //= ns
+        if tensor_dim is not None:
+            local_shape[tensor_dim] //= nt
+        count = 1
+        for size in local_shape:
+            count *= size
+        pieces.append(total[offset : offset + count].reshape(local_shape))
+        offset += count
+    return pieces
 
 
 def forward_pass(block_in, starts, tallied_total, weights, query_position, key_position):
@@ -308,6 +339,13 @@
     sub_grad = back_dot(middle_low, w_out)
     attended_grad, head_gain_grad = norm_back(sub_normed, sub_inv, head_gain, sub_grad)
     attended_low = attended_grad.astype(jnp.bfloat16)
+    early_terms = ((down_grad, 1, 0), (up_grad, 0, 1))
+    middle_terms = ((out_weight_grad, 1, 0),)
+    early_rows, middle_rows, attended_low = lax.optimization_barrier(
+        (pack_rows(early_terms), pack_rows(middle_terms), attended_low)
+    )
+    early_share = scatter_rows(early_rows)
+    middle_share = scatter_rows(middle_rows)
     heads = query_heads.shape[2]
     weights_soft, row_top, row_total = probabilities(query_heads, key_heads, mask_table)
     grad_heads = attended_low.reshape(seq_count, local_len, heads, HD)
@@ -346,6 +384,7 @@
         .reshape(row_count, -1)
     )
     stacked = jnp.stack([query_low, key_low, value_low])
+    early_share, stacked = lax.optimization_barrier((early_share, stacked))
     qkv_grad = jnp.einsum("rd,jre->jde", attn_in, stacked, preferred_element_type=jnp.float32)
     head_bias_grad = jnp.stack(
         [jnp.sum(query_low, 0, dtype=jnp.float32), jnp.sum(value_low, 0, dtype=jnp.float32)]
@@ -353,16 +392,24 @@
     attn_in_grad = jnp.einsum("jre,jde->rd", stacked, w_qkv, preferred_element_type=jnp.float32)
     input_part, first_gain_grad = norm_back(first_normed, first_inv, norm_gains[0], attn_in_grad)
     input_low = (middle_grad + input_part).astype(jnp.bfloat16)
-    big_terms = (qkv_grad, out_weight_grad, up_grad, down_grad)
-    small_terms = (
-        jnp.stack([first_gain_grad, second_gain_grad]),
-        head_bias_grad,
-        head_gain_grad,
-        jnp.stack([first_bias_grad, last_bias_grad]),
-        unit_bias_grad,
-        unit_gain_grad,
-    )
-    return (big_terms, small_terms, input_low.reshape(seq_count, local_len, model_width))
+    heads = model_width // HD
+    unit_rows = unit_bias_grad.shape[0] // HD
+    late_terms = (
+        (qkv_grad, 1, 2),
+        (jnp.stack([first_gain_grad, second_gain_grad]), 1, None),
+        (jnp.stack([first_bias_grad, last_bias_grad]), 1, None),
+        (head_bias_grad.reshape(2, heads, HD), 2, 1),
+        (head_gain_grad.reshape(heads, HD), 1, 0),
+        (unit_bias_grad.reshape(unit_rows, HD), 1, 0),
+        (unit_gain_grad.reshape(unit_rows, HD), 1, 0),
+    )
+    late_share = scatter_rows(pack_rows(late_terms))
+    grad_shares = (
+        unpack_share(early_share, early_terms)
+        + unpack_share(middle_share, middle_terms)
+        + unpack_share(late_share, late_terms)
+    )
+    return (grad_shares, input_low.reshape(seq_count, local_len, model_width))
 
 
 def local(
@@ -428,6 +475,7 @@
     tallied_total = pattern_total(
         query_position, key_position, all_segments, all_dilations, seq_len
     )
+    w_out, w_up, w_down, w_qkv_full = lax.optimization_barrier((w_out, w_up, w_down, w_qkv_full))
     weights = (
         w_qkv_full,
         gather_weight(w_out, 1, 0),
@@ -444,29 +492,20 @@
         block_in, starts, tallied_total, weights, query_position, key_position
     )
     layer_out = pair_gather(layer_block, "tensor", 0)
-    big_terms, small_terms, input_block = backward_pass(kept_state, block_grad, weights)
+    grad_shares, input_block = backward_pass(kept_state, block_grad, weights)
     input_grad = pair_gather(input_block, "tensor", 0)
-    qkv_grad, out_weight_grad, up_grad, down_grad = big_terms
-    down_share = scatter_weight(down_grad, 1, 0)
-    up_share = scatter_weight(up_grad, 0, 1)
-    out_share = scatter_weight(out_weight_grad, 1, 0)
-    qkv_share = scatter_weight(qkv_grad, 1, 2)
-    packed = jnp.concatenate([term.reshape(-1) for term in small_terms])
-    packed = lax.psum(packed, ("shard", "context", "tensor"))
-    unpacked = []
-    offset = 0
-    for term in small_terms:
-        unpacked.append(packed[offset : offset + term.size].reshape(term.shape))
-        offset += term.size
-    gains_full, head_bias_full, head_gain_full, out_bias_full, unit_bias_full, unit_gain_full = unpacked
-    heads = model_width // HD
-    unit_rows = unit_bias_full.shape[0] // HD
-    gains_share = block_of(gains_full, ((1, "shard"),))
-    head_bias_share = block_of(head_bias_full.reshape(2, heads, HD), ((1, "tensor"), (2, "shard")))
-    head_gain_share = block_of(head_gain_full.reshape(heads, HD), ((0, "tensor"), (1, "shard")))
-    out_bias_share = block_of(out_bias_full, ((1, "shard"),))
-    unit_bias_share = block_of(unit_bias_full.reshape(unit_rows, HD), ((0, "tensor"), (1, "shard")))
-    unit_gain_share = block_of(unit_gain_full.reshape(unit_rows, HD), ((0, "tensor"), (1, "shard")))
+    (
+        down_share,
+        up_share,
+        out_share,
+        qkv_share,
+        gains_share,
+        out_bias_share,
+        head_bias_share,
+        head_gain_share,
+        unit_bias_share,
+        unit_gain_share,
+    ) = grad_shares
     return (
         layer_out,
         input_grad,

time: 899 us -> 846 us (0.941)
  blocking collectives: 109 us -> 0 us
  local copies, waits for them, and re-layouts: 227 us -> 296 us
  waiting for transfers between devices: 150 us -> 123 us
    psum x1 -> x0, blocking collectives: 109 us -> none  [local(): packed = lax.psum(packed, ('shard', 'context', 'tensor'))]
    reduce_scatter x4 -> x2, waiting for transfers between devices: 46.6 us -> 0.01 us  [scatter_rows(): lax.psum_scatter(rows, ('shard', 'tensor'), scatter_dimension=0, tiled=Fa...]
    ppermute x4, waiting for transfers between devices: 4.63 us -> 41.2 us  [pair_gather(): other = lax.ppermute(block, axis_name, perm=[(0, 1), (1, 0)])]
    psum x1 -> x0, waiting for transfers between devices: 27.7 us -> none  [scatter_weight(): return lax.psum(share, 'context').astype(jnp.float32)]
    concatenate x1 -> x3, local copies, waits for them, and re-layouts: 0.01 us -> 24.1 us  [pack_rows(): jnp.concatenate([disassemble(full.astype(jnp.bfloat16), shard_dim, tensor...]
    reshape x10 -> x19, local copies, waits for them, and re-layouts: 27.2 us -> 49.8 us  [the longest x5 35.8 us: disassemble(): pieces = full.reshape(split_shape)]
    unnamed x178 -> x153, local copies, waits for them, and re-layouts: 28.4 us -> 50 us
    unnamed x9 -> x8, waiting for transfers between devices: 1.98 us -> 21.6 us
  transfers between devices with their start and end apart: 15 -> 16, of which waited for: 6 -> 5; matrix products, arithmetic and copies ran while one was open for 50% -> 50% of each run, Pallas kernels for 0% -> 0%
where the time goes in v3:
time: 846 us; the launch traced here: 837 us
  local copies, waits for them, and re-layouts  296 us (35%)
  matrix products  242 us (29%)
  other arithmetic  149 us (18%)
  waiting for transfers between devices  123 us (15%)
  between operations  15.6 us (2%)
  starting transfers between devices  10.6 us (1%)
    all_gather x1, waiting for transfers between devices, gather_packed(): lax.all_gather(flat, ('shard', 'tensor'), axis=0, tiled=False)  50.3 us
    unnamed x153, local copies, waits for them, and re-layouts  50 us
    sub x1, matrix products, probabilities(): exponent = mask_table * jnp.exp(masked - row_top)  49.6 us
    convert_element_type x1, other arithmetic, backward_pass(): score_low = (weights_soft * (soft_grad - inner_sum)).astype(jnp.bfloat16)  41.5 us
    ppermute x4, waiting for transfers between devices, pair_gather(): other = lax.ppermute(block, axis_name, perm=[(0, 1), (1, 0)])  41.2 us
    reshape x5, local copies, waits for them, and re-layouts, disassemble(): pieces = full.reshape(split_shape)  35.8 us
    dot_general x1, matrix products, backward_pass(): jnp.einsum('sqhd,skhd->shqk', grad_heads, value_heads, preferred_element_...  35.2 us
    reshape x5, local copies, waits for them, and re-layouts, gather_weight(): stacked.reshape((ns, nt) + local_block.shape)  29.9 us
  transfers between devices with their start and end apart: 16, of which 5 were waited for; matrix products, arithmetic and copies ran while one was open for 50% of the time, Pallas kernels for 0%

profile of v3, /device:TPU:0, one launch (start us, length us, event | category | flops | bytes accessed | tf_op | source)
XLA Modules:
  0.0 836.7 jit_solution(14621180866604188381)
XLA Ops:
  17.2 50.3 %all-gather.8.cloned.1.call-done = bf16[16,880,128]{2,1,0:T(8,128)(2,1)} async-done(((bf16[1,880,128]{2,1,0:T(8,128)(2,1)}), bf16[16,880,128]{2,1,0:T(8,128)(2,1)}) %all-gather.8.cloned.1.call-update) | async-done | bytes 3604496 | tf_op jit(solution)/shard_map/all_gather | solution.py:133
  67.5 6.6 reshape.2011
  76.2 4.8 reshape.2068
  80.9 7.3 copy.193
  88.2 9.1 %reshape.2013 = bf16[3,768,768]{2,1,0:T(8,128)(2,1)} reshape(bf16[3,8,96,2,384]{4,3,2,1,0:T(2,128)(2,1)} %copy.193) | data formatting | bytes 7077888 | tf_op jit(solution)/shard_map/reshape | solution.py:117
  110.8 6.6 convolution_bitcast_fusion
  126.0 5.4 fusion.155
  142.9 4.3 squeeze.39
  147.2 4.1 copy.203
  166.5 25.4 %convert_add_fusion = f32[12,512,1024]{2,1,0:T(8,128)} fusion(s32[12,1024]{1,0:T(8,128)S(1)} %add_select_fusion.1, s32[12,512]{1,0:T(8,128)S(1)} %copy-done.33, s32[12,1024]{1,0:T(8,128)S(1)} %add_select_fusion.3, s32[12,512]{1,0:T(8,128)S(1)} %copy-done.32, s32[12,1024]{1,0:T(8,128)S(1)} %add_select_fusion.5, s32[12,512]{1,0:T(8,128)S(1)} %get-tuple-element.156, ...), kind=kLoop, calls=%fused_computation.12 | loop fusion | flops 138412032 | bytes 25608192 | tf_op jit(solution)/shard_map/add | solution.py:34
  194.8 49.6 %fusion.161 = (f32[2,12,512]{2,1,0:T(8,128)S(1)}, f32[2,12,512,1024]{3,2,1,0:T(8,128)}) fusion(f32[12,512,1024]{2,1,0:T(8,128)} %convert_add_fusion, f32[2,512,1024]{2,1,0:T(8,128)} %or_convert_fusion, bf16[2,512,12,64]{1,3,2,0:T(8,128)(2,1)} %bitcast.255, bf16[2,512,12,64]{1,3,2,0:T(8,128)(2,1)} %copy.203, pred[]{:T(512)S(6)} %eq.264, ...), kind=kOutput, calls=%fused_computation.380 | convolution fusion | flops 1727005696 | bytes 86035456 | tf_op jit(solution)/shard_map/sub | solution.py:88
  247.2 20.4 %fusion.162 = (f32[2,512]{1,0:T(2,128)S(1)}, f32[2,512,12,64]{1,3,2,0:T(8,128)S(1)}) fusion(f32[2,12,512,1024]{3,2,1,0:T(8,128)} %get-tuple-element.165, f32[2,12,512]{2,1,0:T(8,128)S(1)} %get-tuple-element.164, bf16[2,512,12,64]{1,3,2,0:T(8,128)(2,1)} %bitcast.257, bf16[2,512,12,64]{1,3,2,0:T(8,128)(2,1)} %fusion.34, pred[]{:T(512)S(6)} %eq.264), kind=kOutput, calls=%fused_computation.381 | convolution fusion | flops 1650719744 | bytes 56676352 | tf_op jit(solution)/shard_map/shqk,skhd->sqhd/dot_general | solution.py:257
  285.2 9.4 %copy.209 = bf16[8,2,96,1536]{3,1,2,0:T(2,128)(2,1)} copy(bf16[8,2,96,1536]{3,2,1,0:T(8,128)(2,1)} %bitcast.244) | data formatting | bytes 9437184 | tf_op jit(solution)/shard_map/reshape | solution.py:124
  294.6 5.7 copy.253
  300.3 7.6 reshape.2020
  308.0 7.7 copy.214
  315.7 5.8 copy.254
  321.5 7.5 fusion.149
  329.0 5.7 multiply_reduce_fusion.3
  334.8 17.7 %multiply_reduce_fusion.1 = (bf16[3072]{0:T(1024)(128)(2,1)S(1)}, f32[1024]{0:T(1024)S(1)}, f32[1024]{0:T(1024)S(1)}, bf16[1024,3072]{1,0:T(8,128)(2,1)}, f32[1024,3072]{1,0:T(8,128)}) fusion(f32[1024]{0:T(1024)S(1)} %add_rsqrt_fusion, f32[1024]{0:T(1024)S(1)} %broadcast_multiply_fusion.3, f32[1024,3072]{1,0:T(8,128)S(1)} %get-tuple-element.171, ...), kind=kOutput, calls=%fused_computation.23 | convolution fusion | flops 4891601920 | bytes 37795840 | tf_op jit(solution)/shard_map/dot_general | solution.py:62
  352.5 15.9 %fusion.150 = (bf16[3072]{0:T(1024)(128)(2,1)S(1)}, bf16[1024,3072]{1,0:T(8,128)(2,1)S(1)}) fusion(f32[1024]{0:T(1024)S(1)} %broadcast_multiply_fusion.1, f32[1024]{0:T(1024)S(1)} %broadcast_multiply_fusion.3, f32[1024,3072]{1,0:T(8,128)S(1)} %get-tuple-element.171, f32[3072]{0:T(1024)S(1)} %copy-done.34, f32[1024]{0:T(1024)S(1)} %broadcast_multiply_fusion.2, ...), kind=kLoop, calls=%fused_computation.371 | loop fusion | flops 94368768 | bytes 31504384 | tf_op jit(solution)/shard_map/reduce_sum | solution.py:332
  368.5 8.0 multiply_reduce_fusion.6
  376.5 7.7 convolution_convert_fusion
  392.9 12.1 %reshape.2025 = bf16[8,96,2,1536]{3,2,1,0:T(2,128)(2,1)} reshape(bf16[768,3072]{1,0:T(8,128)(2,1)} %convolution_convert_fusion) | data formatting | bytes 9437184 | tf_op jit(solution)/shard_map/reshape | solution.py:187
  405.0 5.4 copy.280
  410.4 9.9 %concatenate.68 = bf16[16,1152,128]{2,1,0:T(8,128)(2,1)} reshape(bf16[8,2,96,1536]{3,2,1,0:T(8,128)(2,1)} %bitcast.235) | data formatting | bytes 9437184 | tf_op jit(solution)/shard_map/concatenate | solution.py:199
  432.5 4.3 reshape.2028
  437.6 9.2 %convolution_convert_fusion.1 = bf16[3072,768]{1,0:T(8,128)(2,1)} fusion(bf16[1024,3072]{1,0:T(8,128)(2,1)} %get-tuple-element.126, bf16[1024,768]{1,0:T(8,128)(2,1)} %bitcast.243), kind=kOutput, calls=%fused_computation.37 | convolution fusion | flops 4834197504 | bytes 12582912 | tf_op jit(solution)/shard_map/dot_general | solution.py:56
  446.8 6.7 copy.215
  453.5 11.6 %reshape.2024 = bf16[2,1536,8,96]{1,0,3,2:T(2,128)(2,1)} reshape(bf16[3072,768]{0,1:T(8,128)(2,1)} %copy.215) | data formatting | bytes 9437184 | tf_op jit(solution)/shard_map/reshape | solution.py:187
  465.1 12.1 %copy.216 = bf16[8,2,1536,96]{3,2,1,0:T(8,128)(2,1)} copy(bf16[8,2,1536,96]{2,1,3,0:T(2,128)(2,1)} %bitcast.236) | data formatting | bytes 9437184 | tf_op jit(solution)/shard_map/transpose | solution.py:190
  477.2 12.8 %concatenate.67 = bf16[16,1152,128]{2,1,0:T(8,128)(2,1)} reshape(bf16[8,2,1536,96]{3,2,1,0:T(8,128)(2,1)} %copy.216) | data formatting | bytes 9437184 | tf_op jit(solution)/shard_map/concatenate | solution.py:199
  489.9 7.5 pad_maximum_fusion
  505.2 22.6 %fusion.14 = f32[2,12,64,1024]{3,2,1,0:T(8,128)S(1)} fusion(bf16[2,512,12,64]{1,0,3,2:T(2,128)(2,1)} %reshape.2029, f32[2,12,512,1024]{3,2,1,0:T(8,128)} %get-tuple-element.165, f32[2,12,512]{2,1,0:T(8,128)S(1)} %get-tuple-element.164), kind=kOutput, calls=%fused_computation.27 | convolution fusion | flops 1635778560 | bytes 58245120 | tf_op jit(solution)/shard_map/shqk,sqhd->skhd/dot_general | solution.py:370
  533.4 35.2 %multiply_reduce_fusion = (f32[2,12,512]{2,1,0:T(8,128)S(1)}, f32[2,12,512,1024]{3,2,1,0:T(8,128)}) fusion(f32[2,12,512,1024]{3,2,1,0:T(8,128)} %get-tuple-element.165, f32[2,12,512]{2,1,0:T(8,128)S(1)} %get-tuple-element.164, bf16[2,512,12,64]{1,3,2,0:T(8,128)(2,1)} %bitcast.258, bf16[2,512,12,64]{1,3,2,0:T(8,128)(2,1)} %fusion.34, pred[]{:T(512)S(6)} %eq.264, ...), kind=kOutput, calls=%fused_computation.4 | convolution fusion | flops 1662504960 | bytes 105480192 | tf_op jit(solution)/shard_map/sqhd,skhd->shqk/dot_general | solution.py:352
  568.6 41.5 %multiply_convert_fusion = bf16[2,12,512,1024]{3,2,1,0:T(8,128)(2,1)} fusion(f32[2,12,512,1024]{3,2,1,0:T(8,128)} %get-tuple-element.176, f32[2,12,512]{2,1,0:T(8,128)S(1)} %get-tuple-element.175, f32[2,12,512,1024]{3,2,1,0:T(8,128)} %get-tuple-element.165, f32[2,12,512]{2,1,0:T(8,128)S(1)} %get-tuple-element.164), kind=kLoop, calls=%fused_computation.3 | loop fusion | flops 50331648 | bytes 125927424 | tf_op jit(solution)/shard_map/convert_element_type | solution.py:356
  610.1 10.6 %broadcast_multiply_fusion = f32[2,12,64,1024]{3,2,1,0:T(8,128)S(1)} fusion(bf16[2,12,512,1024]{3,2,1,0:T(8,128)(2,1)} %multiply_convert_fusion, f32[2,512,12,64]{1,0,3,2:T(2,128)S(1)} %copy-done.10, f32[12,64]{1,0:T(8,128)S(1)} %copy-done.36), kind=kOutput, calls=%fused_computation.78 | convolution fusion | flops 1613758464 | bytes 34606080 | tf_op jit(solution)/shard_map/shqk,sqhd->skhd/dot_general | solution.py:367
  625.0 12.2 %fusion.164 = (bf16[12,64]{1,0:T(8,128)(2,1)S(1)}, bf16[2,512,12,64]{1,3,2,0:T(8,128)(2,1)S(1)}) fusion(bf16[2,12,512,1024]{3,2,1,0:T(8,128)(2,1)} %multiply_convert_fusion, bf16[2,512,12,64]{1,3,2,0:T(8,128)(2,1)S(1)} %bitcast.256, bf16[2,512,12,64]{1,3,2,0:T(8,128)(2,1)S(1)} %copy-done.24, pred[]{:T(512)S(6)} %eq.264), kind=kOutput, calls=%fused_computation.383 | convolution fusion | flops 1627127040 | bytes 29885952 | tf_op jit(solution)/shard_map/shqk,skhd->sqhd/dot_general | solution.py:360
  649.1 9.5 %collective-permute-done.3 = bf16[2,512,768]{1,2,0:T(8,128)(2,1)} collective-permute-done((bf16[2,512,768]{1,2,0:T(8,128)(2,1)}, bf16[2,512,768]{1,2,0:T(8,128)(2,1)}, u32[]{:S(2)}, u32[]{:S(2)}) %collective-permute-start.3) | collective-permute-done | bytes 1572896 | tf_op jit(solution)/shard_map/ppermute | solution.py:162
  671.8 8.4 %convert_bitcast_fusion = bf16[3,768,768]{1,2,0:T(8,128)(2,1)} fusion(bf16[3,1024,768]{1,2,0:T(8,128)(2,1)} %pad_maximum_fusion.1, bf16[1024,768]{1,0:T(8,128)(2,1)} %copy-done.27), kind=kOutput, calls=%fused_computation.42 | convolution fusion | flops 3625648128 | bytes 9830400 | tf_op jit(solution)/shard_map/rd,jre->jde/dot_general | solution.py:388
  680.2 4.3 copy.228
  693.5 4.2 constant_dynamic-update-slice_fusion
  698.8 8.6 %fusion.20 = (bf16[768]{0:T(1024)(128)(2,1)S(1)}, f32[1024]{0:T(1024)S(1)}, f32[1024]{0:T(1024)S(1)}, f32[1024,768,1]{1,0,2:T(8,128)}) fusion(f32[1024]{0:T(1024)S(1)} %bitcast.281, f32[1024]{0:T(1024)S(1)} %bitcast.278, bf16[4,512,768]{2,1,0:T(8,128)(2,1)S(1)} %copy-done.8, s32[]{:T(128)S(6)} %select_n.310, f32[768]{0:T(1024)S(1)} %copy-done.49, ...), kind=kOutput, calls=%fused_computation.51 | convolution fusion | flops 3630953728 | bytes 12997124 | tf_op jit(solution)/shard_map/jre,jde->rd/dot_general | solution.py:392
  721.5 10.3 %add_convert_fusion.2 = bf16[1024,768]{1,0:T(8,128)(2,1)} fusion(f32[1024,768]{1,0:T(8,128)} %copy-done.12, bf16[1024,3072]{1,0:T(8,128)(2,1)} %get-tuple-element.126, bf16[3072,768]{0,1:T(8,128)(2,1)} %bitcast.246, f32[768]{0:T(1024)S(1)} %add.736), kind=kOutput, calls=%fused_computation.86 | convolution fusion | flops 4834197504 | bytes 15731712 | tf_op jit(solution)/shard_map/dot_general | solution.py:275
  739.9 39.1 %collective-permute-done.2 = bf16[2,512,768]{2,1,0:T(8,128)(2,1)} collective-permute-done((bf16[2,512,768]{2,1,0:T(8,128)(2,1)}, bf16[2,512,768]{2,1,0:T(8,128)(2,1)}, u32[]{:S(2)}, u32[]{:S(2)}) %collective-permute-start.2) | collective-permute-done | bytes 1572896 | tf_op jit(solution)/shard_map/ppermute | solution.py:146
  778.9 4.3 maximum_select_fusion.2
  787.7 21.5 %reduce-scatter.10.cloned.1.call-done = bf16[1,872,128]{2,1,0:T(8,128)(2,1)} async-done(((bf16[16,872,128]{2,1,0:T(8,128)(2,1)}), bf16[1,872,128]{2,1,0:T(8,128)(2,1)}) %reduce-scatter.10.cloned.1.call-update) | async-done | bytes 223248
  816.5 6.9 slice.192
  (365 shorter events, 197.8 us)
Async XLA Ops:
  7.2 90.5 %copy-start = (s32[4,2]{0,1:T(2,128)S(1)}, s32[4,2]{0,1:T(2,128)}, u32[]{:S(2)}) copy-start(s32[4,2]{0,1:T(2,128)} %param.21) | copy-start | bytes 100
  7.2 60.3 %all-gather.8.cloned.1.call-start = ((), (), s32[]{:S(2)}) async-start(), calls=%async_computation.3 | async-start | bytes 3829760 | tf_op jit(solution)/shard_map/all_gather | solution.py:133
  17.2 258.7 %all-gather.10.cloned.1.call-start = ((), (), s32[]{:S(2)}) async-start(), calls=%async_computation.6 | async-start | bytes 1253376 | tf_op jit(solution)/shard_map/all_gather | solution.py:123
  88.2 9.1 %copy-start.7 = (bf16[4,512,768]{2,1,0:T(8,128)(2,1)S(1)}, bf16[4,512,768]{2,1,0:T(8,128)(2,1)}, u32[]{:S(2)}) copy-start(bf16[4,512,768]{2,1,0:T(8,128)(2,1)} %param.19) | copy-start | bytes 9437188
  97.3 187.9 %all-gather.12.cloned.1.call-start = ((), (), s32[]{:S(2)}) async-start(), calls=%async_computation.7 | async-start | bytes 5013504 | tf_op jit(solution)/shard_map/all_gather | solution.py:123
  98.5 201.8 %all-gather.14.cloned.1.call-start = ((), (), s32[]{:S(2)}) async-start(), calls=%async_computation.8 | async-start | bytes 5013504 | tf_op jit(solution)/shard_map/all_gather | solution.py:123
  102.1 5.4 slice-start.1
  102.1 8.1 copy-start.44
  102.2 8.1 copy-start.46
  110.2 7.1 copy-start.48
  110.7 6.6 copy-start.27
  141.1 53.7 %copy-start.35 = (f32[12,64]{1,0:T(8,128)}, f32[12,64]{1,0:T(8,128)S(1)}, u32[]{:S(2)}) copy-start(f32[12,64]{1,0:T(8,128)S(1)} %add.722) | copy-start | bytes 9220
  147.2 47.6 %copy-start.9 = (f32[2,512,12,64]{1,0,3,2:T(2,128)}, f32[2,512,12,64]{1,0,3,2:T(2,128)S(1)}, u32[]{:S(2)}) copy-start(f32[2,512,12,64]{1,0,3,2:T(2,128)S(1)} %squeeze.39) | copy-start | bytes 9437188
  147.2 5.5 copy-start.15
  151.3 40.7 %collective-permute-start.1 = (bf16[2,512,768]{1,0,2:T(2,128)(2,1)}, bf16[2,512,768]{1,0,2:T(2,128)(2,1)}, u32[]{:S(2)}, u32[]{:S(2)}) collective-permute-start(bf16[2,512,768]{1,0,2:T(2,128)(2,1)} %convert_element_type.352), channel_id=1, source_target_pairs={{0,2},{2,0},{1,3},{3,1},{4,6},{6,4},{5,7},{7,5},{8,10},{10,8},{9,1... | collective-permute-start | bytes 4718600 | tf_op jit(solution)/shard_map/ppermute | solution.py:146
  156.3 88.0 %collective-permute-start = (bf16[2,512,768]{1,0,2:T(2,128)(2,1)}, bf16[2,512,768]{1,0,2:T(2,128)(2,1)}, u32[]{:S(2)}, u32[]{:S(2)}) collective-permute-start(bf16[2,512,768]{1,0,2:T(2,128)(2,1)} %add_convert_fusion.3), channel_id=1, source_target_pairs={{0,2},{2,0},{1,3},{3,1},{4,6},{6,4},{5,7},{7,5},{8,10},{10,8},{9,1... | collective-permute-start | bytes 4718600 | tf_op jit(solution)/shard_map/ppermute | solution.py:146
  162.6 509.2 %reduce-scatter.6.cloned.1.call-start = ((), (), s32[]{:S(2)}) async-start(), calls=%async_computation.4 | async-start | bytes 10027008 | tf_op jit(solution)/shard_map/reduce_scatter | solution.py:208
  275.9 5.5 copy-start.63
  315.7 5.8 copy-start.13
  315.7 5.8 copy-start.19
  315.7 5.8 copy-start.34
  315.7 5.8 copy-start.58
  329.0 5.8 copy-start.42
  352.5 16.0 %copy-start.14 = (f32[1024,768]{1,0:T(8,128)S(1)}, f32[1024,768]{1,0:T(8,128)}, u32[]{:S(2)}) copy-start(f32[1024,768]{1,0:T(8,128)} %copy-done.12) | copy-start | bytes 9437188
  376.5 7.7 copy-start.18
  501.4 231.5 %reduce-scatter.8.cloned.1.call-start = ((), (), s32[]{:S(2)}) async-start(), calls=%async_computation.5 | async-start | bytes 1253376 | tf_op jit(solution)/shard_map/reduce_scatter | solution.py:208
  531.9 108.5 %collective-permute-start.4 = (bf16[2,512,768]{1,2,0:T(8,128)(2,1)}, bf16[2,512,768]{1,2,0:T(8,128)(2,1)}, u32[]{:S(2)}, u32[]{:S(2)}) collective-permute-start(bf16[2,512,768]{1,2,0:T(8,128)(2,1)} %dynamic-slice_convert_fusion), channel_id=1, source_target_pairs={{0,2},{2,0},{1,3},{3,1},{4,6},{6,4},{5,7},{7,5},{8,10},{10,8},{9,1... | collective-permute-start | bytes 4718600 | tf_op jit(solution)/shard_map/ppermute | solution.py:162
  568.6 41.6 %copy-start.10 = (f32[2,512,12,64]{1,0,3,2:T(2,128)S(1)}, f32[2,512,12,64]{1,0,3,2:T(2,128)}, u32[]{:S(2)}) copy-start(f32[2,512,12,64]{1,0,3,2:T(2,128)} %copy-done.9) | copy-start | bytes 9437188
  568.6 41.6 %copy-start.36 = (f32[12,64]{1,0:T(8,128)S(1)}, f32[12,64]{1,0:T(8,128)}, u32[]{:S(2)}) copy-start(f32[12,64]{1,0:T(8,128)} %copy-done.35) | copy-start | bytes 9220
  620.8 16.4 %copy-start.6 = (f32[2,12,64,1024]{3,2,1,0:T(8,128)}, f32[2,12,64,1024]{3,2,1,0:T(8,128)S(1)}, u32[]{:S(2)}) copy-start(f32[2,12,64,1024]{3,2,1,0:T(8,128)S(1)} %broadcast_multiply_fusion) | copy-start | bytes 18874372
  622.2 36.4 %collective-permute-start.3 = (bf16[2,512,768]{1,2,0:T(8,128)(2,1)}, bf16[2,512,768]{1,2,0:T(8,128)(2,1)}, u32[]{:S(2)}, u32[]{:S(2)}) collective-permute-start(bf16[2,512,768]{1,2,0:T(8,128)(2,1)} %dynamic-slice_convert_fusion.1), channel_id=1, source_target_pairs={{0,2},{2,0},{1,3},{3,1},{4,6},{6,4},{5,7},{7,5},{8,10},{10,8},{9,1... | collective-permute-start | bytes 4718600 | tf_op jit(solution)/shard_map/ppermute | solution.py:162
  640.1 169.0 %reduce-scatter.10.cloned.1.call-start = ((), (), s32[]{:S(2)}) async-start(), calls=%async_computation.9 | async-start | bytes 3794944
  693.5 5.3 copy-start.22
  698.8 8.7 %copy-start.62 = (bf16[1,8,96]{2,1,0:T(8,128)(2,1)S(1)}, bf16[1,8,96]{2,1,0:T(8,128)(2,1)}, u32[]{:S(2)}) copy-start(bf16[1,8,96]{2,1,0:T(8,128)(2,1)} %stack.32) | copy-start | bytes 4612
  698.8 10.2 %copy-start.55 = (bf16[16,192]{1,0:T(8,128)(2,1)S(1)}, bf16[16,192]{1,0:T(8,128)(2,1)}, u32[]{:S(2)}) copy-start(bf16[16,192]{1,0:T(8,128)(2,1)} %reshape.2036) | copy-start | bytes 18436
  698.8 12.9 %copy-start.59 = (bf16[16,48]{1,0:T(8,128)(2,1)S(1)}, bf16[16,48]{1,0:T(8,128)(2,1)}, u32[]{:S(2)}) copy-start(bf16[16,48]{1,0:T(8,128)(2,1)} %reshape.2038) | copy-start | bytes 4612
  698.8 14.4 %copy-start.56 = (bf16[16,192]{1,0:T(8,128)(2,1)S(1)}, bf16[16,192]{1,0:T(8,128)(2,1)}, u32[]{:S(2)}) copy-start(bf16[16,192]{1,0:T(8,128)(2,1)} %reshape.2039) | copy-start | bytes 18436
  698.8 15.8 %copy-start.57 = (bf16[16,192]{1,0:T(8,128)(2,1)S(1)}, bf16[16,192]{1,0:T(8,128)(2,1)}, u32[]{:S(2)}) copy-start(bf16[16,192]{1,0:T(8,128)(2,1)} %reshape.2040) | copy-start | bytes 18436
  721.5 13.5 %copy-start.5 = (f32[1024,768]{1,0:T(8,128)S(1)}, f32[1024,768]{1,0:T(8,128)}, u32[]{:S(2)}) copy-start(f32[1024,768]{1,0:T(8,128)} %copy-done.4) | copy-start | bytes 9437188
  731.8 47.2 %collective-permute-start.2 = (bf16[2,512,768]{2,1,0:T(8,128)(2,1)}, bf16[2,512,768]{2,1,0:T(8,128)(2,1)}, u32[]{:S(2)}, u32[]{:S(2)}) collective-permute-start(bf16[2,512,768]{2,1,0:T(8,128)(2,1)} %bitcast.23), channel_id=1, source_target_pairs={{0,1},{1,0},{2,3},{3,2},{4,5},{5,4},{6,7},{7,6},{8,9},{9,8},{10,11... | collective-permute-start | bytes 4718600 | tf_op jit(solution)/shard_map/ppermute | solution.py:146
  732.9 50.3 %collective-permute-start.7 = (bf16[288,128]{1,0:T(8,128)(2,1)}, bf16[288,128]{1,0:T(8,128)(2,1)S(1)}, u32[]{:S(2)}, u32[]{:S(2)}) collective-permute-start(bf16[288,128]{1,0:T(8,128)(2,1)} %bitcast.270), channel_id=1, source_target_pairs={{0,2},{2,0},{1,3},{3,1},{4,6},{6,4},{5,7},{7,5},{8,10},{10,8},{9,1... | collective-permute-start | bytes 221192 | tf_op jit(solution)/shard_map/ppermute | solution.py:169
  733.6 50.5 %collective-permute-start.8 = (bf16[2304,128]{1,0:T(8,128)(2,1)}, bf16[2304,128]{1,0:T(8,128)(2,1)}, u32[]{:S(2)}, u32[]{:S(2)}) collective-permute-start(bf16[2304,128]{1,0:T(8,128)(2,1)} %bitcast.262), channel_id=1, source_target_pairs={{0,2},{2,0},{1,3},{3,1},{4,6},{6,4},{5,7},{7,5},{8,10},{10,8},{9,1... | collective-permute-start | bytes 1769480 | tf_op jit(solution)/shard_map/ppermute | solution.py:169
  739.0 44.2 %copy-start.37 = (bf16[1,288,128]{2,1,0:T(8,128)(2,1)S(1)}, bf16[1,288,128]{2,1,0:T(8,128)(2,1)}, u32[]{:S(2)}) copy-start(bf16[1,288,128]{2,1,0:T(8,128)(2,1)} %reduce-scatter.8.cloned.1.call-done) | copy-start | bytes 221188
  739.0 45.1 %copy-start.29 = (bf16[1,2304,128]{2,1,0:T(8,128)(2,1)S(1)}, bf16[1,2304,128]{2,1,0:T(8,128)(2,1)}, u32[]{:S(2)}) copy-start(bf16[1,2304,128]{2,1,0:T(8,128)(2,1)} %reduce-scatter.6.cloned.1.call-done) | copy-start | bytes 1769476
  739.0 73.8 %collective-permute-start.5 = (bf16[2,512,768]{2,1,0:T(8,128)(2,1)}, bf16[2,512,768]{2,1,0:T(8,128)(2,1)S(1)}, u32[]{:S(2)}, u32[]{:S(2)}) collective-permute-start(bf16[2,512,768]{2,1,0:T(8,128)(2,1)} %bitcast.37), channel_id=1, source_target_pairs={{0,1},{1,0},{2,3},{3,2},{4,5},{5,4},{6,7},{7,6},{8,9},{9,8},{10,11... | collective-permute-start | bytes 4718600 | tf_op jit(solution)/shard_map/ppermute | solution.py:146
  809.1 7.2 copy-start.30
  809.1 7.1 collective-permute-start.6
  816.4 13.2 %copy-start.1 = (s32[4,2]{0,1:T(2,128)S(1)}, s32[4,2]{0,1:T(2,128)}, u32[]{:S(2)}) copy-start(s32[4,2]{0,1:T(2,128)} %param.21) | copy-start | bytes 100
  (34 other events, 107.8 us)
Sparse Core Ops, SparseCore 0:
  17.3 50.1 all-gather.7
  97.4 35.6 all-gather.9
  135.4 52.5 all-gather.11
  190.3 51.6 all-gather.13
  501.6 110.4 reduce-scatter.5
  640.2 57.1 reduce-scatter.7
  720.9 88.2 reduce-scatter.9

commit v4 on v3

--- a/solution.py
+++ b/solution.py
@@ -3,6 +3,8 @@
 import jax
 import jax.numpy as jnp
 from jax import lax
+from jax.experimental import pallas as pl
+from jax.experimental.pallas import tpu as pltpu
 from jax.sharding import PartitionSpec as P
 
 HD = 64
@@ -88,6 +90,215 @@
     exponent = mask_table * jnp.exp(masked - row_top)
     row_total = jnp.sum(exponent, -1, keepdims=True)
     return (exponent / row_total, row_top, row_total)
+
+
+SCALE = HD ** (-0.5)
+HIDDEN = -1000000000.0
+PAIR = 2
+CODE_WIDTH = 8
+
+
+def pair_masks(patq_ref, patk_ref, pcq_ref, pck_ref):
+    first_q = patq_ref[0]
+    first_k = patk_ref[0]
+    row = first_q[:, 5:6]
+    col = first_k[5:6, :]
+    piece_q = pcq_ref[0][:, 0:1]
+    piece_k = pck_ref[0][0:1, :]
+    allowed = (col <= row) | (piece_q == piece_k)
+    masks = []
+    for head in range(PAIR):
+        codes_q = patq_ref[head]
+        codes_k = patk_ref[head]
+        tally = (codes_q[:, 0:1] == codes_k[0:1, :]).astype(jnp.float32)
+        for pattern in range(1, len(span_parts)):
+            tally = tally + (
+                codes_q[:, pattern : pattern + 1] == codes_k[pattern : pattern + 1, :]
+            ).astype(jnp.float32)
+        masks.append(jnp.where(allowed, tally, 0.0))
+    return masks
+
+
+def soft_rows(query_part, key_block, mask):
+    scores = (
+        lax.dot_general(
+            query_part, key_block, (((1,), (1,)), ((), ())), preferred_element_type=jnp.float32
+        )
+        * SCALE
+    )
+    masked = jnp.where(mask > 0, scores, HIDDEN)
+    top = jnp.max(masked, axis=1, keepdims=True)
+    exponent = mask * jnp.exp(masked - top)
+    return exponent / jnp.sum(exponent, axis=1, keepdims=True)
+
+
+def attention_fwd_kernel(q_ref, k_ref, v_ref, patq_ref, patk_ref, pcq_ref, pck_ref, o_ref):
+    query = q_ref[0]
+    key_block = k_ref[0]
+    value_block = v_ref[0]
+    first = lax.broadcasted_iota(jnp.int32, query.shape, 1) < HD
+    masks = pair_masks(patq_ref, patk_ref, pcq_ref, pck_ref)
+    result = None
+    for head in range(PAIR):
+        keep = first if head == 0 else jnp.logical_not(first)
+        query_part = jnp.where(keep, query, jnp.zeros_like(query))
+        probs = soft_rows(query_part, key_block, masks[head])
+        mixed = jnp.dot(
+            probs.astype(jnp.bfloat16), value_block, preferred_element_type=jnp.float32
+        )
+        result = mixed if result is None else jnp.where(first, result, mixed)
+    o_ref[0] = result
+
+
+def attention_bwd_kernel(
+    q_ref, k_ref, v_ref, do_ref, patq_ref, patk_ref, pcq_ref, pck_ref, dq_ref, dk_ref, dv_ref
+):
+    @pl.when(pl.program_id(2) == 0)
+    def _():
+        dk_ref[...] = jnp.zeros_like(dk_ref)
+        dv_ref[...] = jnp.zeros_like(dv_ref)
+
+    query = q_ref[0]
+    key_block = k_ref[0]
+    value_block = v_ref[0]
+    grad_out = do_ref[0]
+    first = lax.broadcasted_iota(jnp.int32, query.shape, 1) < HD
+    masks = pair_masks(patq_ref, patk_ref, pcq_ref, pck_ref)
+    query_grad = None
+    key_grad = dk_ref[0]
+    value_grad = dv_ref[0]
+    for head in range(PAIR):
+        keep = first if head == 0 else jnp.logical_not(first)
+        query_part = jnp.where(keep, query, jnp.zeros_like(query))
+        grad_part = jnp.where(keep, grad_out, jnp.zeros_like(grad_out))
+        probs = soft_rows(query_part, key_block, masks[head])
+        prob_grad = lax.dot_general(
+            grad_part, value_block, (((1,), (1,)), ((), ())), preferred_element_type=jnp.float32
+        )
+        inner = jnp.sum(probs * prob_grad, axis=1, keepdims=True)
+        score_low = (probs * (prob_grad - inner)).astype(jnp.bfloat16)
+        part = jnp.dot(score_low, key_block, preferred_element_type=jnp.float32)
+        query_grad = part if query_grad is None else jnp.where(first, query_grad, part)
+        key_grad = key_grad + SCALE * lax.dot_general(
+            score_low, query_part, (((0,), (0,)), ((), ())), preferred_element_type=jnp.float32
+        )
+        value_grad = value_grad + lax.dot_general(
+            probs.astype(jnp.bfloat16),
+            grad_part,
+            (((0,), (0,)), ((), ())),
+            preferred_element_type=jnp.float32,
+        )
+    dq_ref[0] = (query_grad * SCALE).astype(jnp.bfloat16)
+    dk_ref[0] = key_grad
+    dv_ref[0] = value_grad
+
+
+def attention_specs(seq_count, local_len, seq_len, block_q):
+    lanes = PAIR * HD
+    query_spec = pl.BlockSpec((1, block_q, lanes), lambda s, g, b: (s, b, g))
+    key_spec = pl.BlockSpec((1, seq_len, lanes), lambda s, g, b: (s, 0, g))
+    patq_spec = pl.BlockSpec((PAIR, block_q, CODE_WIDTH), lambda s, g, b: (g, b, 0))
+    patk_spec = pl.BlockSpec((PAIR, CODE_WIDTH, seq_len), lambda s, g, b: (g, 0, 0))
+    pcq_spec = pl.BlockSpec((1, block_q, CODE_WIDTH), lambda s, g, b: (s, b, 0))
+    pck_spec = pl.BlockSpec((1, CODE_WIDTH, seq_len), lambda s, g, b: (s, 0, 0))
+    return query_spec, key_spec, patq_spec, patk_spec, pcq_spec, pck_spec
+
+
+def attention_forward(query, keys, values, codes):
+    seq_count, local_len, width = query.shape
+    seq_len = keys.shape[1]
+    block_q = min(256, local_len)
+    grid = (seq_count, width // (PAIR * HD), local_len // block_q)
+    query_spec, key_spec, patq_spec, patk_spec, pcq_spec, pck_spec = attention_specs(
+        seq_count, local_len, seq_len, block_q
+    )
+    flops = 8 * seq_count * local_len * seq_len * width
+    return pl.pallas_call(
+        attention_fwd_kernel,
+        grid=grid,
+        in_specs=[query_spec, key_spec, key_spec, patq_spec, patk_spec, pcq_spec, pck_spec],
+        out_specs=query_spec,
+        out_shape=jax.ShapeDtypeStruct((seq_count, local_len, width), jnp.float32),
+        compiler_params=pltpu.CompilerParams(
+            dimension_semantics=("parallel", "parallel", "arbitrary"),
+            vmem_limit_bytes=48 * 1024 * 1024,
+        ),
+        cost_estimate=pl.CostEstimate(
+            flops=flops,
+            transcendentals=seq_count * local_len * seq_len * width // HD,
+            bytes_accessed=2 * query.size + 2 * keys.size * 2 * (local_len // block_q) + 4 * query.size,
+        ),
+    )(query, keys, values, *codes)
+
+
+def attention_backward(query, keys, values, grad_out, codes):
+    seq_count, local_len, width = query.shape
+    seq_len = keys.shape[1]
+    block_q = min(256, local_len)
+    grid = (seq_count, width // (PAIR * HD), local_len // block_q)
+    query_spec, key_spec, patq_spec, patk_spec, pcq_spec, pck_spec = attention_specs(
+        seq_count, local_len, seq_len, block_q
+    )
+    flops = 20 * seq_count * local_len * seq_len * width
+    return pl.pallas_call(
+        attention_bwd_kernel,
+        grid=grid,
+        in_specs=[
+            query_spec,
+            key_spec,
+            key_spec,
+            query_spec,
+            patq_spec,
+            patk_spec,
+            pcq_spec,
+            pck_spec,
+        ],
+        out_specs=[query_spec, key_spec, key_spec],
+        out_shape=[
+            jax.ShapeDtypeStruct((seq_count, local_len, width), jnp.bfloat16),
+            jax.ShapeDtypeStruct((seq_count, seq_len, width), jnp.float32),
+            jax.ShapeDtypeStruct((seq_count, seq_len, width), jnp.float32),
+        ],
+        compiler_params=pltpu.CompilerParams(
+            dimension_semantics=("parallel", "parallel", "arbitrary"),
+            vmem_limit_bytes=48 * 1024 * 1024,
+        ),
+        cost_estimate=pl.CostEstimate(
+            flops=flops,
+            transcendentals=seq_count * local_len * seq_len * width // HD,
+            bytes_accessed=4 * query.size + 2 * keys.size * 2 * (local_len // block_q) + 16 * keys.size,
+        ),
+    )(query, keys, values, grad_out, *codes)
+
+
+def mask_codes(starts, query_position, key_position, segment_offsets, dilation_offsets, seq_len):
+    heads = segment_offsets.shape[0]
+    query_codes = []
+    key_codes = []
+    for pattern in range(len(span_parts)):
+        span = seq_len * span_parts[pattern] // 8
+        rate = dilation_rates[pattern]
+        shift = (segment_offsets[:, pattern] % span)[:, None]
+        phase = (dilation_offsets[:, pattern] % rate)[:, None]
+        query_at = query_position[None, :] + shift
+        key_at = key_position[None, :] + shift
+        query_codes.append(jnp.where(query_at % rate == phase, query_at // span, -1))
+        key_codes.append(jnp.where(key_at % rate == phase, key_at // span, -2))
+    patterns = len(span_parts)
+    query_codes.append(jnp.broadcast_to(query_position[None, :], (heads, query_position.shape[0])))
+    key_codes.append(jnp.broadcast_to(key_position[None, :], (heads, key_position.shape[0])))
+    filler = CODE_WIDTH - patterns - 1
+    query_codes += [jnp.zeros((heads, query_position.shape[0]), jnp.int32)] * filler
+    key_codes += [jnp.zeros((heads, key_position.shape[0]), jnp.int32)] * filler
+    patq = jnp.stack(query_codes, 2).astype(jnp.int32)
+    patk = jnp.stack(key_codes, 1).astype(jnp.int32)
+    query_pic = picture_index(starts, query_position)
+    key_pic = picture_index(starts, key_position)
+    pcq = jnp.where(query_pic > 0, query_pic, -1)[:, :, None]
+    pcq = jnp.pad(pcq, ((0, 0), (0, 0), (0, CODE_WIDTH - 1)))
+    pck = jnp.where(key_pic > 0, key_pic, -2)[:, None, :]
+    pck = jnp.pad(pck, ((0, 0), (0, CODE_WIDTH - 1), (0, 0)))
+    return (patq, patk, pcq.astype(jnp.int32), pck.astype(jnp.int32))
 
 
 def assemble(stacked, shard_dim, tensor_dim):
@@ -228,12 +439,10 @@
     return pieces
 
 
-def forward_pass(block_in, starts, tallied_total, weights, query_position, key_position):
+def forward_pass(block_in, codes, weights):
     w_qkv, w_out, w_up, w_down, norm_gains, out_biases, head_biases, head_gain, unit_bias, unit_gain = weights
     seq_count, local_len, model_width = block_in.shape
-    seq_len = key_position.shape[0]
     row_count = seq_count * local_len
-    heads = model_width // HD
     flattened_input = block_in.reshape(row_count, model_width).astype(jnp.float32)
     first_normed, first_inv, first_out = norm_rows(flattened_input, norm_gains[0])
     attn_in = first_out.astype(jnp.bfloat16)
@@ -245,20 +454,8 @@
     )
     key_all = pair_gather(keys_local, "context", 1)
     value_all = pair_gather(values_local, "context", 1)
-    query_pic = picture_index(starts, query_position)
-    key_pic = picture_index(starts, key_position)
-    mask_table = (
-        allowed_keys(query_pic, key_pic, query_position, key_position)[:, None] * tallied_total[None]
-    )
-    query_heads = query_matrix.reshape(seq_count, local_len, heads, HD)
-    key_heads = key_all.reshape(seq_count, seq_len, heads, HD)
-    value_heads = value_all.reshape(seq_count, seq_len, heads, HD)
-    weights_soft = probabilities(query_heads, key_heads, mask_table)[0]
-    attended = jnp.einsum(
-        "shqk,skhd->sqhd",
-        weights_soft.astype(jnp.bfloat16),
-        value_heads,
-        preferred_element_type=jnp.float32,
+    attended = attention_forward(
+        query_matrix.reshape(seq_count, local_len, model_width), key_all, value_all, codes
     ).reshape(row_count, model_width)
     sub_normed, sub_inv, sub_out = norm_rows(attended, head_gain)
     sub_in = sub_out.astype(jnp.bfloat16)
@@ -278,10 +475,10 @@
         attn_in,
         first_normed,
         first_inv,
-        query_heads,
-        key_heads,
-        value_heads,
-        mask_table,
+        query_matrix,
+        key_all,
+        value_all,
+        codes,
         sub_normed,
         sub_inv,
         sub_in,
@@ -302,10 +499,10 @@
         attn_in,
         first_normed,
         first_inv,
-        query_heads,
-        key_heads,
-        value_heads,
-        mask_table,
+        query_matrix,
+        key_all,
+        value_all,
+        codes,
         sub_normed,
         sub_inv,
         sub_in,
@@ -319,7 +516,7 @@
     ) = kept_state
     seq_count, local_len, model_width = block_grad.shape
     row_count = seq_count * local_len
-    seq_len = key_heads.shape[1]
+    seq_len = key_all.shape[1]
     grad_low = block_grad.reshape(row_count, model_width)
     grad_full = grad_low.astype(jnp.float32)
     down_grad = outer_sum(ffn_mid, grad_low)
@@ -346,42 +543,19 @@
     )
     early_share = scatter_rows(early_rows)
     middle_share = scatter_rows(middle_rows)
-    heads = query_heads.shape[2]
-    weights_soft, row_top, row_total = probabilities(query_heads, key_heads, mask_table)
-    grad_heads = attended_low.reshape(seq_count, local_len, heads, HD)
-    soft_grad = jnp.einsum(
-        "sqhd,skhd->shqk", grad_heads, value_heads, preferred_element_type=jnp.float32
-    )
-    inner_sum = jnp.sum(weights_soft * soft_grad, -1, keepdims=True)
-    score_low = (weights_soft * (soft_grad - inner_sum)).astype(jnp.bfloat16)
-    root_scale = HD ** (-0.5)
-    query_low = (
-        (
-            jnp.einsum("shqk,skhd->sqhd", score_low, key_heads, preferred_element_type=jnp.float32)
-            * root_scale
-        )
-        .astype(jnp.bfloat16)
-        .reshape(row_count, -1)
-    )
-    key_part = (
-        jnp.einsum("shqk,sqhd->skhd", score_low, query_heads, preferred_element_type=jnp.float32)
-        * root_scale
-    )
-    value_part = jnp.einsum(
-        "shqk,sqhd->skhd",
-        weights_soft.astype(jnp.bfloat16),
-        grad_heads,
-        preferred_element_type=jnp.float32,
-    )
+    query_grad, key_part, value_part = attention_backward(
+        query_matrix.reshape(seq_count, local_len, model_width),
+        key_all,
+        value_all,
+        attended_low.reshape(seq_count, local_len, model_width),
+        codes,
+    )
+    query_low = query_grad.reshape(row_count, model_width)
     key_low = (
-        pair_reduce(key_part.reshape(seq_count, seq_len, -1), "context", 1)
-        .astype(jnp.bfloat16)
-        .reshape(row_count, -1)
+        pair_reduce(key_part, "context", 1).astype(jnp.bfloat16).reshape(row_count, model_width)
     )
     value_low = (
-        pair_reduce(value_part.reshape(seq_count, seq_len, -1), "context", 1)
-        .astype(jnp.bfloat16)
-        .reshape(row_count, -1)
+        pair_reduce(value_part, "context", 1).astype(jnp.bfloat16).reshape(row_count, model_width)
     )
     stacked = jnp.stack([query_low, key_low, value_low])
     early_share, stacked = lax.optimization_barrier((early_share, stacked))
@@ -472,9 +646,7 @@
     digits_full = digits_full.astype(jnp.int32)
     all_segments = digits_full[:, :patterns] * 32 + digits_full[:, patterns : 2 * patterns]
     all_dilations = digits_full[:, 2 * patterns :]
-    tallied_total = pattern_total(
-        query_position, key_position, all_segments, all_dilations, seq_len
-    )
+    codes = mask_codes(starts, query_position, key_position, all_segments, all_dilations, seq_len)
     w_out, w_up, w_down, w_qkv_full = lax.optimization_barrier((w_out, w_up, w_down, w_qkv_full))
     weights = (
         w_qkv_full,
@@ -488,9 +660,7 @@
         unit_bias_full.reshape(-1).astype(f32),
         unit_gain_full.reshape(-1).astype(f32),
     )
-    kept_state, layer_block = forward_pass(
-        block_in, starts, tallied_total, weights, query_position, key_position
-    )
+    kept_state, layer_block = forward_pass(block_in, codes, weights)
     layer_out = pair_gather(layer_block, "tensor", 0)
     grad_shares, input_block = backward_pass(kept_state, block_grad, weights)
     input_grad = pair_gather(input_block, "tensor", 0)

time: 846 us -> 872 us (1.031)
  Pallas kernels: 0 us -> 167 us
  matrix products: 242 us -> 97.2 us
  waiting for transfers between devices: 123 us -> 216 us
  other arithmetic: 149 us -> 94.4 us
  local copies, waits for them, and re-layouts: 296 us -> 262 us
    pallas_call x0 -> x2, Pallas kernels: none -> 167 us  [the longest x1 97.3 us: attention_backward(): pl.pallas_call(attention_bwd_kernel, grid=grid, in_specs=[query_spec, key...]
    dot_general x5 -> x0, matrix products: 101 us -> none  [the longest x1 35.2 us: backward_pass(): jnp.einsum('sqhd,skhd->shqk', grad_heads, value_heads, preferred_element_...]
    sub x1 -> x0, matrix products: 49.6 us -> none  [probabilities(): exponent = mask_table * jnp.exp(masked - row_top)]
    ppermute x4, waiting for transfers between devices: 41.2 us -> 90.1 us  [pair_gather(): other = lax.ppermute(block, axis_name, perm=[(0, 1), (1, 0)])]
    ppermute x2, waiting for transfers between devices: 9.52 us -> 52.8 us  [pair_reduce(): received = lax.ppermute(sent, axis_name, perm=[(0, 1), (1, 0)])]
    convert_element_type x3 -> x2, other arithmetic: 47.2 us -> 5.99 us  [the longest x1 3.84 us: backward_pass(): pair_reduce(key_part, 'context', 1).astype(jnp.bfloat16)]
    add x2 -> x0, other arithmetic: 25.5 us -> none  [the longest x1 25.4 us: pattern_total(): tallied_total = tallied_total + merged_heads.astype(jnp.float32)]
    convert_element_type x7 -> x0, local copies, waits for them, and re-layouts: 17.7 us -> none  [the longest x3 8.84 us: forward_pass(): projected[1].astype(jnp.bfloat16).reshape(seq_count, local_len, model_width)]
  transfers between devices with their start and end apart: 16 -> 16, of which waited for: 5 -> 9; matrix products, arithmetic and copies ran while one was open for 50% -> 22% of each run, Pallas kernels for 0% -> 19%
where the time goes in v4:
time: 872 us; the launch traced here: 862 us
  local copies, waits for them, and re-layouts  262 us (30%)
  waiting for transfers between devices  216 us (25%)
  Pallas kernels  167 us (19%)
  matrix products  97.2 us (11%)
  other arithmetic  94.4 us (11%)
  between operations  15.6 us (2%)
  starting transfers between devices  10.3 us (1%)
    pallas_call x1, Pallas kernels, attention_backward(): pl.pallas_call(attention_bwd_kernel, grid=grid, in_specs=[query_spec, key...  97.3 us
    ppermute x4, waiting for transfers between devices, pair_gather(): other = lax.ppermute(block, axis_name, perm=[(0, 1), (1, 0)])  90.1 us
    pallas_call x1, Pallas kernels, attention_forward(): pl.pallas_call(attention_fwd_kernel, grid=grid, in_specs=[query_spec, key...  69.8 us
    ppermute x2, waiting for transfers between devices, pair_reduce(): received = lax.ppermute(sent, axis_name, perm=[(0, 1), (1, 0)])  52.8 us
    all_gather x1, waiting for transfers between devices, gather_packed(): lax.all_gather(flat, ('shard', 'tensor'), axis=0, tiled=False)  50.3 us
    unnamed x153, local copies, waits for them, and re-layouts  42.6 us
    reshape x5, local copies, waits for them, and re-layouts, disassemble(): pieces = full.reshape(split_shape)  35.9 us
    dot_general x3, matrix products, back_dot(): lax.dot_general(left_rows, weight_rows, (((1,), (1,)), ((), ())), preferr...  31.1 us
  transfers between devices with their start and end apart: 16, of which 9 were waited for; matrix products, arithmetic and copies ran while one was open for 22% of the time, Pallas kernels for 19%

profile of v4, /device:TPU:0, one launch (start us, length us, event | category | flops | bytes accessed | tf_op | source)
XLA Modules:
  0.0 862.5 jit_solution(10714965857845564099)
XLA Ops:
  17.2 50.3 %all-gather.8.cloned.1.call-done = bf16[16,880,128]{2,1,0:T(8,128)(2,1)} async-done(((bf16[1,880,128]{2,1,0:T(8,128)(2,1)}), bf16[16,880,128]{2,1,0:T(8,128)(2,1)}) %all-gather.8.cloned.1.call-update) | async-done | bytes 3604496 | tf_op jit(solution)/shard_map/all_gather | solution.py:344
  67.5 6.6 reshape.2051
  76.2 4.7 reshape.2104
  80.9 7.3 copy.177
  88.2 9.0 %reshape.2053 = bf16[3,768,768]{2,1,0:T(8,128)(2,1)} reshape(bf16[3,8,96,2,384]{4,3,2,1,0:T(2,128)(2,1)} %copy.177) | data formatting | bytes 7077888 | tf_op jit(solution)/shard_map/reshape | solution.py:328
  116.2 6.6 convolution_bitcast_fusion
  149.7 20.6 %collective-permute-done = bf16[2,512,768]{2,1,0:T(8,128)(2,1)} collective-permute-done((bf16[2,512,768]{2,1,0:T(8,128)(2,1)}, bf16[2,512,768]{2,1,0:T(8,128)(2,1)}, u32[]{:S(2)}, u32[]{:S(2)}) %collective-permute-start) | collective-permute-done | bytes 1572896 | tf_op jit(solution)/shard_map/ppermute | solution.py:357
  170.3 3.9 maximum_select_fusion.k_ref
  174.2 29.1 %collective-permute-done.1 = bf16[2,512,768]{2,1,0:T(8,128)(2,1)} collective-permute-done((bf16[2,512,768]{2,1,0:T(8,128)(2,1)}, bf16[2,512,768]{2,1,0:T(8,128)(2,1)}, u32[]{:S(2)}, u32[]{:S(2)}) %collective-permute-start.1) | collective-permute-done | bytes 1572896 | tf_op jit(solution)/shard_map/ppermute | solution.py:357
  203.3 4.9 maximum_select_fusion.1.v_ref
  208.2 69.8 %shard_map.256 = f32[2,512,768]{2,1,0:T(8,128)S(1)} custom-call(bf16[2,512,768]{2,1,0:T(8,128)(2,1)S(1)} %add_convert_fusion.4.q_ref, bf16[2,1024,768]{2,1,0:T(8,128)(2,1)} %maximum_select_fusion.k_ref, bf16[2,1024,768]{2,1,0:T(8,128)(2,1)} %maximum_select_fusion.1.v_ref, s32[12,512,8]{2,1,0:T(8,128)} %copy.185.patq_ref, s32[12,8,1024]{2,1,0:T(8,128)S(1)} %stack.55.patk_ref, ...), custom_call_target="tpu_custom_call" | custom-call | flops 6442450944 | bytes 17301504 | tf_op jit(solution)/shard_map/pallas_call | solution.py:216
  292.2 9.4 %copy.189 = bf16[8,2,96,1536]{3,1,2,0:T(2,128)(2,1)} copy(bf16[8,2,96,1536]{3,2,1,0:T(8,128)(2,1)} %bitcast.211) | data formatting | bytes 9437184 | tf_op jit(solution)/shard_map/reshape | solution.py:335
  301.6 5.7 copy.231
  307.3 7.7 reshape.2060
  315.1 7.7 copy.194
  322.8 5.7 copy.232
  328.5 9.8 %fusion.57 = (f32[1024]{0:T(1024)S(1)}, f32[1024,3072]{1,0:T(8,128)S(1)}) fusion(f32[3072]{0:T(1024)S(1)} %copy-done.26, bf16[768,3072]{1,0:T(8,128)(2,1)} %bitcast.212, f32[1024,768]{1,0:T(8,128)S(1)} %get-tuple-element.165, f32[768]{0:T(1024)S(1)} %copy-done.38, f32[1024]{0:T(1024)S(1)} %copy-done.39, f32[1024]{0:T(1024)S(1)} %broadcast_multiply_fusion.9), kind=kOutput, calls=%fused_computation.255 | convolution fusion | flops 4866440192 | bytes 20474880 | tf_op jit(solution)/shard_map/dot_general | solution.py:467
  338.3 5.7 multiply_reduce_fusion.2
  344.1 18.2 %multiply_reduce_fusion = (bf16[3072]{0:T(1024)(128)(2,1)}, f32[1024]{0:T(1024)S(1)}, f32[1024]{0:T(1024)S(1)}, bf16[1024,3072]{1,0:T(8,128)(2,1)}, f32[1024,3072]{1,0:T(8,128)}) fusion(f32[1024]{0:T(1024)S(1)} %add_rsqrt_fusion, f32[1024]{0:T(1024)S(1)} %broadcast_multiply_fusion.2, f32[1024,3072]{1,0:T(8,128)S(1)} %get-tuple-element.167, ...), kind=kOutput, calls=%fused_computation.9 | convolution fusion | flops 4891601920 | bytes 37795840 | tf_op jit(solution)/shard_map/dot_general | solution.py:64
  362.3 16.4 %fusion.58 = (bf16[3072]{0:T(1024)(128)(2,1)}, bf16[1024,3072]{1,0:T(8,128)(2,1)S(1)}) fusion(f32[1024]{0:T(1024)S(1)} %broadcast_multiply_fusion, f32[1024]{0:T(1024)S(1)} %broadcast_multiply_fusion.2, f32[1024,3072]{1,0:T(8,128)S(1)} %get-tuple-element.167, f32[3072]{0:T(1024)S(1)} %copy-done.26, f32[1024]{0:T(1024)S(1)} %broadcast_multiply_fusion.1, ...), kind=kLoop, calls=%fused_computation.256 | loop fusion | flops 94368768 | bytes 31504384 | tf_op jit(solution)/shard_map/reduce_sum | solution.py:529
  378.7 8.6 multiply_reduce_fusion.5
  387.3 7.6 convolution_convert_fusion
  400.9 4.3 multiply_reduce_fusion.4
  405.3 12.0 %reshape.2065 = bf16[8,96,2,1536]{3,2,1,0:T(2,128)(2,1)} reshape(bf16[768,3072]{1,0:T(8,128)(2,1)} %convolution_convert_fusion) | data formatting | bytes 9437184 | tf_op jit(solution)/shard_map/reshape | solution.py:398
  417.3 5.5 copy.241
  422.8 9.9 %concatenate.58 = bf16[16,1152,128]{2,1,0:T(8,128)(2,1)} reshape(bf16[8,2,96,1536]{3,2,1,0:T(8,128)(2,1)} %bitcast.196) | data formatting | bytes 9437184 | tf_op jit(solution)/shard_map/concatenate | solution.py:410
  442.4 4.4 reshape.2068
  448.7 9.2 %convolution_convert_fusion.1 = bf16[3072,768]{1,0:T(8,128)(2,1)} fusion(bf16[1024,3072]{1,0:T(8,128)(2,1)} %get-tuple-element.130, bf16[1024,768]{1,0:T(8,128)(2,1)} %bitcast.208), kind=kOutput, calls=%fused_computation.18 | convolution fusion | flops 4834197504 | bytes 12582912 | tf_op jit(solution)/shard_map/dot_general | solution.py:58
  457.9 6.6 copy.195
  464.6 11.6 %reshape.2064 = bf16[2,1536,8,96]{1,0,3,2:T(2,128)(2,1)} reshape(bf16[3072,768]{0,1:T(8,128)(2,1)} %copy.195) | data formatting | bytes 9437184 | tf_op jit(solution)/shard_map/reshape | solution.py:398
  476.2 12.0 %copy.196 = bf16[8,2,1536,96]{3,2,1,0:T(8,128)(2,1)} copy(bf16[8,2,1536,96]{2,1,3,0:T(2,128)(2,1)} %bitcast.197) | data formatting | bytes 9437184 | tf_op jit(solution)/shard_map/transpose | solution.py:401
  488.2 12.9 %concatenate.57 = bf16[16,1152,128]{2,1,0:T(8,128)(2,1)} reshape(bf16[8,2,1536,96]{3,2,1,0:T(8,128)(2,1)} %copy.196) | data formatting | bytes 9437184 | tf_op jit(solution)/shard_map/concatenate | solution.py:410
  501.1 7.6 pad_maximum_fusion
  508.7 3.9 multiply_convert_fusion.1
  518.1 97.3 %shard_map.257 = (bf16[2,512,768]{2,1,0:T(8,128)(2,1)S(1)}, f32[2,1024,768]{2,1,0:T(8,128)}, f32[2,1024,768]{2,1,0:T(8,128)}) custom-call(bf16[2,512,768]{2,1,0:T(8,128)(2,1)S(1)} %copy-done.3, bf16[2,1024,768]{2,1,0:T(8,128)(2,1)} %maximum_select_fusion.k_ref, bf16[2,1024,768]{2,1,0:T(8,128)(2,1)} %maximum_select_fusion.1.v_ref, ...), custom_call_target="tpu_custom_call" | custom-call | flops 16106127360 | bytes 40894464 | tf_op jit(solution)/shard_map/pallas_call | solution.py:243
  628.7 27.5 %collective-permute-done.4 = bf16[2,512,768]{2,1,0:T(8,128)(2,1)} collective-permute-done((bf16[2,512,768]{2,1,0:T(8,128)(2,1)}, bf16[2,512,768]{2,1,0:T(8,128)(2,1)}, u32[]{:S(2)}, u32[]{:S(2)}) %collective-permute-start.4) | collective-permute-done | bytes 1572896 | tf_op jit(solution)/shard_map/ppermute | solution.py:373
  656.2 3.9 fusion.60
  662.9 25.2 %collective-permute-done.3 = bf16[2,512,768]{2,1,0:T(8,128)(2,1)} collective-permute-done((bf16[2,512,768]{2,1,0:T(8,128)(2,1)}, bf16[2,512,768]{2,1,0:T(8,128)(2,1)}, u32[]{:S(2)}, u32[]{:S(2)}) %collective-permute-start.3) | collective-permute-done | bytes 1572896 | tf_op jit(solution)/shard_map/ppermute | solution.py:373
  698.1 8.5 convert_bitcast_fusion
  706.6 4.3 copy.207
  719.6 4.2 constant_dynamic-update-slice_fusion
  724.9 8.6 fusion.7
  747.7 10.2 %add_convert_fusion.2 = bf16[1024,768]{1,0:T(8,128)(2,1)} fusion(f32[1024,768]{1,0:T(8,128)} %copy-done.14, bf16[1024,3072]{1,0:T(8,128)(2,1)} %get-tuple-element.130, bf16[3072,768]{0,1:T(8,128)(2,1)} %bitcast.210, f32[768]{0:T(1024)S(1)} %add.710), kind=kOutput, calls=%fused_computation.60 | convolution fusion | flops 4834197504 | bytes 15731712 | tf_op jit(solution)/shard_map/dot_general | solution.py:472
  760.7 4.0 fusion.19
  765.9 39.2 %collective-permute-done.2 = bf16[2,512,768]{2,1,0:T(8,128)(2,1)} collective-permute-done((bf16[2,512,768]{2,1,0:T(8,128)(2,1)}, bf16[2,512,768]{2,1,0:T(8,128)(2,1)}, u32[]{:S(2)}, u32[]{:S(2)}) %collective-permute-start.2) | collective-permute-done | bytes 1572896 | tf_op jit(solution)/shard_map/ppermute | solution.py:357
  805.1 4.3 maximum_select_fusion.2
  813.9 21.8 %reduce-scatter.10.cloned.1.call-done = bf16[1,872,128]{2,1,0:T(8,128)(2,1)} async-done(((bf16[16,872,128]{2,1,0:T(8,128)(2,1)}), bf16[1,872,128]{2,1,0:T(8,128)(2,1)}) %reduce-scatter.10.cloned.1.call-update) | async-done | bytes 223248
  842.1 6.9 slice.187
  (347 shorter events, 165.4 us)
Async XLA Ops:
  7.2 93.0 %copy-start = (s32[4,2]{0,1:T(2,128)S(1)}, s32[4,2]{0,1:T(2,128)}, u32[]{:S(2)}) copy-start(s32[4,2]{0,1:T(2,128)} %param.21) | copy-start | bytes 100
  7.2 60.3 %all-gather.8.cloned.1.call-start = ((), (), s32[]{:S(2)}) async-start(), calls=%async_computation.3 | async-start | bytes 3829760 | tf_op jit(solution)/shard_map/all_gather | solution.py:344
  17.2 266.9 %all-gather.10.cloned.1.call-start = ((), (), s32[]{:S(2)}) async-start(), calls=%async_computation.6 | async-start | bytes 1253376 | tf_op jit(solution)/shard_map/all_gather | solution.py:334
  88.2 9.9 %copy-start.11 = (bf16[4,512,768]{2,1,0:T(8,128)(2,1)S(1)}, bf16[4,512,768]{2,1,0:T(8,128)(2,1)}, u32[]{:S(2)}) copy-start(bf16[4,512,768]{2,1,0:T(8,128)(2,1)} %param.19) | copy-start | bytes 9437188
  97.2 195.0 %all-gather.12.cloned.1.call-start = ((), (), s32[]{:S(2)}) async-start(), calls=%async_computation.7 | async-start | bytes 5013504 | tf_op jit(solution)/shard_map/all_gather | solution.py:334
  98.0 209.4 %all-gather.14.cloned.1.call-start = ((), (), s32[]{:S(2)}) async-start(), calls=%async_computation.8 | async-start | bytes 5013504 | tf_op jit(solution)/shard_map/all_gather | solution.py:334
  102.4 7.9 slice-start.1
  105.9 592.3 %reduce-scatter.6.cloned.1.call-start = ((), (), s32[]{:S(2)}) async-start(), calls=%async_computation.4 | async-start | bytes 10027008 | tf_op jit(solution)/shard_map/reduce_scatter | solution.py:419
  116.2 6.6 copy-start.21
  132.7 6.0 copy-start.34
  132.7 37.6 %collective-permute-start = (bf16[2,512,768]{2,1,0:T(8,128)(2,1)}, bf16[2,512,768]{2,1,0:T(8,128)(2,1)}, u32[]{:S(2)}, u32[]{:S(2)}) collective-permute-start(bf16[2,512,768]{2,1,0:T(8,128)(2,1)} %bitcast.203), channel_id=1, source_target_pairs={{0,2},{2,0},{1,3},{3,1},{4,6},{6,4},{5,7},{7,5},{8,10},{10,8},{9,1... | collective-permute-start | bytes 4718600 | tf_op jit(solution)/shard_map/ppermute | solution.py:357
  137.5 65.8 %collective-permute-start.1 = (bf16[2,512,768]{2,1,0:T(8,128)(2,1)}, bf16[2,512,768]{2,1,0:T(8,128)(2,1)}, u32[]{:S(2)}, u32[]{:S(2)}) collective-permute-start(bf16[2,512,768]{2,1,0:T(8,128)(2,1)} %add_convert_fusion.3), channel_id=1, source_target_pairs={{0,2},{2,0},{1,3},{3,1},{4,6},{6,4},{5,7},{7,5},{8,10},{10,8},{9,1... | collective-permute-start | bytes 4718600 | tf_op jit(solution)/shard_map/ppermute | solution.py:357
  144.8 25.5 %copy-start.16 = (bf16[1,1024,768]{2,1,0:T(8,128)(2,1)S(1)}, bf16[1,1024,768]{2,1,0:T(8,128)(2,1)}, u32[]{:S(2)}) copy-start(bf16[1,1024,768]{2,1,0:T(8,128)(2,1)} %copy.182) | copy-start | bytes 4718596
  149.7 58.5 %copy-start.2 = (bf16[2,512,768]{2,1,0:T(8,128)(2,1)}, bf16[2,512,768]{2,1,0:T(8,128)(2,1)S(1)}, u32[]{:S(2)}) copy-start(bf16[2,512,768]{2,1,0:T(8,128)(2,1)S(1)} %add_convert_fusion.4.q_ref) | copy-start | bytes 4718596
  174.2 34.0 %copy-start.4 = (s32[2,512,8]{2,1,0:T(8,128)S(1)}, s32[2,512,8]{2,1,0:T(8,128)}, u32[]{:S(2)}) copy-start(s32[2,512,8]{2,1,0:T(8,128)} %pad.17.pcq_ref) | copy-start | bytes 98308
  174.2 34.0 %copy-start.6 = (s32[2,8,1024]{2,1,0:T(8,128)S(1)}, s32[2,8,1024]{2,1,0:T(8,128)}, u32[]{:S(2)}) copy-start(s32[2,8,1024]{2,1,0:T(8,128)} %pad.18.pck_ref) | copy-start | bytes 196612
  290.7 96.6 %copy-start.14 = (f32[1024,768]{1,0:T(8,128)}, f32[1024,768]{1,0:T(8,128)S(1)}, u32[]{:S(2)}) copy-start(f32[1024,768]{1,0:T(8,128)S(1)} %get-tuple-element.165) | copy-start | bytes 9437188
  322.8 5.7 copy-start.26
  322.8 5.7 copy-start.38
  322.8 5.7 copy-start.39
  338.3 5.8 copy-start.29
  387.3 7.7 copy-start.17
  512.6 246.0 %reduce-scatter.8.cloned.1.call-start = ((), (), s32[]{:S(2)}) async-start(), calls=%async_computation.5 | async-start | bytes 1253376 | tf_op jit(solution)/shard_map/reduce_scatter | solution.py:419
  615.4 8.5 copy-start.44
  615.4 8.6 copy-start.64
  615.4 9.3 %copy-start.46 = (bf16[768]{0:T(1024)(128)(2,1)S(1)}, bf16[768]{0:T(1024)(128)(2,1)}, u32[]{:S(2)}) copy-start(bf16[768]{0:T(1024)(128)(2,1)} %get-tuple-element.126) | copy-start | bytes 4612
  615.4 9.5 %copy-start.37 = (bf16[3072]{0:T(1024)(128)(2,1)S(1)}, bf16[3072]{0:T(1024)(128)(2,1)}, u32[]{:S(2)}) copy-start(bf16[3072]{0:T(1024)(128)(2,1)} %get-tuple-element.122) | copy-start | bytes 18436
  615.4 10.3 %copy-start.48 = (bf16[3072]{0:T(1024)(128)(2,1)S(1)}, bf16[3072]{0:T(1024)(128)(2,1)}, u32[]{:S(2)}) copy-start(bf16[3072]{0:T(1024)(128)(2,1)} %get-tuple-element.97) | copy-start | bytes 18436
  615.4 11.2 %copy-start.47 = (bf16[768]{0:T(1024)(128)(2,1)S(1)}, bf16[768]{0:T(1024)(128)(2,1)}, u32[]{:S(2)}) copy-start(bf16[768]{0:T(1024)(128)(2,1)} %get-tuple-element.100) | copy-start | bytes 4612
  618.6 37.6 %collective-permute-start.4 = (bf16[2,512,768]{2,1,0:T(8,128)(2,1)}, bf16[2,512,768]{2,1,0:T(8,128)(2,1)}, u32[]{:S(2)}, u32[]{:S(2)}) collective-permute-start(bf16[2,512,768]{2,1,0:T(8,128)(2,1)} %dynamic-slice_convert_fusion), channel_id=1, source_target_pairs={{0,2},{2,0},{1,3},{3,1},{4,6},{6,4},{5,7},{7,5},{8,10},{10,8},{9,1... | collective-permute-start | bytes 4718600 | tf_op jit(solution)/shard_map/ppermute | solution.py:373
  623.3 64.9 %collective-permute-start.3 = (bf16[2,512,768]{2,1,0:T(8,128)(2,1)}, bf16[2,512,768]{2,1,0:T(8,128)(2,1)}, u32[]{:S(2)}, u32[]{:S(2)}) collective-permute-start(bf16[2,512,768]{2,1,0:T(8,128)(2,1)} %dynamic-slice_convert_fusion.1), channel_id=1, source_target_pairs={{0,2},{2,0},{1,3},{3,1},{4,6},{6,4},{5,7},{7,5},{8,10},{10,8},{9,1... | collective-permute-start | bytes 4718600 | tf_op jit(solution)/shard_map/ppermute | solution.py:373
  628.6 207.1 %reduce-scatter.10.cloned.1.call-start = ((), (), s32[]{:S(2)}) async-start(), calls=%async_computation.9 | async-start | bytes 3794944
  719.6 5.3 copy-start.30
  719.6 5.3 copy-start.31
  724.9 8.7 %copy-start.45 = (bf16[1,8,96]{2,1,0:T(8,128)(2,1)S(1)}, bf16[1,8,96]{2,1,0:T(8,128)(2,1)}, u32[]{:S(2)}) copy-start(bf16[1,8,96]{2,1,0:T(8,128)(2,1)} %stack.58) | copy-start | bytes 4612
  724.9 11.9 %copy-start.40 = (bf16[16,96]{1,0:T(8,128)(2,1)S(1)}, bf16[16,96]{1,0:T(8,128)(2,1)}, u32[]{:S(2)}) copy-start(bf16[16,96]{1,0:T(8,128)(2,1)} %reshape.2075) | copy-start | bytes 9220
  724.9 14.6 %copy-start.35 = (bf16[16,192]{1,0:T(8,128)(2,1)S(1)}, bf16[16,192]{1,0:T(8,128)(2,1)}, u32[]{:S(2)}) copy-start(bf16[16,192]{1,0:T(8,128)(2,1)} %reshape.2077) | copy-start | bytes 18436
  724.9 16.1 %copy-start.36 = (bf16[16,192]{1,0:T(8,128)(2,1)S(1)}, bf16[16,192]{1,0:T(8,128)(2,1)}, u32[]{:S(2)}) copy-start(bf16[16,192]{1,0:T(8,128)(2,1)} %reshape.2078) | copy-start | bytes 18436
  747.7 13.0 %copy-start.10 = (f32[1024,768]{1,0:T(8,128)S(1)}, f32[1024,768]{1,0:T(8,128)}, u32[]{:S(2)}) copy-start(f32[1024,768]{1,0:T(8,128)} %copy-done.9) | copy-start | bytes 9437188
  758.0 47.1 %collective-permute-start.2 = (bf16[2,512,768]{2,1,0:T(8,128)(2,1)}, bf16[2,512,768]{2,1,0:T(8,128)(2,1)}, u32[]{:S(2)}, u32[]{:S(2)}) collective-permute-start(bf16[2,512,768]{2,1,0:T(8,128)(2,1)} %bitcast.24), channel_id=1, source_target_pairs={{0,1},{1,0},{2,3},{3,2},{4,5},{5,4},{6,7},{7,6},{8,9},{9,8},{10,11... | collective-permute-start | bytes 4718600 | tf_op jit(solution)/shard_map/ppermute | solution.py:357
  758.6 50.8 %collective-permute-start.7 = (bf16[288,128]{1,0:T(8,128)(2,1)}, bf16[288,128]{1,0:T(8,128)(2,1)S(1)}, u32[]{:S(2)}, u32[]{:S(2)}) collective-permute-start(bf16[288,128]{1,0:T(8,128)(2,1)} %bitcast.229), channel_id=1, source_target_pairs={{0,2},{2,0},{1,3},{3,1},{4,6},{6,4},{5,7},{7,5},{8,10},{10,8},{9,1... | collective-permute-start | bytes 221192 | tf_op jit(solution)/shard_map/ppermute | solution.py:380
  760.1 50.3 %collective-permute-start.8 = (bf16[2304,128]{1,0:T(8,128)(2,1)}, bf16[2304,128]{1,0:T(8,128)(2,1)}, u32[]{:S(2)}, u32[]{:S(2)}) collective-permute-start(bf16[2304,128]{1,0:T(8,128)(2,1)} %bitcast.221), channel_id=1, source_target_pairs={{0,2},{2,0},{1,3},{3,1},{4,6},{6,4},{5,7},{7,5},{8,10},{10,8},{9,1... | collective-permute-start | bytes 1769480 | tf_op jit(solution)/shard_map/ppermute | solution.py:380
  764.7 44.8 %copy-start.28 = (bf16[1,288,128]{2,1,0:T(8,128)(2,1)S(1)}, bf16[1,288,128]{2,1,0:T(8,128)(2,1)}, u32[]{:S(2)}) copy-start(bf16[1,288,128]{2,1,0:T(8,128)(2,1)} %reduce-scatter.8.cloned.1.call-done) | copy-start | bytes 221188
  764.7 45.7 %copy-start.24 = (bf16[1,2304,128]{2,1,0:T(8,128)(2,1)S(1)}, bf16[1,2304,128]{2,1,0:T(8,128)(2,1)}, u32[]{:S(2)}) copy-start(bf16[1,2304,128]{2,1,0:T(8,128)(2,1)} %reduce-scatter.6.cloned.1.call-done) | copy-start | bytes 1769476
  764.7 73.6 %collective-permute-start.5 = (bf16[2,512,768]{2,1,0:T(8,128)(2,1)}, bf16[2,512,768]{2,1,0:T(8,128)(2,1)S(1)}, u32[]{:S(2)}, u32[]{:S(2)}) collective-permute-start(bf16[2,512,768]{2,1,0:T(8,128)(2,1)} %bitcast.36), channel_id=1, source_target_pairs={{0,1},{1,0},{2,3},{3,2},{4,5},{5,4},{6,7},{7,6},{8,9},{9,8},{10,11... | collective-permute-start | bytes 4718600 | tf_op jit(solution)/shard_map/ppermute | solution.py:357
  835.7 6.2 copy-start.25
  835.7 6.2 collective-permute-start.6
  842.0 13.2 %copy-start.1 = (s32[4,2]{0,1:T(2,128)S(1)}, s32[4,2]{0,1:T(2,128)}, u32[]{:S(2)}) copy-start(s32[4,2]{0,1:T(2,128)} %param.21) | copy-start | bytes 100
  (35 other events, 87.5 us)
Sparse Core Ops, SparseCore 0:
  17.3 50.1 all-gather.7
  97.4 35.6 all-gather.9
  135.4 52.5 all-gather.11
  190.2 51.6 all-gather.13
  512.8 109.8 reduce-scatter.5
  628.7 56.6 reduce-scatter.7
  747.1 88.5 reduce-scatter.9

commit v5 on v4

--- a/solution.py
+++ b/solution.py
@@ -10,6 +10,7 @@
 HD = 64
 FF = 3072
 PIECE = 256
+PIECES = 2
 
 
 epsilon = 1e-05
@@ -301,6 +302,77 @@
     return (patq, patk, pcq.astype(jnp.int32), pck.astype(jnp.int32))
 
 
+def code_part(codes, begin, end, key_end):
+    patq, patk, pcq, pck = codes
+    return (patq[:, begin:end], patk[:, :, :key_end], pcq[:, begin:end], pck[:, :, :key_end])
+
+
+def split_attention_forward(query, keys, values, codes, span):
+    if span is None:
+        return attention_forward(query, keys, values, codes)
+    head = attention_forward(
+        query[:, :span], keys[:, :span], values[:, :span], code_part(codes, 0, span, span)
+    )
+    seq_len = keys.shape[1]
+    tail = attention_forward(
+        query[:, span:], keys, values, code_part(codes, span, query.shape[1], seq_len)
+    )
+    return jnp.concatenate([head, tail], 1)
+
+
+def split_attention_backward(query, keys, values, grad_out, codes, span):
+    if span is None:
+        return attention_backward(query, keys, values, grad_out, codes)
+    seq_len = keys.shape[1]
+    head_q, head_k, head_v = attention_backward(
+        query[:, :span],
+        keys[:, :span],
+        values[:, :span],
+        grad_out[:, :span],
+        code_part(codes, 0, span, span),
+    )
+    tail_q, tail_k, tail_v = attention_backward(
+        query[:, span:],
+        keys,
+        values,
+        grad_out[:, span:],
+        code_part(codes, span, query.shape[1], seq_len),
+    )
+    padding = ((0, 0), (0, seq_len - span), (0, 0))
+    return (
+        jnp.concatenate([head_q, tail_q], 1),
+        tail_k + jnp.pad(head_k, padding),
+        tail_v + jnp.pad(head_v, padding),
+    )
+
+
+def spread_sequence(block, local_len):
+    me_c = lax.axis_index("context")
+    me_t = lax.axis_index("tensor")
+    swap = [(0, 1), (1, 0)]
+    kept = lax.dynamic_slice_in_dim(block, me_c * local_len, local_len, 1)
+    other = lax.dynamic_slice_in_dim(block, (1 - me_c) * local_len, local_len, 1)
+    from_context = lax.ppermute(other, "context", perm=swap)
+    from_tensor = lax.ppermute(kept, "tensor", perm=swap)
+    from_corner = lax.ppermute(other, ("context", "tensor"), perm=[(0, 3), (3, 0), (1, 2), (2, 1)])
+    first_c = me_c == 0
+    own_pair = jnp.where(
+        first_c,
+        jnp.concatenate([kept, from_context], 0),
+        jnp.concatenate([from_context, kept], 0),
+    )
+    far_pair = jnp.where(
+        first_c,
+        jnp.concatenate([from_tensor, from_corner], 0),
+        jnp.concatenate([from_corner, from_tensor], 0),
+    )
+    return jnp.where(
+        me_t == 0,
+        jnp.concatenate([own_pair, far_pair], 0),
+        jnp.concatenate([far_pair, own_pair], 0),
+    )
+
+
 def assemble(stacked, shard_dim, tensor_dim):
     ns, nt = stacked.shape[0], stacked.shape[1]
     if shard_dim is None:
@@ -439,7 +511,7 @@
     return pieces
 
 
-def forward_pass(block_in, codes, weights):
+def forward_pass(block_in, codes, weights, span):
     w_qkv, w_out, w_up, w_down, norm_gains, out_biases, head_biases, head_gain, unit_bias, unit_gain = weights
     seq_count, local_len, model_width = block_in.shape
     row_count = seq_count * local_len
@@ -452,10 +524,13 @@
     values_local = (projected[2] + head_biases[1]).astype(jnp.bfloat16).reshape(
         seq_count, local_len, model_width
     )
-    key_all = pair_gather(keys_local, "context", 1)
-    value_all = pair_gather(values_local, "context", 1)
-    attended = attention_forward(
-        query_matrix.reshape(seq_count, local_len, model_width), key_all, value_all, codes
+    if span is None:
+        key_all = pair_gather(keys_local, "context", 1)
+        value_all = pair_gather(values_local, "context", 1)
+    else:
+        key_all, value_all = keys_local, values_local
+    attended = split_attention_forward(
+        query_matrix.reshape(seq_count, local_len, model_width), key_all, value_all, codes, span
     ).reshape(row_count, model_width)
     sub_normed, sub_inv, sub_out = norm_rows(attended, head_gain)
     sub_in = sub_out.astype(jnp.bfloat16)
@@ -493,7 +568,7 @@
     return (kept_state, layer_out.reshape(seq_count, local_len, model_width))
 
 
-def backward_pass(kept_state, block_grad, weights):
+def backward_pass(kept_state, block_grad, weights, span):
     w_qkv, w_out, w_up, w_down, norm_gains, out_biases, head_biases, head_gain, unit_bias, unit_gain = weights
     (
         attn_in,
@@ -543,20 +618,23 @@
     )
     early_share = scatter_rows(early_rows)
     middle_share = scatter_rows(middle_rows)
-    query_grad, key_part, value_part = attention_backward(
+    query_grad, key_part, value_part = split_attention_backward(
         query_matrix.reshape(seq_count, local_len, model_width),
         key_all,
         value_all,
         attended_low.reshape(seq_count, local_len, model_width),
         codes,
-    )
+        span,
+    )
+    if span is not None:
+        key_part = key_part.reshape(row_count, model_width)
+        value_part = value_part.reshape(row_count, model_width)
     query_low = query_grad.reshape(row_count, model_width)
-    key_low = (
-        pair_reduce(key_part, "context", 1).astype(jnp.bfloat16).reshape(row_count, model_width)
-    )
-    value_low = (
-        pair_reduce(value_part, "context", 1).astype(jnp.bfloat16).reshape(row_count, model_width)
-    )
+    if span is None:
+        key_part = pair_reduce(key_part, "context", 1)
+        value_part = pair_reduce(value_part, "context", 1)
+    key_low = key_part.astype(jnp.bfloat16).reshape(row_count, model_width)
+    value_low = value_part.astype(jnp.bfloat16).reshape(row_count, model_width)
     stacked = jnp.stack([query_low, key_low, value_low])
     early_share, stacked = lax.optimization_barrier((early_share, stacked))
     qkv_grad = jnp.einsum("rd,jre->jde", attn_in, stacked, preferred_element_type=jnp.float32)
@@ -605,14 +683,41 @@
 ):
     local_seqs, local_len, model_width = inputs.shape
     tensor_count = lax.axis_size("tensor")
-    mine = local_seqs // tensor_count
-    first_seq = lax.axis_index("tensor") * mine
-    block_in = lax.dynamic_slice_in_dim(inputs, first_seq, mine, 0)
-    block_grad = lax.dynamic_slice_in_dim(out_grad, first_seq, mine, 0)
-    starts = lax.dynamic_slice_in_dim(picture_starts, first_seq, mine, 0)
-    seq_len = local_len * lax.axis_size("context")
-    query_position = lax.axis_index("context") * local_len + jnp.arange(local_len, dtype=jnp.int32)
+    context_count = lax.axis_size("context")
+    seq_len = local_len * context_count
     key_position = jnp.arange(seq_len, dtype=jnp.int32)
+    whole = context_count == 2 and tensor_count == 2 and local_seqs == 4
+    if whole:
+        span = seq_len // PIECES
+        me_c = lax.axis_index("context")
+        own_seq = lax.axis_index("tensor") * context_count + me_c
+        partner_seq = lax.axis_index("tensor") * context_count + 1 - me_c
+        swap = [(0, 1), (1, 0)]
+
+        def own_sequence(rows):
+            kept = lax.dynamic_slice_in_dim(rows, own_seq, 1, 0)
+            sent = lax.dynamic_slice_in_dim(rows, partner_seq, 1, 0)
+            received = lax.ppermute(sent, "context", perm=swap)
+            return jnp.where(
+                me_c == 0,
+                jnp.concatenate([kept, received], 1),
+                jnp.concatenate([received, kept], 1),
+            )
+
+        block_in = own_sequence(inputs)
+        block_grad = own_sequence(out_grad)
+        starts = lax.dynamic_slice_in_dim(picture_starts, own_seq, 1, 0)
+        query_position = key_position
+    else:
+        span = None
+        mine = local_seqs // tensor_count
+        first_seq = lax.axis_index("tensor") * mine
+        block_in = lax.dynamic_slice_in_dim(inputs, first_seq, mine, 0)
+        block_grad = lax.dynamic_slice_in_dim(out_grad, first_seq, mine, 0)
+        starts = lax.dynamic_slice_in_dim(picture_starts, first_seq, mine, 0)
+        query_position = lax.axis_index("context") * local_len + jnp.arange(
+            local_len, dtype=jnp.int32
+        )
     spans = jnp.array([seq_len * part // 8 for part in span_parts], jnp.int32)
     rates = jnp.array(dilation_rates, jnp.int32)
     segment_kept = segment_offsets % spans
@@ -660,10 +765,16 @@
         unit_bias_full.reshape(-1).astype(f32),
         unit_gain_full.reshape(-1).astype(f32),
     )
-    kept_state, layer_block = forward_pass(block_in, codes, weights)
-    layer_out = pair_gather(layer_block, "tensor", 0)
-    grad_shares, input_block = backward_pass(kept_state, block_grad, weights)
-    input_grad = pair_gather(input_block, "tensor", 0)
+    kept_state, layer_block = forward_pass(block_in, codes, weights, span)
+    if whole:
+        layer_out = spread_sequence(layer_block, local_len)
+    else:
+        layer_out = pair_gather(layer_block, "tensor", 0)
+    grad_shares, input_block = backward_pass(kept_state, block_grad, weights, span)
+    if whole:
+        input_grad = spread_sequence(input_block, local_len)
+    else:
+        input_grad = pair_gather(input_block, "tensor", 0)
     (
         down_share,
         up_share,

time: 872 us -> 747 us (0.86)
  waiting for transfers between devices: 216 us -> 129 us
  Pallas kernels: 167 us -> 144 us
  local copies, waits for them, and re-layouts: 262 us -> 245 us
    ppermute x6 -> x8, waiting for transfers between devices: 143 us -> 68.9 us  [the longest x2 40.7 us: spread_sequence(): from_context = lax.ppermute(other, 'context', perm=swap)]
    unnamed x8, waiting for transfers between devices: 22.6 us -> 0.8 us
    pallas_call x1 -> x2, Pallas kernels: 97.3 us -> 80.8 us  [attention_backward(): pl.pallas_call(attention_bwd_kernel, grid=grid, in_specs=[query_spec, key...]
    unnamed x153 -> x173, local copies, waits for them, and re-layouts: 42.6 us -> 52.1 us
    pallas_call x1 -> x2, Pallas kernels: 69.8 us -> 63.3 us  [attention_forward(): pl.pallas_call(attention_fwd_kernel, grid=grid, in_specs=[query_spec, key...]
  transfers between devices with their start and end apart: 16 -> 18, of which waited for: 9 -> 9; matrix products, arithmetic and copies ran while one was open for 22% -> 28% of each run, Pallas kernels for 19% -> 19%
where the time goes in v5:
time: 747 us; the launch traced here: 739 us
  local copies, waits for them, and re-layouts  245 us (33%)
  Pallas kernels  144 us (19%)
  waiting for transfers between devices  129 us (17%)
  matrix products  102 us (14%)
  other arithmetic  87.5 us (12%)
  between operations  17.1 us (2%)
  starting transfers between devices  13.9 us (2%)
    pallas_call x2, Pallas kernels, attention_backward(): pl.pallas_call(attention_bwd_kernel, grid=grid, in_specs=[query_spec, key...  80.8 us
    pallas_call x2, Pallas kernels, attention_forward(): pl.pallas_call(attention_fwd_kernel, grid=grid, in_specs=[query_spec, key...  63.3 us
    unnamed x173, local copies, waits for them, and re-layouts  52.1 us
    all_gather x1, waiting for transfers between devices, gather_packed(): lax.all_gather(flat, ('shard', 'tensor'), axis=0, tiled=False)  50.3 us
    ppermute x2, waiting for transfers between devices, spread_sequence(): from_context = lax.ppermute(other, 'context', perm=swap)  40.7 us
    reshape x5, local copies, waits for them, and re-layouts, disassemble(): pieces = full.reshape(split_shape)  35.7 us
    dot_general x3, matrix products, back_dot(): lax.dot_general(left_rows, weight_rows, (((1,), (1,)), ((), ())), preferr...  33.1 us
    reshape x5, local copies, waits for them, and re-layouts, gather_weight(): stacked.reshape((ns, nt) + local_block.shape)  29.4 us
  transfers between devices with their start and end apart: 18, of which 9 were waited for; matrix products, arithmetic and copies ran while one was open for 28% of the time, Pallas kernels for 19%

profile of v5, /device:TPU:0, one launch (start us, length us, event | category | flops | bytes accessed | tf_op | source)
XLA Modules:
  0.0 739.2 jit_solution(1258313862756014383)
XLA Ops:
  16.4 50.3 %all-gather.8.cloned.1.call-done = bf16[16,880,128]{2,1,0:T(8,128)(2,1)} async-done(((bf16[1,880,128]{2,1,0:T(8,128)(2,1)}), bf16[16,880,128]{2,1,0:T(8,128)(2,1)}) %all-gather.8.cloned.1.call-update) | async-done | bytes 3604496 | tf_op jit(solution)/shard_map/all_gather | solution.py:416
  66.7 6.7 reshape.1786
  75.4 4.8 reshape.1836
  80.2 5.5 copy.207
  85.7 4.0 reshape.1788
  107.7 8.0 %collective-permute-done = bf16[1,512,768]{1,2,0:T(8,128)(2,1)S(1)} collective-permute-done((bf16[1,512,768]{1,2,0:T(8,128)(2,1)}, bf16[1,512,768]{1,2,0:T(8,128)(2,1)S(1)}, u32[]{:S(2)}, u32[]{:S(2)}) %collective-permute-start) | collective-permute-done | bytes 786464 | tf_op jit(solution)/shard_map/ppermute | solution.py:700
  117.3 9.5 %fusion.86 = (bf16[3,1024,768]{2,1,0:T(8,128)(2,1)S(1)}, f32[3,1024,768]{2,1,0:T(8,128)}) fusion(bf16[3,768,768]{2,1,0:T(8,128)(2,1)} %reshape.1788, f32[768]{0:T(1024)S(1)} %mul.273, f32[1024]{0:T(1024)S(1)} %add_rsqrt_fusion.3, f32[1024]{0:T(1024)S(1)} %broadcast_multiply_fusion.11, bf16[512,768]{0,1:T(8,128)(2,1)S(1)} %bitcast.172, ...), kind=kOutput, calls=%fused_computation.277 | convolution fusion | flops 3637248000 | bytes 19278848 | tf_op jit(solution)/shard_map/rd,jde->jre/dot_general | solution.py:521
  148.1 28.5 %shard_map.256 = f32[1,512,768]{2,1,0:T(8,128)S(1)} custom-call(bf16[1,512,768]{2,1,0:T(8,128)(2,1)S(1)} %get-tuple-element.154.q_ref, bf16[1,512,768]{2,1,0:T(8,128)(2,1)S(1)} %slice.261.k_ref, bf16[1,512,768]{2,1,0:T(8,128)(2,1)S(1)} %slice.264.v_ref, s32[12,512,8]{2,1,0:T(8,128)} %copy.270.patq_ref, s32[12,8,512]{2,1,0:T(8,128)S(1)} %slice.278.patk_ref, ...), custom_call_target="tpu_custom_call" | custom-call | flops 1610612736 | bytes 5505024 | tf_op jit(solution)/shard_map/pallas_call | solution.py:217
  176.7 34.8 %shard_map.257 = f32[1,512,768]{2,1,0:T(8,128)S(1)} custom-call(bf16[1,512,768]{2,1,0:T(8,128)(2,1)S(1)} %get-tuple-element.155.q_ref, bf16[1,1024,768]{2,1,0:T(8,128)(2,1)S(1)} %copy-done.12, bf16[1,1024,768]{2,1,0:T(8,128)(2,1)S(1)} %get-tuple-element.135.v_ref, s32[12,512,8]{2,1,0:T(8,128)} %copy.271.patq_ref, s32[12,8,1024]{2,1,0:T(8,128)S(1)} %stack.57.patk_ref, ...), custom_call_target="tpu_custom_call" | custom-call | flops 3221225472 | bytes 8650752 | tf_op jit(solution)/shard_map/pallas_call | solution.py:217
  221.6 9.3 %copy.219 = bf16[8,2,96,1536]{3,1,2,0:T(2,128)(2,1)} copy(bf16[8,2,96,1536]{3,2,1,0:T(8,128)(2,1)} %bitcast.187) | data formatting | bytes 9437184 | tf_op jit(solution)/shard_map/reshape | solution.py:407
  230.9 3.8 copy.277
  234.8 12.4 %fusion.73 = (f32[1024]{0:T(1024)S(1)}, f32[1024,3072]{1,0:T(8,128)}) fusion(f32[3072]{0:T(1024)S(1)} %reshape.1821, bf16[768,3072]{1,0:T(8,128)(2,1)S(1)} %bitcast.188, f32[1024,768]{0,1:T(8,128)S(1)} %copy-done.38, f32[768]{0:T(1024)S(1)} %copy-done.66, f32[1024]{0:T(1024)S(1)} %add_rsqrt_fusion.1, f32[1024]{0:T(1024)S(1)} %broadcast_multiply_fusion.9), kind=kOutput, calls=%fused_computation.265 | convolution fusion | flops 4866440192 | bytes 20474880 | tf_op jit(solution)/shard_map/dot_general | solution.py:542
  247.2 8.1 %multiply_reduce_fusion.2 = f32[1024]{0:T(1024)S(1)} fusion(f32[1024]{0:T(1024)S(1)} %broadcast_multiply_fusion.2, f32[1024,3072]{1,0:T(8,128)} %get-tuple-element.177, f32[3072]{0:T(1024)S(1)} %reshape.1821), kind=kLoop, calls=%fused_computation.12 | loop fusion | flops 37747712 | bytes 12603392 | tf_op jit(solution)/shard_map/reduce_sum | solution.py:73
  255.3 7.3 reshape.1796
  262.6 7.7 %copy.224 = bf16[8,2,1536,96]{2,1,3,0:T(2,128)(2,1)} copy(bf16[8,2,1536,96]{2,1,0,3:T(2,128)(2,1)} %reshape.1796) | data formatting | bytes 9437184 | tf_op jit(solution)/shard_map/reshape | solution.py:407
  273.9 21.3 %multiply_reduce_fusion = (bf16[3072]{0:T(1024)(128)(2,1)S(1)}, f32[1024]{0:T(1024)S(1)}, f32[1024]{0:T(1024)S(1)}, bf16[1024,3072]{1,0:T(8,128)(2,1)}, f32[1024,3072]{1,0:T(8,128)}) fusion(f32[1024]{0:T(1024)S(1)} %add_rsqrt_fusion, f32[1024]{0:T(1024)S(1)} %broadcast_multiply_fusion.2, f32[1024,3072]{1,0:T(8,128)} %get-tuple-element.177, ...), kind=kOutput, calls=%fused_computation.9 | convolution fusion | flops 4898679808 | bytes 37795840 | tf_op jit(solution)/shard_map/dot_general | solution.py:65
  295.3 16.6 %fusion.74 = (bf16[3072]{0:T(1024)(128)(2,1)S(1)}, bf16[1024,3072]{1,0:T(8,128)(2,1)S(1)}) fusion(f32[1024]{0:T(1024)S(1)} %broadcast_multiply_fusion, f32[1024]{0:T(1024)S(1)} %broadcast_multiply_fusion.2, f32[1024,3072]{1,0:T(8,128)} %get-tuple-element.177, f32[3072]{0:T(1024)S(1)} %reshape.1821, f32[1024]{0:T(1024)S(1)} %broadcast_multiply_fusion.1, ...), kind=kLoop, calls=%fused_computation.266 | loop fusion | flops 94368768 | bytes 31504384 | tf_op jit(solution)/shard_map/reduce_sum | solution.py:604
  311.9 7.8 %multiply_reduce_fusion.5 = (bf16[768]{0:T(1024)(128)(2,1)S(1)}, f32[1024]{0:T(1024)S(1)}, f32[1024]{0:T(1024)S(1)}, f32[1024,768]{0,1:T(8,128)S(1)}) fusion(f32[1024,768]{0,1:T(8,128)S(1)} %copy-done.39, f32[1024]{0:T(1024)S(1)} %add_rsqrt_fusion.1, f32[1024]{0:T(1024)S(1)} %broadcast_multiply_fusion.9, f32[768]{0:T(1024)S(1)} %copy-done.66, ...), kind=kOutput, calls=%fused_computation.55 | convolution fusion | flops 4838126592 | bytes 17322496 | tf_op jit(solution)/shard_map/dot_general | solution.py:65
  319.7 6.9 convolution_convert_fusion
  333.0 3.9 multiply_reduce_fusion.4
  337.0 8.5 %convolution_convert_fusion.1 = bf16[3072,768]{1,0:T(8,128)(2,1)} fusion(bf16[1024,3072]{1,0:T(8,128)(2,1)S(1)} %bitcast.213, bf16[512,768]{0,1:T(8,128)(2,1)} %bitcast.27, bf16[512,768]{0,1:T(8,128)(2,1)S(1)} %bitcast.194, pred[]{:T(512)S(6)} %eq.183), kind=kOutput, calls=%fused_computation.18 | convolution fusion | flops 4841275392 | bytes 12582913 | tf_op jit(solution)/shard_map/dot_general | solution.py:59
  345.5 6.7 copy.231
  352.2 11.6 %reshape.1798 = bf16[2,1536,8,96]{1,0,3,2:T(2,128)(2,1)} reshape(bf16[3072,768]{0,1:T(8,128)(2,1)} %copy.231) | data formatting | bytes 9437184 | tf_op jit(solution)/shard_map/reshape | solution.py:470
  363.8 12.0 %reshape.1799 = bf16[8,96,2,1536]{3,2,1,0:T(2,128)(2,1)} reshape(bf16[768,3072]{1,0:T(8,128)(2,1)} %convolution_convert_fusion) | data formatting | bytes 9437184 | tf_op jit(solution)/shard_map/reshape | solution.py:470
  375.8 5.4 copy.285
  381.3 9.9 %concatenate.130 = bf16[16,1152,128]{2,1,0:T(8,128)(2,1)} reshape(bf16[8,2,96,1536]{3,2,1,0:T(8,128)(2,1)} %bitcast.165) | data formatting | bytes 9437184 | tf_op jit(solution)/shard_map/concatenate | solution.py:482
  397.1 3.8 copy.235
  400.9 4.3 reshape.1801
  405.3 11.9 %copy.232 = bf16[8,2,1536,96]{3,2,1,0:T(8,128)(2,1)} copy(bf16[8,2,1536,96]{2,1,3,0:T(2,128)(2,1)} %bitcast.166) | data formatting | bytes 9437184 | tf_op jit(solution)/shard_map/transpose | solution.py:473
  417.2 12.8 %concatenate.129 = bf16[16,1152,128]{2,1,0:T(8,128)(2,1)} reshape(bf16[8,2,1536,96]{3,2,1,0:T(8,128)(2,1)} %copy.232) | data formatting | bytes 9437184 | tf_op jit(solution)/shard_map/concatenate | solution.py:482
  430.0 7.6 %pad_maximum_fusion = bf16[16,2304,128]{2,1,0:T(8,128)(2,1)} fusion(bf16[16,1152,128]{2,1,0:T(8,128)(2,1)} %concatenate.130, bf16[16,1152,128]{2,1,0:T(8,128)(2,1)} %concatenate.129), kind=kLoop, calls=%fused_computation.16 | loop fusion | flops 18874368 | bytes 18874368 | tf_op jit(solution)/shard_map/concatenate | solution.py:482
  437.6 3.8 multiply_convert_fusion.1
  451.3 49.9 %shard_map.259 = (bf16[1,512,768]{2,1,0:T(8,128)(2,1)S(1)}, f32[1,1024,768]{2,1,0:T(8,128)}, f32[1,1024,768]{2,1,0:T(8,128)}) custom-call(bf16[1,512,768]{2,1,0:T(8,128)(2,1)S(1)} %copy-done.21, bf16[1,1024,768]{2,1,0:T(8,128)(2,1)S(1)} %copy-done.13, bf16[1,1024,768]{2,1,0:T(8,128)(2,1)S(1)} %copy-done.3, ...), custom_call_target="tpu_custom_call" | custom-call | flops 8053063680 | bytes 20447232 | tf_op jit(solution)/shard_map/pallas_call | solution.py:244
  506.6 31.0 %shard_map.258 = (bf16[1,512,768]{2,1,0:T(8,128)(2,1)S(1)}, f32[1,512,768]{2,1,0:T(8,128)S(1)}, f32[1,512,768]{2,1,0:T(8,128)}) custom-call(bf16[1,512,768]{2,1,0:T(8,128)(2,1)S(1)} %copy-done.9, bf16[1,512,768]{2,1,0:T(8,128)(2,1)S(1)} %copy-done.5, bf16[1,512,768]{2,1,0:T(8,128)(2,1)S(1)} %copy-done.7, bf16[1,512,768]{2,1,0:T(8,128)(2,1)S(1)} %copy-done.22, ...), custom_call_target="tpu_custom_call" | custom-call | flops 4026531840 | bytes 11010048 | tf_op jit(solution)/shard_map/pallas_call | solution.py:244
  538.9 4.0 fusion.76
  548.1 4.2 pad_maximum_fusion.1
  552.4 8.3 %convert_bitcast_fusion = bf16[3,768,768]{1,2,0:T(8,128)(2,1)} fusion(bf16[3,1024,768]{2,1,0:T(8,128)(2,1)} %pad_maximum_fusion.1, f32[768]{0:T(1024)S(1)} %copy-done.63, f32[1024]{0:T(1024)S(1)} %copy-done.61, f32[1024]{0:T(1024)S(1)} %copy-done.57, bf16[512,768]{0,1:T(8,128)(2,1)S(1)} %bitcast.181, bf16[512,768]{0,1:T(8,128)(2,1)S(1)} %bitcast.174, ...), kind=kOutput, calls=%fused_computation.31 | convolution fusion | flops 3636658176 | bytes 9841665 | tf_op jit(solution)/shard_map/rd,jre->jde/dot_general | solution.py:640
  560.7 4.3 copy.241
  573.6 4.1 constant_dynamic-update-slice_fusion
  577.8 8.9 %fusion.19 = (bf16[768]{0:T(1024)(128)(2,1)S(1)}, f32[1024]{0:T(1024)}, f32[1024]{0:T(1024)}, f32[1024,768,1]{0,1,2:T(8,128)}) fusion(f32[1024]{0:T(1024)S(1)} %copy-done.61, f32[1024]{0:T(1024)S(1)} %copy-done.57, bf16[512,768]{0,1:T(8,128)(2,1)S(1)} %bitcast.175, bf16[512,768]{0,1:T(8,128)(2,1)S(1)} %bitcast.182, pred[]{:T(512)S(6)} %eq.183, ...), kind=kOutput, calls=%fused_computation.39 | convolution fusion | flops 3638031616 | bytes 12997121 | tf_op jit(solution)/shard_map/jre,jde->rd/dot_general | solution.py:644
  600.7 10.2 %add_convert_fusion.2 = bf16[1024,768]{0,1:T(8,128)(2,1)S(1)} fusion(f32[1024,768]{0,1:T(8,128)} %copy-done.37, bf16[1024,3072]{1,0:T(8,128)(2,1)} %get-tuple-element.134, bf16[3072,768]{0,1:T(8,128)(2,1)} %bitcast.186, f32[768]{0:T(1024)S(1)} %copy-done.71), kind=kOutput, calls=%fused_computation.63 | convolution fusion | flops 4834197504 | bytes 15731712 | tf_op jit(solution)/shard_map/dot_general | solution.py:547
  616.9 16.1 %collective-permute-done.1 = bf16[1,512,768]{2,1,0:T(8,128)(2,1)} collective-permute-done((bf16[1,512,768]{2,1,0:T(8,128)(2,1)}, bf16[1,512,768]{2,1,0:T(8,128)(2,1)}, u32[]{:S(2)}, u32[]{:S(2)}) %collective-permute-start.1) | collective-permute-done | bytes 786464 | tf_op jit(solution)/shard_map/ppermute | solution.py:355
  635.4 13.2 %collective-permute-done.3 = bf16[1,512,768]{2,1,0:T(8,128)(2,1)} collective-permute-done((bf16[1,512,768]{2,1,0:T(8,128)(2,1)}, bf16[1,512,768]{2,1,0:T(8,128)(2,1)}, u32[]{:S(2)}, u32[]{:S(2)}) %collective-permute-start.3) | collective-permute-done | bytes 786464 | tf_op jit(solution)/shard_map/ppermute | solution.py:357
  648.5 7.0 collective-permute-done.2
  668.1 3.6 fusion.18
  676.9 4.8 collective-permute-done.10
  684.1 24.6 %collective-permute-done.5 = bf16[1,512,768]{2,1,0:T(8,128)(2,1)} collective-permute-done((bf16[1,512,768]{2,1,0:T(8,128)(2,1)}, bf16[1,512,768]{2,1,0:T(8,128)(2,1)}, u32[]{:S(2)}, u32[]{:S(2)}) %collective-permute-start.5) | collective-permute-done | bytes 786464 | tf_op jit(solution)/shard_map/ppermute | solution.py:355
  719.0 6.9 slice.246
  (384 shorter events, 165.5 us)
Async XLA Ops:
  7.2 92.3 %copy-start = (s32[4,2]{0,1:T(2,128)S(1)}, s32[4,2]{0,1:T(2,128)}, u32[]{:S(2)}) copy-start(s32[4,2]{0,1:T(2,128)} %param.21) | copy-start | bytes 100
  7.2 59.5 %all-gather.8.cloned.1.call-start = ((), (), s32[]{:S(2)}) async-start(), calls=%async_computation.3 | async-start | bytes 3829760 | tf_op jit(solution)/shard_map/all_gather | solution.py:416
  16.4 195.9 %all-gather.10.cloned.1.call-start = ((), (), s32[]{:S(2)}) async-start(), calls=%async_computation.6 | async-start | bytes 1253376 | tf_op jit(solution)/shard_map/all_gather | solution.py:406
  89.7 131.9 %all-gather.12.cloned.1.call-start = ((), (), s32[]{:S(2)}) async-start(), calls=%async_computation.7 | async-start | bytes 5013504 | tf_op jit(solution)/shard_map/all_gather | solution.py:406
  90.4 164.8 %all-gather.14.cloned.1.call-start = ((), (), s32[]{:S(2)}) async-start(), calls=%async_computation.8 | async-start | bytes 5013504 | tf_op jit(solution)/shard_map/all_gather | solution.py:406
  95.1 20.6 %collective-permute-start = (bf16[1,512,768]{1,2,0:T(8,128)(2,1)}, bf16[1,512,768]{1,2,0:T(8,128)(2,1)S(1)}, u32[]{:S(2)}, u32[]{:S(2)}) collective-permute-start(bf16[1,512,768]{1,2,0:T(8,128)(2,1)} %copy.268), channel_id=1, source_target_pairs={{0,2},{2,0},{1,3},{3,1},{4,6},{6,4},{5,7},{7,5},{8,10},{10,8},{9,1... | collective-permute-start | bytes 2359304 | tf_op jit(solution)/shard_map/ppermute | solution.py:700
  98.9 175.0 %collective-permute-start.4 = (bf16[1,512,768]{1,2,0:T(8,128)(2,1)}, bf16[1,512,768]{1,2,0:T(8,128)(2,1)}, u32[]{:S(2)}, u32[]{:S(2)}) collective-permute-start(bf16[1,512,768]{1,2,0:T(8,128)(2,1)} %copy.275), channel_id=1, source_target_pairs={{0,2},{2,0},{1,3},{3,1},{4,6},{6,4},{5,7},{7,5},{8,10},{10,8},{9,1... | collective-permute-start | bytes 2359304 | tf_op jit(solution)/shard_map/ppermute | solution.py:700
  104.8 22.0 %copy-start.33 = (bf16[1,512,768]{1,2,0:T(8,128)(2,1)}, bf16[1,512,768]{1,2,0:T(8,128)(2,1)S(1)}, u32[]{:S(2)}) copy-start(bf16[1,512,768]{1,2,0:T(8,128)(2,1)S(1)} %copy.201) | copy-start | bytes 2359300
  104.8 12.1 %copy-start.31 = (bf16[8,2,112640]{2,1,0:T(2,128)(2,1)S(1)}, bf16[8,2,112640]{2,1,0:T(2,128)(2,1)}, u32[]{:S(2)}) copy-start(bf16[8,2,112640]{2,1,0:T(2,128)(2,1)} %reshape.1786) | copy-start | bytes 10813444
  104.8 43.2 %copy-start.27 = (s32[1,8,512]{2,1,0:T(8,128)}, s32[1,8,512]{2,1,0:T(8,128)S(1)}, u32[]{:S(2)}) copy-start(s32[1,8,512]{2,1,0:T(8,128)S(1)} %pad_slice_fusion.2.pck_ref) | copy-start | bytes 49156
  107.7 40.4 %copy-start.16 = (s32[1,512,8]{2,1,0:T(8,128)}, s32[1,512,8]{2,1,0:T(8,128)S(1)}, u32[]{:S(2)}) copy-start(s32[1,512,8]{2,1,0:T(8,128)S(1)} %get-tuple-element.158.pcq_ref) | copy-start | bytes 49156
  115.7 11.0 %copy-start.41 = (bf16[1,512,768]{1,2,0:T(8,128)(2,1)}, bf16[1,512,768]{1,2,0:T(8,128)(2,1)S(1)}, u32[]{:S(2)}) copy-start(bf16[1,512,768]{1,2,0:T(8,128)(2,1)S(1)} %collective-permute-done) | copy-start | bytes 2359300
  116.9 9.9 %copy-start.60 = (f32[1024]{0:T(1024)}, f32[1024]{0:T(1024)S(1)}, u32[]{:S(2)}) copy-start(f32[1024]{0:T(1024)S(1)} %add_rsqrt_fusion.3) | copy-start | bytes 12292
  126.9 21.2 %copy-start.4 = (bf16[1,512,768]{2,1,0:T(8,128)(2,1)}, bf16[1,512,768]{2,1,0:T(8,128)(2,1)S(1)}, u32[]{:S(2)}) copy-start(bf16[1,512,768]{2,1,0:T(8,128)(2,1)S(1)} %slice.261.k_ref) | copy-start | bytes 2359300
  137.0 39.6 %copy-start.18 = (s32[12,8,1024]{2,1,0:T(8,128)}, s32[12,8,1024]{2,1,0:T(8,128)S(1)}, u32[]{:S(2)}) copy-start(s32[12,8,1024]{2,1,0:T(8,128)S(1)} %stack.57.patk_ref) | copy-start | bytes 1179652
  137.0 11.1 %copy-start.23 = (s32[12,8,512]{2,1,0:T(8,128)}, s32[12,8,512]{2,1,0:T(8,128)S(1)}, u32[]{:S(2)}) copy-start(s32[12,8,512]{2,1,0:T(8,128)S(1)} %slice.278.patk_ref) | copy-start | bytes 589828
  137.1 415.3 %reduce-scatter.6.cloned.1.call-start = ((), (), s32[]{:S(2)}) async-start(), calls=%async_computation.4 | async-start | bytes 10027008 | tf_op jit(solution)/shard_map/reduce_scatter | solution.py:491
  147.9 28.8 %copy-start.2 = (bf16[1,1024,768]{2,1,0:T(8,128)(2,1)}, bf16[1,1024,768]{2,1,0:T(8,128)(2,1)S(1)}, u32[]{:S(2)}) copy-start(bf16[1,1024,768]{2,1,0:T(8,128)(2,1)S(1)} %get-tuple-element.135.v_ref) | copy-start | bytes 4718596
  147.9 28.7 %copy-start.6 = (bf16[1,512,768]{2,1,0:T(8,128)(2,1)}, bf16[1,512,768]{2,1,0:T(8,128)(2,1)S(1)}, u32[]{:S(2)}) copy-start(bf16[1,512,768]{2,1,0:T(8,128)(2,1)S(1)} %slice.264.v_ref) | copy-start | bytes 2359300
  148.0 28.6 %copy-start.8 = (bf16[1,512,768]{2,1,0:T(8,128)(2,1)}, bf16[1,512,768]{2,1,0:T(8,128)(2,1)S(1)}, u32[]{:S(2)}) copy-start(bf16[1,512,768]{2,1,0:T(8,128)(2,1)S(1)} %get-tuple-element.154.q_ref) | copy-start | bytes 2359300
  148.1 28.6 %copy-start.20 = (bf16[1,512,768]{2,1,0:T(8,128)(2,1)}, bf16[1,512,768]{2,1,0:T(8,128)(2,1)S(1)}, u32[]{:S(2)}) copy-start(bf16[1,512,768]{2,1,0:T(8,128)(2,1)S(1)} %get-tuple-element.155.q_ref) | copy-start | bytes 2359300
  148.1 28.6 %copy-start.12 = (bf16[1,1024,768]{2,1,0:T(8,128)(2,1)S(1)}, bf16[1,1024,768]{2,1,0:T(8,128)(2,1)}, u32[]{:S(2)}) copy-start(bf16[1,1024,768]{2,1,0:T(8,128)(2,1)} %slice.280.k_ref) | copy-start | bytes 4718596
  148.1 28.6 %copy-start.25 = (s32[1,512,8]{2,1,0:T(8,128)S(1)}, s32[1,512,8]{2,1,0:T(8,128)}, u32[]{:S(2)}) copy-start(s32[1,512,8]{2,1,0:T(8,128)} %get-tuple-element.159.pcq_ref) | copy-start | bytes 49156
  148.1 28.6 %copy-start.29 = (s32[1,8,1024]{2,1,0:T(8,128)S(1)}, s32[1,8,1024]{2,1,0:T(8,128)}, u32[]{:S(2)}) copy-start(s32[1,8,1024]{2,1,0:T(8,128)} %pad.25.pck_ref) | copy-start | bytes 98308
  234.7 12.4 %copy-start.47 = (bf16[96,8,2,1536]{3,1,2,0:T(8,128)(2,1)}, bf16[96,8,2,1536]{3,1,2,0:T(8,128)(2,1)S(1)}, u32[]{:S(2)}) copy-start(bf16[96,8,2,1536]{3,1,2,0:T(8,128)(2,1)S(1)} %copy.277) | copy-start | bytes 14155780
  273.8 21.4 %copy-start.46 = (bf16[96,8,2,1536]{3,1,2,0:T(8,128)(2,1)}, bf16[96,8,2,1536]{3,1,2,0:T(8,128)(2,1)S(1)}, u32[]{:S(2)}) copy-start(bf16[96,8,2,1536]{3,1,2,0:T(8,128)(2,1)S(1)} %copy.278) | copy-start | bytes 14155780
  295.2 16.6 %copy-start.39 = (f32[1024,768]{0,1:T(8,128)S(1)}, f32[1024,768]{0,1:T(8,128)}, u32[]{:S(2)}) copy-start(f32[1024,768]{0,1:T(8,128)} %copy-done.37) | copy-start | bytes 9437188
  441.4 217.5 %reduce-scatter.8.cloned.1.call-start = ((), (), s32[]{:S(2)}) async-start(), calls=%async_computation.5 | async-start | bytes 1253376 | tf_op jit(solution)/shard_map/reduce_scatter | solution.py:491
  451.3 52.1 %copy-start.5 = (bf16[1,512,768]{2,1,0:T(8,128)(2,1)S(1)}, bf16[1,512,768]{2,1,0:T(8,128)(2,1)}, u32[]{:S(2)}) copy-start(bf16[1,512,768]{2,1,0:T(8,128)(2,1)} %copy-done.4) | copy-start | bytes 2359300
  451.3 52.1 %copy-start.7 = (bf16[1,512,768]{2,1,0:T(8,128)(2,1)S(1)}, bf16[1,512,768]{2,1,0:T(8,128)(2,1)}, u32[]{:S(2)}) copy-start(bf16[1,512,768]{2,1,0:T(8,128)(2,1)} %copy-done.6) | copy-start | bytes 2359300
  451.3 52.1 %copy-start.17 = (s32[1,512,8]{2,1,0:T(8,128)S(1)}, s32[1,512,8]{2,1,0:T(8,128)}, u32[]{:S(2)}) copy-start(s32[1,512,8]{2,1,0:T(8,128)} %copy-done.16) | copy-start | bytes 49156
  451.3 52.1 %copy-start.28 = (s32[1,8,512]{2,1,0:T(8,128)S(1)}, s32[1,8,512]{2,1,0:T(8,128)}, u32[]{:S(2)}) copy-start(s32[1,8,512]{2,1,0:T(8,128)} %copy-done.27) | copy-start | bytes 49156
  548.0 164.5 %reduce-scatter.10.cloned.1.call-start = ((), (), s32[]{:S(2)}) async-start(), calls=%async_computation.9 | async-start | bytes 3794944
  577.8 12.0 %copy-start.67 = (bf16[16,96]{1,0:T(8,128)(2,1)S(1)}, bf16[16,96]{1,0:T(8,128)(2,1)}, u32[]{:S(2)}) copy-start(bf16[16,96]{1,0:T(8,128)(2,1)} %reshape.1807) | copy-start | bytes 9220
  577.8 13.3 %copy-start.68 = (bf16[16,48]{1,0:T(8,128)(2,1)S(1)}, bf16[16,48]{1,0:T(8,128)(2,1)}, u32[]{:S(2)}) copy-start(bf16[16,48]{1,0:T(8,128)(2,1)} %reshape.1808) | copy-start | bytes 4612
  577.8 14.8 %copy-start.58 = (bf16[16,192]{1,0:T(8,128)(2,1)S(1)}, bf16[16,192]{1,0:T(8,128)(2,1)}, u32[]{:S(2)}) copy-start(bf16[16,192]{1,0:T(8,128)(2,1)} %reshape.1809) | copy-start | bytes 18436
  577.8 16.3 %copy-start.59 = (bf16[16,192]{1,0:T(8,128)(2,1)S(1)}, bf16[16,192]{1,0:T(8,128)(2,1)}, u32[]{:S(2)}) copy-start(bf16[16,192]{1,0:T(8,128)(2,1)} %reshape.1810) | copy-start | bytes 18436
  612.3 20.7 %collective-permute-start.1 = (bf16[1,512,768]{2,1,0:T(8,128)(2,1)}, bf16[1,512,768]{2,1,0:T(8,128)(2,1)}, u32[]{:S(2)}, u32[]{:S(2)}) collective-permute-start(bf16[1,512,768]{2,1,0:T(8,128)(2,1)} %bitcast.199), channel_id=1, source_target_pairs={{0,2},{2,0},{1,3},{3,1},{4,6},{6,4},{5,7},{7,5},{8,10},{10,8},{9,1... | collective-permute-start | bytes 2359304 | tf_op jit(solution)/shard_map/ppermute | solution.py:355
  613.6 34.9 %collective-permute-start.3 = (bf16[1,512,768]{2,1,0:T(8,128)(2,1)}, bf16[1,512,768]{2,1,0:T(8,128)(2,1)}, u32[]{:S(2)}, u32[]{:S(2)}) collective-permute-start(bf16[1,512,768]{2,1,0:T(8,128)(2,1)} %bitcast.200), channel_id=1, source_target_pairs={{0,3},{3,0},{1,2},{2,1},{4,7},{7,4},{5,6},{6,5},{8,11},{11,8},{9,1... | collective-permute-start | bytes 2359304 | tf_op jit(solution)/shard_map/ppermute | solution.py:357
  615.4 40.1 %collective-permute-start.2 = (bf16[1,512,768]{2,1,0:T(8,128)(2,1)}, bf16[1,512,768]{2,1,0:T(8,128)(2,1)}, u32[]{:S(2)}, u32[]{:S(2)}) collective-permute-start(bf16[1,512,768]{2,1,0:T(8,128)(2,1)} %bitcast.24), channel_id=1, source_target_pairs={{0,1},{1,0},{2,3},{3,2},{4,5},{5,4},{6,7},{7,6},{8,9},{9,8},{10,11... | collective-permute-start | bytes 2359304 | tf_op jit(solution)/shard_map/ppermute | solution.py:356
  658.9 5.4 collective-permute-start.9
  665.3 16.4 %collective-permute-start.10 = (bf16[2304,128]{1,0:T(8,128)(2,1)}, bf16[2304,128]{1,0:T(8,128)(2,1)S(1)}, u32[]{:S(2)}, u32[]{:S(2)}) collective-permute-start(bf16[2304,128]{1,0:T(8,128)(2,1)} %bitcast.203), channel_id=1, source_target_pairs={{0,2},{2,0},{1,3},{3,1},{4,6},{6,4},{5,7},{7,5},{8,10},{10,8},{9,1... | collective-permute-start | bytes 1769480 | tf_op jit(solution)/shard_map/ppermute | solution.py:452
  671.7 10.0 %copy-start.52 = (bf16[1,2304,128]{2,1,0:T(8,128)(2,1)S(1)}, bf16[1,2304,128]{2,1,0:T(8,128)(2,1)}, u32[]{:S(2)}) copy-start(bf16[1,2304,128]{2,1,0:T(8,128)(2,1)} %reduce-scatter.6.cloned.1.call-done) | copy-start | bytes 1769476
  673.1 37.3 %collective-permute-start.7 = (bf16[1,512,768]{2,1,0:T(8,128)(2,1)}, bf16[1,512,768]{2,1,0:T(8,128)(2,1)}, u32[]{:S(2)}, u32[]{:S(2)}) collective-permute-start(bf16[1,512,768]{2,1,0:T(8,128)(2,1)} %bitcast.35), channel_id=1, source_target_pairs={{0,3},{3,0},{1,2},{2,1},{4,7},{7,4},{5,6},{6,5},{8,11},{11,8},{9,1... | collective-permute-start | bytes 2359304 | tf_op jit(solution)/shard_map/ppermute | solution.py:357
  674.4 34.3 %collective-permute-start.5 = (bf16[1,512,768]{2,1,0:T(8,128)(2,1)}, bf16[1,512,768]{2,1,0:T(8,128)(2,1)}, u32[]{:S(2)}, u32[]{:S(2)}) collective-permute-start(bf16[1,512,768]{2,1,0:T(8,128)(2,1)} %bitcast.35), channel_id=1, source_target_pairs={{0,2},{2,0},{1,3},{3,1},{4,6},{6,4},{5,7},{7,5},{8,10},{10,8},{9,1... | collective-permute-start | bytes 2359304 | tf_op jit(solution)/shard_map/ppermute | solution.py:355
  676.3 34.1 %collective-permute-start.6 = (bf16[1,512,768]{2,1,0:T(8,128)(2,1)S(1)}, bf16[1,512,768]{2,1,0:T(8,128)(2,1)}, u32[]{:S(2)}, u32[]{:S(2)}) collective-permute-start(bf16[1,512,768]{2,1,0:T(8,128)(2,1)S(1)} %bitcast.195), channel_id=1, source_target_pairs={{0,1},{1,0},{2,3},{3,2},{4,5},{5,4},{6,7},{7,6},{8,9},{9,8},{10,11... | collective-permute-start | bytes 2359304 | tf_op jit(solution)/shard_map/ppermute | solution.py:356
  712.6 6.2 collective-permute-start.8
  719.0 13.2 %copy-start.1 = (s32[4,2]{0,1:T(2,128)S(1)}, s32[4,2]{0,1:T(2,128)}, u32[]{:S(2)}) copy-start(s32[4,2]{0,1:T(2,128)} %param.21) | copy-start | bytes 100
  (47 other events, 168.7 us)
Sparse Core Ops, SparseCore 0:
  16.5 50.1 all-gather.7
  89.8 35.6 all-gather.9
  127.8 52.5 all-gather.11
  182.6 51.6 all-gather.13
  441.5 109.8 reduce-scatter.5
  554.9 57.7 reduce-scatter.7
  616.6 91.2 reduce-scatter.9

commit v6 on v5

--- a/solution.py
+++ b/solution.py
@@ -511,6 +511,15 @@
     return pieces
 
 
+def shard_stage(grad, dim):
+    return lax.psum_scatter(grad.astype(jnp.bfloat16), "shard", scatter_dimension=dim, tiled=True)
+
+
+def finish_stage(share, tensor_dim):
+    summed = pair_reduce(share, "tensor", tensor_dim)
+    return pair_sum(summed.astype(jnp.bfloat16), "context")
+
+
 def forward_pass(block_in, codes, weights, span):
     w_qkv, w_out, w_up, w_down, norm_gains, out_biases, head_biases, head_gain, unit_bias, unit_gain = weights
     seq_count, local_len, model_width = block_in.shape
@@ -594,7 +603,7 @@
     seq_len = key_all.shape[1]
     grad_low = block_grad.reshape(row_count, model_width)
     grad_full = grad_low.astype(jnp.float32)
-    down_grad = outer_sum(ffn_mid, grad_low)
+    down_grad = outer_sum(grad_low, ffn_mid)
     last_bias_grad = jnp.sum(grad_full, 0)
     unit_grad = back_dot(grad_low, w_down)
     activated_grad, unit_gain_grad = norm_back(unit_normed, unit_inv, unit_gain, unit_grad)
@@ -606,18 +615,22 @@
     middle_part, second_gain_grad = norm_back(second_normed, second_inv, norm_gains[1], ffn_in_grad)
     middle_grad = grad_full + middle_part
     middle_low = middle_grad.astype(jnp.bfloat16)
-    out_weight_grad = outer_sum(sub_in, middle_low)
+    out_weight_grad = outer_sum(middle_low, sub_in)
     first_bias_grad = jnp.sum(middle_low, 0, dtype=jnp.float32)
     sub_grad = back_dot(middle_low, w_out)
     attended_grad, head_gain_grad = norm_back(sub_normed, sub_inv, head_gain, sub_grad)
     attended_low = attended_grad.astype(jnp.bfloat16)
-    early_terms = ((down_grad, 1, 0), (up_grad, 0, 1))
-    middle_terms = ((out_weight_grad, 1, 0),)
-    early_rows, middle_rows, attended_low = lax.optimization_barrier(
-        (pack_rows(early_terms), pack_rows(middle_terms), attended_low)
-    )
-    early_share = scatter_rows(early_rows)
-    middle_share = scatter_rows(middle_rows)
+    down_grad, up_grad, out_weight_grad, attended_low = lax.optimization_barrier(
+        (
+            down_grad.astype(jnp.bfloat16),
+            up_grad.astype(jnp.bfloat16),
+            out_weight_grad.astype(jnp.bfloat16),
+            attended_low,
+        )
+    )
+    down_share = shard_stage(down_grad, 0)
+    up_share = shard_stage(up_grad, 0)
+    out_share = shard_stage(out_weight_grad, 0)
     query_grad, key_part, value_part = split_attention_backward(
         query_matrix.reshape(seq_count, local_len, model_width),
         key_all,
@@ -636,8 +649,8 @@
     key_low = key_part.astype(jnp.bfloat16).reshape(row_count, model_width)
     value_low = value_part.astype(jnp.bfloat16).reshape(row_count, model_width)
     stacked = jnp.stack([query_low, key_low, value_low])
-    early_share, stacked = lax.optimization_barrier((early_share, stacked))
-    qkv_grad = jnp.einsum("rd,jre->jde", attn_in, stacked, preferred_element_type=jnp.float32)
+    down_share, up_share, stacked = lax.optimization_barrier((down_share, up_share, stacked))
+    qkv_grad = jnp.einsum("rd,jre->dje", attn_in, stacked, preferred_element_type=jnp.float32)
     head_bias_grad = jnp.stack(
         [jnp.sum(query_low, 0, dtype=jnp.float32), jnp.sum(value_low, 0, dtype=jnp.float32)]
     )
@@ -646,8 +659,7 @@
     input_low = (middle_grad + input_part).astype(jnp.bfloat16)
     heads = model_width // HD
     unit_rows = unit_bias_grad.shape[0] // HD
-    late_terms = (
-        (qkv_grad, 1, 2),
+    small_terms = (
         (jnp.stack([first_gain_grad, second_gain_grad]), 1, None),
         (jnp.stack([first_bias_grad, last_bias_grad]), 1, None),
         (head_bias_grad.reshape(2, heads, HD), 2, 1),
@@ -655,12 +667,42 @@
         (unit_bias_grad.reshape(unit_rows, HD), 1, 0),
         (unit_gain_grad.reshape(unit_rows, HD), 1, 0),
     )
-    late_share = scatter_rows(pack_rows(late_terms))
+    ns = lax.axis_size("shard")
+    nt = lax.axis_size("tensor")
+    small_rows = jnp.concatenate(
+        [disassemble(full, shard_dim, tensor_dim) for full, shard_dim, tensor_dim in small_terms], 1
+    )
+    small_width = small_rows.shape[1]
+    block_rows = model_width // ns
+    block_cols = model_width // nt
+    small_plane = (
+        jnp.pad(small_rows, ((0, 0), (0, block_rows * block_cols - small_width)))
+        .reshape(ns, nt, block_rows, block_cols)
+        .transpose(0, 2, 1, 3)
+        .reshape(model_width, 1, model_width)
+    )
+    qkv_share = shard_stage(jnp.concatenate([qkv_grad, small_plane], 1), 0)
+    qkv_total = finish_stage(qkv_share, 2)
+    small_total = qkv_total[:, 3].reshape(-1)[:small_width]
+    small_pieces = []
+    offset = 0
+    for full, shard_dim, tensor_dim in small_terms:
+        local_shape = list(full.shape)
+        if shard_dim is not None:
+            local_shape[shard_dim] //= ns
+        if tensor_dim is not None:
+            local_shape[tensor_dim] //= nt
+        count = 1
+        for size in local_shape:
+            count *= size
+        small_pieces.append(small_total[offset : offset + count].reshape(local_shape))
+        offset += count
     grad_shares = (
-        unpack_share(early_share, early_terms)
-        + unpack_share(middle_share, middle_terms)
-        + unpack_share(late_share, late_terms)
-    )
+        finish_stage(down_share, 1).transpose(1, 0),
+        finish_stage(up_share, 1),
+        finish_stage(out_share, 1).transpose(1, 0),
+        qkv_total[:, :3].transpose(1, 0, 2),
+    ) + tuple(small_pieces)
     return (grad_shares, input_low.reshape(seq_count, local_len, model_width))
 
 

time: 747 us -> 636 us (0.85)
  local copies, waits for them, and re-layouts: 245 us -> 130 us
  other arithmetic: 87.5 us -> 79.8 us
    reshape x12 -> x1, local copies, waits for them, and re-layouts: 43.4 us -> 3.14 us  [backward_pass(): small_plane = jnp.pad(small_rows, ((0, 0), (0, block_rows * block_cols -...]
    ppermute x0 -> x4, waiting for transfers between devices: none -> 24.3 us  [pair_reduce(): received = lax.ppermute(sent, axis_name, perm=[(0, 1), (1, 0)])]
    concatenate x3 -> x1, local copies, waits for them, and re-layouts: 24.1 us -> 0.09 us  [backward_pass(): jnp.concatenate([disassemble(full, shard_dim, tensor_dim) for full, shard...]
    ppermute x2, waiting for transfers between devices: 40.7 us -> 16.9 us  [spread_sequence(): from_context = lax.ppermute(other, 'context', perm=swap)]
    transpose x9 -> x4, local copies, waits for them, and re-layouts: 18.5 us -> 1.33 us  [disassemble(): pieces = pieces.transpose(lead + rest)]
    unnamed x173 -> x138, local copies, waits for them, and re-layouts: 52.1 us -> 35.5 us
    convert_element_type x6 -> x0, local copies, waits for them, and re-layouts: 13.8 us -> none  [pack_rows(): full.astype(jnp.bfloat16)]
    ppermute x3 -> x4, waiting for transfers between devices: 8.83 us -> 17.6 us  [pair_sum(): received = lax.ppermute(share, axis_name, perm=[(0, 1), (1, 0)])]
  transfers between devices with their start and end apart: 18 -> 24, of which waited for: 9 -> 12; matrix products, arithmetic and copies ran while one was open for 28% -> 28% of each run, Pallas kernels for 19% -> 23%
where the time goes in v6:
time: 636 us; the launch traced here: 630 us
  Pallas kernels  144 us (23%)
  waiting for transfers between devices  132 us (21%)
  local copies, waits for them, and re-layouts  130 us (20%)
  matrix products  107 us (17%)
  other arithmetic  79.8 us (13%)
  starting transfers between devices  20.3 us (3%)
  between operations  17.1 us (3%)
    pallas_call x2, Pallas kernels, attention_backward(): pl.pallas_call(attention_bwd_kernel, grid=grid, in_specs=[query_spec, key...  80.5 us
    pallas_call x2, Pallas kernels, attention_forward(): pl.pallas_call(attention_fwd_kernel, grid=grid, in_specs=[query_spec, key...  63.3 us
    all_gather x1, waiting for transfers between devices, gather_packed(): lax.all_gather(flat, ('shard', 'tensor'), axis=0, tiled=False)  50.3 us
    dot_general x3, matrix products, back_dot(): lax.dot_general(left_rows, weight_rows, (((1,), (1,)), ((), ())), preferr...  37.1 us
    unnamed x138, local copies, waits for them, and re-layouts  35.5 us
    reshape x5, local copies, waits for them, and re-layouts, gather_weight(): stacked.reshape((ns, nt) + local_block.shape)  29.6 us
    ppermute x4, waiting for transfers between devices, pair_reduce(): received = lax.ppermute(sent, axis_name, perm=[(0, 1), (1, 0)])  24.3 us
    dot_general x3, matrix products, outer_sum(): lax.dot_general(left_rows, right_rows, (((0,), (0,)), ((), ())), preferre...  19.8 us
  transfers between devices with their start and end apart: 24, of which 12 were waited for; matrix products, arithmetic and copies ran while one was open for 28% of the time, Pallas kernels for 23%

profile of v6, /device:TPU:0, one launch (start us, length us, event | category | flops | bytes accessed | tf_op | source)
XLA Modules:
  0.0 630.4 jit_solution(5334568232232305609)
XLA Ops:
  17.2 50.3 %all-gather.8.cloned.1.call-done = bf16[16,880,128]{2,1,0:T(8,128)(2,1)} async-done(((bf16[1,880,128]{2,1,0:T(8,128)(2,1)}), bf16[16,880,128]{2,1,0:T(8,128)(2,1)}) %all-gather.8.cloned.1.call-update) | async-done | bytes 3604496 | tf_op jit(solution)/shard_map/all_gather | solution.py:416
  67.5 6.6 %reshape.1729 = bf16[8,2,112640]{2,1,0:T(2,128)(2,1)} reshape(bf16[16,880,128]{2,1,0:T(8,128)(2,1)} %all-gather.8.cloned.1.call-done) | data formatting | bytes 7208960 | tf_op jit(solution)/shard_map/reshape | solution.py:416
  76.2 4.7 reshape.1767
  80.9 5.5 copy.171
  86.4 4.0 reshape.1731
  91.4 2.9 constant_dynamic-slice_fusion.7
  97.0 2.3 copy.224
  107.4 8.7 %collective-permute-done = bf16[1,512,768]{1,2,0:T(8,128)(2,1)S(1)} collective-permute-done((bf16[1,512,768]{1,2,0:T(8,128)(2,1)}, bf16[1,512,768]{1,2,0:T(8,128)(2,1)S(1)}, u32[]{:S(2)}, u32[]{:S(2)}) %collective-permute-start) | collective-permute-done | bytes 786464 | tf_op jit(solution)/shard_map/ppermute | solution.py:742
  118.3 9.5 %fusion.85 = (bf16[3,1024,768]{2,1,0:T(8,128)(2,1)S(1)}, f32[3,1024,768]{2,1,0:T(8,128)}) fusion(bf16[3,768,768]{2,1,0:T(8,128)(2,1)} %reshape.1731, f32[768]{0:T(1024)S(1)} %mul.289, f32[1024]{0:T(1024)S(1)} %add_rsqrt_fusion.3, f32[1024]{0:T(1024)S(1)} %broadcast_multiply_fusion.11, bf16[512,768]{0,1:T(8,128)(2,1)S(1)} %bitcast.152, ...), kind=kOutput, calls=%fused_computation.284 | convolution fusion | flops 3637248000 | bytes 19278848 | tf_op jit(solution)/shard_map/rd,jde->jre/dot_general | solution.py:530
  142.9 3.4 fusion.21
  146.6 28.5 %shard_map.256 = f32[1,512,768]{2,1,0:T(8,128)S(1)} custom-call(bf16[1,512,768]{2,1,0:T(8,128)(2,1)S(1)} %get-tuple-element.146.q_ref, bf16[1,512,768]{2,1,0:T(8,128)(2,1)S(1)} %slice.270.k_ref, bf16[1,512,768]{2,1,0:T(8,128)(2,1)S(1)} %slice.273.v_ref, s32[12,512,8]{2,1,0:T(8,128)} %copy.219.patq_ref, s32[12,8,512]{2,1,0:T(8,128)S(1)} %slice.287.patk_ref, ...), custom_call_target="tpu_custom_call" | custom-call | flops 1610612736 | bytes 5505024 | tf_op jit(solution)/shard_map/pallas_call | solution.py:217
  175.1 34.8 %shard_map.257 = f32[1,512,768]{2,1,0:T(8,128)S(1)} custom-call(bf16[1,512,768]{2,1,0:T(8,128)(2,1)S(1)} %get-tuple-element.147.q_ref, bf16[1,1024,768]{2,1,0:T(8,128)(2,1)S(1)} %copy-done.12, bf16[1,1024,768]{2,1,0:T(8,128)(2,1)S(1)} %get-tuple-element.127.v_ref, s32[12,512,8]{2,1,0:T(8,128)} %copy.220.patq_ref, s32[12,8,1024]{2,1,0:T(8,128)S(1)} %copy-done.17, ...), custom_call_target="tpu_custom_call" | custom-call | flops 3221225472 | bytes 8650752 | tf_op jit(solution)/shard_map/pallas_call | solution.py:217
  210.7 3.1 reshape.1734
  220.2 9.3 %copy.183 = bf16[8,2,96,1536]{3,1,2,0:T(2,128)(2,1)} copy(bf16[8,2,96,1536]{3,2,1,0:T(8,128)(2,1)} %bitcast.165) | data formatting | bytes 9437184 | tf_op jit(solution)/shard_map/reshape | solution.py:407
  229.5 3.7 copy.226
  233.3 12.2 %fusion.73 = (f32[1024]{0:T(1024)S(1)}, f32[1024,3072]{1,0:T(8,128)}) fusion(f32[3072]{0:T(1024)S(1)} %reshape.1752, bf16[768,3072]{1,0:T(8,128)(2,1)S(1)} %bitcast.168, f32[1024,768]{0,1:T(8,128)S(1)} %copy-done.32, f32[768]{0:T(1024)S(1)} %mul.304, f32[1024]{0:T(1024)S(1)} %add_rsqrt_fusion.1, f32[1024]{0:T(1024)S(1)} %broadcast_multiply_fusion.9), kind=kOutput, calls=%fused_computation.273 | convolution fusion | flops 4866440192 | bytes 20474880 | tf_op jit(solution)/shard_map/dot_general | solution.py:551
  245.5 8.1 %multiply_reduce_fusion.2 = f32[1024]{0:T(1024)S(1)} fusion(f32[1024]{0:T(1024)S(1)} %broadcast_multiply_fusion.2, f32[1024,3072]{1,0:T(8,128)} %get-tuple-element.165, f32[3072]{0:T(1024)S(1)} %reshape.1752), kind=kLoop, calls=%fused_computation.12 | loop fusion | flops 37747712 | bytes 12603392 | tf_op jit(solution)/shard_map/reduce_sum | solution.py:73
  253.6 7.3 %reshape.1739 = bf16[8,2,1536,96]{2,1,0,3:T(2,128)(2,1)} reshape(bf16[24576,96]{0,1:T(8,128)(2,1)} %all-gather.14.cloned.1.call-done) | data formatting | bytes 9437184 | tf_op jit(solution)/shard_map/reshape | solution.py:407
  260.9 7.7 %copy.188 = bf16[8,2,1536,96]{2,1,3,0:T(2,128)(2,1)} copy(bf16[8,2,1536,96]{2,1,0,3:T(2,128)(2,1)} %reshape.1739) | data formatting | bytes 9437184 | tf_op jit(solution)/shard_map/reshape | solution.py:407
  268.6 3.6 copy.227
  272.2 22.0 %multiply_reduce_fusion = (bf16[3072]{0:T(1024)(128)(2,1)}, f32[1024]{0:T(1024)S(1)}, f32[1024]{0:T(1024)S(1)}, bf16[1024,3072]{1,0:T(8,128)(2,1)}, f32[1024,3072]{1,0:T(8,128)}) fusion(f32[1024]{0:T(1024)S(1)} %add_rsqrt_fusion, f32[1024]{0:T(1024)S(1)} %broadcast_multiply_fusion.2, f32[1024,3072]{1,0:T(8,128)} %get-tuple-element.165, ...), kind=kOutput, calls=%fused_computation.9 | convolution fusion | flops 4898679808 | bytes 37795840 | tf_op jit(solution)/shard_map/dot_general | solution.py:65
  294.2 17.2 %fusion.74 = (bf16[3072]{0:T(1024)(128)(2,1)}, bf16[1024,3072]{1,0:T(8,128)(2,1)S(1)}) fusion(f32[1024]{0:T(1024)S(1)} %broadcast_multiply_fusion, f32[1024]{0:T(1024)S(1)} %broadcast_multiply_fusion.2, f32[1024,3072]{1,0:T(8,128)} %get-tuple-element.165, f32[3072]{0:T(1024)S(1)} %reshape.1752, f32[1024]{0:T(1024)S(1)} %broadcast_multiply_fusion.1, ...), kind=kLoop, calls=%fused_computation.274 | loop fusion | flops 94368768 | bytes 31504384 | tf_op jit(solution)/shard_map/reduce_sum | solution.py:613
  311.4 8.6 %multiply_reduce_fusion.5 = (bf16[768]{0:T(1024)(128)(2,1)S(1)}, f32[1024]{0:T(1024)S(1)}, f32[1024]{0:T(1024)S(1)}, f32[1024,768]{0,1:T(8,128)}) fusion(f32[1024,768]{0,1:T(8,128)S(1)} %copy-done.33, f32[1024]{0:T(1024)S(1)} %add_rsqrt_fusion.1, f32[1024]{0:T(1024)S(1)} %broadcast_multiply_fusion.9, f32[768]{0:T(1024)S(1)} %mul.304, ...), kind=kOutput, calls=%fused_computation.55 | convolution fusion | flops 4838126592 | bytes 17322496 | tf_op jit(solution)/shard_map/dot_general | solution.py:65
  320.0 7.3 %convolution_convert_fusion = bf16[768,3072]{1,0:T(8,128)(2,1)} fusion(bf16[1024,3072]{1,0:T(8,128)(2,1)S(1)} %get-tuple-element.121, f32[1024,768]{0,1:T(8,128)S(1)} %copy-done.33, f32[768]{0:T(1024)S(1)} %mul.304, f32[1024]{0:T(1024)S(1)} %add_rsqrt_fusion.1, f32[1024]{0:T(1024)S(1)} %broadcast_multiply_fusion.9), kind=kOutput, calls=%fused_computation.16 | convolution fusion | flops 4837343232 | bytes 14167040 | tf_op jit(solution)/shard_map/dot_general | solution.py:59
  327.3 5.5 convert_reduce_fusion.2
  334.5 2.7 fusion.37
  337.1 6.5 %multiply_reduce_fusion.4 = (bf16[768]{0:T(1024)(128)(2,1)}, f32[1024]{0:T(1024)S(1)}, f32[1024]{0:T(1024)S(1)}, f32[1024,768]{1,0:T(8,128)}) fusion(f32[1024]{0:T(1024)S(1)} %add_rsqrt_fusion.2, f32[1024]{0:T(1024)S(1)} %broadcast_multiply_fusion.10, f32[1,512,768]{2,1,0:T(8,128)S(1)} %shard_map.257, f32[1,512,768]{2,1,0:T(8,128)S(1)} %shard_map.256, ...), kind=kOutput, calls=%fused_computation.53 | convolution fusion | flops 1215821056 | bytes 10637824 | tf_op jit(solution)/shard_map/dot_general | solution.py:65
  343.6 9.8 %convolution_convert_fusion.1 = bf16[768,3072]{1,0:T(8,128)(2,1)} fusion(bf16[1024,3072]{1,0:T(8,128)(2,1)} %get-tuple-element.126, bf16[512,768]{0,1:T(8,128)(2,1)} %bitcast.27, bf16[512,768]{0,1:T(8,128)(2,1)S(1)} %bitcast.175, pred[]{:T(512)S(6)} %eq.183), kind=kOutput, calls=%fused_computation.17 | convolution fusion | flops 4841275392 | bytes 12582913 | tf_op jit(solution)/shard_map/dot_general | solution.py:59
  353.5 3.7 multiply_convert_fusion.1
  371.4 49.5 %shard_map.259 = (bf16[1,512,768]{2,1,0:T(8,128)(2,1)S(1)}, f32[1,1024,768]{2,1,0:T(8,128)}, f32[1,1024,768]{2,1,0:T(8,128)}) custom-call(bf16[1,512,768]{2,1,0:T(8,128)(2,1)S(1)} %copy-done.20, bf16[1,1024,768]{2,1,0:T(8,128)(2,1)S(1)} %copy-done.13, bf16[1,1024,768]{2,1,0:T(8,128)(2,1)S(1)} %copy-done.3, ...), custom_call_target="tpu_custom_call" | custom-call | flops 8053063680 | bytes 20447232 | tf_op jit(solution)/shard_map/pallas_call | solution.py:244
  426.4 30.9 %shard_map.258 = (bf16[1,512,768]{2,1,0:T(8,128)(2,1)S(1)}, f32[1,512,768]{2,1,0:T(8,128)S(1)}, f32[1,512,768]{2,1,0:T(8,128)}) custom-call(bf16[1,512,768]{2,1,0:T(8,128)(2,1)S(1)} %copy-done.9, bf16[1,512,768]{2,1,0:T(8,128)(2,1)S(1)} %copy-done.5, bf16[1,512,768]{2,1,0:T(8,128)(2,1)S(1)} %copy-done.7, bf16[1,512,768]{2,1,0:T(8,128)(2,1)S(1)} %copy-done.21, ...), custom_call_target="tpu_custom_call" | custom-call | flops 4026531840 | bytes 11010048 | tf_op jit(solution)/shard_map/pallas_call | solution.py:244
  458.6 4.0 fusion.76
  462.9 2.3 add_convert_fusion.1
  465.6 2.8 pad_maximum_fusion
  468.7 10.0 %fusion.19 = (bf16[768]{0:T(1024)(128)(2,1)S(1)}, f32[1024]{0:T(1024)}, f32[1024]{0:T(1024)S(1)}, f32[1024,768,1]{0,1,2:T(8,128)}) fusion(f32[1024]{0:T(1024)S(1)} %copy-done.56, f32[1024]{0:T(1024)S(1)} %copy-done.52, bf16[512,768]{0,1:T(8,128)(2,1)S(1)} %bitcast.154, bf16[512,768]{0,1:T(8,128)(2,1)S(1)} %bitcast.161, pred[]{:T(512)S(6)} %eq.183, ...), kind=kOutput, calls=%fused_computation.38 | convolution fusion | flops 3638031616 | bytes 12997121 | tf_op jit(solution)/shard_map/jre,jde->rd/dot_general | solution.py:657
  481.2 3.1 reshape.1749
  484.4 6.9 %convolution_convert_fusion.2 = bf16[768,3,768]{2,0,1:T(8,128)(2,1)S(1)} fusion(bf16[3,1024,768]{2,1,0:T(8,128)(2,1)} %pad_maximum_fusion, f32[768]{0:T(1024)S(1)} %copy-done.58, f32[1024]{0:T(1024)S(1)} %copy-done.56, f32[1024]{0:T(1024)S(1)} %copy-done.52, bf16[512,768]{0,1:T(8,128)(2,1)S(1)} %bitcast.162, bf16[512,768]{0,1:T(8,128)(2,1)S(1)} %bitcast.155, ...), kind=kOutput, calls=%fused_computation.71 | convolution fusion | flops 3636658176 | bytes 9841665 | tf_op jit(solution)/shard_map/rd,jre->dje/dot_general | solution.py:653
  491.3 2.5 pad_maximum_fusion.1
  494.6 10.2 %add_convert_fusion.2 = bf16[1024,768]{0,1:T(8,128)(2,1)S(1)} fusion(f32[1024,768]{0,1:T(8,128)} %copy-done.31, bf16[1024,3072]{1,0:T(8,128)(2,1)} %get-tuple-element.126, bf16[3072,768]{0,1:T(8,128)(2,1)} %bitcast.167, f32[768]{0:T(1024)S(1)} %add.753), kind=kOutput, calls=%fused_computation.62 | convolution fusion | flops 4834197504 | bytes 15731712 | tf_op jit(solution)/shard_map/dot_general | solution.py:556
  510.1 16.9 %collective-permute-done.1 = bf16[1,512,768]{2,1,0:T(8,128)(2,1)} collective-permute-done((bf16[1,512,768]{2,1,0:T(8,128)(2,1)}, bf16[1,512,768]{2,1,0:T(8,128)(2,1)}, u32[]{:S(2)}, u32[]{:S(2)}) %collective-permute-start.1) | collective-permute-done | bytes 786464 | tf_op jit(solution)/shard_map/ppermute | solution.py:355
  527.0 2.8 maximum_select_fusion.3
  531.5 10.2 %collective-permute-done.3 = bf16[1,512,768]{2,1,0:T(8,128)(2,1)} collective-permute-done((bf16[1,512,768]{2,1,0:T(8,128)(2,1)}, bf16[1,512,768]{2,1,0:T(8,128)(2,1)}, u32[]{:S(2)}, u32[]{:S(2)}) %collective-permute-start.3) | collective-permute-done | bytes 786464 | tf_op jit(solution)/shard_map/ppermute | solution.py:357
  560.6 17.3 %collective-permute-done.14 = bf16[96,1536]{1,0:T(8,128)(2,1)S(1)} collective-permute-done((bf16[96,1536]{1,0:T(8,128)(2,1)}, bf16[96,1536]{1,0:T(8,128)(2,1)S(1)}, u32[]{:S(2)}, u32[]{:S(2)}) %collective-permute-start.14) | collective-permute-done | bytes 294944 | tf_op jit(solution)/shard_map/ppermute | solution.py:445
  580.4 3.8 collective-permute-done.12
  586.8 11.1 %collective-permute-done.15 = bf16[96,1536]{1,0:T(8,128)(2,1)S(1)} collective-permute-done((bf16[96,1536]{1,0:T(8,128)(2,1)S(1)}, bf16[96,1536]{1,0:T(8,128)(2,1)S(1)}, u32[]{:S(2)}, u32[]{:S(2)}) %collective-permute-start.15) | collective-permute-done | bytes 294944 | tf_op jit(solution)/shard_map/ppermute | solution.py:452
  598.7 2.3 collective-permute-done.13
  606.5 3.2 collective-permute-done.8
  613.2 3.3 collective-permute-done.9
  (349 shorter events, 120.4 us)
Async XLA Ops:
  7.2 92.7 %copy-start = (s32[4,2]{0,1:T(2,128)S(1)}, s32[4,2]{0,1:T(2,128)}, u32[]{:S(2)}) copy-start(s32[4,2]{0,1:T(2,128)} %param.21) | copy-start | bytes 100
  7.2 60.3 %all-gather.8.cloned.1.call-start = ((), (), s32[]{:S(2)}) async-start(), calls=%async_computation.4 | async-start | bytes 3829760 | tf_op jit(solution)/shard_map/all_gather | solution.py:416
  17.2 193.5 %all-gather.10.cloned.1.call-start = ((), (), s32[]{:S(2)}) async-start(), calls=%async_computation.9 | async-start | bytes 1253376 | tf_op jit(solution)/shard_map/all_gather | solution.py:406
  90.4 129.8 %all-gather.12.cloned.1.call-start = ((), (), s32[]{:S(2)}) async-start(), calls=%async_computation.10 | async-start | bytes 5013504 | tf_op jit(solution)/shard_map/all_gather | solution.py:406
  91.2 162.4 %all-gather.14.cloned.1.call-start = ((), (), s32[]{:S(2)}) async-start(), calls=%async_computation.11 | async-start | bytes 5013504 | tf_op jit(solution)/shard_map/all_gather | solution.py:406
  95.5 20.6 %collective-permute-start = (bf16[1,512,768]{1,2,0:T(8,128)(2,1)}, bf16[1,512,768]{1,2,0:T(8,128)(2,1)S(1)}, u32[]{:S(2)}, u32[]{:S(2)}) collective-permute-start(bf16[1,512,768]{1,2,0:T(8,128)(2,1)} %copy.217), channel_id=1, source_target_pairs={{0,2},{2,0},{1,3},{3,1},{4,6},{6,4},{5,7},{7,5},{8,10},{10,8},{9,1... | collective-permute-start | bytes 2359304 | tf_op jit(solution)/shard_map/ppermute | solution.py:742
  99.3 172.9 %collective-permute-start.4 = (bf16[1,512,768]{1,2,0:T(8,128)(2,1)}, bf16[1,512,768]{1,2,0:T(8,128)(2,1)}, u32[]{:S(2)}, u32[]{:S(2)}) collective-permute-start(bf16[1,512,768]{1,2,0:T(8,128)(2,1)} %copy.224), channel_id=1, source_target_pairs={{0,2},{2,0},{1,3},{3,1},{4,6},{6,4},{5,7},{7,5},{8,10},{10,8},{9,1... | collective-permute-start | bytes 2359304 | tf_op jit(solution)/shard_map/ppermute | solution.py:742
  104.5 23.3 %copy-start.28 = (bf16[1,512,768]{1,2,0:T(8,128)(2,1)}, bf16[1,512,768]{1,2,0:T(8,128)(2,1)S(1)}, u32[]{:S(2)}) copy-start(bf16[1,512,768]{1,2,0:T(8,128)(2,1)S(1)} %copy.165) | copy-start | bytes 2359300
  104.5 12.8 %copy-start.26 = (bf16[8,2,112640]{2,1,0:T(2,128)(2,1)S(1)}, bf16[8,2,112640]{2,1,0:T(2,128)(2,1)}, u32[]{:S(2)}) copy-start(bf16[8,2,112640]{2,1,0:T(2,128)(2,1)} %reshape.1729) | copy-start | bytes 10813444
  116.1 11.7 %copy-start.36 = (bf16[1,512,768]{1,2,0:T(8,128)(2,1)}, bf16[1,512,768]{1,2,0:T(8,128)(2,1)S(1)}, u32[]{:S(2)}) copy-start(bf16[1,512,768]{1,2,0:T(8,128)(2,1)S(1)} %collective-permute-done) | copy-start | bytes 2359300
  116.6 11.2 %copy-start.51 = (f32[1024]{0:T(1024)}, f32[1024]{0:T(1024)S(1)}, u32[]{:S(2)}) copy-start(f32[1024]{0:T(1024)S(1)} %broadcast_multiply_fusion.11) | copy-start | bytes 12292
  117.3 10.6 %copy-start.55 = (f32[1024]{0:T(1024)}, f32[1024]{0:T(1024)S(1)}, u32[]{:S(2)}) copy-start(f32[1024]{0:T(1024)S(1)} %add_rsqrt_fusion.3) | copy-start | bytes 12292
  127.9 18.6 %copy-start.4 = (bf16[1,512,768]{2,1,0:T(8,128)(2,1)}, bf16[1,512,768]{2,1,0:T(8,128)(2,1)S(1)}, u32[]{:S(2)}) copy-start(bf16[1,512,768]{2,1,0:T(8,128)(2,1)S(1)} %slice.270.k_ref) | copy-start | bytes 2359300
  135.2 11.4 %copy-start.22 = (s32[12,8,512]{2,1,0:T(8,128)}, s32[12,8,512]{2,1,0:T(8,128)S(1)}, u32[]{:S(2)}) copy-start(s32[12,8,512]{2,1,0:T(8,128)S(1)} %slice.287.patk_ref) | copy-start | bytes 589828
  135.5 333.1 %reduce-scatter.5.cloned.1.call-start = ((), (), s32[]{:S(2)}) async-start(), calls=%async_computation.5 | async-start | bytes 5308416 | tf_op jit(solution)/shard_map/reduce_scatter | solution.py:515
  146.3 28.8 %copy-start.2 = (bf16[1,1024,768]{2,1,0:T(8,128)(2,1)}, bf16[1,1024,768]{2,1,0:T(8,128)(2,1)S(1)}, u32[]{:S(2)}) copy-start(bf16[1,1024,768]{2,1,0:T(8,128)(2,1)S(1)} %get-tuple-element.127.v_ref) | copy-start | bytes 4718596
  146.4 28.7 %copy-start.6 = (bf16[1,512,768]{2,1,0:T(8,128)(2,1)}, bf16[1,512,768]{2,1,0:T(8,128)(2,1)S(1)}, u32[]{:S(2)}) copy-start(bf16[1,512,768]{2,1,0:T(8,128)(2,1)S(1)} %slice.273.v_ref) | copy-start | bytes 2359300
  146.5 28.6 %copy-start.8 = (bf16[1,512,768]{2,1,0:T(8,128)(2,1)}, bf16[1,512,768]{2,1,0:T(8,128)(2,1)S(1)}, u32[]{:S(2)}) copy-start(bf16[1,512,768]{2,1,0:T(8,128)(2,1)S(1)} %get-tuple-element.146.q_ref) | copy-start | bytes 2359300
  146.5 28.6 %copy-start.19 = (bf16[1,512,768]{2,1,0:T(8,128)(2,1)}, bf16[1,512,768]{2,1,0:T(8,128)(2,1)S(1)}, u32[]{:S(2)}) copy-start(bf16[1,512,768]{2,1,0:T(8,128)(2,1)S(1)} %get-tuple-element.147.q_ref) | copy-start | bytes 2359300
  146.5 28.6 %copy-start.12 = (bf16[1,1024,768]{2,1,0:T(8,128)(2,1)S(1)}, bf16[1,1024,768]{2,1,0:T(8,128)(2,1)}, u32[]{:S(2)}) copy-start(bf16[1,1024,768]{2,1,0:T(8,128)(2,1)} %slice.289.k_ref) | copy-start | bytes 4718596
  146.6 28.6 %copy-start.17 = (s32[12,8,1024]{2,1,0:T(8,128)S(1)}, s32[12,8,1024]{2,1,0:T(8,128)}, u32[]{:S(2)}) copy-start(s32[12,8,1024]{2,1,0:T(8,128)} %copy-done.16) | copy-start | bytes 1179652
  146.6 28.6 %copy-start.24 = (s32[1,512,8]{2,1,0:T(8,128)S(1)}, s32[1,512,8]{2,1,0:T(8,128)}, u32[]{:S(2)}) copy-start(s32[1,512,8]{2,1,0:T(8,128)} %get-tuple-element.149.pcq_ref) | copy-start | bytes 49156
  233.3 12.2 %copy-start.43 = (bf16[96,8,2,1536]{3,1,2,0:T(8,128)(2,1)}, bf16[96,8,2,1536]{3,1,2,0:T(8,128)(2,1)S(1)}, u32[]{:S(2)}) copy-start(bf16[96,8,2,1536]{3,1,2,0:T(8,128)(2,1)S(1)} %copy.226) | copy-start | bytes 14155780
  272.2 22.0 %copy-start.42 = (bf16[96,8,2,1536]{3,1,2,0:T(8,128)(2,1)}, bf16[96,8,2,1536]{3,1,2,0:T(8,128)(2,1)S(1)}, u32[]{:S(2)}) copy-start(bf16[96,8,2,1536]{3,1,2,0:T(8,128)(2,1)S(1)} %copy.227) | copy-start | bytes 14155780
  294.2 17.2 %copy-start.33 = (f32[1024,768]{0,1:T(8,128)S(1)}, f32[1024,768]{0,1:T(8,128)}, u32[]{:S(2)}) copy-start(f32[1024,768]{0,1:T(8,128)} %copy-done.31) | copy-start | bytes 9437188
  357.2 111.4 %reduce-scatter.7.cloned.1.call-start = ((), (), s32[]{:S(2)}) async-start(), calls=%async_computation.6 | async-start | bytes 5308416 | tf_op jit(solution)/shard_map/reduce_scatter | solution.py:515
  357.8 172.0 %reduce-scatter.11.cloned.1.call-start = ((), (), s32[]{:S(2)}) async-start(), calls=%async_computation.8 | async-start | bytes 1327104 | tf_op jit(solution)/shard_map/reduce_scatter | solution.py:515
  371.4 51.7 %copy-start.5 = (bf16[1,512,768]{2,1,0:T(8,128)(2,1)S(1)}, bf16[1,512,768]{2,1,0:T(8,128)(2,1)}, u32[]{:S(2)}) copy-start(bf16[1,512,768]{2,1,0:T(8,128)(2,1)} %copy-done.4) | copy-start | bytes 2359300
  371.4 51.7 %copy-start.7 = (bf16[1,512,768]{2,1,0:T(8,128)(2,1)S(1)}, bf16[1,512,768]{2,1,0:T(8,128)(2,1)}, u32[]{:S(2)}) copy-start(bf16[1,512,768]{2,1,0:T(8,128)(2,1)} %copy-done.6) | copy-start | bytes 2359300
  462.8 139.1 %reduce-scatter.9.cloned.1.call-start = ((), (), s32[]{:S(2)}) async-start(), calls=%async_computation.7 | async-start | bytes 5308416 | tf_op jit(solution)/shard_map/reduce_scatter | solution.py:515
  468.6 10.4 %copy-start.53 = (bf16[16,192]{1,0:T(8,128)(2,1)S(1)}, bf16[16,192]{1,0:T(8,128)(2,1)}, u32[]{:S(2)}) copy-start(bf16[16,192]{1,0:T(8,128)(2,1)} %reshape.1743) | copy-start | bytes 18436
  468.6 10.4 %copy-start.54 = (bf16[16,192]{1,0:T(8,128)(2,1)S(1)}, bf16[16,192]{1,0:T(8,128)(2,1)}, u32[]{:S(2)}) copy-start(bf16[16,192]{1,0:T(8,128)(2,1)} %reshape.1746) | copy-start | bytes 18436
  506.2 20.7 %collective-permute-start.1 = (bf16[1,512,768]{2,1,0:T(8,128)(2,1)}, bf16[1,512,768]{2,1,0:T(8,128)(2,1)}, u32[]{:S(2)}, u32[]{:S(2)}) collective-permute-start(bf16[1,512,768]{2,1,0:T(8,128)(2,1)} %bitcast.184), channel_id=1, source_target_pairs={{0,2},{2,0},{1,3},{3,1},{4,6},{6,4},{5,7},{7,5},{8,10},{10,8},{9,1... | collective-permute-start | bytes 2359304 | tf_op jit(solution)/shard_map/ppermute | solution.py:355
  507.7 34.0 %collective-permute-start.3 = (bf16[1,512,768]{2,1,0:T(8,128)(2,1)}, bf16[1,512,768]{2,1,0:T(8,128)(2,1)}, u32[]{:S(2)}, u32[]{:S(2)}) collective-permute-start(bf16[1,512,768]{2,1,0:T(8,128)(2,1)} %bitcast.185), channel_id=1, source_target_pairs={{0,3},{3,0},{1,2},{2,1},{4,7},{7,4},{5,6},{6,5},{8,11},{11,8},{9,1... | collective-permute-start | bytes 2359304 | tf_op jit(solution)/shard_map/ppermute | solution.py:357
  508.6 35.2 %collective-permute-start.2 = (bf16[1,512,768]{2,1,0:T(8,128)(2,1)S(1)}, bf16[1,512,768]{2,1,0:T(8,128)(2,1)S(1)}, u32[]{:S(2)}, u32[]{:S(2)}) collective-permute-start(bf16[1,512,768]{2,1,0:T(8,128)(2,1)S(1)} %bitcast.178), channel_id=1, source_target_pairs={{0,1},{1,0},{2,3},{3,2},{4,5},{5,4},{6,7},{7,6},{8,9},{9,8},{10,11... | collective-permute-start | bytes 2359304 | tf_op jit(solution)/shard_map/ppermute | solution.py:356
  529.8 15.7 %copy-start.50 = (bf16[96,768]{1,0:T(8,128)(2,1)S(1)}, bf16[96,768]{1,0:T(8,128)(2,1)}, u32[]{:S(2)}) copy-start(bf16[96,768]{1,0:T(8,128)(2,1)} %reduce-scatter.11.cloned.1.call-done) | copy-start | bytes 442372
  529.8 17.4 %copy-start.41 = (bf16[2,512,768]{2,1,0:T(8,128)(2,1)S(1)}, bf16[2,512,768]{2,1,0:T(8,128)(2,1)}, u32[]{:S(2)}) copy-start(bf16[2,512,768]{2,1,0:T(8,128)(2,1)} %maximum_select_fusion.3) | copy-start | bytes 4718596
  530.8 14.7 %collective-permute-start.10 = (bf16[96,384]{1,0:T(8,128)(2,1)S(1)}, bf16[96,384]{1,0:T(8,128)(2,1)S(1)}, u32[]{:S(2)}, u32[]{:S(2)}) collective-permute-start(bf16[96,384]{1,0:T(8,128)(2,1)S(1)} %constant_dynamic-slice_fusion.2), channel_id=1, source_target_pairs={{0,1},{1,0},{2,3},{3,2},{4,5},{5,4},{6,7},{7,6},{8,9},{9,8},{10,11... | collective-permute-start | bytes 221192 | tf_op jit(solution)/shard_map/ppermute | solution.py:445
  545.6 4.4 collective-permute-start.11
  551.4 26.5 %collective-permute-start.14 = (bf16[96,1536]{1,0:T(8,128)(2,1)}, bf16[96,1536]{1,0:T(8,128)(2,1)S(1)}, u32[]{:S(2)}, u32[]{:S(2)}) collective-permute-start(bf16[96,1536]{1,0:T(8,128)(2,1)} %constant_dynamic-slice_fusion), channel_id=1, source_target_pairs={{0,1},{1,0},{2,3},{3,2},{4,5},{5,4},{6,7},{7,6},{8,9},{9,8},{10,11... | collective-permute-start | bytes 884744 | tf_op jit(solution)/shard_map/ppermute | solution.py:445
  555.2 51.0 %collective-permute-start.7 = (bf16[1,512,768]{2,1,0:T(8,128)(2,1)S(1)}, bf16[1,512,768]{2,1,0:T(8,128)(2,1)S(1)}, u32[]{:S(2)}, u32[]{:S(2)}) collective-permute-start(bf16[1,512,768]{2,1,0:T(8,128)(2,1)S(1)} %bitcast.182), channel_id=1, source_target_pairs={{0,3},{3,0},{1,2},{2,1},{4,7},{7,4},{5,6},{6,5},{8,11},{11,8},{9,1... | collective-permute-start | bytes 2359304 | tf_op jit(solution)/shard_map/ppermute | solution.py:357
  556.7 47.8 %collective-permute-start.5 = (bf16[1,512,768]{2,1,0:T(8,128)(2,1)S(1)}, bf16[1,512,768]{2,1,0:T(8,128)(2,1)}, u32[]{:S(2)}, u32[]{:S(2)}) collective-permute-start(bf16[1,512,768]{2,1,0:T(8,128)(2,1)S(1)} %bitcast.183), channel_id=1, source_target_pairs={{0,2},{2,0},{1,3},{3,1},{4,6},{6,4},{5,7},{7,5},{8,10},{10,8},{9,1... | collective-permute-start | bytes 2359304 | tf_op jit(solution)/shard_map/ppermute | solution.py:355
  558.5 25.7 %collective-permute-start.12 = (bf16[96,1536]{1,0:T(8,128)(2,1)S(1)}, bf16[96,1536]{1,0:T(8,128)(2,1)S(1)}, u32[]{:S(2)}, u32[]{:S(2)}) collective-permute-start(bf16[96,1536]{1,0:T(8,128)(2,1)S(1)} %constant_dynamic-slice_fusion.1), channel_id=1, source_target_pairs={{0,1},{1,0},{2,3},{3,2},{4,5},{5,4},{6,7},{7,6},{8,9},{9,8},{10,11... | collective-permute-start | bytes 884744 | tf_op jit(solution)/shard_map/ppermute | solution.py:445
  560.1 46.1 %collective-permute-start.6 = (bf16[1,512,768]{2,1,0:T(8,128)(2,1)S(1)}, bf16[1,512,768]{2,1,0:T(8,128)(2,1)S(1)}, u32[]{:S(2)}, u32[]{:S(2)}) collective-permute-start(bf16[1,512,768]{2,1,0:T(8,128)(2,1)S(1)} %bitcast.176), channel_id=1, source_target_pairs={{0,1},{1,0},{2,3},{3,2},{4,5},{5,4},{6,7},{7,6},{8,9},{9,8},{10,11... | collective-permute-start | bytes 2359304 | tf_op jit(solution)/shard_map/ppermute | solution.py:356
  578.9 18.9 %collective-permute-start.15 = (bf16[96,1536]{1,0:T(8,128)(2,1)S(1)}, bf16[96,1536]{1,0:T(8,128)(2,1)S(1)}, u32[]{:S(2)}, u32[]{:S(2)}) collective-permute-start(bf16[96,1536]{1,0:T(8,128)(2,1)S(1)} %add_convert_fusion.3), channel_id=1, source_target_pairs={{0,2},{2,0},{1,3},{3,1},{4,6},{6,4},{5,7},{7,5},{8,10},{10,8},{9,1... | collective-permute-start | bytes 884744 | tf_op jit(solution)/shard_map/ppermute | solution.py:452
  585.3 15.7 %collective-permute-start.13 = (bf16[96,1536]{1,0:T(8,128)(2,1)S(1)}, bf16[96,1536]{1,0:T(8,128)(2,1)S(1)}, u32[]{:S(2)}, u32[]{:S(2)}) collective-permute-start(bf16[96,1536]{1,0:T(8,128)(2,1)S(1)} %add_convert_fusion.4), channel_id=1, source_target_pairs={{0,2},{2,0},{1,3},{3,1},{4,6},{6,4},{5,7},{7,5},{8,10},{10,8},{9,1... | collective-permute-start | bytes 884744 | tf_op jit(solution)/shard_map/ppermute | solution.py:452
  602.9 6.8 %collective-permute-start.8 = (bf16[96,4,384]{2,0,1:T(8,128)(2,1)S(1)}, bf16[96,4,384]{2,0,1:T(8,128)(2,1)S(1)}, u32[]{:S(2)}, u32[]{:S(2)}) collective-permute-start(bf16[96,4,384]{2,0,1:T(8,128)(2,1)S(1)} %constant_dynamic-slice_fusion.3), channel_id=1, source_target_pairs={{0,1},{1,0},{2,3},{3,2},{4,5},{5,4},{6,7},{7,6},{8,9},{9,8},{10,11... | collective-permute-start | bytes 884744 | tf_op jit(solution)/shard_map/ppermute | solution.py:445
  609.8 6.8 %collective-permute-start.9 = (bf16[96,4,384]{2,0,1:T(8,128)(2,1)S(1)}, bf16[96,4,384]{2,0,1:T(8,128)(2,1)S(1)}, u32[]{:S(2)}, u32[]{:S(2)}) collective-permute-start(bf16[96,4,384]{2,0,1:T(8,128)(2,1)S(1)} %add_convert_fusion.5), channel_id=1, source_target_pairs={{0,2},{2,0},{1,3},{3,1},{4,6},{6,4},{5,7},{7,5},{8,10},{10,8},{9,1... | collective-permute-start | bytes 884744 | tf_op jit(solution)/shard_map/ppermute | solution.py:452
  (40 other events, 151.5 us)
Sparse Core Ops, SparseCore 0:
  17.3 50.1 all-gather.7
  90.6 35.6 all-gather.9
  128.6 52.5 all-gather.11
  183.4 51.6 all-gather.13
  357.3 53.6 reduce-scatter.4
  413.2 53.3 reduce-scatter.6
  468.9 31.4 reduce-scatter.10
  502.7 53.0 reduce-scatter.8

commit v7 on v6

--- a/solution.py
+++ b/solution.py
@@ -654,6 +654,7 @@
     head_bias_grad = jnp.stack(
         [jnp.sum(query_low, 0, dtype=jnp.float32), jnp.sum(value_low, 0, dtype=jnp.float32)]
     )
+    qkv_grad, stacked = lax.optimization_barrier((qkv_grad, stacked))
     attn_in_grad = jnp.einsum("jre,jde->rd", stacked, w_qkv, preferred_element_type=jnp.float32)
     input_part, first_gain_grad = norm_back(first_normed, first_inv, norm_gains[0], attn_in_grad)
     input_low = (middle_grad + input_part).astype(jnp.bfloat16)
@@ -674,16 +675,21 @@
     )
     small_width = small_rows.shape[1]
     block_rows = model_width // ns
-    block_cols = model_width // nt
-    small_plane = (
-        jnp.pad(small_rows, ((0, 0), (0, block_rows * block_cols - small_width)))
-        .reshape(ns, nt, block_rows, block_cols)
-        .transpose(0, 2, 1, 3)
-        .reshape(model_width, 1, model_width)
-    )
-    qkv_share = shard_stage(jnp.concatenate([qkv_grad, small_plane], 1), 0)
+    extra_rows = 8
+    planes = qkv_grad.shape[1]
+    slots = extra_rows * planes * (model_width // nt)
+    small_block = (
+        jnp.pad(small_rows, ((0, 0), (0, slots - small_width)))
+        .reshape(ns, nt, extra_rows, planes, model_width // nt)
+        .transpose(0, 2, 3, 1, 4)
+        .reshape(ns, extra_rows, planes, model_width)
+    )
+    widened = jnp.concatenate(
+        [qkv_grad.reshape(ns, block_rows, planes, model_width), small_block.astype(qkv_grad.dtype)], 1
+    ).reshape(ns * (block_rows + extra_rows), planes, model_width)
+    qkv_share = shard_stage(widened, 0)
     qkv_total = finish_stage(qkv_share, 2)
-    small_total = qkv_total[:, 3].reshape(-1)[:small_width]
+    small_total = qkv_total[block_rows:].reshape(-1)[:small_width]
     small_pieces = []
     offset = 0
     for full, shard_dim, tensor_dim in small_terms:
@@ -701,7 +707,7 @@
         finish_stage(down_share, 1).transpose(1, 0),
         finish_stage(up_share, 1),
         finish_stage(out_share, 1).transpose(1, 0),
-        qkv_total[:, :3].transpose(1, 0, 2),
+        qkv_total[:block_rows].transpose(1, 0, 2),
     ) + tuple(small_pieces)
     return (grad_shares, input_low.reshape(seq_count, local_len, model_width))
 

time: 636 us -> 631 us (level)
  transfers between devices with their start and end apart: 24 -> 24, of which waited for: 12 -> 12; matrix products, arithmetic and copies ran while one was open for 28% -> 29% of each run, Pallas kernels for 23% -> 23%
where the time goes in v7:
time: 631 us; the launch traced here: 625 us
  Pallas kernels  143 us (23%)
  local copies, waits for them, and re-layouts  128 us (20%)
  waiting for transfers between devices  128 us (20%)
  matrix products  107 us (17%)
  other arithmetic  81.3 us (13%)
  starting transfers between devices  21 us (3%)
  between operations  17.2 us (3%)
    pallas_call x2, Pallas kernels, attention_backward(): pl.pallas_call(attention_bwd_kernel, grid=grid, in_specs=[query_spec, key...  80.2 us
    pallas_call x2, Pallas kernels, attention_forward(): pl.pallas_call(attention_fwd_kernel, grid=grid, in_specs=[query_spec, key...  63.3 us
    all_gather x1, waiting for transfers between devices, gather_packed(): lax.all_gather(flat, ('shard', 'tensor'), axis=0, tiled=False)  50.3 us
    unnamed x138, local copies, waits for them, and re-layouts  39.1 us
    dot_general x3, matrix products, back_dot(): lax.dot_general(left_rows, weight_rows, (((1,), (1,)), ((), ())), preferr...  37.1 us
    reshape x5, local copies, waits for them, and re-layouts, gather_weight(): stacked.reshape((ns, nt) + local_block.shape)  29.7 us
    ppermute x4, waiting for transfers between devices, pair_reduce(): received = lax.ppermute(sent, axis_name, perm=[(0, 1), (1, 0)])  20.8 us
    dot_general x3, matrix products, outer_sum(): lax.dot_general(left_rows, right_rows, (((0,), (0,)), ((), ())), preferre...  19.6 us
  transfers between devices with their start and end apart: 24, of which 12 were waited for; matrix products, arithmetic and copies ran while one was open for 29% of the time, Pallas kernels for 23%

profile of v7, /device:TPU:0, one launch (start us, length us, event | category | flops | bytes accessed | tf_op | source)
XLA Modules:
  0.0 625.1 jit_solution(15489478507647083977)
XLA Ops:
  17.2 50.3 %all-gather.8.cloned.1.call-done = bf16[16,880,128]{2,1,0:T(8,128)(2,1)} async-done(((bf16[1,880,128]{2,1,0:T(8,128)(2,1)}), bf16[16,880,128]{2,1,0:T(8,128)(2,1)}) %all-gather.8.cloned.1.call-update) | async-done | bytes 3604496 | tf_op jit(solution)/shard_map/all_gather | solution.py:416
  67.5 6.6 %reshape.1736 = bf16[8,2,112640]{2,1,0:T(2,128)(2,1)} reshape(bf16[16,880,128]{2,1,0:T(8,128)(2,1)} %all-gather.8.cloned.1.call-done) | data formatting | bytes 7208960 | tf_op jit(solution)/shard_map/reshape | solution.py:416
  76.2 4.7 reshape.1775
  80.9 5.5 copy.180
  86.4 4.0 reshape.1738
  91.4 2.9 constant_dynamic-slice_fusion.8
  97.0 2.3 copy.241
  107.4 8.7 %collective-permute-done = bf16[1,512,768]{1,2,0:T(8,128)(2,1)S(1)} collective-permute-done((bf16[1,512,768]{1,2,0:T(8,128)(2,1)}, bf16[1,512,768]{1,2,0:T(8,128)(2,1)S(1)}, u32[]{:S(2)}, u32[]{:S(2)}) %collective-permute-start) | collective-permute-done | bytes 786464 | tf_op jit(solution)/shard_map/ppermute | solution.py:748
  117.8 9.5 %fusion.86 = (bf16[3,1024,768]{2,1,0:T(8,128)(2,1)S(1)}, f32[3,1024,768]{2,1,0:T(8,128)}) fusion(bf16[3,768,768]{2,1,0:T(8,128)(2,1)} %reshape.1738, f32[768]{0:T(1024)S(1)} %mul.289, f32[1024]{0:T(1024)S(1)} %add_rsqrt_fusion.3, f32[1024]{0:T(1024)S(1)} %broadcast_multiply_fusion.11, bf16[512,768]{0,1:T(8,128)(2,1)S(1)} %bitcast.151, ...), kind=kOutput, calls=%fused_computation.285 | convolution fusion | flops 3637248000 | bytes 19278848 | tf_op jit(solution)/shard_map/rd,jde->jre/dot_general | solution.py:530
  142.5 3.4 fusion.21
  146.1 28.5 %shard_map.256 = f32[1,512,768]{2,1,0:T(8,128)S(1)} custom-call(bf16[1,512,768]{2,1,0:T(8,128)(2,1)S(1)} %get-tuple-element.160.q_ref, bf16[1,512,768]{2,1,0:T(8,128)(2,1)S(1)} %slice.270.k_ref, bf16[1,512,768]{2,1,0:T(8,128)(2,1)S(1)} %slice.273.v_ref, s32[12,512,8]{2,1,0:T(8,128)} %copy.236.patq_ref, s32[12,8,512]{2,1,0:T(8,128)S(1)} %slice.287.patk_ref, ...), custom_call_target="tpu_custom_call" | custom-call | flops 1610612736 | bytes 5505024 | tf_op jit(solution)/shard_map/pallas_call | solution.py:217
  174.6 34.8 %shard_map.257 = f32[1,512,768]{2,1,0:T(8,128)S(1)} custom-call(bf16[1,512,768]{2,1,0:T(8,128)(2,1)S(1)} %get-tuple-element.161.q_ref, bf16[1,1024,768]{2,1,0:T(8,128)(2,1)S(1)} %copy-done.12, bf16[1,1024,768]{2,1,0:T(8,128)(2,1)S(1)} %get-tuple-element.143.v_ref, s32[12,512,8]{2,1,0:T(8,128)} %copy.237.patq_ref, s32[12,8,1024]{2,1,0:T(8,128)S(1)} %copy-done.17, ...), custom_call_target="tpu_custom_call" | custom-call | flops 3221225472 | bytes 8650752 | tf_op jit(solution)/shard_map/pallas_call | solution.py:217
  210.2 3.2 reshape.1741
  213.4 2.2 copy.191
  219.7 9.3 %copy.192 = bf16[8,2,96,1536]{3,1,2,0:T(2,128)(2,1)} copy(bf16[8,2,96,1536]{3,2,1,0:T(8,128)(2,1)} %bitcast.164) | data formatting | bytes 9437184 | tf_op jit(solution)/shard_map/reshape | solution.py:407
  229.1 3.7 copy.246
  232.8 12.2 %fusion.74 = (f32[1024]{0:T(1024)S(1)}, f32[1024,3072]{1,0:T(8,128)}) fusion(f32[3072]{0:T(1024)S(1)} %reshape.1760, bf16[768,3072]{1,0:T(8,128)(2,1)S(1)} %bitcast.167, f32[1024,768]{0,1:T(8,128)S(1)} %copy-done.32, f32[768]{0:T(1024)S(1)} %mul.304, f32[1024]{0:T(1024)S(1)} %add_rsqrt_fusion.1, f32[1024]{0:T(1024)S(1)} %broadcast_multiply_fusion.9), kind=kOutput, calls=%fused_computation.274 | convolution fusion | flops 4866440192 | bytes 20474880 | tf_op jit(solution)/shard_map/dot_general | solution.py:551
  245.0 8.1 %multiply_reduce_fusion.2 = f32[1024]{0:T(1024)S(1)} fusion(f32[1024]{0:T(1024)S(1)} %broadcast_multiply_fusion.2, f32[1024,3072]{1,0:T(8,128)} %get-tuple-element.183, f32[3072]{0:T(1024)S(1)} %reshape.1760), kind=kLoop, calls=%fused_computation.12 | loop fusion | flops 37747712 | bytes 12603392 | tf_op jit(solution)/shard_map/reduce_sum | solution.py:73
  253.1 7.3 %reshape.1746 = bf16[8,2,1536,96]{2,1,0,3:T(2,128)(2,1)} reshape(bf16[24576,96]{0,1:T(8,128)(2,1)} %all-gather.14.cloned.1.call-done) | data formatting | bytes 9437184 | tf_op jit(solution)/shard_map/reshape | solution.py:407
  260.4 7.7 %copy.197 = bf16[8,2,1536,96]{2,1,3,0:T(2,128)(2,1)} copy(bf16[8,2,1536,96]{2,1,0,3:T(2,128)(2,1)} %reshape.1746) | data formatting | bytes 9437184 | tf_op jit(solution)/shard_map/reshape | solution.py:407
  268.1 3.6 copy.247
  271.7 22.0 %multiply_reduce_fusion = (bf16[3072]{0:T(1024)(128)(2,1)}, f32[1024]{0:T(1024)S(1)}, f32[1024]{0:T(1024)S(1)}, bf16[1024,3072]{1,0:T(8,128)(2,1)}, f32[1024,3072]{1,0:T(8,128)}) fusion(f32[1024]{0:T(1024)S(1)} %add_rsqrt_fusion, f32[1024]{0:T(1024)S(1)} %broadcast_multiply_fusion.2, f32[1024,3072]{1,0:T(8,128)} %get-tuple-element.183, ...), kind=kOutput, calls=%fused_computation.9 | convolution fusion | flops 4898679808 | bytes 37795840 | tf_op jit(solution)/shard_map/dot_general | solution.py:65
  293.7 17.2 %fusion.75 = (bf16[3072]{0:T(1024)(128)(2,1)}, bf16[1024,3072]{1,0:T(8,128)(2,1)S(1)}) fusion(f32[1024]{0:T(1024)S(1)} %broadcast_multiply_fusion, f32[1024]{0:T(1024)S(1)} %broadcast_multiply_fusion.2, f32[1024,3072]{1,0:T(8,128)} %get-tuple-element.183, f32[3072]{0:T(1024)S(1)} %reshape.1760, f32[1024]{0:T(1024)S(1)} %broadcast_multiply_fusion.1, ...), kind=kLoop, calls=%fused_computation.275 | loop fusion | flops 94368768 | bytes 31504384 | tf_op jit(solution)/shard_map/reduce_sum | solution.py:613
  310.9 8.6 %multiply_reduce_fusion.5 = (bf16[768]{0:T(1024)(128)(2,1)S(1)}, f32[1024]{0:T(1024)S(1)}, f32[1024]{0:T(1024)S(1)}, f32[1024,768]{0,1:T(8,128)}) fusion(f32[1024,768]{0,1:T(8,128)S(1)} %copy-done.33, f32[1024]{0:T(1024)S(1)} %add_rsqrt_fusion.1, f32[1024]{0:T(1024)S(1)} %broadcast_multiply_fusion.9, f32[768]{0:T(1024)S(1)} %mul.304, ...), kind=kOutput, calls=%fused_computation.55 | convolution fusion | flops 4838126592 | bytes 17322496 | tf_op jit(solution)/shard_map/dot_general | solution.py:65
  319.5 7.1 %convolution_convert_fusion = bf16[768,3072]{1,0:T(8,128)(2,1)} fusion(bf16[1024,3072]{1,0:T(8,128)(2,1)S(1)} %get-tuple-element.137, f32[1024,768]{0,1:T(8,128)S(1)} %copy-done.33, f32[768]{0:T(1024)S(1)} %mul.304, f32[1024]{0:T(1024)S(1)} %add_rsqrt_fusion.1, f32[1024]{0:T(1024)S(1)} %broadcast_multiply_fusion.9), kind=kOutput, calls=%fused_computation.16 | convolution fusion | flops 4837343232 | bytes 14167040 | tf_op jit(solution)/shard_map/dot_general | solution.py:59
  326.6 5.5 convert_reduce_fusion.2
  333.7 2.7 fusion.37
  336.4 6.5 %multiply_reduce_fusion.4 = (bf16[768]{0:T(1024)(128)(2,1)}, f32[1024]{0:T(1024)S(1)}, f32[1024]{0:T(1024)S(1)}, f32[1024,768]{1,0:T(8,128)}) fusion(f32[1024]{0:T(1024)S(1)} %add_rsqrt_fusion.2, f32[1024]{0:T(1024)S(1)} %broadcast_multiply_fusion.10, f32[1,512,768]{2,1,0:T(8,128)S(1)} %shard_map.257, f32[1,512,768]{2,1,0:T(8,128)S(1)} %shard_map.256, ...), kind=kOutput, calls=%fused_computation.53 | convolution fusion | flops 1215821056 | bytes 10637824 | tf_op jit(solution)/shard_map/dot_general | solution.py:65
  342.9 9.8 %convolution_convert_fusion.1 = bf16[768,3072]{1,0:T(8,128)(2,1)} fusion(bf16[1024,3072]{1,0:T(8,128)(2,1)} %get-tuple-element.142, bf16[512,768]{0,1:T(8,128)(2,1)} %bitcast.27, bf16[512,768]{0,1:T(8,128)(2,1)S(1)} %bitcast.173, pred[]{:T(512)S(6)} %eq.183), kind=kOutput, calls=%fused_computation.17 | convolution fusion | flops 4841275392 | bytes 12582913 | tf_op jit(solution)/shard_map/dot_general | solution.py:59
  352.7 3.7 multiply_convert_fusion.1
  371.4 49.3 %shard_map.259 = (bf16[1,512,768]{2,1,0:T(8,128)(2,1)S(1)}, f32[1,1024,768]{2,1,0:T(8,128)}, f32[1,1024,768]{2,1,0:T(8,128)}) custom-call(bf16[1,512,768]{2,1,0:T(8,128)(2,1)S(1)} %copy-done.20, bf16[1,1024,768]{2,1,0:T(8,128)(2,1)S(1)} %copy-done.13, bf16[1,1024,768]{2,1,0:T(8,128)(2,1)S(1)} %copy-done.3, ...), custom_call_target="tpu_custom_call" | custom-call | flops 8053063680 | bytes 20447232 | tf_op jit(solution)/shard_map/pallas_call | solution.py:244
  426.0 31.0 %shard_map.258 = (bf16[1,512,768]{2,1,0:T(8,128)(2,1)S(1)}, f32[1,512,768]{2,1,0:T(8,128)S(1)}, f32[1,512,768]{2,1,0:T(8,128)}) custom-call(bf16[1,512,768]{2,1,0:T(8,128)(2,1)S(1)} %copy-done.9, bf16[1,512,768]{2,1,0:T(8,128)(2,1)S(1)} %copy-done.5, bf16[1,512,768]{2,1,0:T(8,128)(2,1)S(1)} %copy-done.7, bf16[1,512,768]{2,1,0:T(8,128)(2,1)S(1)} %copy-done.21, ...), custom_call_target="tpu_custom_call" | custom-call | flops 4026531840 | bytes 11010048 | tf_op jit(solution)/shard_map/pallas_call | solution.py:244
  458.3 4.0 fusion.77
  462.6 2.3 add_convert_fusion.1
  465.3 2.8 pad_maximum_fusion
  468.4 8.3 %fusion.38 = bf16[768,3,768]{2,0,1:T(8,128)(2,1)} fusion(bf16[3,1024,768]{2,1,0:T(8,128)(2,1)} %pad_maximum_fusion, f32[768]{0:T(1024)S(1)} %copy-done.58, f32[1024]{0:T(1024)S(1)} %copy-done.56, f32[1024]{0:T(1024)S(1)} %copy-done.52, bf16[512,768]{0,1:T(8,128)(2,1)S(1)} %bitcast.160, bf16[512,768]{0,1:T(8,128)(2,1)S(1)} %bitcast.153, pred[]{:T(512)S(6)} %eq.183), kind=kOutput, calls=%fused_computation.87 | convolution fusion | flops 3634888704 | bytes 9841665 | tf_op jit(solution)/shard_map/rd,jre->dje/dot_general | solution.py:653
  476.6 8.5 %fusion.19 = (bf16[768]{0:T(1024)(128)(2,1)S(1)}, f32[1024]{0:T(1024)S(1)}, f32[1024]{0:T(1024)S(1)}, f32[1024,768,1]{0,1,2:T(8,128)}) fusion(f32[1024]{0:T(1024)S(1)} %copy-done.56, f32[1024]{0:T(1024)S(1)} %copy-done.52, bf16[512,768]{0,1:T(8,128)(2,1)S(1)} %bitcast.154, bf16[512,768]{0,1:T(8,128)(2,1)S(1)} %bitcast.161, pred[]{:T(512)S(6)} %eq.183, ...), kind=kOutput, calls=%fused_computation.38 | convolution fusion | flops 3638031616 | bytes 12997121 | tf_op jit(solution)/shard_map/jre,jde->rd/dot_general | solution.py:658
  486.3 2.3 pad_maximum_fusion.1
  491.4 10.0 %add_convert_fusion.2 = bf16[1024,768]{0,1:T(8,128)(2,1)S(1)} fusion(f32[1024,768]{0,1:T(8,128)} %copy-done.31, bf16[1024,3072]{1,0:T(8,128)(2,1)} %get-tuple-element.142, bf16[3072,768]{0,1:T(8,128)(2,1)} %bitcast.166, f32[768]{0:T(1024)S(1)} %copy-done.60), kind=kOutput, calls=%fused_computation.62 | convolution fusion | flops 4834197504 | bytes 15731712 | tf_op jit(solution)/shard_map/dot_general | solution.py:556
  506.6 16.9 %collective-permute-done.1 = bf16[1,512,768]{2,1,0:T(8,128)(2,1)} collective-permute-done((bf16[1,512,768]{2,1,0:T(8,128)(2,1)}, bf16[1,512,768]{2,1,0:T(8,128)(2,1)}, u32[]{:S(2)}, u32[]{:S(2)}) %collective-permute-start.1) | collective-permute-done | bytes 786464 | tf_op jit(solution)/shard_map/ppermute | solution.py:355
  523.5 2.9 maximum_select_fusion.3
  528.2 10.0 %collective-permute-done.3 = bf16[1,512,768]{2,1,0:T(8,128)(2,1)} collective-permute-done((bf16[1,512,768]{2,1,0:T(8,128)(2,1)}, bf16[1,512,768]{2,1,0:T(8,128)(2,1)}, u32[]{:S(2)}, u32[]{:S(2)}) %collective-permute-start.3) | collective-permute-done | bytes 786464 | tf_op jit(solution)/shard_map/ppermute | solution.py:357
  538.2 2.2 collective-permute-done.2
  558.1 16.0 %collective-permute-done.14 = bf16[96,1536]{1,0:T(8,128)(2,1)S(1)} collective-permute-done((bf16[96,1536]{1,0:T(8,128)(2,1)}, bf16[96,1536]{1,0:T(8,128)(2,1)S(1)}, u32[]{:S(2)}, u32[]{:S(2)}) %collective-permute-start.14) | collective-permute-done | bytes 294944 | tf_op jit(solution)/shard_map/ppermute | solution.py:445
  576.8 3.7 collective-permute-done.12
  583.3 11.3 %collective-permute-done.15 = bf16[96,1536]{1,0:T(8,128)(2,1)S(1)} collective-permute-done((bf16[96,1536]{1,0:T(8,128)(2,1)S(1)}, bf16[96,1536]{1,0:T(8,128)(2,1)S(1)}, u32[]{:S(2)}, u32[]{:S(2)}) %collective-permute-start.15) | collective-permute-done | bytes 294944 | tf_op jit(solution)/shard_map/ppermute | solution.py:452
  595.5 2.3 collective-permute-done.13
  610.2 2.8 collective-permute-done.9
  (351 shorter events, 120.0 us)
Async XLA Ops:
  7.2 92.7 %copy-start = (s32[4,2]{0,1:T(2,128)S(1)}, s32[4,2]{0,1:T(2,128)}, u32[]{:S(2)}) copy-start(s32[4,2]{0,1:T(2,128)} %param.21) | copy-start | bytes 100
  7.2 60.3 %all-gather.8.cloned.1.call-start = ((), (), s32[]{:S(2)}) async-start(), calls=%async_computation.4 | async-start | bytes 3829760 | tf_op jit(solution)/shard_map/all_gather | solution.py:416
  17.2 193.0 %all-gather.10.cloned.1.call-start = ((), (), s32[]{:S(2)}) async-start(), calls=%async_computation.8 | async-start | bytes 1253376 | tf_op jit(solution)/shard_map/all_gather | solution.py:406
  90.4 129.3 %all-gather.12.cloned.1.call-start = ((), (), s32[]{:S(2)}) async-start(), calls=%async_computation.9 | async-start | bytes 5013504 | tf_op jit(solution)/shard_map/all_gather | solution.py:406
  91.2 161.9 %all-gather.14.cloned.1.call-start = ((), (), s32[]{:S(2)}) async-start(), calls=%async_computation.10 | async-start | bytes 5013504 | tf_op jit(solution)/shard_map/all_gather | solution.py:406
  95.5 20.6 %collective-permute-start = (bf16[1,512,768]{1,2,0:T(8,128)(2,1)}, bf16[1,512,768]{1,2,0:T(8,128)(2,1)S(1)}, u32[]{:S(2)}, u32[]{:S(2)}) collective-permute-start(bf16[1,512,768]{1,2,0:T(8,128)(2,1)} %copy.234), channel_id=1, source_target_pairs={{0,2},{2,0},{1,3},{3,1},{4,6},{6,4},{5,7},{7,5},{8,10},{10,8},{9,1... | collective-permute-start | bytes 2359304 | tf_op jit(solution)/shard_map/ppermute | solution.py:748
  99.3 172.4 %collective-permute-start.4 = (bf16[1,512,768]{1,2,0:T(8,128)(2,1)}, bf16[1,512,768]{1,2,0:T(8,128)(2,1)}, u32[]{:S(2)}, u32[]{:S(2)}) collective-permute-start(bf16[1,512,768]{1,2,0:T(8,128)(2,1)} %copy.241), channel_id=1, source_target_pairs={{0,2},{2,0},{1,3},{3,1},{4,6},{6,4},{5,7},{7,5},{8,10},{10,8},{9,1... | collective-permute-start | bytes 2359304 | tf_op jit(solution)/shard_map/ppermute | solution.py:748
  104.5 22.8 %copy-start.28 = (bf16[1,512,768]{1,2,0:T(8,128)(2,1)}, bf16[1,512,768]{1,2,0:T(8,128)(2,1)S(1)}, u32[]{:S(2)}) copy-start(bf16[1,512,768]{1,2,0:T(8,128)(2,1)S(1)} %copy.174) | copy-start | bytes 2359300
  104.5 12.8 %copy-start.26 = (bf16[8,2,112640]{2,1,0:T(2,128)(2,1)S(1)}, bf16[8,2,112640]{2,1,0:T(2,128)(2,1)}, u32[]{:S(2)}) copy-start(bf16[8,2,112640]{2,1,0:T(2,128)(2,1)} %reshape.1736) | copy-start | bytes 10813444
  116.2 11.1 %copy-start.36 = (bf16[1,512,768]{1,2,0:T(8,128)(2,1)}, bf16[1,512,768]{1,2,0:T(8,128)(2,1)S(1)}, u32[]{:S(2)}) copy-start(bf16[1,512,768]{1,2,0:T(8,128)(2,1)S(1)} %collective-permute-done) | copy-start | bytes 2359300
  116.6 10.7 %copy-start.51 = (f32[1024]{0:T(1024)}, f32[1024]{0:T(1024)S(1)}, u32[]{:S(2)}) copy-start(f32[1024]{0:T(1024)S(1)} %broadcast_multiply_fusion.11) | copy-start | bytes 12292
  117.3 10.0 %copy-start.55 = (f32[1024]{0:T(1024)}, f32[1024]{0:T(1024)S(1)}, u32[]{:S(2)}) copy-start(f32[1024]{0:T(1024)S(1)} %add_rsqrt_fusion.3) | copy-start | bytes 12292
  117.8 9.5 %copy-start.57 = (f32[768]{0:T(1024)}, f32[768]{0:T(1024)S(1)}, u32[]{:S(2)}) copy-start(f32[768]{0:T(1024)S(1)} %mul.289) | copy-start | bytes 9220
  127.4 18.6 %copy-start.4 = (bf16[1,512,768]{2,1,0:T(8,128)(2,1)}, bf16[1,512,768]{2,1,0:T(8,128)(2,1)S(1)}, u32[]{:S(2)}) copy-start(bf16[1,512,768]{2,1,0:T(8,128)(2,1)S(1)} %slice.270.k_ref) | copy-start | bytes 2359300
  134.6 11.4 %copy-start.22 = (s32[12,8,512]{2,1,0:T(8,128)}, s32[12,8,512]{2,1,0:T(8,128)S(1)}, u32[]{:S(2)}) copy-start(s32[12,8,512]{2,1,0:T(8,128)S(1)} %slice.287.patk_ref) | copy-start | bytes 589828
  135.0 333.3 %reduce-scatter.7.cloned.1.call-start = ((), (), s32[]{:S(2)}) async-start(), calls=%async_computation.5 | async-start | bytes 5308416 | tf_op jit(solution)/shard_map/reduce_scatter | solution.py:515
  145.8 28.8 %copy-start.2 = (bf16[1,1024,768]{2,1,0:T(8,128)(2,1)}, bf16[1,1024,768]{2,1,0:T(8,128)(2,1)S(1)}, u32[]{:S(2)}) copy-start(bf16[1,1024,768]{2,1,0:T(8,128)(2,1)S(1)} %get-tuple-element.143.v_ref) | copy-start | bytes 4718596
  145.9 28.7 %copy-start.6 = (bf16[1,512,768]{2,1,0:T(8,128)(2,1)}, bf16[1,512,768]{2,1,0:T(8,128)(2,1)S(1)}, u32[]{:S(2)}) copy-start(bf16[1,512,768]{2,1,0:T(8,128)(2,1)S(1)} %slice.273.v_ref) | copy-start | bytes 2359300
  146.0 28.6 %copy-start.8 = (bf16[1,512,768]{2,1,0:T(8,128)(2,1)}, bf16[1,512,768]{2,1,0:T(8,128)(2,1)S(1)}, u32[]{:S(2)}) copy-start(bf16[1,512,768]{2,1,0:T(8,128)(2,1)S(1)} %get-tuple-element.160.q_ref) | copy-start | bytes 2359300
  146.0 28.6 %copy-start.19 = (bf16[1,512,768]{2,1,0:T(8,128)(2,1)}, bf16[1,512,768]{2,1,0:T(8,128)(2,1)S(1)}, u32[]{:S(2)}) copy-start(bf16[1,512,768]{2,1,0:T(8,128)(2,1)S(1)} %get-tuple-element.161.q_ref) | copy-start | bytes 2359300
  146.1 28.6 %copy-start.12 = (bf16[1,1024,768]{2,1,0:T(8,128)(2,1)S(1)}, bf16[1,1024,768]{2,1,0:T(8,128)(2,1)}, u32[]{:S(2)}) copy-start(bf16[1,1024,768]{2,1,0:T(8,128)(2,1)} %slice.289.k_ref) | copy-start | bytes 4718596
  146.1 28.6 %copy-start.17 = (s32[12,8,1024]{2,1,0:T(8,128)S(1)}, s32[12,8,1024]{2,1,0:T(8,128)}, u32[]{:S(2)}) copy-start(s32[12,8,1024]{2,1,0:T(8,128)} %copy-done.16) | copy-start | bytes 1179652
  146.1 28.6 %copy-start.24 = (s32[1,512,8]{2,1,0:T(8,128)S(1)}, s32[1,512,8]{2,1,0:T(8,128)}, u32[]{:S(2)}) copy-start(s32[1,512,8]{2,1,0:T(8,128)} %get-tuple-element.167.pcq_ref) | copy-start | bytes 49156
  232.8 12.2 %copy-start.43 = (bf16[96,8,2,1536]{3,1,2,0:T(8,128)(2,1)}, bf16[96,8,2,1536]{3,1,2,0:T(8,128)(2,1)S(1)}, u32[]{:S(2)}) copy-start(bf16[96,8,2,1536]{3,1,2,0:T(8,128)(2,1)S(1)} %copy.246) | copy-start | bytes 14155780
  271.7 22.0 %copy-start.42 = (bf16[96,8,2,1536]{3,1,2,0:T(8,128)(2,1)}, bf16[96,8,2,1536]{3,1,2,0:T(8,128)(2,1)S(1)}, u32[]{:S(2)}) copy-start(bf16[96,8,2,1536]{3,1,2,0:T(8,128)(2,1)S(1)} %copy.247) | copy-start | bytes 14155780
  293.7 17.2 %copy-start.33 = (f32[1024,768]{0,1:T(8,128)S(1)}, f32[1024,768]{0,1:T(8,128)}, u32[]{:S(2)}) copy-start(f32[1024,768]{0,1:T(8,128)} %copy-done.31) | copy-start | bytes 9437188
  356.5 111.8 %reduce-scatter.9.cloned.1.call-start = ((), (), s32[]{:S(2)}) async-start(), calls=%async_computation.6 | async-start | bytes 5308416 | tf_op jit(solution)/shard_map/reduce_scatter | solution.py:515
  357.0 9.8 %copy-start.3 = (bf16[1,1024,768]{2,1,0:T(8,128)(2,1)S(1)}, bf16[1,1024,768]{2,1,0:T(8,128)(2,1)}, u32[]{:S(2)}) copy-start(bf16[1,1024,768]{2,1,0:T(8,128)(2,1)} %copy-done.2) | copy-start | bytes 4718596
  357.1 169.3 %reduce-scatter.11.cloned.1.call-start = ((), (), s32[]{:S(2)}) async-start(), calls=%async_computation.7 | async-start | bytes 1327104 | tf_op jit(solution)/shard_map/reduce_scatter | solution.py:515
  371.4 51.5 %copy-start.5 = (bf16[1,512,768]{2,1,0:T(8,128)(2,1)S(1)}, bf16[1,512,768]{2,1,0:T(8,128)(2,1)}, u32[]{:S(2)}) copy-start(bf16[1,512,768]{2,1,0:T(8,128)(2,1)} %copy-done.4) | copy-start | bytes 2359300
  371.4 51.5 %copy-start.7 = (bf16[1,512,768]{2,1,0:T(8,128)(2,1)S(1)}, bf16[1,512,768]{2,1,0:T(8,128)(2,1)}, u32[]{:S(2)}) copy-start(bf16[1,512,768]{2,1,0:T(8,128)(2,1)} %copy-done.6) | copy-start | bytes 2359300
  462.5 136.1 %reduce-scatter.13.cloned.1.call-start = ((), (), s32[]{:S(2)}) async-start(), calls=%async_computation.11 | async-start | bytes 4313088
  502.8 20.7 %collective-permute-start.1 = (bf16[1,512,768]{2,1,0:T(8,128)(2,1)}, bf16[1,512,768]{2,1,0:T(8,128)(2,1)}, u32[]{:S(2)}, u32[]{:S(2)}) collective-permute-start(bf16[1,512,768]{2,1,0:T(8,128)(2,1)} %bitcast.183), channel_id=1, source_target_pairs={{0,2},{2,0},{1,3},{3,1},{4,6},{6,4},{5,7},{7,5},{8,10},{10,8},{9,1... | collective-permute-start | bytes 2359304 | tf_op jit(solution)/shard_map/ppermute | solution.py:355
  504.2 33.9 %collective-permute-start.3 = (bf16[1,512,768]{2,1,0:T(8,128)(2,1)}, bf16[1,512,768]{2,1,0:T(8,128)(2,1)}, u32[]{:S(2)}, u32[]{:S(2)}) collective-permute-start(bf16[1,512,768]{2,1,0:T(8,128)(2,1)} %bitcast.184), channel_id=1, source_target_pairs={{0,3},{3,0},{1,2},{2,1},{4,7},{7,4},{5,6},{6,5},{8,11},{11,8},{9,1... | collective-permute-start | bytes 2359304 | tf_op jit(solution)/shard_map/ppermute | solution.py:357
  505.3 35.1 %collective-permute-start.2 = (bf16[1,512,768]{2,1,0:T(8,128)(2,1)S(1)}, bf16[1,512,768]{2,1,0:T(8,128)(2,1)S(1)}, u32[]{:S(2)}, u32[]{:S(2)}) collective-permute-start(bf16[1,512,768]{2,1,0:T(8,128)(2,1)S(1)} %bitcast.176), channel_id=1, source_target_pairs={{0,1},{1,0},{2,3},{3,2},{4,5},{5,4},{6,7},{7,6},{8,9},{9,8},{10,11... | collective-permute-start | bytes 2359304 | tf_op jit(solution)/shard_map/ppermute | solution.py:356
  526.4 15.7 %copy-start.50 = (bf16[96,768]{1,0:T(8,128)(2,1)S(1)}, bf16[96,768]{1,0:T(8,128)(2,1)}, u32[]{:S(2)}) copy-start(bf16[96,768]{1,0:T(8,128)(2,1)} %reduce-scatter.11.cloned.1.call-done) | copy-start | bytes 442372
  526.4 17.3 %copy-start.41 = (bf16[2,512,768]{2,1,0:T(8,128)(2,1)S(1)}, bf16[2,512,768]{2,1,0:T(8,128)(2,1)}, u32[]{:S(2)}) copy-start(bf16[2,512,768]{2,1,0:T(8,128)(2,1)} %maximum_select_fusion.3) | copy-start | bytes 4718596
  527.4 14.7 %collective-permute-start.10 = (bf16[96,384]{1,0:T(8,128)(2,1)S(1)}, bf16[96,384]{1,0:T(8,128)(2,1)S(1)}, u32[]{:S(2)}, u32[]{:S(2)}) collective-permute-start(bf16[96,384]{1,0:T(8,128)(2,1)S(1)} %constant_dynamic-slice_fusion.2), channel_id=1, source_target_pairs={{0,1},{1,0},{2,3},{3,2},{4,5},{5,4},{6,7},{7,6},{8,9},{9,8},{10,11... | collective-permute-start | bytes 221192 | tf_op jit(solution)/shard_map/ppermute | solution.py:445
  542.2 4.4 collective-permute-start.11
  548.0 26.1 %collective-permute-start.14 = (bf16[96,1536]{1,0:T(8,128)(2,1)}, bf16[96,1536]{1,0:T(8,128)(2,1)S(1)}, u32[]{:S(2)}, u32[]{:S(2)}) collective-permute-start(bf16[96,1536]{1,0:T(8,128)(2,1)} %constant_dynamic-slice_fusion), channel_id=1, source_target_pairs={{0,1},{1,0},{2,3},{3,2},{4,5},{5,4},{6,7},{7,6},{8,9},{9,8},{10,11... | collective-permute-start | bytes 884744 | tf_op jit(solution)/shard_map/ppermute | solution.py:445
  552.3 51.7 %collective-permute-start.7 = (bf16[1,512,768]{2,1,0:T(8,128)(2,1)S(1)}, bf16[1,512,768]{2,1,0:T(8,128)(2,1)S(1)}, u32[]{:S(2)}, u32[]{:S(2)}) collective-permute-start(bf16[1,512,768]{2,1,0:T(8,128)(2,1)S(1)} %bitcast.181), channel_id=1, source_target_pairs={{0,3},{3,0},{1,2},{2,1},{4,7},{7,4},{5,6},{6,5},{8,11},{11,8},{9,1... | collective-permute-start | bytes 2359304 | tf_op jit(solution)/shard_map/ppermute | solution.py:357
  553.5 48.9 %collective-permute-start.5 = (bf16[1,512,768]{2,1,0:T(8,128)(2,1)S(1)}, bf16[1,512,768]{2,1,0:T(8,128)(2,1)}, u32[]{:S(2)}, u32[]{:S(2)}) collective-permute-start(bf16[1,512,768]{2,1,0:T(8,128)(2,1)S(1)} %bitcast.182), channel_id=1, source_target_pairs={{0,2},{2,0},{1,3},{3,1},{4,6},{6,4},{5,7},{7,5},{8,10},{10,8},{9,1... | collective-permute-start | bytes 2359304 | tf_op jit(solution)/shard_map/ppermute | solution.py:355
  555.8 24.8 %collective-permute-start.12 = (bf16[96,1536]{1,0:T(8,128)(2,1)}, bf16[96,1536]{1,0:T(8,128)(2,1)}, u32[]{:S(2)}, u32[]{:S(2)}) collective-permute-start(bf16[96,1536]{1,0:T(8,128)(2,1)} %constant_dynamic-slice_fusion.1), channel_id=1, source_target_pairs={{0,1},{1,0},{2,3},{3,2},{4,5},{5,4},{6,7},{7,6},{8,9},{9,8},{10,11... | collective-permute-start | bytes 884744 | tf_op jit(solution)/shard_map/ppermute | solution.py:445
  557.8 46.2 %collective-permute-start.6 = (bf16[1,512,768]{2,1,0:T(8,128)(2,1)S(1)}, bf16[1,512,768]{2,1,0:T(8,128)(2,1)}, u32[]{:S(2)}, u32[]{:S(2)}) collective-permute-start(bf16[1,512,768]{2,1,0:T(8,128)(2,1)S(1)} %bitcast.174), channel_id=1, source_target_pairs={{0,1},{1,0},{2,3},{3,2},{4,5},{5,4},{6,7},{7,6},{8,9},{9,8},{10,11... | collective-permute-start | bytes 2359304 | tf_op jit(solution)/shard_map/ppermute | solution.py:356
  575.1 19.5 %collective-permute-start.15 = (bf16[96,1536]{1,0:T(8,128)(2,1)S(1)}, bf16[96,1536]{1,0:T(8,128)(2,1)S(1)}, u32[]{:S(2)}, u32[]{:S(2)}) collective-permute-start(bf16[96,1536]{1,0:T(8,128)(2,1)S(1)} %add_convert_fusion.3), channel_id=1, source_target_pairs={{0,2},{2,0},{1,3},{3,1},{4,6},{6,4},{5,7},{7,5},{8,10},{10,8},{9,1... | collective-permute-start | bytes 884744 | tf_op jit(solution)/shard_map/ppermute | solution.py:452
  581.7 16.1 %collective-permute-start.13 = (bf16[96,1536]{1,0:T(8,128)(2,1)S(1)}, bf16[96,1536]{1,0:T(8,128)(2,1)S(1)}, u32[]{:S(2)}, u32[]{:S(2)}) collective-permute-start(bf16[96,1536]{1,0:T(8,128)(2,1)S(1)} %add_convert_fusion.4), channel_id=1, source_target_pairs={{0,2},{2,0},{1,3},{3,1},{4,6},{6,4},{5,7},{7,5},{8,10},{10,8},{9,1... | collective-permute-start | bytes 884744 | tf_op jit(solution)/shard_map/ppermute | solution.py:452
  600.6 6.2 collective-permute-start.8
  606.8 6.2 collective-permute-start.9
  (39 other events, 146.2 us)
Sparse Core Ops, SparseCore 0:
  17.3 50.1 all-gather.7
  90.6 35.6 all-gather.9
  128.6 52.5 all-gather.11
  183.4 51.6 all-gather.13
  356.6 53.7 reduce-scatter.6
  412.5 53.3 reduce-scatter.8
  468.1 31.3 reduce-scatter.10
  501.9 45.0 reduce-scatter.12

commit v8 on v7

--- a/solution.py
+++ b/solution.py
@@ -628,9 +628,18 @@
             attended_low,
         )
     )
-    down_share = shard_stage(down_grad, 0)
-    up_share = shard_stage(up_grad, 0)
-    out_share = shard_stage(out_weight_grad, 0)
+    tensor_count = lax.axis_size("tensor")
+    early_widths = (down_grad.shape[1], up_grad.shape[1], out_weight_grad.shape[1])
+    early_share = shard_stage(
+        jnp.concatenate(
+            [
+                part.reshape(part.shape[0], tensor_count, part.shape[1] // tensor_count)
+                for part in (down_grad, up_grad, out_weight_grad)
+            ],
+            2,
+        ),
+        0,
+    )
     query_grad, key_part, value_part = split_attention_backward(
         query_matrix.reshape(seq_count, local_len, model_width),
         key_all,
@@ -649,7 +658,7 @@
     key_low = key_part.astype(jnp.bfloat16).reshape(row_count, model_width)
     value_low = value_part.astype(jnp.bfloat16).reshape(row_count, model_width)
     stacked = jnp.stack([query_low, key_low, value_low])
-    down_share, up_share, stacked = lax.optimization_barrier((down_share, up_share, stacked))
+    early_share, stacked = lax.optimization_barrier((early_share, stacked))
     qkv_grad = jnp.einsum("rd,jre->dje", attn_in, stacked, preferred_element_type=jnp.float32)
     head_bias_grad = jnp.stack(
         [jnp.sum(query_low, 0, dtype=jnp.float32), jnp.sum(value_low, 0, dtype=jnp.float32)]
@@ -703,10 +712,13 @@
             count *= size
         small_pieces.append(small_total[offset : offset + count].reshape(local_shape))
         offset += count
+    early_total = finish_stage(early_share, 1).reshape(early_share.shape[0], -1)
+    down_width = early_widths[0] // nt
+    up_width = early_widths[1] // nt
     grad_shares = (
-        finish_stage(down_share, 1).transpose(1, 0),
-        finish_stage(up_share, 1),
-        finish_stage(out_share, 1).transpose(1, 0),
+        early_total[:, :down_width].transpose(1, 0),
+        early_total[:, down_width : down_width + up_width],
+        early_total[:, down_width + up_width :].transpose(1, 0),
         qkv_total[:block_rows].transpose(1, 0, 2),
     ) + tuple(small_pieces)
     return (grad_shares, input_low.reshape(seq_count, local_len, model_width))

time: 631 us -> 614 us (0.973)
  matrix products: 107 us -> 94.7 us
    ppermute x4 -> x2, waiting for transfers between devices: 17.4 us -> 2.93 us  [pair_sum(): received = lax.ppermute(share, axis_name, perm=[(0, 1), (1, 0)])]
    ppermute x4 -> x2, waiting for transfers between devices: 20.8 us -> 31.4 us  [pair_reduce(): received = lax.ppermute(sent, axis_name, perm=[(0, 1), (1, 0)])]
    unnamed x138 -> x142, local copies, waits for them, and re-layouts: 39.1 us -> 38 us
  transfers between devices with their start and end apart: 24 -> 18, of which waited for: 12 -> 10; matrix products, arithmetic and copies ran while one was open for 29% -> 25% of each run, Pallas kernels for 23% -> 24%
where the time goes in v8:
time: 614 us; the launch traced here: 608 us
  Pallas kernels  144 us (23%)
  waiting for transfers between devices  133 us (22%)
  local copies, waits for them, and re-layouts  128 us (21%)
  matrix products  94.7 us (15%)
  other arithmetic  77.4 us (13%)
  between operations  17.1 us (3%)
  starting transfers between devices  15.4 us (3%)
    pallas_call x2, Pallas kernels, attention_backward(): pl.pallas_call(attention_bwd_kernel, grid=grid, in_specs=[query_spec, key...  80.2 us
    pallas_call x2, Pallas kernels, attention_forward(): pl.pallas_call(attention_fwd_kernel, grid=grid, in_specs=[query_spec, key...  63.3 us
    all_gather x1, waiting for transfers between devices, gather_packed(): lax.all_gather(flat, ('shard', 'tensor'), axis=0, tiled=False)  50.3 us
    unnamed x142, local copies, waits for them, and re-layouts  38 us
    dot_general x3, matrix products, back_dot(): lax.dot_general(left_rows, weight_rows, (((1,), (1,)), ((), ())), preferr...  32.8 us
    ppermute x2, waiting for transfers between devices, pair_reduce(): received = lax.ppermute(sent, axis_name, perm=[(0, 1), (1, 0)])  31.4 us
    reshape x5, local copies, waits for them, and re-layouts, gather_weight(): stacked.reshape((ns, nt) + local_block.shape)  29.6 us
    ppermute x2, waiting for transfers between devices, spread_sequence(): from_context = lax.ppermute(other, 'context', perm=swap)  22.1 us
  transfers between devices with their start and end apart: 18, of which 10 were waited for; matrix products, arithmetic and copies ran while one was open for 25% of the time, Pallas kernels for 24%

profile of v8, /device:TPU:0, one launch (start us, length us, event | category | flops | bytes accessed | tf_op | source)
XLA Modules:
  0.0 608.2 jit_solution(13665033093138567905)
XLA Ops:
  16.4 50.3 %all-gather.8.cloned.1.call-done = bf16[16,880,128]{2,1,0:T(8,128)(2,1)} async-done(((bf16[1,880,128]{2,1,0:T(8,128)(2,1)}), bf16[16,880,128]{2,1,0:T(8,128)(2,1)}) %all-gather.8.cloned.1.call-update) | async-done | bytes 3604496 | tf_op jit(solution)/shard_map/all_gather | solution.py:416
  66.7 6.6 %reshape.1748 = bf16[8,2,112640]{2,1,0:T(2,128)(2,1)} reshape(bf16[16,880,128]{2,1,0:T(8,128)(2,1)} %all-gather.8.cloned.1.call-done) | data formatting | bytes 7208960 | tf_op jit(solution)/shard_map/reshape | solution.py:416
  75.4 4.7 reshape.1791
  80.1 5.5 copy.192
  85.6 4.0 reshape.1750
  90.6 2.9 constant_dynamic-slice_fusion.6
  96.2 2.3 copy.256
  106.6 8.7 %collective-permute-done = bf16[1,512,768]{1,2,0:T(8,128)(2,1)S(1)} collective-permute-done((bf16[1,512,768]{1,2,0:T(8,128)(2,1)}, bf16[1,512,768]{1,2,0:T(8,128)(2,1)S(1)}, u32[]{:S(2)}, u32[]{:S(2)}) %collective-permute-start) | collective-permute-done | bytes 786464 | tf_op jit(solution)/shard_map/ppermute | solution.py:760
  116.9 9.5 %fusion.86 = (bf16[3,1024,768]{2,1,0:T(8,128)(2,1)S(1)}, f32[3,1024,768]{2,1,0:T(8,128)}) fusion(bf16[3,768,768]{2,1,0:T(8,128)(2,1)} %reshape.1750, f32[768]{0:T(1024)S(1)} %mul.279, f32[1024]{0:T(1024)S(1)} %add_rsqrt_fusion.3, f32[1024]{0:T(1024)S(1)} %broadcast_multiply_fusion.11, bf16[512,768]{0,1:T(8,128)(2,1)S(1)} %bitcast.167, ...), kind=kOutput, calls=%fused_computation.285 | convolution fusion | flops 3637248000 | bytes 19278848 | tf_op jit(solution)/shard_map/rd,jde->jre/dot_general | solution.py:530
  138.0 2.2 copy.251.patq_ref
  142.3 3.4 fusion.21
  146.0 28.5 %shard_map.256 = f32[1,512,768]{2,1,0:T(8,128)S(1)} custom-call(bf16[1,512,768]{2,1,0:T(8,128)(2,1)S(1)} %get-tuple-element.158.q_ref, bf16[1,512,768]{2,1,0:T(8,128)(2,1)S(1)} %slice.282.k_ref, bf16[1,512,768]{2,1,0:T(8,128)(2,1)S(1)} %slice.285.v_ref, s32[12,512,8]{2,1,0:T(8,128)} %copy.251.patq_ref, s32[12,8,512]{2,1,0:T(8,128)S(1)} %slice.299.patk_ref, ...), custom_call_target="tpu_custom_call" | custom-call | flops 1610612736 | bytes 5505024 | tf_op jit(solution)/shard_map/pallas_call | solution.py:217
  174.5 34.8 %shard_map.257 = f32[1,512,768]{2,1,0:T(8,128)S(1)} custom-call(bf16[1,512,768]{2,1,0:T(8,128)(2,1)S(1)} %get-tuple-element.159.q_ref, bf16[1,1024,768]{2,1,0:T(8,128)(2,1)S(1)} %copy-done.12, bf16[1,1024,768]{2,1,0:T(8,128)(2,1)S(1)} %get-tuple-element.141.v_ref, s32[12,512,8]{2,1,0:T(8,128)} %copy.252.patq_ref, s32[12,8,1024]{2,1,0:T(8,128)S(1)} %copy-done.17, ...), custom_call_target="tpu_custom_call" | custom-call | flops 3221225472 | bytes 8650752 | tf_op jit(solution)/shard_map/pallas_call | solution.py:217
  210.1 3.1 reshape.1753
  213.3 2.2 copy.203
  219.6 9.4 %copy.204 = bf16[8,2,96,1536]{3,1,2,0:T(2,128)(2,1)} copy(bf16[8,2,96,1536]{3,2,1,0:T(8,128)(2,1)} %bitcast.180) | data formatting | bytes 9437184 | tf_op jit(solution)/shard_map/reshape | solution.py:407
  228.9 3.7 copy.264
  232.7 12.2 %fusion.74 = (f32[1024]{0:T(1024)S(1)}, f32[1024,3072]{1,0:T(8,128)}) fusion(f32[3072]{0:T(1024)S(1)} %reshape.1776, bf16[768,3072]{1,0:T(8,128)(2,1)S(1)} %bitcast.183, f32[1024,768]{0,1:T(8,128)S(1)} %copy-done.32, f32[768]{0:T(1024)S(1)} %mul.294, f32[1024]{0:T(1024)S(1)} %add_rsqrt_fusion.1, f32[1024]{0:T(1024)S(1)} %broadcast_multiply_fusion.9), kind=kOutput, calls=%fused_computation.274 | convolution fusion | flops 4866440192 | bytes 20474880 | tf_op jit(solution)/shard_map/dot_general | solution.py:551
  244.9 8.1 %multiply_reduce_fusion.2 = f32[1024]{0:T(1024)S(1)} fusion(f32[1024]{0:T(1024)S(1)} %broadcast_multiply_fusion.2, f32[1024,3072]{1,0:T(8,128)} %get-tuple-element.183, f32[3072]{0:T(1024)S(1)} %reshape.1776), kind=kLoop, calls=%fused_computation.12 | loop fusion | flops 37747712 | bytes 12603392 | tf_op jit(solution)/shard_map/reduce_sum | solution.py:73
  253.0 7.3 %reshape.1758 = bf16[8,2,1536,96]{2,1,0,3:T(2,128)(2,1)} reshape(bf16[24576,96]{0,1:T(8,128)(2,1)} %all-gather.14.cloned.1.call-done) | data formatting | bytes 9437184 | tf_op jit(solution)/shard_map/reshape | solution.py:407
  260.3 7.7 %copy.209 = bf16[8,2,1536,96]{2,1,3,0:T(2,128)(2,1)} copy(bf16[8,2,1536,96]{2,1,0,3:T(2,128)(2,1)} %reshape.1758) | data formatting | bytes 9437184 | tf_op jit(solution)/shard_map/reshape | solution.py:407
  268.0 3.6 copy.265
  271.6 22.0 %multiply_reduce_fusion = (bf16[3072]{0:T(1024)(128)(2,1)}, f32[1024]{0:T(1024)S(1)}, f32[1024]{0:T(1024)S(1)}, bf16[1024,3072]{1,0:T(8,128)(2,1)}, f32[1024,3072]{1,0:T(8,128)}) fusion(f32[1024]{0:T(1024)S(1)} %add_rsqrt_fusion, f32[1024]{0:T(1024)S(1)} %broadcast_multiply_fusion.2, f32[1024,3072]{1,0:T(8,128)} %get-tuple-element.183, ...), kind=kOutput, calls=%fused_computation.9 | convolution fusion | flops 4898679808 | bytes 37795840 | tf_op jit(solution)/shard_map/dot_general | solution.py:65
  293.6 17.2 %fusion.75 = (bf16[3072]{0:T(1024)(128)(2,1)}, bf16[1024,3072]{1,0:T(8,128)(2,1)S(1)}) fusion(f32[1024]{0:T(1024)S(1)} %broadcast_multiply_fusion, f32[1024]{0:T(1024)S(1)} %broadcast_multiply_fusion.2, f32[1024,3072]{1,0:T(8,128)} %get-tuple-element.183, f32[3072]{0:T(1024)S(1)} %reshape.1776, f32[1024]{0:T(1024)S(1)} %broadcast_multiply_fusion.1, ...), kind=kLoop, calls=%fused_computation.275 | loop fusion | flops 94368768 | bytes 31504384 | tf_op jit(solution)/shard_map/reduce_sum | solution.py:613
  310.8 8.0 %multiply_reduce_fusion.5 = (bf16[768]{0:T(1024)(128)(2,1)S(1)}, f32[1024]{0:T(1024)S(1)}, f32[1024]{0:T(1024)S(1)}, f32[1024,768]{0,1:T(8,128)S(1)}) fusion(f32[1024,768]{0,1:T(8,128)S(1)} %copy-done.33, f32[1024]{0:T(1024)S(1)} %add_rsqrt_fusion.1, f32[1024]{0:T(1024)S(1)} %broadcast_multiply_fusion.9, f32[768]{0:T(1024)S(1)} %mul.294, ...), kind=kOutput, calls=%fused_computation.58 | convolution fusion | flops 4838126592 | bytes 17322496 | tf_op jit(solution)/shard_map/dot_general | solution.py:65
  318.8 5.4 convolution_convert_fusion
  324.3 3.5 convert_reduce_fusion.2
  330.0 2.8 multiply_reduce_fusion.4
  332.7 6.8 %convolution_convert_fusion.1 = bf16[768,3072]{1,0:T(8,128)(2,1)S(1)} fusion(bf16[1024,3072]{1,0:T(8,128)(2,1)S(1)} %bitcast.213, bf16[512,768]{0,1:T(8,128)(2,1)} %bitcast.27, bf16[512,768]{0,1:T(8,128)(2,1)S(1)} %bitcast.192, pred[]{:T(512)S(6)} %eq.183), kind=kOutput, calls=%fused_computation.18 | convolution fusion | flops 4841275392 | bytes 12582913 | tf_op jit(solution)/shard_map/dot_general | solution.py:59
  339.6 2.5 multiply_convert_fusion.1
  342.9 4.7 pad_maximum_fusion
  361.2 49.3 %shard_map.259 = (bf16[1,512,768]{2,1,0:T(8,128)(2,1)S(1)}, f32[1,1024,768]{2,1,0:T(8,128)}, f32[1,1024,768]{2,1,0:T(8,128)}) custom-call(bf16[1,512,768]{2,1,0:T(8,128)(2,1)S(1)} %copy-done.20, bf16[1,1024,768]{2,1,0:T(8,128)(2,1)S(1)} %copy-done.13, bf16[1,1024,768]{2,1,0:T(8,128)(2,1)S(1)} %copy-done.3, ...), custom_call_target="tpu_custom_call" | custom-call | flops 8053063680 | bytes 20447232 | tf_op jit(solution)/shard_map/pallas_call | solution.py:244
  415.9 31.0 %shard_map.258 = (bf16[1,512,768]{2,1,0:T(8,128)(2,1)S(1)}, f32[1,512,768]{2,1,0:T(8,128)S(1)}, f32[1,512,768]{2,1,0:T(8,128)}) custom-call(bf16[1,512,768]{2,1,0:T(8,128)(2,1)S(1)} %copy-done.9, bf16[1,512,768]{2,1,0:T(8,128)(2,1)S(1)} %copy-done.5, bf16[1,512,768]{2,1,0:T(8,128)(2,1)S(1)} %copy-done.7, bf16[1,512,768]{2,1,0:T(8,128)(2,1)S(1)} %copy-done.21, ...), custom_call_target="tpu_custom_call" | custom-call | flops 4026531840 | bytes 11010048 | tf_op jit(solution)/shard_map/pallas_call | solution.py:244
  448.2 4.1 fusion.77
  452.6 2.3 add_convert_fusion.1
  455.3 2.5 pad_maximum_fusion.1
  457.9 8.5 %fusion.38 = bf16[768,3,768]{2,0,1:T(8,128)(2,1)} fusion(bf16[3,1024,768]{2,1,0:T(8,128)(2,1)} %pad_maximum_fusion.1, f32[768]{0:T(1024)S(1)} %copy-done.58, f32[1024]{0:T(1024)S(1)} %copy-done.56, f32[1024]{0:T(1024)S(1)} %copy-done.52, bf16[512,768]{0,1:T(8,128)(2,1)S(1)} %bitcast.176, bf16[512,768]{0,1:T(8,128)(2,1)S(1)} %bitcast.169, pred[]{:T(512)S(6)} %eq.183), kind=kOutput, calls=%fused_computation.93 | convolution fusion | flops 3634888704 | bytes 9841665 | tf_op jit(solution)/shard_map/rd,jre->dje/dot_general | solution.py:662
  466.4 6.1 %fusion.19 = (bf16[768]{0:T(1024)(128)(2,1)S(1)}, f32[1024]{0:T(1024)S(1)}, f32[1024]{0:T(1024)S(1)}, f32[1024,768,1]{0,1,2:T(8,128)}) fusion(f32[1024]{0:T(1024)S(1)} %copy-done.56, f32[1024]{0:T(1024)S(1)} %copy-done.52, bf16[512,768]{0,1:T(8,128)(2,1)S(1)} %bitcast.170, bf16[512,768]{0,1:T(8,128)(2,1)S(1)} %bitcast.177, pred[]{:T(512)S(6)} %eq.183, ...), kind=kOutput, calls=%fused_computation.41 | convolution fusion | flops 3638031616 | bytes 12997121 | tf_op jit(solution)/shard_map/jre,jde->rd/dot_general | solution.py:667
  473.7 2.3 pad_maximum_fusion.2
  478.8 10.3 %add_convert_fusion.2 = bf16[1024,768]{0,1:T(8,128)(2,1)S(1)} fusion(f32[1024,768]{0,1:T(8,128)} %copy-done.31, bf16[1024,3072]{1,0:T(8,128)(2,1)} %get-tuple-element.140, bf16[3072,768]{0,1:T(8,128)(2,1)} %bitcast.182, f32[768]{0:T(1024)S(1)} %add.734), kind=kOutput, calls=%fused_computation.65 | convolution fusion | flops 4834197504 | bytes 15731712 | tf_op jit(solution)/shard_map/dot_general | solution.py:556
  494.3 16.9 %collective-permute-done.1 = bf16[1,512,768]{2,1,0:T(8,128)(2,1)} collective-permute-done((bf16[1,512,768]{2,1,0:T(8,128)(2,1)}, bf16[1,512,768]{2,1,0:T(8,128)(2,1)}, u32[]{:S(2)}, u32[]{:S(2)}) %collective-permute-start.1) | collective-permute-done | bytes 786464 | tf_op jit(solution)/shard_map/ppermute | solution.py:355
  512.9 12.6 %collective-permute-done.3 = bf16[1,512,768]{2,1,0:T(8,128)(2,1)} collective-permute-done((bf16[1,512,768]{2,1,0:T(8,128)(2,1)}, bf16[1,512,768]{2,1,0:T(8,128)(2,1)}, u32[]{:S(2)}, u32[]{:S(2)}) %collective-permute-start.3) | collective-permute-done | bytes 786464 | tf_op jit(solution)/shard_map/ppermute | solution.py:357
  536.0 2.3 collective-permute-start.7
  539.8 26.6 %collective-permute-done.10 = bf16[96,1,3456]{2,0,1:T(8,128)(2,1)} collective-permute-done((bf16[96,1,3456]{2,0,1:T(8,128)(2,1)}, bf16[96,1,3456]{2,0,1:T(8,128)(2,1)}, u32[]{:S(2)}, u32[]{:S(2)}) %collective-permute-start.10) | collective-permute-done | bytes 663584 | tf_op jit(solution)/shard_map/ppermute | solution.py:445
  569.2 5.2 collective-permute-done.5
  576.1 2.3 collective-permute-done.6
  585.3 4.8 collective-permute-done.8
  593.4 2.9 collective-permute-done.9
  (344 shorter events, 107.8 us)
Async XLA Ops:
  7.2 91.9 %copy-start = (s32[4,2]{0,1:T(2,128)S(1)}, s32[4,2]{0,1:T(2,128)}, u32[]{:S(2)}) copy-start(s32[4,2]{0,1:T(2,128)} %param.21) | copy-start | bytes 100
  7.2 59.5 %all-gather.8.cloned.1.call-start = ((), (), s32[]{:S(2)}) async-start(), calls=%async_computation.2 | async-start | bytes 3829760 | tf_op jit(solution)/shard_map/all_gather | solution.py:416
  16.4 193.7 %all-gather.10.cloned.1.call-start = ((), (), s32[]{:S(2)}) async-start(), calls=%async_computation.4 | async-start | bytes 1253376 | tf_op jit(solution)/shard_map/all_gather | solution.py:406
  89.6 129.9 %all-gather.12.cloned.1.call-start = ((), (), s32[]{:S(2)}) async-start(), calls=%async_computation.5 | async-start | bytes 5013504 | tf_op jit(solution)/shard_map/all_gather | solution.py:406
  90.4 162.6 %all-gather.14.cloned.1.call-start = ((), (), s32[]{:S(2)}) async-start(), calls=%async_computation.6 | async-start | bytes 5013504 | tf_op jit(solution)/shard_map/all_gather | solution.py:406
  94.7 20.6 %collective-permute-start = (bf16[1,512,768]{1,2,0:T(8,128)(2,1)}, bf16[1,512,768]{1,2,0:T(8,128)(2,1)S(1)}, u32[]{:S(2)}, u32[]{:S(2)}) collective-permute-start(bf16[1,512,768]{1,2,0:T(8,128)(2,1)} %copy.249), channel_id=1, source_target_pairs={{0,2},{2,0},{1,3},{3,1},{4,6},{6,4},{5,7},{7,5},{8,10},{10,8},{9,1... | collective-permute-start | bytes 2359304 | tf_op jit(solution)/shard_map/ppermute | solution.py:760
  98.5 173.1 %collective-permute-start.4 = (bf16[1,512,768]{1,2,0:T(8,128)(2,1)}, bf16[1,512,768]{1,2,0:T(8,128)(2,1)}, u32[]{:S(2)}, u32[]{:S(2)}) collective-permute-start(bf16[1,512,768]{1,2,0:T(8,128)(2,1)} %copy.256), channel_id=1, source_target_pairs={{0,2},{2,0},{1,3},{3,1},{4,6},{6,4},{5,7},{7,5},{8,10},{10,8},{9,1... | collective-permute-start | bytes 2359304 | tf_op jit(solution)/shard_map/ppermute | solution.py:760
  103.8 22.6 %copy-start.28 = (bf16[1,512,768]{1,2,0:T(8,128)(2,1)}, bf16[1,512,768]{1,2,0:T(8,128)(2,1)S(1)}, u32[]{:S(2)}) copy-start(bf16[1,512,768]{1,2,0:T(8,128)(2,1)S(1)} %copy.186) | copy-start | bytes 2359300
  103.8 12.7 %copy-start.26 = (bf16[8,2,112640]{2,1,0:T(2,128)(2,1)S(1)}, bf16[8,2,112640]{2,1,0:T(2,128)(2,1)}, u32[]{:S(2)}) copy-start(bf16[8,2,112640]{2,1,0:T(2,128)(2,1)} %reshape.1748) | copy-start | bytes 10813444
  115.3 11.0 %copy-start.36 = (bf16[1,512,768]{1,2,0:T(8,128)(2,1)}, bf16[1,512,768]{1,2,0:T(8,128)(2,1)S(1)}, u32[]{:S(2)}) copy-start(bf16[1,512,768]{1,2,0:T(8,128)(2,1)S(1)} %collective-permute-done) | copy-start | bytes 2359300
  115.8 10.6 %copy-start.51 = (f32[1024]{0:T(1024)}, f32[1024]{0:T(1024)S(1)}, u32[]{:S(2)}) copy-start(f32[1024]{0:T(1024)S(1)} %broadcast_multiply_fusion.11) | copy-start | bytes 12292
  116.5 9.9 %copy-start.55 = (f32[1024]{0:T(1024)}, f32[1024]{0:T(1024)S(1)}, u32[]{:S(2)}) copy-start(f32[1024]{0:T(1024)S(1)} %add_rsqrt_fusion.3) | copy-start | bytes 12292
  116.9 9.5 %copy-start.57 = (f32[768]{0:T(1024)}, f32[768]{0:T(1024)S(1)}, u32[]{:S(2)}) copy-start(f32[768]{0:T(1024)S(1)} %mul.279) | copy-start | bytes 9220
  126.5 19.5 %copy-start.4 = (bf16[1,512,768]{2,1,0:T(8,128)(2,1)}, bf16[1,512,768]{2,1,0:T(8,128)(2,1)S(1)}, u32[]{:S(2)}) copy-start(bf16[1,512,768]{2,1,0:T(8,128)(2,1)S(1)} %slice.282.k_ref) | copy-start | bytes 2359300
  134.8 7.5 %copy-start.16 = (s32[12,8,1024]{2,1,0:T(8,128)}, s32[12,8,1024]{2,1,0:T(8,128)S(1)}, u32[]{:S(2)}) copy-start(s32[12,8,1024]{2,1,0:T(8,128)S(1)} %stack.57.patk_ref) | copy-start | bytes 1179652
  134.9 11.1 %copy-start.22 = (s32[12,8,512]{2,1,0:T(8,128)}, s32[12,8,512]{2,1,0:T(8,128)S(1)}, u32[]{:S(2)}) copy-start(s32[12,8,512]{2,1,0:T(8,128)S(1)} %slice.299.patk_ref) | copy-start | bytes 589828
  134.9 322.9 %reduce-scatter.5.cloned.1.call-start = ((), (), s32[]{:S(2)}) async-start(), calls=%async_computation.3 | async-start | bytes 11943936 | tf_op jit(solution)/shard_map/reduce_scatter | solution.py:515
  145.7 28.8 %copy-start.2 = (bf16[1,1024,768]{2,1,0:T(8,128)(2,1)}, bf16[1,1024,768]{2,1,0:T(8,128)(2,1)S(1)}, u32[]{:S(2)}) copy-start(bf16[1,1024,768]{2,1,0:T(8,128)(2,1)S(1)} %get-tuple-element.141.v_ref) | copy-start | bytes 4718596
  145.8 28.7 %copy-start.6 = (bf16[1,512,768]{2,1,0:T(8,128)(2,1)}, bf16[1,512,768]{2,1,0:T(8,128)(2,1)S(1)}, u32[]{:S(2)}) copy-start(bf16[1,512,768]{2,1,0:T(8,128)(2,1)S(1)} %slice.285.v_ref) | copy-start | bytes 2359300
  145.9 28.6 %copy-start.8 = (bf16[1,512,768]{2,1,0:T(8,128)(2,1)}, bf16[1,512,768]{2,1,0:T(8,128)(2,1)S(1)}, u32[]{:S(2)}) copy-start(bf16[1,512,768]{2,1,0:T(8,128)(2,1)S(1)} %get-tuple-element.158.q_ref) | copy-start | bytes 2359300
  145.9 28.6 %copy-start.19 = (bf16[1,512,768]{2,1,0:T(8,128)(2,1)}, bf16[1,512,768]{2,1,0:T(8,128)(2,1)S(1)}, u32[]{:S(2)}) copy-start(bf16[1,512,768]{2,1,0:T(8,128)(2,1)S(1)} %get-tuple-element.159.q_ref) | copy-start | bytes 2359300
  145.9 28.6 %copy-start.12 = (bf16[1,1024,768]{2,1,0:T(8,128)(2,1)S(1)}, bf16[1,1024,768]{2,1,0:T(8,128)(2,1)}, u32[]{:S(2)}) copy-start(bf16[1,1024,768]{2,1,0:T(8,128)(2,1)} %slice.301.k_ref) | copy-start | bytes 4718596
  146.0 28.6 %copy-start.17 = (s32[12,8,1024]{2,1,0:T(8,128)S(1)}, s32[12,8,1024]{2,1,0:T(8,128)}, u32[]{:S(2)}) copy-start(s32[12,8,1024]{2,1,0:T(8,128)} %copy-done.16) | copy-start | bytes 1179652
  146.0 28.6 %copy-start.24 = (s32[1,512,8]{2,1,0:T(8,128)S(1)}, s32[1,512,8]{2,1,0:T(8,128)}, u32[]{:S(2)}) copy-start(s32[1,512,8]{2,1,0:T(8,128)} %get-tuple-element.167.pcq_ref) | copy-start | bytes 49156
  232.7 12.2 %copy-start.42 = (bf16[96,8,2,1536]{3,1,2,0:T(8,128)(2,1)}, bf16[96,8,2,1536]{3,1,2,0:T(8,128)(2,1)S(1)}, u32[]{:S(2)}) copy-start(bf16[96,8,2,1536]{3,1,2,0:T(8,128)(2,1)S(1)} %copy.264) | copy-start | bytes 14155780
  271.6 22.0 %copy-start.41 = (bf16[96,8,2,1536]{3,1,2,0:T(8,128)(2,1)}, bf16[96,8,2,1536]{3,1,2,0:T(8,128)(2,1)S(1)}, u32[]{:S(2)}) copy-start(bf16[96,8,2,1536]{3,1,2,0:T(8,128)(2,1)S(1)} %copy.265) | copy-start | bytes 14155780
  293.6 17.2 %copy-start.33 = (f32[1024,768]{0,1:T(8,128)S(1)}, f32[1024,768]{0,1:T(8,128)}, u32[]{:S(2)}) copy-start(f32[1024,768]{0,1:T(8,128)} %copy-done.31) | copy-start | bytes 9437188
  347.6 8.1 %copy-start.39 = (bf16[1024,768]{1,0:T(8,128)(2,1)S(1)}, bf16[1024,768]{1,0:T(8,128)(2,1)}, u32[]{:S(2)}) copy-start(bf16[1024,768]{1,0:T(8,128)(2,1)} %multiply_convert_fusion.1) | copy-start | bytes 4718596
  347.6 9.1 %copy-start.3 = (bf16[1,1024,768]{2,1,0:T(8,128)(2,1)S(1)}, bf16[1,1024,768]{2,1,0:T(8,128)(2,1)}, u32[]{:S(2)}) copy-start(bf16[1,1024,768]{2,1,0:T(8,128)(2,1)} %copy-done.2) | copy-start | bytes 4718596
  347.6 234.3 %reduce-scatter.7.cloned.1.call-start = ((), (), s32[]{:S(2)}) async-start(), calls=%async_computation.7 | async-start | bytes 4313088
  361.2 51.4 %copy-start.5 = (bf16[1,512,768]{2,1,0:T(8,128)(2,1)S(1)}, bf16[1,512,768]{2,1,0:T(8,128)(2,1)}, u32[]{:S(2)}) copy-start(bf16[1,512,768]{2,1,0:T(8,128)(2,1)} %copy-done.4) | copy-start | bytes 2359300
  361.2 51.4 %copy-start.7 = (bf16[1,512,768]{2,1,0:T(8,128)(2,1)S(1)}, bf16[1,512,768]{2,1,0:T(8,128)(2,1)}, u32[]{:S(2)}) copy-start(bf16[1,512,768]{2,1,0:T(8,128)(2,1)} %copy-done.6) | copy-start | bytes 2359300
  457.9 8.5 %copy-start.43 = (bf16[3,1024,768]{2,1,0:T(8,128)(2,1)S(1)}, bf16[3,1024,768]{2,1,0:T(8,128)(2,1)}, u32[]{:S(2)}) copy-start(bf16[3,1024,768]{2,1,0:T(8,128)(2,1)} %pad_maximum_fusion.1) | copy-start | bytes 14155780
  457.9 8.5 %copy-start.44 = (bf16[3,768,768]{2,1,0:T(8,128)(2,1)S(1)}, bf16[3,768,768]{2,1,0:T(8,128)(2,1)}, u32[]{:S(2)}) copy-start(bf16[3,768,768]{2,1,0:T(8,128)(2,1)} %reshape.1750) | copy-start | bytes 10616836
  466.4 6.3 %copy-start.53 = (bf16[16,192]{1,0:T(8,128)(2,1)S(1)}, bf16[16,192]{1,0:T(8,128)(2,1)}, u32[]{:S(2)}) copy-start(bf16[16,192]{1,0:T(8,128)(2,1)} %reshape.1766) | copy-start | bytes 18436
  466.4 6.3 %copy-start.54 = (bf16[16,192]{1,0:T(8,128)(2,1)S(1)}, bf16[16,192]{1,0:T(8,128)(2,1)}, u32[]{:S(2)}) copy-start(bf16[16,192]{1,0:T(8,128)(2,1)} %reshape.1769) | copy-start | bytes 18436
  490.5 20.7 %collective-permute-start.1 = (bf16[1,512,768]{2,1,0:T(8,128)(2,1)}, bf16[1,512,768]{2,1,0:T(8,128)(2,1)}, u32[]{:S(2)}, u32[]{:S(2)}) collective-permute-start(bf16[1,512,768]{2,1,0:T(8,128)(2,1)} %bitcast.201), channel_id=1, source_target_pairs={{0,2},{2,0},{1,3},{3,1},{4,6},{6,4},{5,7},{7,5},{8,10},{10,8},{9,1... | collective-permute-start | bytes 2359304 | tf_op jit(solution)/shard_map/ppermute | solution.py:355
  491.8 33.7 %collective-permute-start.3 = (bf16[1,512,768]{2,1,0:T(8,128)(2,1)}, bf16[1,512,768]{2,1,0:T(8,128)(2,1)}, u32[]{:S(2)}, u32[]{:S(2)}) collective-permute-start(bf16[1,512,768]{2,1,0:T(8,128)(2,1)} %bitcast.202), channel_id=1, source_target_pairs={{0,3},{3,0},{1,2},{2,1},{4,7},{7,4},{5,6},{6,5},{8,11},{11,8},{9,1... | collective-permute-start | bytes 2359304 | tf_op jit(solution)/shard_map/ppermute | solution.py:357
  492.6 34.3 %collective-permute-start.2 = (bf16[1,512,768]{2,1,0:T(8,128)(2,1)S(1)}, bf16[1,512,768]{2,1,0:T(8,128)(2,1)S(1)}, u32[]{:S(2)}, u32[]{:S(2)}) collective-permute-start(bf16[1,512,768]{2,1,0:T(8,128)(2,1)S(1)} %bitcast.193), channel_id=1, source_target_pairs={{0,1},{1,0},{2,3},{3,2},{4,5},{5,4},{6,7},{7,6},{8,9},{9,8},{10,11... | collective-permute-start | bytes 2359304 | tf_op jit(solution)/shard_map/ppermute | solution.py:356
  531.5 34.9 %collective-permute-start.10 = (bf16[96,1,3456]{2,0,1:T(8,128)(2,1)}, bf16[96,1,3456]{2,0,1:T(8,128)(2,1)}, u32[]{:S(2)}, u32[]{:S(2)}) collective-permute-start(bf16[96,1,3456]{2,0,1:T(8,128)(2,1)} %constant_dynamic-slice_fusion), channel_id=1, source_target_pairs={{0,1},{1,0},{2,3},{3,2},{4,5},{5,4},{6,7},{7,6},{8,9},{9,8},{10,11... | collective-permute-start | bytes 1990664 | tf_op jit(solution)/shard_map/ppermute | solution.py:445
  534.7 31.8 %copy-start.48 = (bf16[96,2,3456]{2,0,1:T(8,128)(2,1)S(1)}, bf16[96,2,3456]{2,0,1:T(8,128)(2,1)}, u32[]{:S(2)}) copy-start(bf16[96,2,3456]{2,0,1:T(8,128)(2,1)} %reduce-scatter.5.cloned.1.call-done) | copy-start | bytes 3981316
  536.0 40.1 %collective-permute-start.7 = (bf16[1,512,768]{2,1,0:T(8,128)(2,1)}, bf16[1,512,768]{2,1,0:T(8,128)(2,1)}, u32[]{:S(2)}, u32[]{:S(2)}) collective-permute-start(bf16[1,512,768]{2,1,0:T(8,128)(2,1)} %bitcast.203), channel_id=1, source_target_pairs={{0,3},{3,0},{1,2},{2,1},{4,7},{7,4},{5,6},{6,5},{8,11},{11,8},{9,1... | collective-permute-start | bytes 2359304 | tf_op jit(solution)/shard_map/ppermute | solution.py:357
  538.3 36.1 %collective-permute-start.5 = (bf16[1,512,768]{2,1,0:T(8,128)(2,1)}, bf16[1,512,768]{2,1,0:T(8,128)(2,1)}, u32[]{:S(2)}, u32[]{:S(2)}) collective-permute-start(bf16[1,512,768]{2,1,0:T(8,128)(2,1)} %bitcast.204), channel_id=1, source_target_pairs={{0,2},{2,0},{1,3},{3,1},{4,6},{6,4},{5,7},{7,5},{8,10},{10,8},{9,1... | collective-permute-start | bytes 2359304 | tf_op jit(solution)/shard_map/ppermute | solution.py:355
  539.1 39.3 %collective-permute-start.6 = (bf16[1,512,768]{2,1,0:T(8,128)(2,1)S(1)}, bf16[1,512,768]{2,1,0:T(8,128)(2,1)S(1)}, u32[]{:S(2)}, u32[]{:S(2)}) collective-permute-start(bf16[1,512,768]{2,1,0:T(8,128)(2,1)S(1)} %bitcast.195), channel_id=1, source_target_pairs={{0,1},{1,0},{2,3},{3,2},{4,5},{5,4},{6,7},{7,6},{8,9},{9,8},{10,11... | collective-permute-start | bytes 2359304 | tf_op jit(solution)/shard_map/ppermute | solution.py:356
  567.7 17.5 %collective-permute-start.11 = (bf16[96,1,3456]{2,0,1:T(8,128)(2,1)S(1)}, bf16[96,1,3456]{2,0,1:T(8,128)(2,1)S(1)}, u32[]{:S(2)}, u32[]{:S(2)}) collective-permute-start(bf16[96,1,3456]{2,0,1:T(8,128)(2,1)S(1)} %add_convert_fusion.3), channel_id=1, source_target_pairs={{0,2},{2,0},{1,3},{3,1},{4,6},{6,4},{5,7},{7,5},{8,10},{10,8},{9,1... | collective-permute-start | bytes 1990664 | tf_op jit(solution)/shard_map/ppermute | solution.py:452
  583.9 6.2 %collective-permute-start.8 = (bf16[104,3,384]{2,0,1:T(8,128)(2,1)S(1)}, bf16[104,3,384]{2,0,1:T(8,128)(2,1)S(1)}, u32[]{:S(2)}, u32[]{:S(2)}) collective-permute-start(bf16[104,3,384]{2,0,1:T(8,128)(2,1)S(1)} %copy.258), channel_id=1, source_target_pairs={{0,1},{1,0},{2,3},{3,2},{4,5},{5,4},{6,7},{7,6},{8,9},{9,8},{10,11... | collective-permute-start | bytes 718856 | tf_op jit(solution)/shard_map/ppermute | solution.py:445
  590.1 11.0 %copy-start.1 = (s32[4,2]{0,1:T(2,128)S(1)}, s32[4,2]{0,1:T(2,128)}, u32[]{:S(2)}) copy-start(s32[4,2]{0,1:T(2,128)} %param.21) | copy-start | bytes 100
  590.1 6.2 %collective-permute-start.9 = (bf16[104,3,384]{2,0,1:T(8,128)(2,1)S(1)}, bf16[104,3,384]{2,0,1:T(8,128)(2,1)S(1)}, u32[]{:S(2)}, u32[]{:S(2)}) collective-permute-start(bf16[104,3,384]{2,0,1:T(8,128)(2,1)S(1)} %add_convert_fusion.4), channel_id=1, source_target_pairs={{0,2},{2,0},{1,3},{3,1},{4,6},{6,4},{5,7},{7,5},{8,10},{10,8},{9,1... | collective-permute-start | bytes 718856 | tf_op jit(solution)/shard_map/ppermute | solution.py:452
  (35 other events, 87.3 us)
Sparse Core Ops, SparseCore 0:
  16.5 50.1 all-gather.7
  89.8 35.6 all-gather.9
  127.8 52.6 all-gather.11
  182.6 51.6 all-gather.13
  347.8 109.2 reduce-scatter.4
  478.2 45.3 reduce-scatter.6

commit v9 on v8

--- a/solution.py
+++ b/solution.py
@@ -577,7 +577,7 @@
     return (kept_state, layer_out.reshape(seq_count, local_len, model_width))
 
 
-def backward_pass(kept_state, block_grad, weights, span):
+def backward_pass(kept_state, block_grad, weights, span, carried):
     w_qkv, w_out, w_up, w_down, norm_gains, out_biases, head_biases, head_gain, unit_bias, unit_gain = weights
     (
         attn_in,
@@ -620,12 +620,13 @@
     sub_grad = back_dot(middle_low, w_out)
     attended_grad, head_gain_grad = norm_back(sub_normed, sub_inv, head_gain, sub_grad)
     attended_low = attended_grad.astype(jnp.bfloat16)
-    down_grad, up_grad, out_weight_grad, attended_low = lax.optimization_barrier(
+    down_grad, up_grad, out_weight_grad, attended_low, carried = lax.optimization_barrier(
         (
             down_grad.astype(jnp.bfloat16),
             up_grad.astype(jnp.bfloat16),
             out_weight_grad.astype(jnp.bfloat16),
             attended_low,
+            carried,
         )
     )
     tensor_count = lax.axis_size("tensor")
@@ -665,6 +666,8 @@
     )
     qkv_grad, stacked = lax.optimization_barrier((qkv_grad, stacked))
     attn_in_grad = jnp.einsum("jre,jde->rd", stacked, w_qkv, preferred_element_type=jnp.float32)
+    early_total = finish_stage(early_share, 1).reshape(early_share.shape[0], -1)
+    early_total, attn_in_grad = lax.optimization_barrier((early_total, attn_in_grad))
     input_part, first_gain_grad = norm_back(first_normed, first_inv, norm_gains[0], attn_in_grad)
     input_low = (middle_grad + input_part).astype(jnp.bfloat16)
     heads = model_width // HD
@@ -712,7 +715,6 @@
             count *= size
         small_pieces.append(small_total[offset : offset + count].reshape(local_shape))
         offset += count
-    early_total = finish_stage(early_share, 1).reshape(early_share.shape[0], -1)
     down_width = early_widths[0] // nt
     up_width = early_widths[1] // nt
     grad_shares = (
@@ -721,7 +723,7 @@
         early_total[:, down_width + up_width :].transpose(1, 0),
         qkv_total[:block_rows].transpose(1, 0, 2),
     ) + tuple(small_pieces)
-    return (grad_shares, input_low.reshape(seq_count, local_len, model_width))
+    return (grad_shares, input_low.reshape(seq_count, local_len, model_width), carried)
 
 
 def local(
@@ -830,7 +832,9 @@
         layer_out = spread_sequence(layer_block, local_len)
     else:
         layer_out = pair_gather(layer_block, "tensor", 0)
-    grad_shares, input_block = backward_pass(kept_state, block_grad, weights, span)
+    grad_shares, input_block, layer_out = backward_pass(
+        kept_state, block_grad, weights, span, layer_out
+    )
     if whole:
         input_grad = spread_sequence(input_block, local_len)
     else:

time: 614 us -> 633 us (1.031)
  local copies, waits for them, and re-layouts: 128 us -> 138 us
  other arithmetic: 77.4 us -> 85.3 us
    unnamed x7, waiting for transfers between devices: 0.76 us -> 38.9 us
    ppermute x2, waiting for transfers between devices: 31.4 us -> 6.12 us  [pair_reduce(): received = lax.ppermute(sent, axis_name, perm=[(0, 1), (1, 0)])]
    ppermute x2, waiting for transfers between devices: 12.6 us -> 0.01 us  [spread_sequence(): lax.ppermute(other, ('context', 'tensor'), perm=[(0, 3), (3, 0), (1, 2),...]
    ppermute x2, waiting for transfers between devices: 2.93 us -> 9.67 us  [pair_sum(): received = lax.ppermute(share, axis_name, perm=[(0, 1), (1, 0)])]
    reduce_scatter x1, waiting for transfers between devices: 0.01 us -> 6.52 us  [shard_stage(): lax.psum_scatter(grad.astype(jnp.bfloat16), 'shard', scatter_dimension=di...]
    unnamed x142 -> x168, local copies, waits for them, and re-layouts: 38 us -> 42 us
  transfers between devices with their start and end apart: 18 -> 18, of which waited for: 10 -> 9; matrix products, arithmetic and copies ran while one was open for 25% -> 26% of each run, Pallas kernels for 24% -> 23%
where the time goes in v9:
time: 633 us; the launch traced here: 627 us
  Pallas kernels  143 us (23%)
  local copies, waits for them, and re-layouts  138 us (22%)
  waiting for transfers between devices  138 us (22%)
  matrix products  89.8 us (14%)
  other arithmetic  85.3 us (13%)
  between operations  17.4 us (3%)
  starting transfers between devices  15.9 us (3%)
    pallas_call x2, Pallas kernels, attention_backward(): pl.pallas_call(attention_bwd_kernel, grid=grid, in_specs=[query_spec, key...  80.2 us
    pallas_call x2, Pallas kernels, attention_forward(): pl.pallas_call(attention_fwd_kernel, grid=grid, in_specs=[query_spec, key...  63.3 us
    all_gather x1, waiting for transfers between devices, gather_packed(): lax.all_gather(flat, ('shard', 'tensor'), axis=0, tiled=False)  50.3 us
    unnamed x168, local copies, waits for them, and re-layouts  42 us
    unnamed x7, waiting for transfers between devices  38.9 us
    dot_general x3, matrix products, back_dot(): lax.dot_general(left_rows, weight_rows, (((1,), (1,)), ((), ())), preferr...  30.4 us
    reshape x5, local copies, waits for them, and re-layouts, gather_weight(): stacked.reshape((ns, nt) + local_block.shape)  29.7 us
    ppermute x2, waiting for transfers between devices, spread_sequence(): from_context = lax.ppermute(other, 'context', perm=swap)  17.8 us
  transfers between devices with their start and end apart: 18, of which 9 were waited for; matrix products, arithmetic and copies ran while one was open for 26% of the time, Pallas kernels for 23%

profile of v9, /device:TPU:0, one launch (start us, length us, event | category | flops | bytes accessed | tf_op | source)
XLA Modules:
  0.0 627.3 jit_solution(437521560581480536)
XLA Ops:
  16.4 50.3 %all-gather.8.cloned.1.call-done = bf16[16,880,128]{2,1,0:T(8,128)(2,1)} async-done(((bf16[1,880,128]{2,1,0:T(8,128)(2,1)}), bf16[16,880,128]{2,1,0:T(8,128)(2,1)}) %all-gather.8.cloned.1.call-update) | async-done | bytes 3604496 | tf_op jit(solution)/shard_map/all_gather | solution.py:416
  66.7 6.7 %reshape.1748 = bf16[8,2,112640]{2,1,0:T(2,128)(2,1)} reshape(bf16[16,880,128]{2,1,0:T(8,128)(2,1)} %all-gather.8.cloned.1.call-done) | data formatting | bytes 7208960 | tf_op jit(solution)/shard_map/reshape | solution.py:416
  75.4 4.7 reshape.1791
  80.1 5.5 copy.202
  85.6 4.0 reshape.1750
  90.7 2.9 constant_dynamic-slice_fusion.8
  96.2 2.3 copy.259
  107.0 8.4 %collective-permute-done.1 = bf16[1,512,768]{1,2,0:T(8,128)(2,1)S(1)} collective-permute-done((bf16[1,512,768]{1,2,0:T(8,128)(2,1)}, bf16[1,512,768]{1,2,0:T(8,128)(2,1)S(1)}, u32[]{:S(2)}, u32[]{:S(2)}) %collective-permute-start.1) | collective-permute-done | bytes 786464 | tf_op jit(solution)/shard_map/ppermute | solution.py:762
  116.9 9.4 %fusion.85 = (bf16[3,1024,768]{2,1,0:T(8,128)(2,1)S(1)}, f32[3,1024,768]{2,1,0:T(8,128)}) fusion(bf16[3,768,768]{2,1,0:T(8,128)(2,1)} %reshape.1750, f32[768]{0:T(1024)S(1)} %mul.279, f32[1024]{0:T(1024)S(1)} %add_rsqrt_fusion.3, f32[1024]{0:T(1024)S(1)} %broadcast_multiply_fusion.11, bf16[512,768]{0,1:T(8,128)(2,1)S(1)} %bitcast.153, ...), kind=kOutput, calls=%fused_computation.285 | convolution fusion | flops 3637248000 | bytes 19278848 | tf_op jit(solution)/shard_map/rd,jde->jre/dot_general | solution.py:530
  144.3 3.4 fusion.21
  148.0 28.5 %shard_map.256 = f32[1,512,768]{2,1,0:T(8,128)S(1)} custom-call(bf16[1,512,768]{2,1,0:T(8,128)(2,1)S(1)} %get-tuple-element.164.q_ref, bf16[1,512,768]{2,1,0:T(8,128)(2,1)S(1)} %slice.282.k_ref, bf16[1,512,768]{2,1,0:T(8,128)(2,1)S(1)} %slice.285.v_ref, s32[12,512,8]{2,1,0:T(8,128)} %copy.262.patq_ref, s32[12,8,512]{2,1,0:T(8,128)S(1)} %slice.299.patk_ref, ...), custom_call_target="tpu_custom_call" | custom-call | flops 1610612736 | bytes 5505024 | tf_op jit(solution)/shard_map/pallas_call | solution.py:217
  176.5 34.8 %shard_map.257 = f32[1,512,768]{2,1,0:T(8,128)S(1)} custom-call(bf16[1,512,768]{2,1,0:T(8,128)(2,1)S(1)} %get-tuple-element.165.q_ref, bf16[1,1024,768]{2,1,0:T(8,128)(2,1)S(1)} %copy-done.12, bf16[1,1024,768]{2,1,0:T(8,128)(2,1)S(1)} %get-tuple-element.147.v_ref, s32[12,512,8]{2,1,0:T(8,128)} %copy.263.patq_ref, s32[12,8,1024]{2,1,0:T(8,128)S(1)} %stack.57.patk_ref, ...), custom_call_target="tpu_custom_call" | custom-call | flops 3221225472 | bytes 8650752 | tf_op jit(solution)/shard_map/pallas_call | solution.py:217
  212.1 3.2 reshape.1753
  221.6 9.3 %copy.214 = bf16[8,2,96,1536]{3,1,2,0:T(2,128)(2,1)} copy(bf16[8,2,96,1536]{3,2,1,0:T(8,128)(2,1)} %bitcast.173) | data formatting | bytes 9437184 | tf_op jit(solution)/shard_map/reshape | solution.py:407
  231.0 3.8 copy.274
  234.8 12.2 %fusion.73 = (f32[1024]{0:T(1024)S(1)}, f32[1024,3072]{1,0:T(8,128)}) fusion(f32[3072]{0:T(1024)S(1)} %reshape.1776, bf16[768,3072]{1,0:T(8,128)(2,1)S(1)} %bitcast.180, f32[1024,768]{0,1:T(8,128)S(1)} %copy-done.37, f32[768]{0:T(1024)S(1)} %copy-done.60, f32[1024]{0:T(1024)S(1)} %add_rsqrt_fusion.1, f32[1024]{0:T(1024)S(1)} %broadcast_multiply_fusion.9), kind=kOutput, calls=%fused_computation.274 | convolution fusion | flops 4866440192 | bytes 20474880 | tf_op jit(solution)/shard_map/dot_general | solution.py:551
  247.0 8.1 %multiply_reduce_fusion.2 = f32[1024]{0:T(1024)S(1)} fusion(f32[1024]{0:T(1024)S(1)} %broadcast_multiply_fusion.2, f32[1024,3072]{1,0:T(8,128)} %get-tuple-element.189, f32[3072]{0:T(1024)S(1)} %reshape.1776), kind=kLoop, calls=%fused_computation.12 | loop fusion | flops 37747712 | bytes 12603392 | tf_op jit(solution)/shard_map/reduce_sum | solution.py:73
  255.1 7.3 %reshape.1758 = bf16[8,2,1536,96]{2,1,0,3:T(2,128)(2,1)} reshape(bf16[24576,96]{0,1:T(8,128)(2,1)} %all-gather.14.cloned.1.call-done) | data formatting | bytes 9437184 | tf_op jit(solution)/shard_map/reshape | solution.py:407
  262.4 7.7 %copy.219 = bf16[8,2,1536,96]{2,1,3,0:T(2,128)(2,1)} copy(bf16[8,2,1536,96]{2,1,0,3:T(2,128)(2,1)} %reshape.1758) | data formatting | bytes 9437184 | tf_op jit(solution)/shard_map/reshape | solution.py:407
  270.1 5.8 copy.275
  275.9 20.9 %multiply_reduce_fusion = (bf16[3072]{0:T(1024)(128)(2,1)S(1)}, f32[1024]{0:T(1024)S(1)}, f32[1024]{0:T(1024)S(1)}, bf16[1024,3072]{1,0:T(8,128)(2,1)}, f32[1024,3072]{1,0:T(8,128)}) fusion(f32[1024]{0:T(1024)S(1)} %add_rsqrt_fusion, f32[1024]{0:T(1024)S(1)} %broadcast_multiply_fusion.2, f32[1024,3072]{1,0:T(8,128)} %get-tuple-element.189, ...), kind=kOutput, calls=%fused_computation.9 | convolution fusion | flops 4898679808 | bytes 37795840 | tf_op jit(solution)/shard_map/dot_general | solution.py:65
  296.9 17.0 %fusion.74 = (bf16[3072]{0:T(1024)(128)(2,1)S(1)}, bf16[1024,3072]{1,0:T(8,128)(2,1)S(1)}) fusion(f32[1024]{0:T(1024)S(1)} %broadcast_multiply_fusion, f32[1024]{0:T(1024)S(1)} %broadcast_multiply_fusion.2, f32[1024,3072]{1,0:T(8,128)} %get-tuple-element.189, f32[3072]{0:T(1024)S(1)} %reshape.1776, f32[1024]{0:T(1024)S(1)} %broadcast_multiply_fusion.1, ...), kind=kLoop, calls=%fused_computation.275 | loop fusion | flops 94368768 | bytes 31504384 | tf_op jit(solution)/shard_map/reduce_sum | solution.py:613
  313.9 7.4 %multiply_reduce_fusion.5 = (bf16[768]{0:T(1024)(128)(2,1)S(1)}, f32[1024]{0:T(1024)S(1)}, f32[1024]{0:T(1024)S(1)}, f32[1024,768]{0,1:T(8,128)}) fusion(f32[1024,768]{0,1:T(8,128)S(1)} %copy-done.38, f32[1024]{0:T(1024)S(1)} %add_rsqrt_fusion.1, f32[1024]{0:T(1024)S(1)} %broadcast_multiply_fusion.9, f32[768]{0:T(1024)S(1)} %copy-done.60, ...), kind=kOutput, calls=%fused_computation.57 | convolution fusion | flops 4838126592 | bytes 17322496 | tf_op jit(solution)/shard_map/dot_general | solution.py:65
  321.3 6.9 %convolution_convert_fusion = bf16[768,3072]{1,0:T(8,128)(2,1)} fusion(bf16[1024,3072]{1,0:T(8,128)(2,1)S(1)} %get-tuple-element.141, f32[1024,768]{0,1:T(8,128)S(1)} %copy-done.38, f32[768]{0:T(1024)S(1)} %copy-done.60, f32[1024]{0:T(1024)S(1)} %add_rsqrt_fusion.1, f32[1024]{0:T(1024)S(1)} %broadcast_multiply_fusion.9), kind=kOutput, calls=%fused_computation.17 | convolution fusion | flops 4837343232 | bytes 14167040 | tf_op jit(solution)/shard_map/dot_general | solution.py:59
  328.2 8.6 %convolution_convert_fusion.1 = bf16[768,3072]{1,0:T(8,128)(2,1)} fusion(bf16[1024,3072]{1,0:T(8,128)(2,1)S(1)} %bitcast.216, bf16[512,768]{0,1:T(8,128)(2,1)} %bitcast.1, bf16[512,768]{0,1:T(8,128)(2,1)S(1)} %bitcast.195, pred[]{:T(512)S(6)} %eq.182), kind=kOutput, calls=%fused_computation.18 | convolution fusion | flops 4841275392 | bytes 12582913 | tf_op jit(solution)/shard_map/dot_general | solution.py:59
  336.8 5.1 add_convert_fusion.2
  343.3 2.3 copy.224
  347.6 2.3 copy.223
  351.3 5.5 convert_reduce_fusion.2
  359.0 2.3 multiply_convert_fusion.1
  363.0 17.8 %collective-permute-done.2 = bf16[1,512,768]{2,1,0:T(8,128)(2,1)} collective-permute-done((bf16[1,512,768]{2,1,0:T(8,128)(2,1)}, bf16[1,512,768]{2,1,0:T(8,128)(2,1)}, u32[]{:S(2)}, u32[]{:S(2)}) %collective-permute-start.2) | collective-permute-done | bytes 786464 | tf_op jit(solution)/shard_map/ppermute | solution.py:355
  389.0 4.8 pad_maximum_fusion
  400.9 49.3 %shard_map.259 = (bf16[1,512,768]{2,1,0:T(8,128)(2,1)S(1)}, f32[1,1024,768]{2,1,0:T(8,128)}, f32[1,1024,768]{2,1,0:T(8,128)}) custom-call(bf16[1,512,768]{2,1,0:T(8,128)(2,1)S(1)} %copy-done.21, bf16[1,1024,768]{2,1,0:T(8,128)(2,1)S(1)} %copy-done.13, bf16[1,1024,768]{2,1,0:T(8,128)(2,1)S(1)} %copy-done.3, ...), custom_call_target="tpu_custom_call" | custom-call | flops 8053063680 | bytes 20447232 | tf_op jit(solution)/shard_map/pallas_call | solution.py:244
  455.6 30.9 %shard_map.258 = (bf16[1,512,768]{2,1,0:T(8,128)(2,1)S(1)}, f32[1,512,768]{2,1,0:T(8,128)S(1)}, f32[1,512,768]{2,1,0:T(8,128)}) custom-call(bf16[1,512,768]{2,1,0:T(8,128)(2,1)S(1)} %copy-done.9, bf16[1,512,768]{2,1,0:T(8,128)(2,1)S(1)} %copy-done.5, bf16[1,512,768]{2,1,0:T(8,128)(2,1)S(1)} %copy-done.7, bf16[1,512,768]{2,1,0:T(8,128)(2,1)S(1)} %copy-done.22, ...), custom_call_target="tpu_custom_call" | custom-call | flops 4026531840 | bytes 11010048 | tf_op jit(solution)/shard_map/pallas_call | solution.py:244
  487.9 4.0 fusion.76
  492.3 2.4 add_convert_fusion.1
  495.0 2.5 pad_maximum_fusion.1
  497.5 6.5 %reduce-scatter.5.cloned.1.call-done = bf16[96,2,3456]{2,0,1:T(8,128)(2,1)} async-done(((bf16[768,2,3456]{2,0,1:T(8,128)(2,1)}), bf16[96,2,3456]{2,0,1:T(8,128)(2,1)}) %reduce-scatter.5.cloned.1.call-update) | async-done | bytes 1327120 | tf_op jit(solution)/shard_map/reduce_scatter | solution.py:515
  506.9 8.5 %fusion.37 = bf16[768,3,768]{2,0,1:T(8,128)(2,1)} fusion(bf16[3,1024,768]{2,1,0:T(8,128)(2,1)} %pad_maximum_fusion.1, f32[768]{0:T(1024)S(1)} %copy-done.59, f32[1024]{0:T(1024)S(1)} %copy-done.57, f32[1024]{0:T(1024)S(1)} %copy-done.54, bf16[512,768]{0,1:T(8,128)(2,1)S(1)} %bitcast.171, bf16[512,768]{0,1:T(8,128)(2,1)S(1)} %bitcast.157, pred[]{:T(512)S(6)} %eq.182), kind=kOutput, calls=%fused_computation.93 | convolution fusion | flops 3634888704 | bytes 9841665 | tf_op jit(solution)/shard_map/rd,jre->dje/dot_general | solution.py:663
  515.4 4.8 collective-permute-done.5
  521.9 5.5 convolution_bitcast_fusion.1
  527.5 6.9 %collective-permute-done.6 = bf16[96,1,3456]{2,0,1:T(8,128)(2,1)S(1)} collective-permute-done((bf16[96,1,3456]{2,0,1:T(8,128)(2,1)S(1)}, bf16[96,1,3456]{2,0,1:T(8,128)(2,1)S(1)}, u32[]{:S(2)}, u32[]{:S(2)}) %collective-permute-start.6) | collective-permute-done | bytes 663584 | tf_op jit(solution)/shard_map/ppermute | solution.py:452
  535.6 2.4 copy.228
  538.0 4.0 fusion.19
  551.5 4.3 fusion.18
  557.2 2.4 collective-permute-start.9
  562.8 38.1 %reduce-scatter.7.cloned.1.call-done = bf16[104,2304]{1,0:T(8,128)(2,1)} async-done(((bf16[832,2304]{1,0:T(8,128)(2,1)}), bf16[104,2304]{1,0:T(8,128)(2,1)}) %reduce-scatter.7.cloned.1.call-update) | async-done | bytes 479248
  612.5 2.8 collective-permute-done.11
  (377 shorter events, 115.6 us)
Async XLA Ops:
  7.2 91.9 %copy-start = (s32[4,2]{0,1:T(2,128)S(1)}, s32[4,2]{0,1:T(2,128)}, u32[]{:S(2)}) copy-start(s32[4,2]{0,1:T(2,128)} %param.21) | copy-start | bytes 100
  7.2 59.5 %all-gather.8.cloned.1.call-start = ((), (), s32[]{:S(2)}) async-start(), calls=%async_computation.2 | async-start | bytes 3829760 | tf_op jit(solution)/shard_map/all_gather | solution.py:416
  16.4 195.7 %all-gather.10.cloned.1.call-start = ((), (), s32[]{:S(2)}) async-start(), calls=%async_computation.4 | async-start | bytes 1253376 | tf_op jit(solution)/shard_map/all_gather | solution.py:406
  89.7 131.9 %all-gather.12.cloned.1.call-start = ((), (), s32[]{:S(2)}) async-start(), calls=%async_computation.5 | async-start | bytes 5013504 | tf_op jit(solution)/shard_map/all_gather | solution.py:406
  90.4 164.7 %all-gather.14.cloned.1.call-start = ((), (), s32[]{:S(2)}) async-start(), calls=%async_computation.6 | async-start | bytes 5013504 | tf_op jit(solution)/shard_map/all_gather | solution.py:406
  94.8 20.6 %collective-permute-start.1 = (bf16[1,512,768]{1,2,0:T(8,128)(2,1)}, bf16[1,512,768]{1,2,0:T(8,128)(2,1)S(1)}, u32[]{:S(2)}, u32[]{:S(2)}) collective-permute-start(bf16[1,512,768]{1,2,0:T(8,128)(2,1)} %copy.260), channel_id=1, source_target_pairs={{0,2},{2,0},{1,3},{3,1},{4,6},{6,4},{5,7},{7,5},{8,10},{10,8},{9,1... | collective-permute-start | bytes 2359304 | tf_op jit(solution)/shard_map/ppermute | solution.py:762
  98.5 177.3 %collective-permute-start = (bf16[1,512,768]{1,2,0:T(8,128)(2,1)}, bf16[1,512,768]{1,2,0:T(8,128)(2,1)}, u32[]{:S(2)}, u32[]{:S(2)}) collective-permute-start(bf16[1,512,768]{1,2,0:T(8,128)(2,1)} %copy.259), channel_id=1, source_target_pairs={{0,2},{2,0},{1,3},{3,1},{4,6},{6,4},{5,7},{7,5},{8,10},{10,8},{9,1... | collective-permute-start | bytes 2359304 | tf_op jit(solution)/shard_map/ppermute | solution.py:762
  103.2 23.2 %copy-start.31 = (bf16[1,512,768]{1,2,0:T(8,128)(2,1)}, bf16[1,512,768]{1,2,0:T(8,128)(2,1)S(1)}, u32[]{:S(2)}) copy-start(bf16[1,512,768]{1,2,0:T(8,128)(2,1)S(1)} %copy.196) | copy-start | bytes 2359300
  104.4 43.5 %copy-start.27 = (s32[1,8,512]{2,1,0:T(8,128)}, s32[1,8,512]{2,1,0:T(8,128)S(1)}, u32[]{:S(2)}) copy-start(s32[1,8,512]{2,1,0:T(8,128)S(1)} %pad_slice_fusion.2.pck_ref) | copy-start | bytes 49156
  107.0 41.0 %copy-start.16 = (s32[1,512,8]{2,1,0:T(8,128)}, s32[1,512,8]{2,1,0:T(8,128)S(1)}, u32[]{:S(2)}) copy-start(s32[1,512,8]{2,1,0:T(8,128)S(1)} %get-tuple-element.172.pcq_ref) | copy-start | bytes 49156
  126.5 21.5 %copy-start.4 = (bf16[1,512,768]{2,1,0:T(8,128)(2,1)}, bf16[1,512,768]{2,1,0:T(8,128)(2,1)S(1)}, u32[]{:S(2)}) copy-start(bf16[1,512,768]{2,1,0:T(8,128)(2,1)S(1)} %slice.282.k_ref) | copy-start | bytes 2359300
  136.7 39.8 %copy-start.18 = (s32[12,8,1024]{2,1,0:T(8,128)}, s32[12,8,1024]{2,1,0:T(8,128)S(1)}, u32[]{:S(2)}) copy-start(s32[12,8,1024]{2,1,0:T(8,128)S(1)} %stack.57.patk_ref) | copy-start | bytes 1179652
  136.8 367.3 %reduce-scatter.5.cloned.1.call-start = ((), (), s32[]{:S(2)}) async-start(), calls=%async_computation.3 | async-start | bytes 11943936 | tf_op jit(solution)/shard_map/reduce_scatter | solution.py:515
  147.7 28.8 %copy-start.2 = (bf16[1,1024,768]{2,1,0:T(8,128)(2,1)}, bf16[1,1024,768]{2,1,0:T(8,128)(2,1)S(1)}, u32[]{:S(2)}) copy-start(bf16[1,1024,768]{2,1,0:T(8,128)(2,1)S(1)} %get-tuple-element.147.v_ref) | copy-start | bytes 4718596
  147.8 28.7 %copy-start.6 = (bf16[1,512,768]{2,1,0:T(8,128)(2,1)}, bf16[1,512,768]{2,1,0:T(8,128)(2,1)S(1)}, u32[]{:S(2)}) copy-start(bf16[1,512,768]{2,1,0:T(8,128)(2,1)S(1)} %slice.285.v_ref) | copy-start | bytes 2359300
  147.9 28.6 %copy-start.8 = (bf16[1,512,768]{2,1,0:T(8,128)(2,1)}, bf16[1,512,768]{2,1,0:T(8,128)(2,1)S(1)}, u32[]{:S(2)}) copy-start(bf16[1,512,768]{2,1,0:T(8,128)(2,1)S(1)} %get-tuple-element.164.q_ref) | copy-start | bytes 2359300
  147.9 28.6 %copy-start.20 = (bf16[1,512,768]{2,1,0:T(8,128)(2,1)}, bf16[1,512,768]{2,1,0:T(8,128)(2,1)S(1)}, u32[]{:S(2)}) copy-start(bf16[1,512,768]{2,1,0:T(8,128)(2,1)S(1)} %get-tuple-element.165.q_ref) | copy-start | bytes 2359300
  148.0 28.6 %copy-start.12 = (bf16[1,1024,768]{2,1,0:T(8,128)(2,1)S(1)}, bf16[1,1024,768]{2,1,0:T(8,128)(2,1)}, u32[]{:S(2)}) copy-start(bf16[1,1024,768]{2,1,0:T(8,128)(2,1)} %slice.301.k_ref) | copy-start | bytes 4718596
  148.0 28.6 %copy-start.25 = (s32[1,512,8]{2,1,0:T(8,128)S(1)}, s32[1,512,8]{2,1,0:T(8,128)}, u32[]{:S(2)}) copy-start(s32[1,512,8]{2,1,0:T(8,128)} %get-tuple-element.173.pcq_ref) | copy-start | bytes 49156
  148.0 28.5 %copy-start.29 = (s32[1,8,1024]{2,1,0:T(8,128)S(1)}, s32[1,8,1024]{2,1,0:T(8,128)}, u32[]{:S(2)}) copy-start(s32[1,8,1024]{2,1,0:T(8,128)} %pad.26.pck_ref) | copy-start | bytes 98308
  270.1 43.8 %slice-start.6 = ((s8[4718592]{0:T(1024)(128)(4,1)}), s8[4194304]{0:T(1024)(128)(4,1)S(1)}, s32[]{:S(2)}) async-start(s8[4718592]{0:T(1024)(128)(4,1)} %bitcast.181), calls=%async_computation.14 | async-start | bytes 8388608
  275.9 38.0 %slice-start.7 = ((s8[4718592]{0:T(1024)(128)(4,1)}), s8[524288]{0:T(1024)(128)(4,1)S(1)}, s32[]{:S(2)}) async-start(s8[4718592]{0:T(1024)(128)(4,1)} %bitcast.181), calls=%async_computation.15 | async-start | bytes 1048576
  296.8 17.0 %copy-start.38 = (f32[1024,768]{0,1:T(8,128)S(1)}, f32[1024,768]{0,1:T(8,128)}, u32[]{:S(2)}) copy-start(f32[1024,768]{0,1:T(8,128)} %copy-done.36) | copy-start | bytes 9437188
  296.8 31.3 %slice-start.12 = ((s8[6291456]{0:T(1024)(128)(4,1)}), s8[4194304]{0:T(1024)(128)(4,1)S(1)}, s32[]{:S(2)}) async-start(s8[6291456]{0:T(1024)(128)(4,1)} %bitcast.215), calls=%async_computation.20 | async-start | bytes 8388608
  313.9 14.3 %slice-start.13 = ((s8[6291456]{0:T(1024)(128)(4,1)}), s8[2097152]{0:T(1024)(128)(4,1)S(1)}, s32[]{:S(2)}) async-start(s8[6291456]{0:T(1024)(128)(4,1)} %bitcast.215), calls=%async_computation.21 | async-start | bytes 4194304
  321.3 15.5 %slice-start.8 = ((s8[4718592]{0:T(1024)(128)(4,1)}), s8[524288]{0:T(1024)(128)(4,1)S(1)}, s32[]{:S(2)}) async-start(s8[4718592]{0:T(1024)(128)(4,1)} %bitcast.185), calls=%async_computation.16 | async-start | bytes 1048576
  345.6 36.9 %collective-permute-start.4 = (bf16[1,512,768]{2,1,0:T(8,128)(2,1)}, bf16[1,512,768]{2,1,0:T(8,128)(2,1)}, u32[]{:S(2)}, u32[]{:S(2)}) collective-permute-start(bf16[1,512,768]{2,1,0:T(8,128)(2,1)} %bitcast.204), channel_id=1, source_target_pairs={{0,3},{3,0},{1,2},{2,1},{4,7},{7,4},{5,6},{6,5},{8,11},{11,8},{9,1... | collective-permute-start | bytes 2359304 | tf_op jit(solution)/shard_map/ppermute | solution.py:357
  347.1 33.8 %collective-permute-start.2 = (bf16[1,512,768]{2,1,0:T(8,128)(2,1)}, bf16[1,512,768]{2,1,0:T(8,128)(2,1)}, u32[]{:S(2)}, u32[]{:S(2)}) collective-permute-start(bf16[1,512,768]{2,1,0:T(8,128)(2,1)} %bitcast.205), channel_id=1, source_target_pairs={{0,2},{2,0},{1,3},{3,1},{4,6},{6,4},{5,7},{7,5},{8,10},{10,8},{9,1... | collective-permute-start | bytes 2359304 | tf_op jit(solution)/shard_map/ppermute | solution.py:355
  349.9 32.6 %collective-permute-start.3 = (bf16[1,512,768]{2,1,0:T(8,128)(2,1)}, bf16[1,512,768]{2,1,0:T(8,128)(2,1)S(1)}, u32[]{:S(2)}, u32[]{:S(2)}) collective-permute-start(bf16[1,512,768]{2,1,0:T(8,128)(2,1)} %bitcast.196), channel_id=1, source_target_pairs={{0,1},{1,0},{2,3},{3,2},{4,5},{5,4},{6,7},{7,6},{8,9},{9,8},{10,11... | collective-permute-start | bytes 2359304 | tf_op jit(solution)/shard_map/ppermute | solution.py:356
  361.4 19.5 %copy-start.49 = (bf16[512,768]{1,0:T(8,128)(2,1)S(1)}, bf16[512,768]{1,0:T(8,128)(2,1)}, u32[]{:S(2)}) copy-start(bf16[512,768]{1,0:T(8,128)(2,1)} %copy.223) | copy-start | bytes 2359300
  361.4 24.9 %slice-start.4 = ((s8[4718592]{0:T(1024)(128)(4,1)}), s8[4194304]{0:T(1024)(128)(4,1)S(1)}, s32[]{:S(2)}) async-start(s8[4718592]{0:T(1024)(128)(4,1)} %bitcast.177), calls=%async_computation.12 | async-start | bytes 8388608
  363.0 23.3 %slice-start.5 = ((s8[4718592]{0:T(1024)(128)(4,1)}), s8[524288]{0:T(1024)(128)(4,1)S(1)}, s32[]{:S(2)}) async-start(s8[4718592]{0:T(1024)(128)(4,1)} %bitcast.177), calls=%async_computation.13 | async-start | bytes 1048576
  393.8 207.2 %reduce-scatter.7.cloned.1.call-start = ((), (), s32[]{:S(2)}) async-start(), calls=%async_computation.7 | async-start | bytes 4313088
  400.9 51.5 %copy-start.5 = (bf16[1,512,768]{2,1,0:T(8,128)(2,1)S(1)}, bf16[1,512,768]{2,1,0:T(8,128)(2,1)}, u32[]{:S(2)}) copy-start(bf16[1,512,768]{2,1,0:T(8,128)(2,1)} %copy-done.4) | copy-start | bytes 2359300
  400.9 51.5 %copy-start.7 = (bf16[1,512,768]{2,1,0:T(8,128)(2,1)S(1)}, bf16[1,512,768]{2,1,0:T(8,128)(2,1)}, u32[]{:S(2)}) copy-start(bf16[1,512,768]{2,1,0:T(8,128)(2,1)} %copy-done.6) | copy-start | bytes 2359300
  400.9 51.5 %copy-start.17 = (s32[1,512,8]{2,1,0:T(8,128)S(1)}, s32[1,512,8]{2,1,0:T(8,128)}, u32[]{:S(2)}) copy-start(s32[1,512,8]{2,1,0:T(8,128)} %copy-done.16) | copy-start | bytes 49156
  400.9 51.5 %copy-start.28 = (s32[1,8,512]{2,1,0:T(8,128)S(1)}, s32[1,8,512]{2,1,0:T(8,128)}, u32[]{:S(2)}) copy-start(s32[1,8,512]{2,1,0:T(8,128)} %copy-done.27) | copy-start | bytes 49156
  504.1 17.9 %slice-start.10 = ((s8[4718592]{0:T(1024)(128)(4,1)}), s8[4194304]{0:T(1024)(128)(4,1)S(1)}, s32[]{:S(2)}) async-start(s8[4718592]{0:T(1024)(128)(4,1)} %bitcast.188), calls=%async_computation.18 | async-start | bytes 8388608
  505.3 14.9 %copy-start.50 = (bf16[96,2,3456]{2,0,1:T(8,128)(2,1)S(1)}, bf16[96,2,3456]{2,0,1:T(8,128)(2,1)}, u32[]{:S(2)}) copy-start(bf16[96,2,3456]{2,0,1:T(8,128)(2,1)} %reduce-scatter.5.cloned.1.call-done) | copy-start | bytes 3981316
  505.4 16.6 %slice-start.11 = ((s8[4718592]{0:T(1024)(128)(4,1)}), s8[524288]{0:T(1024)(128)(4,1)S(1)}, s32[]{:S(2)}) async-start(s8[4718592]{0:T(1024)(128)(4,1)} %bitcast.188), calls=%async_computation.19 | async-start | bytes 1048576
  505.4 16.6 %copy-start.47 = (bf16[3,768,768]{2,1,0:T(8,128)(2,1)S(1)}, bf16[3,768,768]{2,1,0:T(8,128)(2,1)}, u32[]{:S(2)}) copy-start(bf16[3,768,768]{2,1,0:T(8,128)(2,1)} %reshape.1750) | copy-start | bytes 10616836
  505.4 14.8 %collective-permute-start.5 = (bf16[96,1,3456]{2,0,1:T(8,128)(2,1)S(1)}, bf16[96,1,3456]{2,0,1:T(8,128)(2,1)S(1)}, u32[]{:S(2)}, u32[]{:S(2)}) collective-permute-start(bf16[96,1,3456]{2,0,1:T(8,128)(2,1)S(1)} %constant_dynamic-slice_fusion.4), channel_id=1, source_target_pairs={{0,1},{1,0},{2,3},{3,2},{4,5},{5,4},{6,7},{7,6},{8,9},{9,8},{10,11... | collective-permute-start | bytes 1990664 | tf_op jit(solution)/shard_map/ppermute | solution.py:445
  520.4 14.0 %collective-permute-start.6 = (bf16[96,1,3456]{2,0,1:T(8,128)(2,1)S(1)}, bf16[96,1,3456]{2,0,1:T(8,128)(2,1)S(1)}, u32[]{:S(2)}, u32[]{:S(2)}) collective-permute-start(bf16[96,1,3456]{2,0,1:T(8,128)(2,1)S(1)} %add_convert_fusion.3), channel_id=1, source_target_pairs={{0,2},{2,0},{1,3},{3,1},{4,6},{6,4},{5,7},{7,5},{8,10},{10,8},{9,1... | collective-permute-start | bytes 1990664 | tf_op jit(solution)/shard_map/ppermute | solution.py:452
  557.2 48.9 %collective-permute-start.9 = (bf16[1,512,768]{2,1,0:T(8,128)(2,1)}, bf16[1,512,768]{2,1,0:T(8,128)(2,1)}, u32[]{:S(2)}, u32[]{:S(2)}) collective-permute-start(bf16[1,512,768]{2,1,0:T(8,128)(2,1)} %bitcast.206), channel_id=1, source_target_pairs={{0,3},{3,0},{1,2},{2,1},{4,7},{7,4},{5,6},{6,5},{8,11},{11,8},{9,1... | collective-permute-start | bytes 2359304 | tf_op jit(solution)/shard_map/ppermute | solution.py:357
  559.6 44.8 %collective-permute-start.7 = (bf16[1,512,768]{2,1,0:T(8,128)(2,1)}, bf16[1,512,768]{2,1,0:T(8,128)(2,1)}, u32[]{:S(2)}, u32[]{:S(2)}) collective-permute-start(bf16[1,512,768]{2,1,0:T(8,128)(2,1)} %bitcast.207), channel_id=1, source_target_pairs={{0,2},{2,0},{1,3},{3,1},{4,6},{6,4},{5,7},{7,5},{8,10},{10,8},{9,1... | collective-permute-start | bytes 2359304 | tf_op jit(solution)/shard_map/ppermute | solution.py:355
  560.4 45.7 %collective-permute-start.8 = (bf16[1,512,768]{2,1,0:T(8,128)(2,1)S(1)}, bf16[1,512,768]{2,1,0:T(8,128)(2,1)S(1)}, u32[]{:S(2)}, u32[]{:S(2)}) collective-permute-start(bf16[1,512,768]{2,1,0:T(8,128)(2,1)S(1)} %bitcast.198), channel_id=1, source_target_pairs={{0,1},{1,0},{2,3},{3,2},{4,5},{5,4},{6,7},{7,6},{8,9},{9,8},{10,11... | collective-permute-start | bytes 2359304 | tf_op jit(solution)/shard_map/ppermute | solution.py:356
  602.8 6.2 collective-permute-start.10
  609.1 6.2 collective-permute-start.11
  (48 other events, 243.0 us)
Sparse Core Ops, SparseCore 0:
  16.5 50.1 all-gather.7
  89.8 35.6 all-gather.9
  127.8 52.5 all-gather.11
  182.6 51.6 all-gather.13
  393.9 110.1 reduce-scatter.4
  551.0 49.9 reduce-scatter.6

commit v10 on v8

--- a/solution.py
+++ b/solution.py
@@ -665,6 +665,8 @@
     )
     qkv_grad, stacked = lax.optimization_barrier((qkv_grad, stacked))
     attn_in_grad = jnp.einsum("jre,jde->rd", stacked, w_qkv, preferred_element_type=jnp.float32)
+    early_total = finish_stage(early_share, 1).reshape(early_share.shape[0], -1)
+    early_total, attn_in_grad = lax.optimization_barrier((early_total, attn_in_grad))
     input_part, first_gain_grad = norm_back(first_normed, first_inv, norm_gains[0], attn_in_grad)
     input_low = (middle_grad + input_part).astype(jnp.bfloat16)
     heads = model_width // HD
@@ -712,7 +714,6 @@
             count *= size
         small_pieces.append(small_total[offset : offset + count].reshape(local_shape))
         offset += count
-    early_total = finish_stage(early_share, 1).reshape(early_share.shape[0], -1)
     down_width = early_widths[0] // nt
     up_width = early_widths[1] // nt
     grad_shares = (

time: 614 us -> 626 us (1.020)
  local copies, waits for them, and re-layouts: 128 us -> 140 us
    ppermute x2, waiting for transfers between devices: 31.4 us -> 8.06 us  [pair_reduce(): received = lax.ppermute(sent, axis_name, perm=[(0, 1), (1, 0)])]
    ppermute x2, waiting for transfers between devices: 22.1 us -> 35.5 us  [spread_sequence(): from_context = lax.ppermute(other, 'context', perm=swap)]
    ppermute x2, waiting for transfers between devices: 2.93 us -> 10.7 us  [pair_sum(): received = lax.ppermute(share, axis_name, perm=[(0, 1), (1, 0)])]
    unnamed x142 -> x148, local copies, waits for them, and re-layouts: 38 us -> 39.7 us
  transfers between devices with their start and end apart: 18 -> 18, of which waited for: 10 -> 10; matrix products, arithmetic and copies ran while one was open for 25% -> 27% of each run, Pallas kernels for 24% -> 23%
where the time goes in v10:
time: 626 us; the launch traced here: 620 us
  Pallas kernels  144 us (23%)
  local copies, waits for them, and re-layouts  140 us (22%)
  waiting for transfers between devices  128 us (20%)
  matrix products  93.9 us (15%)
  other arithmetic  81.9 us (13%)
  between operations  17.1 us (3%)
  starting transfers between devices  14.9 us (2%)
    pallas_call x2, Pallas kernels, attention_backward(): pl.pallas_call(attention_bwd_kernel, grid=grid, in_specs=[query_spec, key...  80.3 us
    pallas_call x2, Pallas kernels, attention_forward(): pl.pallas_call(attention_fwd_kernel, grid=grid, in_specs=[query_spec, key...  63.3 us
    all_gather x1, waiting for transfers between devices, gather_packed(): lax.all_gather(flat, ('shard', 'tensor'), axis=0, tiled=False)  50.3 us
    unnamed x148, local copies, waits for them, and re-layouts  39.7 us
    ppermute x2, waiting for transfers between devices, spread_sequence(): from_context = lax.ppermute(other, 'context', perm=swap)  35.5 us
    dot_general x3, matrix products, back_dot(): lax.dot_general(left_rows, weight_rows, (((1,), (1,)), ((), ())), preferr...  32.7 us
    reshape x5, local copies, waits for them, and re-layouts, gather_weight(): stacked.reshape((ns, nt) + local_block.shape)  29.6 us
    reduce_sum x1, other arithmetic, backward_pass(): unit_bias_grad = jnp.sum(hidden_low, 0, dtype=jnp.float32)  17.2 us
  transfers between devices with their start and end apart: 18, of which 10 were waited for; matrix products, arithmetic and copies ran while one was open for 27% of the time, Pallas kernels for 23%

profile of v10, /device:TPU:0, one launch (start us, length us, event | category | flops | bytes accessed | tf_op | source)
XLA Modules:
  0.0 619.6 jit_solution(11088498323178755054)
XLA Ops:
  16.4 50.3 %all-gather.8.cloned.1.call-done = bf16[16,880,128]{2,1,0:T(8,128)(2,1)} async-done(((bf16[1,880,128]{2,1,0:T(8,128)(2,1)}), bf16[16,880,128]{2,1,0:T(8,128)(2,1)}) %all-gather.8.cloned.1.call-update) | async-done | bytes 3604496 | tf_op jit(solution)/shard_map/all_gather | solution.py:416
  66.7 6.6 %reshape.1748 = bf16[8,2,112640]{2,1,0:T(2,128)(2,1)} reshape(bf16[16,880,128]{2,1,0:T(8,128)(2,1)} %all-gather.8.cloned.1.call-done) | data formatting | bytes 7208960 | tf_op jit(solution)/shard_map/reshape | solution.py:416
  75.4 4.8 reshape.1791
  80.1 5.5 copy.200
  85.6 4.0 reshape.1750
  90.6 2.9 constant_dynamic-slice_fusion.6
  96.2 2.3 copy.266
  106.7 8.7 %collective-permute-done = bf16[1,512,768]{1,2,0:T(8,128)(2,1)S(1)} collective-permute-done((bf16[1,512,768]{1,2,0:T(8,128)(2,1)}, bf16[1,512,768]{1,2,0:T(8,128)(2,1)S(1)}, u32[]{:S(2)}, u32[]{:S(2)}) %collective-permute-start) | collective-permute-done | bytes 786464 | tf_op jit(solution)/shard_map/ppermute | solution.py:761
  116.9 9.5 %fusion.85 = (bf16[3,1024,768]{2,1,0:T(8,128)(2,1)S(1)}, f32[3,1024,768]{2,1,0:T(8,128)}) fusion(bf16[3,768,768]{2,1,0:T(8,128)(2,1)} %reshape.1750, f32[768]{0:T(1024)S(1)} %mul.279, f32[1024]{0:T(1024)S(1)} %add_rsqrt_fusion.3, f32[1024]{0:T(1024)S(1)} %broadcast_multiply_fusion.11, bf16[512,768]{0,1:T(8,128)(2,1)S(1)} %bitcast.153, ...), kind=kOutput, calls=%fused_computation.285 | convolution fusion | flops 3637248000 | bytes 19278848 | tf_op jit(solution)/shard_map/rd,jde->jre/dot_general | solution.py:530
  142.4 3.4 fusion.21
  146.0 28.5 %shard_map.256 = f32[1,512,768]{2,1,0:T(8,128)S(1)} custom-call(bf16[1,512,768]{2,1,0:T(8,128)(2,1)S(1)} %get-tuple-element.162.q_ref, bf16[1,512,768]{2,1,0:T(8,128)(2,1)S(1)} %slice.282.k_ref, bf16[1,512,768]{2,1,0:T(8,128)(2,1)S(1)} %slice.285.v_ref, s32[12,512,8]{2,1,0:T(8,128)} %copy.261.patq_ref, s32[12,8,512]{2,1,0:T(8,128)S(1)} %slice.299.patk_ref, ...), custom_call_target="tpu_custom_call" | custom-call | flops 1610612736 | bytes 5505024 | tf_op jit(solution)/shard_map/pallas_call | solution.py:217
  174.6 34.8 %shard_map.257 = f32[1,512,768]{2,1,0:T(8,128)S(1)} custom-call(bf16[1,512,768]{2,1,0:T(8,128)(2,1)S(1)} %get-tuple-element.163.q_ref, bf16[1,1024,768]{2,1,0:T(8,128)(2,1)S(1)} %copy-done.12, bf16[1,1024,768]{2,1,0:T(8,128)(2,1)S(1)} %get-tuple-element.145.v_ref, s32[12,512,8]{2,1,0:T(8,128)} %copy.262.patq_ref, s32[12,8,1024]{2,1,0:T(8,128)S(1)} %copy-done.17, ...), custom_call_target="tpu_custom_call" | custom-call | flops 3221225472 | bytes 8650752 | tf_op jit(solution)/shard_map/pallas_call | solution.py:217
  210.1 3.1 reshape.1753
  219.6 9.4 %copy.212 = bf16[8,2,96,1536]{3,1,2,0:T(2,128)(2,1)} copy(bf16[8,2,96,1536]{3,2,1,0:T(8,128)(2,1)} %bitcast.175) | data formatting | bytes 9437184 | tf_op jit(solution)/shard_map/reshape | solution.py:407
  229.0 3.7 copy.274
  232.8 12.2 %fusion.73 = (f32[1024]{0:T(1024)S(1)}, f32[1024,3072]{1,0:T(8,128)}) fusion(f32[3072]{0:T(1024)S(1)} %reshape.1776, bf16[768,3072]{1,0:T(8,128)(2,1)S(1)} %bitcast.176, f32[1024,768]{0,1:T(8,128)S(1)} %copy-done.33, f32[768]{0:T(1024)S(1)} %mul.294, f32[1024]{0:T(1024)S(1)} %add_rsqrt_fusion.1, f32[1024]{0:T(1024)S(1)} %broadcast_multiply_fusion.9), kind=kOutput, calls=%fused_computation.274 | convolution fusion | flops 4866440192 | bytes 20474880 | tf_op jit(solution)/shard_map/dot_general | solution.py:551
  245.0 8.1 %multiply_reduce_fusion.2 = f32[1024]{0:T(1024)S(1)} fusion(f32[1024]{0:T(1024)S(1)} %broadcast_multiply_fusion.2, f32[1024,3072]{1,0:T(8,128)} %get-tuple-element.187, f32[3072]{0:T(1024)S(1)} %reshape.1776), kind=kLoop, calls=%fused_computation.12 | loop fusion | flops 37747712 | bytes 12603392 | tf_op jit(solution)/shard_map/reduce_sum | solution.py:73
  253.1 7.3 %reshape.1758 = bf16[8,2,1536,96]{2,1,0,3:T(2,128)(2,1)} reshape(bf16[24576,96]{0,1:T(8,128)(2,1)} %all-gather.14.cloned.1.call-done) | data formatting | bytes 9437184 | tf_op jit(solution)/shard_map/reshape | solution.py:407
  260.3 7.7 %copy.217 = bf16[8,2,1536,96]{2,1,3,0:T(2,128)(2,1)} copy(bf16[8,2,1536,96]{2,1,0,3:T(2,128)(2,1)} %reshape.1758) | data formatting | bytes 9437184 | tf_op jit(solution)/shard_map/reshape | solution.py:407
  268.0 3.6 copy.275
  271.6 22.0 %multiply_reduce_fusion = (bf16[3072]{0:T(1024)(128)(2,1)}, f32[1024]{0:T(1024)S(1)}, f32[1024]{0:T(1024)S(1)}, bf16[1024,3072]{1,0:T(8,128)(2,1)}, f32[1024,3072]{1,0:T(8,128)}) fusion(f32[1024]{0:T(1024)S(1)} %add_rsqrt_fusion, f32[1024]{0:T(1024)S(1)} %broadcast_multiply_fusion.2, f32[1024,3072]{1,0:T(8,128)} %get-tuple-element.187, ...), kind=kOutput, calls=%fused_computation.9 | convolution fusion | flops 4898679808 | bytes 37795840 | tf_op jit(solution)/shard_map/dot_general | solution.py:65
  293.6 17.2 %fusion.74 = (bf16[3072]{0:T(1024)(128)(2,1)}, bf16[1024,3072]{1,0:T(8,128)(2,1)S(1)}) fusion(f32[1024]{0:T(1024)S(1)} %broadcast_multiply_fusion, f32[1024]{0:T(1024)S(1)} %broadcast_multiply_fusion.2, f32[1024,3072]{1,0:T(8,128)} %get-tuple-element.187, f32[3072]{0:T(1024)S(1)} %reshape.1776, f32[1024]{0:T(1024)S(1)} %broadcast_multiply_fusion.1, ...), kind=kLoop, calls=%fused_computation.275 | loop fusion | flops 94368768 | bytes 31504384 | tf_op jit(solution)/shard_map/reduce_sum | solution.py:613
  310.9 8.0 %multiply_reduce_fusion.5 = (bf16[768]{0:T(1024)(128)(2,1)S(1)}, f32[1024]{0:T(1024)S(1)}, f32[1024]{0:T(1024)S(1)}, f32[1024,768]{0,1:T(8,128)S(1)}) fusion(f32[1024,768]{0,1:T(8,128)S(1)} %copy-done.34, f32[1024]{0:T(1024)S(1)} %add_rsqrt_fusion.1, f32[1024]{0:T(1024)S(1)} %broadcast_multiply_fusion.9, f32[768]{0:T(1024)S(1)} %mul.294, ...), kind=kOutput, calls=%fused_computation.57 | convolution fusion | flops 4838126592 | bytes 17322496 | tf_op jit(solution)/shard_map/dot_general | solution.py:65
  318.9 5.4 convolution_convert_fusion
  324.3 3.4 convert_reduce_fusion.2
  329.8 2.7 multiply_reduce_fusion.4
  332.6 6.8 %convolution_convert_fusion.1 = bf16[768,3072]{1,0:T(8,128)(2,1)S(1)} fusion(bf16[1024,3072]{1,0:T(8,128)(2,1)S(1)} %bitcast.208, bf16[512,768]{0,1:T(8,128)(2,1)} %bitcast.27, bf16[512,768]{0,1:T(8,128)(2,1)S(1)} %bitcast.187, pred[]{:T(512)S(6)} %eq.183), kind=kOutput, calls=%fused_computation.18 | convolution fusion | flops 4841275392 | bytes 12582913 | tf_op jit(solution)/shard_map/dot_general | solution.py:59
  339.4 2.5 multiply_convert_fusion.1
  342.8 4.7 pad_maximum_fusion
  361.0 49.3 %shard_map.259 = (bf16[1,512,768]{2,1,0:T(8,128)(2,1)S(1)}, f32[1,1024,768]{2,1,0:T(8,128)}, f32[1,1024,768]{2,1,0:T(8,128)}) custom-call(bf16[1,512,768]{2,1,0:T(8,128)(2,1)S(1)} %copy-done.20, bf16[1,1024,768]{2,1,0:T(8,128)(2,1)S(1)} %copy-done.13, bf16[1,1024,768]{2,1,0:T(8,128)(2,1)S(1)} %copy-done.3, ...), custom_call_target="tpu_custom_call" | custom-call | flops 8053063680 | bytes 20447232 | tf_op jit(solution)/shard_map/pallas_call | solution.py:244
  415.8 31.0 %shard_map.258 = (bf16[1,512,768]{2,1,0:T(8,128)(2,1)S(1)}, f32[1,512,768]{2,1,0:T(8,128)S(1)}, f32[1,512,768]{2,1,0:T(8,128)}) custom-call(bf16[1,512,768]{2,1,0:T(8,128)(2,1)S(1)} %copy-done.9, bf16[1,512,768]{2,1,0:T(8,128)(2,1)S(1)} %copy-done.5, bf16[1,512,768]{2,1,0:T(8,128)(2,1)S(1)} %copy-done.7, bf16[1,512,768]{2,1,0:T(8,128)(2,1)S(1)} %copy-done.21, ...), custom_call_target="tpu_custom_call" | custom-call | flops 4026531840 | bytes 11010048 | tf_op jit(solution)/shard_map/pallas_call | solution.py:244
  448.0 4.1 fusion.76
  452.5 2.3 add_convert_fusion.1
  455.2 2.5 pad_maximum_fusion.1
  459.7 8.5 %fusion.37 = bf16[768,3,768]{2,0,1:T(8,128)(2,1)} fusion(bf16[3,1024,768]{2,1,0:T(8,128)(2,1)} %pad_maximum_fusion.1, f32[768]{0:T(1024)S(1)} %copy-done.56, f32[1024]{0:T(1024)S(1)} %copy-done.54, f32[1024]{0:T(1024)S(1)} %copy-done.52, bf16[512,768]{0,1:T(8,128)(2,1)S(1)} %bitcast.170, bf16[512,768]{0,1:T(8,128)(2,1)S(1)} %bitcast.156, pred[]{:T(512)S(6)} %eq.183), kind=kOutput, calls=%fused_computation.93 | convolution fusion | flops 3634888704 | bytes 9841665 | tf_op jit(solution)/shard_map/rd,jre->dje/dot_general | solution.py:662
  468.3 6.2 collective-permute-done.5
  476.2 5.5 convolution_bitcast_fusion.1
  481.7 7.5 %collective-permute-done.6 = bf16[96,1,3456]{2,0,1:T(8,128)(2,1)S(1)} collective-permute-done((bf16[96,1,3456]{2,0,1:T(8,128)(2,1)S(1)}, bf16[96,1,3456]{2,0,1:T(8,128)(2,1)S(1)}, u32[]{:S(2)}, u32[]{:S(2)}) %collective-permute-start.6) | collective-permute-done | bytes 663584 | tf_op jit(solution)/shard_map/ppermute | solution.py:452
  490.5 2.4 copy.228
  492.9 3.9 fusion.19
  506.5 10.0 %add_convert_fusion.2 = bf16[1024,768]{0,1:T(8,128)(2,1)S(1)} fusion(f32[1024,768]{0,1:T(8,128)} %copy-done.32, bf16[1024,3072]{1,0:T(8,128)(2,1)} %get-tuple-element.144, bf16[3072,768]{0,1:T(8,128)(2,1)} %bitcast.174, f32[768]{0:T(1024)S(1)} %add.734), kind=kOutput, calls=%fused_computation.64 | convolution fusion | flops 4834197504 | bytes 15731712 | tf_op jit(solution)/shard_map/dot_general | solution.py:556
  517.8 2.3 copy.220
  522.2 2.3 copy.219
  525.9 14.9 %collective-permute-done.1 = bf16[1,512,768]{2,1,0:T(8,128)(2,1)} collective-permute-done((bf16[1,512,768]{2,1,0:T(8,128)(2,1)}, bf16[1,512,768]{2,1,0:T(8,128)(2,1)}, u32[]{:S(2)}, u32[]{:S(2)}) %collective-permute-start.1) | collective-permute-done | bytes 786464 | tf_op jit(solution)/shard_map/ppermute | solution.py:355
  543.0 10.8 %collective-permute-done.3 = bf16[1,512,768]{2,1,0:T(8,128)(2,1)} collective-permute-done((bf16[1,512,768]{2,1,0:T(8,128)(2,1)}, bf16[1,512,768]{2,1,0:T(8,128)(2,1)}, u32[]{:S(2)}, u32[]{:S(2)}) %collective-permute-start.3) | collective-permute-done | bytes 786464 | tf_op jit(solution)/shard_map/ppermute | solution.py:357
  553.8 3.7 collective-permute-done.2
  575.4 20.5 %collective-permute-done.7 = bf16[1,512,768]{2,1,0:T(8,128)(2,1)} collective-permute-done((bf16[1,512,768]{2,1,0:T(8,128)(2,1)}, bf16[1,512,768]{2,1,0:T(8,128)(2,1)}, u32[]{:S(2)}, u32[]{:S(2)}) %collective-permute-start.7) | collective-permute-done | bytes 786464 | tf_op jit(solution)/shard_map/ppermute | solution.py:355
  604.5 3.2 collective-permute-done.11
  (353 shorter events, 122.6 us)
Async XLA Ops:
  7.2 91.9 %copy-start = (s32[4,2]{0,1:T(2,128)S(1)}, s32[4,2]{0,1:T(2,128)}, u32[]{:S(2)}) copy-start(s32[4,2]{0,1:T(2,128)} %param.21) | copy-start | bytes 100
  7.2 59.5 %all-gather.8.cloned.1.call-start = ((), (), s32[]{:S(2)}) async-start(), calls=%async_computation.2 | async-start | bytes 3829760 | tf_op jit(solution)/shard_map/all_gather | solution.py:416
  16.4 193.7 %all-gather.10.cloned.1.call-start = ((), (), s32[]{:S(2)}) async-start(), calls=%async_computation.4 | async-start | bytes 1253376 | tf_op jit(solution)/shard_map/all_gather | solution.py:406
  89.7 129.9 %all-gather.12.cloned.1.call-start = ((), (), s32[]{:S(2)}) async-start(), calls=%async_computation.5 | async-start | bytes 5013504 | tf_op jit(solution)/shard_map/all_gather | solution.py:406
  90.4 162.6 %all-gather.14.cloned.1.call-start = ((), (), s32[]{:S(2)}) async-start(), calls=%async_computation.6 | async-start | bytes 5013504 | tf_op jit(solution)/shard_map/all_gather | solution.py:406
  94.7 20.6 %collective-permute-start = (bf16[1,512,768]{1,2,0:T(8,128)(2,1)}, bf16[1,512,768]{1,2,0:T(8,128)(2,1)S(1)}, u32[]{:S(2)}, u32[]{:S(2)}) collective-permute-start(bf16[1,512,768]{1,2,0:T(8,128)(2,1)} %copy.259), channel_id=1, source_target_pairs={{0,2},{2,0},{1,3},{3,1},{4,6},{6,4},{5,7},{7,5},{8,10},{10,8},{9,1... | collective-permute-start | bytes 2359304 | tf_op jit(solution)/shard_map/ppermute | solution.py:761
  98.5 173.1 %collective-permute-start.4 = (bf16[1,512,768]{1,2,0:T(8,128)(2,1)}, bf16[1,512,768]{1,2,0:T(8,128)(2,1)}, u32[]{:S(2)}, u32[]{:S(2)}) collective-permute-start(bf16[1,512,768]{1,2,0:T(8,128)(2,1)} %copy.266), channel_id=1, source_target_pairs={{0,2},{2,0},{1,3},{3,1},{4,6},{6,4},{5,7},{7,5},{8,10},{10,8},{9,1... | collective-permute-start | bytes 2359304 | tf_op jit(solution)/shard_map/ppermute | solution.py:761
  103.8 22.6 %copy-start.26 = (bf16[1,512,768]{1,2,0:T(8,128)(2,1)}, bf16[1,512,768]{1,2,0:T(8,128)(2,1)S(1)}, u32[]{:S(2)}) copy-start(bf16[1,512,768]{1,2,0:T(8,128)(2,1)S(1)} %copy.194) | copy-start | bytes 2359300
  103.8 12.7 %copy-start.30 = (bf16[8,2,112640]{2,1,0:T(2,128)(2,1)S(1)}, bf16[8,2,112640]{2,1,0:T(2,128)(2,1)}, u32[]{:S(2)}) copy-start(bf16[8,2,112640]{2,1,0:T(2,128)(2,1)} %reshape.1748) | copy-start | bytes 10813444
  115.8 10.6 %copy-start.51 = (f32[1024]{0:T(1024)}, f32[1024]{0:T(1024)S(1)}, u32[]{:S(2)}) copy-start(f32[1024]{0:T(1024)S(1)} %broadcast_multiply_fusion.11) | copy-start | bytes 12292
  116.5 9.9 %copy-start.53 = (f32[1024]{0:T(1024)}, f32[1024]{0:T(1024)S(1)}, u32[]{:S(2)}) copy-start(f32[1024]{0:T(1024)S(1)} %add_rsqrt_fusion.3) | copy-start | bytes 12292
  116.9 9.5 %copy-start.55 = (f32[768]{0:T(1024)}, f32[768]{0:T(1024)S(1)}, u32[]{:S(2)}) copy-start(f32[768]{0:T(1024)S(1)} %mul.279) | copy-start | bytes 9220
  126.5 19.5 %copy-start.4 = (bf16[1,512,768]{2,1,0:T(8,128)(2,1)}, bf16[1,512,768]{2,1,0:T(8,128)(2,1)S(1)}, u32[]{:S(2)}) copy-start(bf16[1,512,768]{2,1,0:T(8,128)(2,1)S(1)} %slice.282.k_ref) | copy-start | bytes 2359300
  134.9 7.5 %copy-start.16 = (s32[12,8,1024]{2,1,0:T(8,128)}, s32[12,8,1024]{2,1,0:T(8,128)S(1)}, u32[]{:S(2)}) copy-start(s32[12,8,1024]{2,1,0:T(8,128)S(1)} %stack.57.patk_ref) | copy-start | bytes 1179652
  134.9 11.1 %copy-start.22 = (s32[12,8,512]{2,1,0:T(8,128)}, s32[12,8,512]{2,1,0:T(8,128)S(1)}, u32[]{:S(2)}) copy-start(s32[12,8,512]{2,1,0:T(8,128)S(1)} %slice.299.patk_ref) | copy-start | bytes 589828
  134.9 322.8 %reduce-scatter.5.cloned.1.call-start = ((), (), s32[]{:S(2)}) async-start(), calls=%async_computation.3 | async-start | bytes 11943936 | tf_op jit(solution)/shard_map/reduce_scatter | solution.py:515
  145.8 28.8 %copy-start.2 = (bf16[1,1024,768]{2,1,0:T(8,128)(2,1)}, bf16[1,1024,768]{2,1,0:T(8,128)(2,1)S(1)}, u32[]{:S(2)}) copy-start(bf16[1,1024,768]{2,1,0:T(8,128)(2,1)S(1)} %get-tuple-element.145.v_ref) | copy-start | bytes 4718596
  145.8 28.7 %copy-start.6 = (bf16[1,512,768]{2,1,0:T(8,128)(2,1)}, bf16[1,512,768]{2,1,0:T(8,128)(2,1)S(1)}, u32[]{:S(2)}) copy-start(bf16[1,512,768]{2,1,0:T(8,128)(2,1)S(1)} %slice.285.v_ref) | copy-start | bytes 2359300
  146.0 28.6 %copy-start.8 = (bf16[1,512,768]{2,1,0:T(8,128)(2,1)}, bf16[1,512,768]{2,1,0:T(8,128)(2,1)S(1)}, u32[]{:S(2)}) copy-start(bf16[1,512,768]{2,1,0:T(8,128)(2,1)S(1)} %get-tuple-element.162.q_ref) | copy-start | bytes 2359300
  146.0 28.6 %copy-start.19 = (bf16[1,512,768]{2,1,0:T(8,128)(2,1)}, bf16[1,512,768]{2,1,0:T(8,128)(2,1)S(1)}, u32[]{:S(2)}) copy-start(bf16[1,512,768]{2,1,0:T(8,128)(2,1)S(1)} %get-tuple-element.163.q_ref) | copy-start | bytes 2359300
  146.0 28.6 %copy-start.12 = (bf16[1,1024,768]{2,1,0:T(8,128)(2,1)S(1)}, bf16[1,1024,768]{2,1,0:T(8,128)(2,1)}, u32[]{:S(2)}) copy-start(bf16[1,1024,768]{2,1,0:T(8,128)(2,1)} %slice.301.k_ref) | copy-start | bytes 4718596
  146.0 28.6 %copy-start.17 = (s32[12,8,1024]{2,1,0:T(8,128)S(1)}, s32[12,8,1024]{2,1,0:T(8,128)}, u32[]{:S(2)}) copy-start(s32[12,8,1024]{2,1,0:T(8,128)} %copy-done.16) | copy-start | bytes 1179652
  146.0 28.6 %copy-start.24 = (s32[1,512,8]{2,1,0:T(8,128)S(1)}, s32[1,512,8]{2,1,0:T(8,128)}, u32[]{:S(2)}) copy-start(s32[1,512,8]{2,1,0:T(8,128)} %get-tuple-element.171.pcq_ref) | copy-start | bytes 49156
  232.7 12.2 %copy-start.45 = (bf16[96,8,2,1536]{3,1,2,0:T(8,128)(2,1)}, bf16[96,8,2,1536]{3,1,2,0:T(8,128)(2,1)S(1)}, u32[]{:S(2)}) copy-start(bf16[96,8,2,1536]{3,1,2,0:T(8,128)(2,1)S(1)} %copy.274) | copy-start | bytes 14155780
  271.6 22.0 %copy-start.44 = (bf16[96,8,2,1536]{3,1,2,0:T(8,128)(2,1)}, bf16[96,8,2,1536]{3,1,2,0:T(8,128)(2,1)S(1)}, u32[]{:S(2)}) copy-start(bf16[96,8,2,1536]{3,1,2,0:T(8,128)(2,1)S(1)} %copy.275) | copy-start | bytes 14155780
  293.6 17.2 %copy-start.34 = (f32[1024,768]{0,1:T(8,128)S(1)}, f32[1024,768]{0,1:T(8,128)}, u32[]{:S(2)}) copy-start(f32[1024,768]{0,1:T(8,128)} %copy-done.32) | copy-start | bytes 9437188
  327.7 4.9 slice-start.4
  347.4 8.1 %copy-start.41 = (bf16[1024,768]{1,0:T(8,128)(2,1)S(1)}, bf16[1024,768]{1,0:T(8,128)(2,1)}, u32[]{:S(2)}) copy-start(bf16[1024,768]{1,0:T(8,128)(2,1)} %multiply_convert_fusion.1) | copy-start | bytes 4718596
  347.5 9.0 %copy-start.3 = (bf16[1,1024,768]{2,1,0:T(8,128)(2,1)S(1)}, bf16[1,1024,768]{2,1,0:T(8,128)(2,1)}, u32[]{:S(2)}) copy-start(bf16[1,1024,768]{2,1,0:T(8,128)(2,1)} %copy-done.2) | copy-start | bytes 4718596
  347.5 224.4 %reduce-scatter.7.cloned.1.call-start = ((), (), s32[]{:S(2)}) async-start(), calls=%async_computation.7 | async-start | bytes 4313088
  361.0 51.5 %copy-start.5 = (bf16[1,512,768]{2,1,0:T(8,128)(2,1)S(1)}, bf16[1,512,768]{2,1,0:T(8,128)(2,1)}, u32[]{:S(2)}) copy-start(bf16[1,512,768]{2,1,0:T(8,128)(2,1)} %copy-done.4) | copy-start | bytes 2359300
  361.0 51.5 %copy-start.7 = (bf16[1,512,768]{2,1,0:T(8,128)(2,1)S(1)}, bf16[1,512,768]{2,1,0:T(8,128)(2,1)}, u32[]{:S(2)}) copy-start(bf16[1,512,768]{2,1,0:T(8,128)(2,1)} %copy-done.6) | copy-start | bytes 2359300
  457.7 18.5 %slice-start.2 = ((s8[4718592]{0:T(1024)(128)(4,1)}), s8[4194304]{0:T(1024)(128)(4,1)S(1)}, s32[]{:S(2)}) async-start(s8[4718592]{0:T(1024)(128)(4,1)} %bitcast.179), calls=%async_computation.10 | async-start | bytes 8388608
  459.0 15.5 %copy-start.48 = (bf16[96,2,3456]{2,0,1:T(8,128)(2,1)S(1)}, bf16[96,2,3456]{2,0,1:T(8,128)(2,1)}, u32[]{:S(2)}) copy-start(bf16[96,2,3456]{2,0,1:T(8,128)(2,1)} %reduce-scatter.5.cloned.1.call-done) | copy-start | bytes 3981316
  459.0 17.2 %slice-start.3 = ((s8[4718592]{0:T(1024)(128)(4,1)}), s8[524288]{0:T(1024)(128)(4,1)S(1)}, s32[]{:S(2)}) async-start(s8[4718592]{0:T(1024)(128)(4,1)} %bitcast.179), calls=%async_computation.11 | async-start | bytes 1048576
  459.0 17.2 %copy-start.46 = (bf16[3,768,768]{2,1,0:T(8,128)(2,1)S(1)}, bf16[3,768,768]{2,1,0:T(8,128)(2,1)}, u32[]{:S(2)}) copy-start(bf16[3,768,768]{2,1,0:T(8,128)(2,1)} %reshape.1750) | copy-start | bytes 10616836
  459.0 15.4 %collective-permute-start.5 = (bf16[96,1,3456]{2,0,1:T(8,128)(2,1)S(1)}, bf16[96,1,3456]{2,0,1:T(8,128)(2,1)S(1)}, u32[]{:S(2)}, u32[]{:S(2)}) collective-permute-start(bf16[96,1,3456]{2,0,1:T(8,128)(2,1)S(1)} %constant_dynamic-slice_fusion.4), channel_id=1, source_target_pairs={{0,1},{1,0},{2,3},{3,2},{4,5},{5,4},{6,7},{7,6},{8,9},{9,8},{10,11... | collective-permute-start | bytes 1990664 | tf_op jit(solution)/shard_map/ppermute | solution.py:445
  474.6 14.6 %collective-permute-start.6 = (bf16[96,1,3456]{2,0,1:T(8,128)(2,1)S(1)}, bf16[96,1,3456]{2,0,1:T(8,128)(2,1)S(1)}, u32[]{:S(2)}, u32[]{:S(2)}) collective-permute-start(bf16[96,1,3456]{2,0,1:T(8,128)(2,1)S(1)} %add_convert_fusion.3), channel_id=1, source_target_pairs={{0,2},{2,0},{1,3},{3,1},{4,6},{6,4},{5,7},{7,5},{8,10},{10,8},{9,1... | collective-permute-start | bytes 1990664 | tf_op jit(solution)/shard_map/ppermute | solution.py:452
  520.1 20.7 %collective-permute-start.1 = (bf16[1,512,768]{2,1,0:T(8,128)(2,1)}, bf16[1,512,768]{2,1,0:T(8,128)(2,1)}, u32[]{:S(2)}, u32[]{:S(2)}) collective-permute-start(bf16[1,512,768]{2,1,0:T(8,128)(2,1)} %bitcast.198), channel_id=1, source_target_pairs={{0,2},{2,0},{1,3},{3,1},{4,6},{6,4},{5,7},{7,5},{8,10},{10,8},{9,1... | collective-permute-start | bytes 2359304 | tf_op jit(solution)/shard_map/ppermute | solution.py:355
  521.6 32.2 %collective-permute-start.3 = (bf16[1,512,768]{2,1,0:T(8,128)(2,1)}, bf16[1,512,768]{2,1,0:T(8,128)(2,1)}, u32[]{:S(2)}, u32[]{:S(2)}) collective-permute-start(bf16[1,512,768]{2,1,0:T(8,128)(2,1)} %bitcast.199), channel_id=1, source_target_pairs={{0,3},{3,0},{1,2},{2,1},{4,7},{7,4},{5,6},{6,5},{8,11},{11,8},{9,1... | collective-permute-start | bytes 2359304 | tf_op jit(solution)/shard_map/ppermute | solution.py:357
  524.5 32.9 %collective-permute-start.2 = (bf16[1,512,768]{2,1,0:T(8,128)(2,1)}, bf16[1,512,768]{2,1,0:T(8,128)(2,1)}, u32[]{:S(2)}, u32[]{:S(2)}) collective-permute-start(bf16[1,512,768]{2,1,0:T(8,128)(2,1)} %bitcast.190), channel_id=1, source_target_pairs={{0,1},{1,0},{2,3},{3,2},{4,5},{5,4},{6,7},{7,6},{8,9},{9,8},{10,11... | collective-permute-start | bytes 2359304 | tf_op jit(solution)/shard_map/ppermute | solution.py:356
  564.8 5.2 copy-start.43
  566.2 31.3 %collective-permute-start.9 = (bf16[1,512,768]{2,1,0:T(8,128)(2,1)}, bf16[1,512,768]{2,1,0:T(8,128)(2,1)}, u32[]{:S(2)}, u32[]{:S(2)}) collective-permute-start(bf16[1,512,768]{2,1,0:T(8,128)(2,1)} %bitcast.196), channel_id=1, source_target_pairs={{0,3},{3,0},{1,2},{2,1},{4,7},{7,4},{5,6},{6,5},{8,11},{11,8},{9,1... | collective-permute-start | bytes 2359304 | tf_op jit(solution)/shard_map/ppermute | solution.py:357
  568.5 27.4 %collective-permute-start.7 = (bf16[1,512,768]{2,1,0:T(8,128)(2,1)}, bf16[1,512,768]{2,1,0:T(8,128)(2,1)}, u32[]{:S(2)}, u32[]{:S(2)}) collective-permute-start(bf16[1,512,768]{2,1,0:T(8,128)(2,1)} %bitcast.197), channel_id=1, source_target_pairs={{0,2},{2,0},{1,3},{3,1},{4,6},{6,4},{5,7},{7,5},{8,10},{10,8},{9,1... | collective-permute-start | bytes 2359304 | tf_op jit(solution)/shard_map/ppermute | solution.py:355
  569.3 28.3 %collective-permute-start.8 = (bf16[1,512,768]{2,1,0:T(8,128)(2,1)S(1)}, bf16[1,512,768]{2,1,0:T(8,128)(2,1)S(1)}, u32[]{:S(2)}, u32[]{:S(2)}) collective-permute-start(bf16[1,512,768]{2,1,0:T(8,128)(2,1)S(1)} %bitcast.188), channel_id=1, source_target_pairs={{0,1},{1,0},{2,3},{3,2},{4,5},{5,4},{6,7},{7,6},{8,9},{9,8},{10,11... | collective-permute-start | bytes 2359304 | tf_op jit(solution)/shard_map/ppermute | solution.py:356
  574.0 27.1 %collective-permute-start.10 = (bf16[104,3,384]{2,0,1:T(8,128)(2,1)S(1)}, bf16[104,3,384]{2,0,1:T(8,128)(2,1)S(1)}, u32[]{:S(2)}, u32[]{:S(2)}) collective-permute-start(bf16[104,3,384]{2,0,1:T(8,128)(2,1)S(1)} %copy.268), channel_id=1, source_target_pairs={{0,1},{1,0},{2,3},{3,2},{4,5},{5,4},{6,7},{7,6},{8,9},{9,8},{10,11... | collective-permute-start | bytes 718856 | tf_op jit(solution)/shard_map/ppermute | solution.py:445
  601.1 6.6 %collective-permute-start.11 = (bf16[104,3,384]{2,0,1:T(8,128)(2,1)S(1)}, bf16[104,3,384]{2,0,1:T(8,128)(2,1)S(1)}, u32[]{:S(2)}, u32[]{:S(2)}) collective-permute-start(bf16[104,3,384]{2,0,1:T(8,128)(2,1)S(1)} %add_convert_fusion.4), channel_id=1, source_target_pairs={{0,2},{2,0},{1,3},{3,1},{4,6},{6,4},{5,7},{7,5},{8,10},{10,8},{9,1... | collective-permute-start | bytes 718856 | tf_op jit(solution)/shard_map/ppermute | solution.py:452
  602.6 9.9 %copy-start.1 = (s32[4,2]{0,1:T(2,128)S(1)}, s32[4,2]{0,1:T(2,128)}, u32[]{:S(2)}) copy-start(s32[4,2]{0,1:T(2,128)} %param.21) | copy-start | bytes 100
  (38 other events, 97.5 us)
Sparse Core Ops, SparseCore 0:
  16.5 50.1 all-gather.7
  89.8 35.6 all-gather.9
  127.8 52.5 all-gather.11
  182.6 51.6 all-gather.13
  347.6 109.2 reduce-scatter.4
  505.9 46.2 reduce-scatter.6

commit v11 on v9

--- a/solution.py
+++ b/solution.py
@@ -620,13 +620,12 @@
     sub_grad = back_dot(middle_low, w_out)
     attended_grad, head_gain_grad = norm_back(sub_normed, sub_inv, head_gain, sub_grad)
     attended_low = attended_grad.astype(jnp.bfloat16)
-    down_grad, up_grad, out_weight_grad, attended_low, carried = lax.optimization_barrier(
+    down_grad, up_grad, out_weight_grad, attended_low = lax.optimization_barrier(
         (
             down_grad.astype(jnp.bfloat16),
             up_grad.astype(jnp.bfloat16),
             out_weight_grad.astype(jnp.bfloat16),
             attended_low,
-            carried,
         )
     )
     tensor_count = lax.axis_size("tensor")
@@ -659,15 +658,13 @@
     key_low = key_part.astype(jnp.bfloat16).reshape(row_count, model_width)
     value_low = value_part.astype(jnp.bfloat16).reshape(row_count, model_width)
     stacked = jnp.stack([query_low, key_low, value_low])
-    early_share, stacked = lax.optimization_barrier((early_share, stacked))
+    early_share, stacked, carried = lax.optimization_barrier((early_share, stacked, carried))
     qkv_grad = jnp.einsum("rd,jre->dje", attn_in, stacked, preferred_element_type=jnp.float32)
     head_bias_grad = jnp.stack(
         [jnp.sum(query_low, 0, dtype=jnp.float32), jnp.sum(value_low, 0, dtype=jnp.float32)]
     )
     qkv_grad, stacked = lax.optimization_barrier((qkv_grad, stacked))
     attn_in_grad = jnp.einsum("jre,jde->rd", stacked, w_qkv, preferred_element_type=jnp.float32)
-    early_total = finish_stage(early_share, 1).reshape(early_share.shape[0], -1)
-    early_total, attn_in_grad = lax.optimization_barrier((early_total, attn_in_grad))
     input_part, first_gain_grad = norm_back(first_normed, first_inv, norm_gains[0], attn_in_grad)
     input_low = (middle_grad + input_part).astype(jnp.bfloat16)
     heads = model_width // HD
@@ -715,6 +712,7 @@
             count *= size
         small_pieces.append(small_total[offset : offset + count].reshape(local_shape))
         offset += count
+    early_total = finish_stage(early_share, 1).reshape(early_share.shape[0], -1)
     down_width = early_widths[0] // nt
     up_width = early_widths[1] // nt
     grad_shares = (

time: 633 us -> 592 us (0.935)
  waiting for transfers between devices: 138 us -> 108 us
  local copies, waits for them, and re-layouts: 138 us -> 129 us
  other arithmetic: 85.3 us -> 78.4 us
    unnamed x7, waiting for transfers between devices: 38.9 us -> 0.76 us
    ppermute x2, waiting for transfers between devices: 6.12 us -> 29.3 us  [pair_reduce(): received = lax.ppermute(sent, axis_name, perm=[(0, 1), (1, 0)])]
    ppermute x2, waiting for transfers between devices: 17.8 us -> 6.27 us  [spread_sequence(): from_context = lax.ppermute(other, 'context', perm=swap)]
    ppermute x2, waiting for transfers between devices: 0.01 us -> 10.3 us  [spread_sequence(): from_tensor = lax.ppermute(kept, 'tensor', perm=swap)]
    ppermute x2, waiting for transfers between devices: 9.67 us -> 2.76 us  [pair_sum(): received = lax.ppermute(share, axis_name, perm=[(0, 1), (1, 0)])]
    reduce_scatter x1, waiting for transfers between devices: 6.52 us -> 0.01 us  [shard_stage(): lax.psum_scatter(grad.astype(jnp.bfloat16), 'shard', scatter_dimension=di...]
    unnamed x168 -> x150, local copies, waits for them, and re-layouts: 42 us -> 40.5 us
  transfers between devices with their start and end apart: 18 -> 18, of which waited for: 9 -> 8; matrix products, arithmetic and copies ran while one was open for 26% -> 26% of each run, Pallas kernels for 23% -> 24%
where the time goes in v11:
time: 592 us; the launch traced here: 587 us
  Pallas kernels  144 us (24%)
  local copies, waits for them, and re-layouts  129 us (22%)
  waiting for transfers between devices  108 us (18%)
  matrix products  94.8 us (16%)
  other arithmetic  78.4 us (13%)
  between operations  17.1 us (3%)
  starting transfers between devices  15.5 us (3%)
    pallas_call x2, Pallas kernels, attention_backward(): pl.pallas_call(attention_bwd_kernel, grid=grid, in_specs=[query_spec, key...  80.3 us
    pallas_call x2, Pallas kernels, attention_forward(): pl.pallas_call(attention_fwd_kernel, grid=grid, in_specs=[query_spec, key...  63.3 us
    all_gather x1, waiting for transfers between devices, gather_packed(): lax.all_gather(flat, ('shard', 'tensor'), axis=0, tiled=False)  50.3 us
    unnamed x150, local copies, waits for them, and re-layouts  40.5 us
    dot_general x3, matrix products, back_dot(): lax.dot_general(left_rows, weight_rows, (((1,), (1,)), ((), ())), preferr...  31.6 us
    reshape x5, local copies, waits for them, and re-layouts, gather_weight(): stacked.reshape((ns, nt) + local_block.shape)  29.6 us
    ppermute x2, waiting for transfers between devices, pair_reduce(): received = lax.ppermute(sent, axis_name, perm=[(0, 1), (1, 0)])  29.3 us
    reduce_sum x1, other arithmetic, backward_pass(): unit_bias_grad = jnp.sum(hidden_low, 0, dtype=jnp.float32)  16.6 us
  transfers between devices with their start and end apart: 18, of which 8 were waited for; matrix products, arithmetic and copies ran while one was open for 26% of the time, Pallas kernels for 24%

profile of v11, /device:TPU:0, one launch (start us, length us, event | category | flops | bytes accessed | tf_op | source)
XLA Modules:
  0.0 586.5 jit_solution(6667034412515202825)
XLA Ops:
  16.4 50.3 %all-gather.8.cloned.1.call-done = bf16[16,880,128]{2,1,0:T(8,128)(2,1)} async-done(((bf16[1,880,128]{2,1,0:T(8,128)(2,1)}), bf16[16,880,128]{2,1,0:T(8,128)(2,1)}) %all-gather.8.cloned.1.call-update) | async-done | bytes 3604496 | tf_op jit(solution)/shard_map/all_gather | solution.py:416
  66.7 6.6 %reshape.1748 = bf16[8,2,112640]{2,1,0:T(2,128)(2,1)} reshape(bf16[16,880,128]{2,1,0:T(8,128)(2,1)} %all-gather.8.cloned.1.call-done) | data formatting | bytes 7208960 | tf_op jit(solution)/shard_map/reshape | solution.py:416
  75.4 4.8 reshape.1791
  80.1 5.5 copy.194
  85.6 4.0 reshape.1750
  90.7 2.9 constant_dynamic-slice_fusion.8
  96.2 2.3 copy.249
  107.0 8.4 %collective-permute-done.1 = bf16[1,512,768]{1,2,0:T(8,128)(2,1)S(1)} collective-permute-done((bf16[1,512,768]{1,2,0:T(8,128)(2,1)}, bf16[1,512,768]{1,2,0:T(8,128)(2,1)S(1)}, u32[]{:S(2)}, u32[]{:S(2)}) %collective-permute-start.1) | collective-permute-done | bytes 786464 | tf_op jit(solution)/shard_map/ppermute | solution.py:760
  116.9 9.5 %fusion.86 = (bf16[3,1024,768]{2,1,0:T(8,128)(2,1)S(1)}, f32[3,1024,768]{2,1,0:T(8,128)}) fusion(bf16[3,768,768]{2,1,0:T(8,128)(2,1)} %reshape.1750, f32[768]{0:T(1024)S(1)} %mul.279, f32[1024]{0:T(1024)S(1)} %add_rsqrt_fusion.3, f32[1024]{0:T(1024)S(1)} %broadcast_multiply_fusion.11, bf16[512,768]{0,1:T(8,128)(2,1)S(1)} %bitcast.167, ...), kind=kOutput, calls=%fused_computation.285 | convolution fusion | flops 3637248000 | bytes 19278848 | tf_op jit(solution)/shard_map/rd,jde->jre/dot_general | solution.py:530
  139.8 2.2 copy.252.patq_ref
  142.0 2.2 copy.253.patq_ref
  144.2 3.4 fusion.21
  147.9 28.5 %shard_map.256 = f32[1,512,768]{2,1,0:T(8,128)S(1)} custom-call(bf16[1,512,768]{2,1,0:T(8,128)(2,1)S(1)} %get-tuple-element.160.q_ref, bf16[1,512,768]{2,1,0:T(8,128)(2,1)S(1)} %slice.282.k_ref, bf16[1,512,768]{2,1,0:T(8,128)(2,1)S(1)} %slice.285.v_ref, s32[12,512,8]{2,1,0:T(8,128)} %copy.252.patq_ref, s32[12,8,512]{2,1,0:T(8,128)S(1)} %slice.299.patk_ref, ...), custom_call_target="tpu_custom_call" | custom-call | flops 1610612736 | bytes 5505024 | tf_op jit(solution)/shard_map/pallas_call | solution.py:217
  176.4 34.8 %shard_map.257 = f32[1,512,768]{2,1,0:T(8,128)S(1)} custom-call(bf16[1,512,768]{2,1,0:T(8,128)(2,1)S(1)} %get-tuple-element.161.q_ref, bf16[1,1024,768]{2,1,0:T(8,128)(2,1)S(1)} %copy-done.12, bf16[1,1024,768]{2,1,0:T(8,128)(2,1)S(1)} %get-tuple-element.143.v_ref, s32[12,512,8]{2,1,0:T(8,128)} %copy.253.patq_ref, s32[12,8,1024]{2,1,0:T(8,128)S(1)} %stack.57.patk_ref, ...), custom_call_target="tpu_custom_call" | custom-call | flops 3221225472 | bytes 8650752 | tf_op jit(solution)/shard_map/pallas_call | solution.py:217
  212.0 3.1 reshape.1753
  215.1 2.2 copy.205
  221.5 9.3 %copy.206 = bf16[8,2,96,1536]{3,1,2,0:T(2,128)(2,1)} copy(bf16[8,2,96,1536]{3,2,1,0:T(8,128)(2,1)} %bitcast.180) | data formatting | bytes 9437184 | tf_op jit(solution)/shard_map/reshape | solution.py:407
  230.8 3.8 copy.264
  234.7 12.2 %fusion.74 = (f32[1024]{0:T(1024)S(1)}, f32[1024,3072]{1,0:T(8,128)}) fusion(f32[3072]{0:T(1024)S(1)} %reshape.1776, bf16[768,3072]{1,0:T(8,128)(2,1)S(1)} %bitcast.183, f32[1024,768]{0,1:T(8,128)S(1)} %copy-done.37, f32[768]{0:T(1024)S(1)} %copy-done.62, f32[1024]{0:T(1024)S(1)} %add_rsqrt_fusion.1, f32[1024]{0:T(1024)S(1)} %broadcast_multiply_fusion.9), kind=kOutput, calls=%fused_computation.274 | convolution fusion | flops 4866440192 | bytes 20474880 | tf_op jit(solution)/shard_map/dot_general | solution.py:551
  246.9 8.1 %multiply_reduce_fusion.2 = f32[1024]{0:T(1024)S(1)} fusion(f32[1024]{0:T(1024)S(1)} %broadcast_multiply_fusion.2, f32[1024,3072]{1,0:T(8,128)} %get-tuple-element.185, f32[3072]{0:T(1024)S(1)} %reshape.1776), kind=kLoop, calls=%fused_computation.12 | loop fusion | flops 37747712 | bytes 12603392 | tf_op jit(solution)/shard_map/reduce_sum | solution.py:73
  255.0 7.3 %reshape.1758 = bf16[8,2,1536,96]{2,1,0,3:T(2,128)(2,1)} reshape(bf16[24576,96]{0,1:T(8,128)(2,1)} %all-gather.14.cloned.1.call-done) | data formatting | bytes 9437184 | tf_op jit(solution)/shard_map/reshape | solution.py:407
  262.3 7.7 %copy.211 = bf16[8,2,1536,96]{2,1,3,0:T(2,128)(2,1)} copy(bf16[8,2,1536,96]{2,1,0,3:T(2,128)(2,1)} %reshape.1758) | data formatting | bytes 9437184 | tf_op jit(solution)/shard_map/reshape | solution.py:407
  269.9 3.6 copy.265
  273.6 21.3 %multiply_reduce_fusion = (bf16[3072]{0:T(1024)(128)(2,1)S(1)}, f32[1024]{0:T(1024)S(1)}, f32[1024]{0:T(1024)S(1)}, bf16[1024,3072]{1,0:T(8,128)(2,1)}, f32[1024,3072]{1,0:T(8,128)}) fusion(f32[1024]{0:T(1024)S(1)} %add_rsqrt_fusion, f32[1024]{0:T(1024)S(1)} %broadcast_multiply_fusion.2, f32[1024,3072]{1,0:T(8,128)} %get-tuple-element.185, ...), kind=kOutput, calls=%fused_computation.9 | convolution fusion | flops 4898679808 | bytes 37795840 | tf_op jit(solution)/shard_map/dot_general | solution.py:65
  295.0 16.6 %fusion.75 = (bf16[3072]{0:T(1024)(128)(2,1)S(1)}, bf16[1024,3072]{1,0:T(8,128)(2,1)S(1)}) fusion(f32[1024]{0:T(1024)S(1)} %broadcast_multiply_fusion, f32[1024]{0:T(1024)S(1)} %broadcast_multiply_fusion.2, f32[1024,3072]{1,0:T(8,128)} %get-tuple-element.185, f32[3072]{0:T(1024)S(1)} %reshape.1776, f32[1024]{0:T(1024)S(1)} %broadcast_multiply_fusion.1, ...), kind=kLoop, calls=%fused_computation.275 | loop fusion | flops 94368768 | bytes 31504384 | tf_op jit(solution)/shard_map/reduce_sum | solution.py:613
  311.6 8.0 %multiply_reduce_fusion.5 = (bf16[768]{0:T(1024)(128)(2,1)S(1)}, f32[1024]{0:T(1024)S(1)}, f32[1024]{0:T(1024)S(1)}, f32[1024,768]{0,1:T(8,128)S(1)}) fusion(f32[1024,768]{0,1:T(8,128)S(1)} %copy-done.38, f32[1024]{0:T(1024)S(1)} %add_rsqrt_fusion.1, f32[1024]{0:T(1024)S(1)} %broadcast_multiply_fusion.9, f32[768]{0:T(1024)S(1)} %copy-done.62, ...), kind=kOutput, calls=%fused_computation.58 | convolution fusion | flops 4838126592 | bytes 17322496 | tf_op jit(solution)/shard_map/dot_general | solution.py:65
  319.6 5.4 convolution_convert_fusion
  325.0 3.4 convert_reduce_fusion.2
  330.6 2.3 multiply_reduce_fusion.4
  333.0 6.8 %convolution_convert_fusion.1 = bf16[768,3072]{1,0:T(8,128)(2,1)S(1)} fusion(bf16[1024,3072]{1,0:T(8,128)(2,1)S(1)} %bitcast.213, bf16[512,768]{0,1:T(8,128)(2,1)} %bitcast.1, bf16[512,768]{0,1:T(8,128)(2,1)S(1)} %bitcast.192, pred[]{:T(512)S(6)} %eq.182), kind=kOutput, calls=%fused_computation.18 | convolution fusion | flops 4841275392 | bytes 12582913 | tf_op jit(solution)/shard_map/dot_general | solution.py:59
  339.8 2.4 multiply_convert_fusion.1
  343.0 4.7 pad_maximum_fusion
  349.6 9.4 %add_convert_fusion = bf16[1024,768]{0,1:T(8,128)(2,1)S(1)} fusion(f32[1024,768]{0,1:T(8,128)S(1)} %copy-done.39, bf16[1024,3072]{1,0:T(8,128)(2,1)} %get-tuple-element.142, bf16[3072,768]{0,1:T(8,128)(2,1)} %bitcast.182, f32[768]{0:T(1024)S(1)} %add.737), kind=kOutput, calls=%fused_computation.59 | convolution fusion | flops 4834197504 | bytes 15731712 | tf_op jit(solution)/shard_map/dot_general | solution.py:556
  360.2 2.4 copy.219
  369.8 49.4 %shard_map.259 = (bf16[1,512,768]{2,1,0:T(8,128)(2,1)S(1)}, f32[1,1024,768]{2,1,0:T(8,128)}, f32[1,1024,768]{2,1,0:T(8,128)}) custom-call(bf16[1,512,768]{2,1,0:T(8,128)(2,1)S(1)} %copy-done.21, bf16[1,1024,768]{2,1,0:T(8,128)(2,1)S(1)} %copy-done.13, bf16[1,1024,768]{2,1,0:T(8,128)(2,1)S(1)} %copy-done.3, ...), custom_call_target="tpu_custom_call" | custom-call | flops 8053063680 | bytes 20447232 | tf_op jit(solution)/shard_map/pallas_call | solution.py:244
  424.6 31.0 %shard_map.258 = (bf16[1,512,768]{2,1,0:T(8,128)(2,1)S(1)}, f32[1,512,768]{2,1,0:T(8,128)S(1)}, f32[1,512,768]{2,1,0:T(8,128)}) custom-call(bf16[1,512,768]{2,1,0:T(8,128)(2,1)S(1)} %copy-done.9, bf16[1,512,768]{2,1,0:T(8,128)(2,1)S(1)} %copy-done.5, bf16[1,512,768]{2,1,0:T(8,128)(2,1)S(1)} %copy-done.7, bf16[1,512,768]{2,1,0:T(8,128)(2,1)S(1)} %copy-done.22, ...), custom_call_target="tpu_custom_call" | custom-call | flops 4026531840 | bytes 11010048 | tf_op jit(solution)/shard_map/pallas_call | solution.py:244
  456.9 4.0 fusion.77
  465.6 2.3 add_convert_fusion.2
  468.1 2.7 pad_maximum_fusion.1
  472.6 8.2 %collective-permute-done.3 = bf16[1,512,768]{2,1,0:T(8,128)(2,1)S(1)} collective-permute-done((bf16[1,512,768]{2,1,0:T(8,128)(2,1)}, bf16[1,512,768]{2,1,0:T(8,128)(2,1)S(1)}, u32[]{:S(2)}, u32[]{:S(2)}) %collective-permute-start.3) | collective-permute-done | bytes 786464 | tf_op jit(solution)/shard_map/ppermute | solution.py:356
  484.5 8.2 %fusion.38 = bf16[768,3,768]{2,0,1:T(8,128)(2,1)} fusion(bf16[3,1024,768]{2,1,0:T(8,128)(2,1)} %pad_maximum_fusion.1, f32[768]{0:T(1024)S(1)} %copy-done.61, f32[1024]{0:T(1024)S(1)} %copy-done.59, f32[1024]{0:T(1024)S(1)} %copy-done.57, bf16[512,768]{0,1:T(8,128)(2,1)S(1)} %bitcast.176, bf16[512,768]{0,1:T(8,128)(2,1)S(1)} %bitcast.169, pred[]{:T(512)S(6)} %eq.182), kind=kOutput, calls=%fused_computation.93 | convolution fusion | flops 3634888704 | bytes 9841665 | tf_op jit(solution)/shard_map/rd,jre->dje/dot_general | solution.py:662
  492.7 8.4 %fusion.19 = (bf16[768]{0:T(1024)(128)(2,1)S(1)}, f32[1024]{0:T(1024)S(1)}, f32[1024]{0:T(1024)S(1)}, f32[1024,768,1]{0,1,2:T(8,128)}) fusion(f32[1024]{0:T(1024)S(1)} %copy-done.59, f32[1024]{0:T(1024)S(1)} %copy-done.57, bf16[512,768]{0,1:T(8,128)(2,1)S(1)} %bitcast.170, bf16[512,768]{0,1:T(8,128)(2,1)S(1)} %bitcast.177, pred[]{:T(512)S(6)} %eq.182, ...), kind=kOutput, calls=%fused_computation.41 | convolution fusion | flops 3638031616 | bytes 12997121 | tf_op jit(solution)/shard_map/jre,jde->rd/dot_general | solution.py:667
  502.3 2.3 pad_maximum_fusion.2
  510.4 4.0 fusion.18
  519.6 24.3 %collective-permute-done.10 = bf16[96,1,3456]{2,0,1:T(8,128)(2,1)} collective-permute-done((bf16[96,1,3456]{2,0,1:T(8,128)(2,1)}, bf16[96,1,3456]{2,0,1:T(8,128)(2,1)}, u32[]{:S(2)}, u32[]{:S(2)}) %collective-permute-start.10) | collective-permute-done | bytes 663584 | tf_op jit(solution)/shard_map/ppermute | solution.py:445
  546.7 6.3 %collective-permute-done.5 = bf16[1,512,768]{2,1,0:T(8,128)(2,1)} collective-permute-done((bf16[1,512,768]{2,1,0:T(8,128)(2,1)}, bf16[1,512,768]{2,1,0:T(8,128)(2,1)}, u32[]{:S(2)}, u32[]{:S(2)}) %collective-permute-start.5) | collective-permute-done | bytes 786464 | tf_op jit(solution)/shard_map/ppermute | solution.py:355
  563.4 5.0 collective-permute-done.8
  571.9 2.8 collective-permute-done.9
  (352 shorter events, 105.4 us)
Async XLA Ops:
  7.2 91.9 %copy-start = (s32[4,2]{0,1:T(2,128)S(1)}, s32[4,2]{0,1:T(2,128)}, u32[]{:S(2)}) copy-start(s32[4,2]{0,1:T(2,128)} %param.21) | copy-start | bytes 100
  7.2 59.5 %all-gather.8.cloned.1.call-start = ((), (), s32[]{:S(2)}) async-start(), calls=%async_computation.2 | async-start | bytes 3829760 | tf_op jit(solution)/shard_map/all_gather | solution.py:416
  16.4 195.6 %all-gather.10.cloned.1.call-start = ((), (), s32[]{:S(2)}) async-start(), calls=%async_computation.4 | async-start | bytes 1253376 | tf_op jit(solution)/shard_map/all_gather | solution.py:406
  89.7 131.8 %all-gather.12.cloned.1.call-start = ((), (), s32[]{:S(2)}) async-start(), calls=%async_computation.5 | async-start | bytes 5013504 | tf_op jit(solution)/shard_map/all_gather | solution.py:406
  90.4 164.6 %all-gather.14.cloned.1.call-start = ((), (), s32[]{:S(2)}) async-start(), calls=%async_computation.6 | async-start | bytes 5013504 | tf_op jit(solution)/shard_map/all_gather | solution.py:406
  94.8 20.6 %collective-permute-start.1 = (bf16[1,512,768]{1,2,0:T(8,128)(2,1)}, bf16[1,512,768]{1,2,0:T(8,128)(2,1)S(1)}, u32[]{:S(2)}, u32[]{:S(2)}) collective-permute-start(bf16[1,512,768]{1,2,0:T(8,128)(2,1)} %copy.250), channel_id=1, source_target_pairs={{0,2},{2,0},{1,3},{3,1},{4,6},{6,4},{5,7},{7,5},{8,10},{10,8},{9,1... | collective-permute-start | bytes 2359304 | tf_op jit(solution)/shard_map/ppermute | solution.py:760
  98.5 175.0 %collective-permute-start = (bf16[1,512,768]{1,2,0:T(8,128)(2,1)}, bf16[1,512,768]{1,2,0:T(8,128)(2,1)}, u32[]{:S(2)}, u32[]{:S(2)}) collective-permute-start(bf16[1,512,768]{1,2,0:T(8,128)(2,1)} %copy.249), channel_id=1, source_target_pairs={{0,2},{2,0},{1,3},{3,1},{4,6},{6,4},{5,7},{7,5},{8,10},{10,8},{9,1... | collective-permute-start | bytes 2359304 | tf_op jit(solution)/shard_map/ppermute | solution.py:760
  103.2 13.7 %copy-start.33 = (bf16[1,512,768]{1,2,0:T(8,128)(2,1)}, bf16[1,512,768]{1,2,0:T(8,128)(2,1)S(1)}, u32[]{:S(2)}) copy-start(bf16[1,512,768]{1,2,0:T(8,128)(2,1)S(1)} %copy.188) | copy-start | bytes 2359300
  104.4 12.1 %copy-start.31 = (bf16[8,2,112640]{2,1,0:T(2,128)(2,1)S(1)}, bf16[8,2,112640]{2,1,0:T(2,128)(2,1)}, u32[]{:S(2)}) copy-start(bf16[8,2,112640]{2,1,0:T(2,128)(2,1)} %reshape.1748) | copy-start | bytes 10813444
  104.4 43.4 %copy-start.27 = (s32[1,8,512]{2,1,0:T(8,128)}, s32[1,8,512]{2,1,0:T(8,128)S(1)}, u32[]{:S(2)}) copy-start(s32[1,8,512]{2,1,0:T(8,128)S(1)} %pad_slice_fusion.2.pck_ref) | copy-start | bytes 49156
  107.0 40.8 %copy-start.16 = (s32[1,512,8]{2,1,0:T(8,128)}, s32[1,512,8]{2,1,0:T(8,128)S(1)}, u32[]{:S(2)}) copy-start(s32[1,512,8]{2,1,0:T(8,128)S(1)} %get-tuple-element.168.pcq_ref) | copy-start | bytes 49156
  115.4 11.1 %copy-start.41 = (bf16[1,512,768]{1,2,0:T(8,128)(2,1)}, bf16[1,512,768]{1,2,0:T(8,128)(2,1)S(1)}, u32[]{:S(2)}) copy-start(bf16[1,512,768]{1,2,0:T(8,128)(2,1)S(1)} %collective-permute-done.1) | copy-start | bytes 2359300
  116.5 9.9 %copy-start.58 = (f32[1024]{0:T(1024)}, f32[1024]{0:T(1024)S(1)}, u32[]{:S(2)}) copy-start(f32[1024]{0:T(1024)S(1)} %add_rsqrt_fusion.3) | copy-start | bytes 12292
  116.9 9.5 %copy-start.60 = (f32[768]{0:T(1024)}, f32[768]{0:T(1024)S(1)}, u32[]{:S(2)}) copy-start(f32[768]{0:T(1024)S(1)} %mul.279) | copy-start | bytes 9220
  126.5 21.3 %copy-start.4 = (bf16[1,512,768]{2,1,0:T(8,128)(2,1)}, bf16[1,512,768]{2,1,0:T(8,128)(2,1)S(1)}, u32[]{:S(2)}) copy-start(bf16[1,512,768]{2,1,0:T(8,128)(2,1)S(1)} %slice.282.k_ref) | copy-start | bytes 2359300
  136.7 39.7 %copy-start.18 = (s32[12,8,1024]{2,1,0:T(8,128)}, s32[12,8,1024]{2,1,0:T(8,128)S(1)}, u32[]{:S(2)}) copy-start(s32[12,8,1024]{2,1,0:T(8,128)S(1)} %stack.57.patk_ref) | copy-start | bytes 1179652
  136.7 11.1 %copy-start.23 = (s32[12,8,512]{2,1,0:T(8,128)}, s32[12,8,512]{2,1,0:T(8,128)S(1)}, u32[]{:S(2)}) copy-start(s32[12,8,512]{2,1,0:T(8,128)S(1)} %slice.299.patk_ref) | copy-start | bytes 589828
  136.7 347.7 %reduce-scatter.5.cloned.1.call-start = ((), (), s32[]{:S(2)}) async-start(), calls=%async_computation.3 | async-start | bytes 11943936 | tf_op jit(solution)/shard_map/reduce_scatter | solution.py:515
  147.6 28.8 %copy-start.2 = (bf16[1,1024,768]{2,1,0:T(8,128)(2,1)}, bf16[1,1024,768]{2,1,0:T(8,128)(2,1)S(1)}, u32[]{:S(2)}) copy-start(bf16[1,1024,768]{2,1,0:T(8,128)(2,1)S(1)} %get-tuple-element.143.v_ref) | copy-start | bytes 4718596
  147.6 28.7 %copy-start.6 = (bf16[1,512,768]{2,1,0:T(8,128)(2,1)}, bf16[1,512,768]{2,1,0:T(8,128)(2,1)S(1)}, u32[]{:S(2)}) copy-start(bf16[1,512,768]{2,1,0:T(8,128)(2,1)S(1)} %slice.285.v_ref) | copy-start | bytes 2359300
  147.8 28.6 %copy-start.8 = (bf16[1,512,768]{2,1,0:T(8,128)(2,1)}, bf16[1,512,768]{2,1,0:T(8,128)(2,1)S(1)}, u32[]{:S(2)}) copy-start(bf16[1,512,768]{2,1,0:T(8,128)(2,1)S(1)} %get-tuple-element.160.q_ref) | copy-start | bytes 2359300
  147.8 28.6 %copy-start.20 = (bf16[1,512,768]{2,1,0:T(8,128)(2,1)}, bf16[1,512,768]{2,1,0:T(8,128)(2,1)S(1)}, u32[]{:S(2)}) copy-start(bf16[1,512,768]{2,1,0:T(8,128)(2,1)S(1)} %get-tuple-element.161.q_ref) | copy-start | bytes 2359300
  147.8 28.6 %copy-start.12 = (bf16[1,1024,768]{2,1,0:T(8,128)(2,1)S(1)}, bf16[1,1024,768]{2,1,0:T(8,128)(2,1)}, u32[]{:S(2)}) copy-start(bf16[1,1024,768]{2,1,0:T(8,128)(2,1)} %slice.301.k_ref) | copy-start | bytes 4718596
  147.8 28.6 %copy-start.25 = (s32[1,512,8]{2,1,0:T(8,128)S(1)}, s32[1,512,8]{2,1,0:T(8,128)}, u32[]{:S(2)}) copy-start(s32[1,512,8]{2,1,0:T(8,128)} %get-tuple-element.169.pcq_ref) | copy-start | bytes 49156
  147.8 28.6 %copy-start.29 = (s32[1,8,1024]{2,1,0:T(8,128)S(1)}, s32[1,8,1024]{2,1,0:T(8,128)}, u32[]{:S(2)}) copy-start(s32[1,8,1024]{2,1,0:T(8,128)} %pad.26.pck_ref) | copy-start | bytes 98308
  212.0 5.7 copy-start.64
  234.7 12.2 %copy-start.47 = (bf16[96,8,2,1536]{3,1,2,0:T(8,128)(2,1)}, bf16[96,8,2,1536]{3,1,2,0:T(8,128)(2,1)S(1)}, u32[]{:S(2)}) copy-start(bf16[96,8,2,1536]{3,1,2,0:T(8,128)(2,1)S(1)} %copy.264) | copy-start | bytes 14155780
  273.5 21.4 %copy-start.46 = (bf16[96,8,2,1536]{3,1,2,0:T(8,128)(2,1)}, bf16[96,8,2,1536]{3,1,2,0:T(8,128)(2,1)S(1)}, u32[]{:S(2)}) copy-start(bf16[96,8,2,1536]{3,1,2,0:T(8,128)(2,1)S(1)} %copy.265) | copy-start | bytes 14155780
  294.9 16.6 %copy-start.38 = (f32[1024,768]{0,1:T(8,128)S(1)}, f32[1024,768]{0,1:T(8,128)}, u32[]{:S(2)}) copy-start(f32[1024,768]{0,1:T(8,128)} %copy-done.36) | copy-start | bytes 9437188
  347.7 212.6 %reduce-scatter.7.cloned.1.call-start = ((), (), s32[]{:S(2)}) async-start(), calls=%async_computation.7 | async-start | bytes 4313088
  358.9 5.3 copy-start.44
  362.7 109.9 %collective-permute-start.4 = (bf16[1,512,768]{2,1,0:T(8,128)(2,1)}, bf16[1,512,768]{2,1,0:T(8,128)(2,1)}, u32[]{:S(2)}, u32[]{:S(2)}) collective-permute-start(bf16[1,512,768]{2,1,0:T(8,128)(2,1)} %bitcast.201), channel_id=1, source_target_pairs={{0,3},{3,0},{1,2},{2,1},{4,7},{7,4},{5,6},{6,5},{8,11},{11,8},{9,1... | collective-permute-start | bytes 2359304 | tf_op jit(solution)/shard_map/ppermute | solution.py:357
  363.5 107.4 %collective-permute-start.2 = (bf16[1,512,768]{2,1,0:T(8,128)(2,1)}, bf16[1,512,768]{2,1,0:T(8,128)(2,1)}, u32[]{:S(2)}, u32[]{:S(2)}) collective-permute-start(bf16[1,512,768]{2,1,0:T(8,128)(2,1)} %bitcast.202), channel_id=1, source_target_pairs={{0,2},{2,0},{1,3},{3,1},{4,6},{6,4},{5,7},{7,5},{8,10},{10,8},{9,1... | collective-permute-start | bytes 2359304 | tf_op jit(solution)/shard_map/ppermute | solution.py:355
  369.8 51.5 %copy-start.5 = (bf16[1,512,768]{2,1,0:T(8,128)(2,1)S(1)}, bf16[1,512,768]{2,1,0:T(8,128)(2,1)}, u32[]{:S(2)}) copy-start(bf16[1,512,768]{2,1,0:T(8,128)(2,1)} %copy-done.4) | copy-start | bytes 2359300
  369.8 51.5 %copy-start.7 = (bf16[1,512,768]{2,1,0:T(8,128)(2,1)S(1)}, bf16[1,512,768]{2,1,0:T(8,128)(2,1)}, u32[]{:S(2)}) copy-start(bf16[1,512,768]{2,1,0:T(8,128)(2,1)} %copy-done.6) | copy-start | bytes 2359300
  369.8 51.5 %copy-start.17 = (s32[1,512,8]{2,1,0:T(8,128)S(1)}, s32[1,512,8]{2,1,0:T(8,128)}, u32[]{:S(2)}) copy-start(s32[1,512,8]{2,1,0:T(8,128)} %copy-done.16) | copy-start | bytes 49156
  369.8 51.6 %copy-start.28 = (s32[1,8,512]{2,1,0:T(8,128)S(1)}, s32[1,8,512]{2,1,0:T(8,128)}, u32[]{:S(2)}) copy-start(s32[1,8,512]{2,1,0:T(8,128)} %copy-done.27) | copy-start | bytes 49156
  456.9 8.7 %copy-start.15 = (f32[1,512,768]{2,1,0:T(8,128)S(1)}, f32[1,512,768]{2,1,0:T(8,128)}, u32[]{:S(2)}) copy-start(f32[1,512,768]{2,1,0:T(8,128)} %copy-done.14) | copy-start | bytes 4718596
  463.1 17.7 %collective-permute-start.3 = (bf16[1,512,768]{2,1,0:T(8,128)(2,1)}, bf16[1,512,768]{2,1,0:T(8,128)(2,1)S(1)}, u32[]{:S(2)}, u32[]{:S(2)}) collective-permute-start(bf16[1,512,768]{2,1,0:T(8,128)(2,1)} %bitcast.193), channel_id=1, source_target_pairs={{0,1},{1,0},{2,3},{3,2},{4,5},{5,4},{6,7},{7,6},{8,9},{9,8},{10,11... | collective-permute-start | bytes 2359304 | tf_op jit(solution)/shard_map/ppermute | solution.py:356
  484.5 8.3 %copy-start.48 = (bf16[3,768,768]{2,1,0:T(8,128)(2,1)S(1)}, bf16[3,768,768]{2,1,0:T(8,128)(2,1)}, u32[]{:S(2)}) copy-start(bf16[3,768,768]{2,1,0:T(8,128)(2,1)} %reshape.1750) | copy-start | bytes 10616836
  508.9 34.9 %collective-permute-start.10 = (bf16[96,1,3456]{2,0,1:T(8,128)(2,1)}, bf16[96,1,3456]{2,0,1:T(8,128)(2,1)}, u32[]{:S(2)}, u32[]{:S(2)}) collective-permute-start(bf16[96,1,3456]{2,0,1:T(8,128)(2,1)} %constant_dynamic-slice_fusion), channel_id=1, source_target_pairs={{0,1},{1,0},{2,3},{3,2},{4,5},{5,4},{6,7},{7,6},{8,9},{9,8},{10,11... | collective-permute-start | bytes 1990664 | tf_op jit(solution)/shard_map/ppermute | solution.py:445
  515.7 38.9 %collective-permute-start.7 = (bf16[1,512,768]{2,1,0:T(8,128)(2,1)}, bf16[1,512,768]{2,1,0:T(8,128)(2,1)}, u32[]{:S(2)}, u32[]{:S(2)}) collective-permute-start(bf16[1,512,768]{2,1,0:T(8,128)(2,1)} %bitcast.203), channel_id=1, source_target_pairs={{0,3},{3,0},{1,2},{2,1},{4,7},{7,4},{5,6},{6,5},{8,11},{11,8},{9,1... | collective-permute-start | bytes 2359304 | tf_op jit(solution)/shard_map/ppermute | solution.py:357
  516.8 36.1 %collective-permute-start.5 = (bf16[1,512,768]{2,1,0:T(8,128)(2,1)}, bf16[1,512,768]{2,1,0:T(8,128)(2,1)}, u32[]{:S(2)}, u32[]{:S(2)}) collective-permute-start(bf16[1,512,768]{2,1,0:T(8,128)(2,1)} %bitcast.204), channel_id=1, source_target_pairs={{0,2},{2,0},{1,3},{3,1},{4,6},{6,4},{5,7},{7,5},{8,10},{10,8},{9,1... | collective-permute-start | bytes 2359304 | tf_op jit(solution)/shard_map/ppermute | solution.py:355
  517.6 39.1 %collective-permute-start.6 = (bf16[1,512,768]{2,1,0:T(8,128)(2,1)S(1)}, bf16[1,512,768]{2,1,0:T(8,128)(2,1)S(1)}, u32[]{:S(2)}, u32[]{:S(2)}) collective-permute-start(bf16[1,512,768]{2,1,0:T(8,128)(2,1)S(1)} %bitcast.195), channel_id=1, source_target_pairs={{0,1},{1,0},{2,3},{3,2},{4,5},{5,4},{6,7},{7,6},{8,9},{9,8},{10,11... | collective-permute-start | bytes 2359304 | tf_op jit(solution)/shard_map/ppermute | solution.py:356
  545.1 18.2 %collective-permute-start.11 = (bf16[96,1,3456]{2,0,1:T(8,128)(2,1)S(1)}, bf16[96,1,3456]{2,0,1:T(8,128)(2,1)S(1)}, u32[]{:S(2)}, u32[]{:S(2)}) collective-permute-start(bf16[96,1,3456]{2,0,1:T(8,128)(2,1)S(1)} %add_convert_fusion.3), channel_id=1, source_target_pairs={{0,2},{2,0},{1,3},{3,1},{4,6},{6,4},{5,7},{7,5},{8,10},{10,8},{9,1... | collective-permute-start | bytes 1990664 | tf_op jit(solution)/shard_map/ppermute | solution.py:452
  562.2 6.2 %collective-permute-start.8 = (bf16[104,3,384]{2,0,1:T(8,128)(2,1)S(1)}, bf16[104,3,384]{2,0,1:T(8,128)(2,1)S(1)}, u32[]{:S(2)}, u32[]{:S(2)}) collective-permute-start(bf16[104,3,384]{2,0,1:T(8,128)(2,1)S(1)} %copy.258), channel_id=1, source_target_pairs={{0,1},{1,0},{2,3},{3,2},{4,5},{5,4},{6,7},{7,6},{8,9},{9,8},{10,11... | collective-permute-start | bytes 718856 | tf_op jit(solution)/shard_map/ppermute | solution.py:445
  568.4 11.0 %copy-start.1 = (s32[4,2]{0,1:T(2,128)S(1)}, s32[4,2]{0,1:T(2,128)}, u32[]{:S(2)}) copy-start(s32[4,2]{0,1:T(2,128)} %param.21) | copy-start | bytes 100
  568.5 6.2 %collective-permute-start.9 = (bf16[104,3,384]{2,0,1:T(8,128)(2,1)S(1)}, bf16[104,3,384]{2,0,1:T(8,128)(2,1)S(1)}, u32[]{:S(2)}, u32[]{:S(2)}) collective-permute-start(bf16[104,3,384]{2,0,1:T(8,128)(2,1)S(1)} %add_convert_fusion.4), channel_id=1, source_target_pairs={{0,2},{2,0},{1,3},{3,1},{4,6},{6,4},{5,7},{7,5},{8,10},{10,8},{9,1... | collective-permute-start | bytes 718856 | tf_op jit(solution)/shard_map/ppermute | solution.py:452
  (39 other events, 90.7 us)
Sparse Core Ops, SparseCore 0:
  16.5 50.1 all-gather.7
  89.8 35.6 all-gather.9
  127.8 52.6 all-gather.11
  182.7 51.4 all-gather.13
  347.8 109.1 reduce-scatter.4
  506.8 46.4 reduce-scatter.6

commit v12 on v11

--- a/solution.py
+++ b/solution.py
@@ -665,8 +665,7 @@
     )
     qkv_grad, stacked = lax.optimization_barrier((qkv_grad, stacked))
     attn_in_grad = jnp.einsum("jre,jde->rd", stacked, w_qkv, preferred_element_type=jnp.float32)
-    input_part, first_gain_grad = norm_back(first_normed, first_inv, norm_gains[0], attn_in_grad)
-    input_low = (middle_grad + input_part).astype(jnp.bfloat16)
+    first_gain_grad = jnp.sum(attn_in_grad * first_normed, 0)
     heads = model_width // HD
     unit_rows = unit_bias_grad.shape[0] // HD
     small_terms = (
@@ -696,7 +695,10 @@
     widened = jnp.concatenate(
         [qkv_grad.reshape(ns, block_rows, planes, model_width), small_block.astype(qkv_grad.dtype)], 1
     ).reshape(ns * (block_rows + extra_rows), planes, model_width)
+    widened, attn_in_grad = lax.optimization_barrier((widened, attn_in_grad))
     qkv_share = shard_stage(widened, 0)
+    input_part = norm_back(first_normed, first_inv, norm_gains[0], attn_in_grad)[0]
+    input_low = (middle_grad + input_part).astype(jnp.bfloat16)
     qkv_total = finish_stage(qkv_share, 2)
     small_total = qkv_total[block_rows:].reshape(-1)[:small_width]
     small_pieces = []

time: 592 us -> 602 us (1.017)
  local copies, waits for them, and re-layouts: 129 us -> 144 us
  waiting for transfers between devices: 108 us -> 99.9 us
    ppermute x2, waiting for transfers between devices: 29.3 us -> 5.59 us  [pair_reduce(): received = lax.ppermute(sent, axis_name, perm=[(0, 1), (1, 0)])]
    reshape x5, local copies, waits for them, and re-layouts: 29.6 us -> 38.2 us  [gather_weight(): stacked.reshape((ns, nt) + local_block.shape)]
    ppermute x2, waiting for transfers between devices: 10.3 us -> 16.4 us  [spread_sequence(): from_tensor = lax.ppermute(kept, 'tensor', perm=swap)]
    unnamed x150 -> x139, local copies, waits for them, and re-layouts: 40.5 us -> 38.4 us
  transfers between devices with their start and end apart: 18 -> 18, of which waited for: 8 -> 8; matrix products, arithmetic and copies ran while one was open for 26% -> 27% of each run, Pallas kernels for 24% -> 25%
where the time goes in v12:
time: 602 us; the launch traced here: 591 us
  Pallas kernels  145 us (24%)
  local copies, waits for them, and re-layouts  144 us (24%)
  waiting for transfers between devices  99.9 us (17%)
  matrix products  89.3 us (15%)
  other arithmetic  82.6 us (14%)
  between operations  17.2 us (3%)
  starting transfers between devices  13.5 us (2%)
    pallas_call x2, Pallas kernels, attention_backward(): pl.pallas_call(attention_bwd_kernel, grid=grid, in_specs=[query_spec, key...  81.2 us
    pallas_call x2, Pallas kernels, attention_forward(): pl.pallas_call(attention_fwd_kernel, grid=grid, in_specs=[query_spec, key...  63.6 us
    all_gather x1, waiting for transfers between devices, gather_packed(): lax.all_gather(flat, ('shard', 'tensor'), axis=0, tiled=False)  50.3 us
    unnamed x139, local copies, waits for them, and re-layouts  38.4 us
    reshape x5, local copies, waits for them, and re-layouts, gather_weight(): stacked.reshape((ns, nt) + local_block.shape)  38.2 us
    dot_general x3, matrix products, back_dot(): lax.dot_general(left_rows, weight_rows, (((1,), (1,)), ((), ())), preferr...  31 us
    reduce_sum x1, other arithmetic, backward_pass(): unit_bias_grad = jnp.sum(hidden_low, 0, dtype=jnp.float32)  17 us
    ppermute x2, waiting for transfers between devices, spread_sequence(): from_tensor = lax.ppermute(kept, 'tensor', perm=swap)  16.4 us
  transfers between devices with their start and end apart: 18, of which 8 were waited for; matrix products, arithmetic and copies ran while one was open for 27% of the time, Pallas kernels for 25%

profile of v12, /device:TPU:0, one launch (start us, length us, event | category | flops | bytes accessed | tf_op | source)
XLA Modules:
  0.0 590.9 jit_solution(10758193978514058511)
XLA Ops:
  16.4 50.3 %all-gather.8.cloned.1.call-done = bf16[16,880,128]{2,1,0:T(8,128)(2,1)} async-done(((bf16[1,880,128]{2,1,0:T(8,128)(2,1)}), bf16[16,880,128]{2,1,0:T(8,128)(2,1)}) %all-gather.8.cloned.1.call-update) | async-done | bytes 3604496 | tf_op jit(solution)/shard_map/all_gather | solution.py:416
  66.7 6.7 %reshape.1738 = bf16[8,2,112640]{2,1,0:T(2,128)(2,1)} reshape(bf16[16,880,128]{2,1,0:T(8,128)(2,1)} %all-gather.8.cloned.1.call-done) | data formatting | bytes 7208960 | tf_op jit(solution)/shard_map/reshape | solution.py:416
  75.4 4.8 reshape.1782
  80.2 5.5 copy.202
  85.7 4.0 reshape.1740
  104.3 10.0 %collective-permute-done.1 = bf16[1,512,768]{1,2,0:T(8,128)(2,1)S(1)} collective-permute-done((bf16[1,512,768]{1,2,0:T(8,128)(2,1)}, bf16[1,512,768]{1,2,0:T(8,128)(2,1)S(1)}, u32[]{:S(2)}, u32[]{:S(2)}) %collective-permute-start.1) | collective-permute-done | bytes 786464 | tf_op jit(solution)/shard_map/ppermute | solution.py:762
  124.7 6.5 %fusion.81 = (bf16[3,1024,768]{2,1,0:T(8,128)(2,1)S(1)}, f32[3,1024,768]{2,1,0:T(8,128)S(1)}) fusion(bf16[3,768,768]{2,1,0:T(8,128)(2,1)} %reshape.1740, f32[768]{0:T(1024)S(1)} %mul.279, f32[1024]{0:T(1024)S(1)} %add_rsqrt_fusion.3, f32[1024]{0:T(1024)S(1)} %broadcast_multiply_fusion.11, bf16[512,768]{0,1:T(8,128)(2,1)S(1)} %bitcast.157, ...), kind=kOutput, calls=%fused_computation.287 | convolution fusion | flops 3637248000 | bytes 19278848 | tf_op jit(solution)/shard_map/rd,jde->jre/dot_general | solution.py:530
  150.0 28.0 %shard_map.256 = f32[1,512,768]{2,1,0:T(8,128)S(1)} custom-call(bf16[1,512,768]{2,1,0:T(8,128)(2,1)S(1)} %get-tuple-element.163.q_ref, bf16[1,512,768]{2,1,0:T(8,128)(2,1)S(1)} %slice.282.k_ref, bf16[1,512,768]{2,1,0:T(8,128)(2,1)S(1)} %slice.285.v_ref, s32[12,512,8]{2,1,0:T(8,128)} %copy.262.patq_ref, s32[12,8,512]{2,1,0:T(8,128)S(1)} %copy-done.20, ...), custom_call_target="tpu_custom_call" | custom-call | flops 1610612736 | bytes 5505024 | tf_op jit(solution)/shard_map/pallas_call | solution.py:217
  178.1 35.6 %shard_map.257 = f32[1,512,768]{2,1,0:T(8,128)S(1)} custom-call(bf16[1,512,768]{2,1,0:T(8,128)(2,1)S(1)} %get-tuple-element.164.q_ref, bf16[1,1024,768]{2,1,0:T(8,128)(2,1)S(1)} %copy-done.11, bf16[1,1024,768]{2,1,0:T(8,128)(2,1)S(1)} %copy-done.3, s32[12,512,8]{2,1,0:T(8,128)} %copy.263.patq_ref, s32[12,8,1024]{2,1,0:T(8,128)S(1)} %copy-done.16, ...), custom_call_target="tpu_custom_call" | custom-call | flops 3221225472 | bytes 8650752 | tf_op jit(solution)/shard_map/pallas_call | solution.py:217
  214.5 11.3 %reshape.1743 = bf16[8,2,384,96]{2,1,0,3:T(2,128)(2,1)} reshape(bf16[6144,96]{0,1:T(8,128)(2,1)} %all-gather.10.cloned.1.call-done) | data formatting | bytes 2359296 | tf_op jit(solution)/shard_map/reshape | solution.py:407
  232.1 9.4 %copy.214 = bf16[8,2,96,1536]{3,1,2,0:T(2,128)(2,1)} copy(bf16[8,2,96,1536]{3,2,1,0:T(8,128)(2,1)} %bitcast.179) | data formatting | bytes 9437184 | tf_op jit(solution)/shard_map/reshape | solution.py:407
  241.5 3.7 copy.274
  245.2 9.2 %fusion.71 = (f32[1024]{0:T(1024)S(1)}, f32[1024,3072]{1,0:T(8,128)S(1)}) fusion(f32[3072]{0:T(1024)S(1)} %reshape.1767, bf16[768,3072]{1,0:T(8,128)(2,1)S(1)} %bitcast.182, f32[1024,768]{0,1:T(8,128)S(1)} %copy-done.36, f32[768]{0:T(1024)S(1)} %mul.294, f32[1024]{0:T(1024)S(1)} %add_rsqrt_fusion.1, f32[1024]{0:T(1024)S(1)} %broadcast_multiply_fusion.9), kind=kOutput, calls=%fused_computation.278 | convolution fusion | flops 4866440192 | bytes 20474880 | tf_op jit(solution)/shard_map/dot_general | solution.py:551
  254.5 4.5 copy-done.24
  259.0 5.6 multiply_reduce_fusion.2
  264.6 7.7 %reshape.1748 = bf16[8,2,1536,96]{2,1,0,3:T(2,128)(2,1)} reshape(bf16[24576,96]{0,1:T(8,128)(2,1)} %all-gather.14.cloned.1.call-done) | data formatting | bytes 9437184 | tf_op jit(solution)/shard_map/reshape | solution.py:407
  272.2 7.7 %copy.219 = bf16[8,2,1536,96]{2,1,3,0:T(2,128)(2,1)} copy(bf16[8,2,1536,96]{2,1,0,3:T(2,128)(2,1)} %reshape.1748) | data formatting | bytes 9437184 | tf_op jit(solution)/shard_map/reshape | solution.py:407
  279.9 5.8 copy.275
  285.7 19.3 %multiply_reduce_fusion = (bf16[3072]{0:T(1024)(128)(2,1)S(1)}, f32[1024]{0:T(1024)S(1)}, f32[1024]{0:T(1024)S(1)}, f32[1024,3072]{1,0:T(8,128)}) fusion(f32[1024]{0:T(1024)S(1)} %add_rsqrt_fusion, f32[1024]{0:T(1024)S(1)} %broadcast_multiply_fusion.2, f32[1024,3072]{1,0:T(8,128)} %copy-done.24, f32[3072]{0:T(1024)S(1)} %reshape.1767, ...), kind=kOutput, calls=%fused_computation.9 | convolution fusion | flops 4892388352 | bytes 31504384 | tf_op jit(solution)/shard_map/dot_general | solution.py:65
  305.1 17.0 %convert_reduce_fusion = (bf16[3072]{0:T(1024)(128)(2,1)S(1)}, bf16[1024,3072]{1,0:T(8,128)(2,1)S(1)}, bf16[1024,3072]{1,0:T(8,128)(2,1)S(1)}) fusion(f32[1024]{0:T(1024)S(1)} %broadcast_multiply_fusion, f32[1024]{0:T(1024)S(1)} %broadcast_multiply_fusion.2, f32[1024,3072]{1,0:T(8,128)S(1)} %bitcast.154, f32[3072]{0:T(1024)S(1)} %reshape.1767, ...), kind=kLoop, calls=%fused_computation.10 | loop fusion | flops 103805952 | bytes 37795840 | tf_op jit(solution)/shard_map/reduce_sum | solution.py:613
  322.1 9.4 %multiply_reduce_fusion.5 = (bf16[768]{0:T(1024)(128)(2,1)S(1)}, f32[1024]{0:T(1024)S(1)}, f32[1024]{0:T(1024)S(1)}, f32[1024,768]{0,1:T(8,128)S(1)}) fusion(f32[1024,768]{0,1:T(8,128)S(1)} %copy-done.37, f32[1024]{0:T(1024)S(1)} %add_rsqrt_fusion.1, f32[1024]{0:T(1024)S(1)} %broadcast_multiply_fusion.9, f32[768]{0:T(1024)S(1)} %mul.294, ...), kind=kOutput, calls=%fused_computation.61 | convolution fusion | flops 4838126592 | bytes 17322496 | tf_op jit(solution)/shard_map/dot_general | solution.py:65
  331.5 3.5 convert_reduce_fusion.5
  335.1 2.3 multiply_reduce_fusion.4
  337.4 2.7 fusion.36
  340.1 5.4 convolution_convert_fusion
  345.6 6.8 %convolution_convert_fusion.1 = bf16[768,3072]{1,0:T(8,128)(2,1)S(1)} fusion(bf16[1024,3072]{1,0:T(8,128)(2,1)S(1)} %get-tuple-element.145, bf16[512,768]{0,1:T(8,128)(2,1)} %bitcast.1, bf16[512,768]{0,1:T(8,128)(2,1)S(1)} %bitcast.191, pred[]{:T(512)S(6)} %eq.182), kind=kOutput, calls=%fused_computation.20 | convolution fusion | flops 4841275392 | bytes 12582913 | tf_op jit(solution)/shard_map/dot_general | solution.py:59
  352.4 2.4 multiply_convert_fusion.1
  356.5 4.7 pad_maximum_fusion
  363.1 9.8 %add_convert_fusion = bf16[1024,768]{0,1:T(8,128)(2,1)S(1)} fusion(f32[1024,768]{0,1:T(8,128)S(1)} %copy-done.38, bf16[1024,3072]{1,0:T(8,128)(2,1)} %copy-done.41, bf16[3072,768]{0,1:T(8,128)(2,1)} %bitcast.181, f32[768]{0:T(1024)S(1)} %add.737), kind=kOutput, calls=%fused_computation.62 | convolution fusion | flops 4834197504 | bytes 15731712 | tf_op jit(solution)/shard_map/dot_general | solution.py:556
  374.2 2.5 copy.227
  377.9 2.3 copy.226
  384.0 31.3 %shard_map.258 = (bf16[1,512,768]{2,1,0:T(8,128)(2,1)S(1)}, f32[1,512,768]{2,1,0:T(8,128)S(1)}, f32[1,512,768]{2,1,0:T(8,128)}) custom-call(bf16[1,512,768]{2,1,0:T(8,128)(2,1)S(1)} %copy-done.10, bf16[1,512,768]{2,1,0:T(8,128)(2,1)S(1)} %copy-done.6, bf16[1,512,768]{2,1,0:T(8,128)(2,1)S(1)} %copy-done.8, ...), custom_call_target="tpu_custom_call" | custom-call | flops 4026531840 | bytes 11010048 | tf_op jit(solution)/shard_map/pallas_call | solution.py:244
  416.6 49.9 %shard_map.259 = (bf16[1,512,768]{2,1,0:T(8,128)(2,1)S(1)}, f32[1,1024,768]{2,1,0:T(8,128)}, f32[1,1024,768]{2,1,0:T(8,128)}) custom-call(bf16[1,512,768]{2,1,0:T(8,128)(2,1)S(1)} %copy-done.19, bf16[1,1024,768]{2,1,0:T(8,128)(2,1)S(1)} %copy-done.12, bf16[1,1024,768]{2,1,0:T(8,128)(2,1)S(1)} %copy-done.4, ...), custom_call_target="tpu_custom_call" | custom-call | flops 8053063680 | bytes 20447232 | tf_op jit(solution)/shard_map/pallas_call | solution.py:244
  467.0 4.0 convert_reduce_fusion.3
  472.4 2.4 add_convert_fusion.2
  474.8 2.7 pad_maximum_fusion.2
  483.3 8.2 %fusion.37 = bf16[768,3,768]{2,0,1:T(8,128)(2,1)} fusion(bf16[3,1024,768]{2,1,0:T(8,128)(2,1)} %pad_maximum_fusion.2, f32[768]{0:T(1024)S(1)} %copy-done.57, f32[1024]{0:T(1024)S(1)} %copy-done.55, f32[1024]{0:T(1024)S(1)} %copy-done.53, bf16[512,768]{0,1:T(8,128)(2,1)S(1)} %bitcast.168, bf16[512,768]{0,1:T(8,128)(2,1)S(1)} %bitcast.160, pred[]{:T(512)S(6)} %eq.182), kind=kOutput, calls=%fused_computation.97 | convolution fusion | flops 3634888704 | bytes 9841665 | tf_op jit(solution)/shard_map/rd,jre->dje/dot_general | solution.py:662
  491.5 7.9 %convolution_bitcast_fusion.1 = f32[1024,768]{1,0:T(8,128)} fusion(bf16[3,1024,768]{2,1,0:T(8,128)(2,1)} %pad_maximum_fusion.2, bf16[3,768,768]{2,1,0:T(8,128)(2,1)S(1)} %copy-done.44), kind=kOutput, calls=%fused_computation.77 | convolution fusion | flops 3623878656 | bytes 11403264 | tf_op jit(solution)/shard_map/jre,jde->rd/dot_general | solution.py:667
  499.4 3.6 copy.228
  503.0 2.6 fusion.14
  506.8 2.3 pad_maximum_fusion.1
  513.5 2.4 copy.237
  515.9 3.0 multiply_reduce_fusion.10
  526.1 3.9 collective-permute-done.10
  532.9 10.2 %collective-permute-done.5 = bf16[1,512,768]{2,1,0:T(8,128)(2,1)} collective-permute-done((bf16[1,512,768]{2,1,0:T(8,128)(2,1)}, bf16[1,512,768]{2,1,0:T(8,128)(2,1)}, u32[]{:S(2)}, u32[]{:S(2)}) %collective-permute-start.5) | collective-permute-done | bytes 786464 | tf_op jit(solution)/shard_map/ppermute | solution.py:355
  544.8 16.4 %collective-permute-done.6 = bf16[1,512,768]{2,1,0:T(8,128)(2,1)S(1)} collective-permute-done((bf16[1,512,768]{2,1,0:T(8,128)(2,1)S(1)}, bf16[1,512,768]{2,1,0:T(8,128)(2,1)S(1)}, u32[]{:S(2)}, u32[]{:S(2)}) %collective-permute-start.6) | collective-permute-done | bytes 786464 | tf_op jit(solution)/shard_map/ppermute | solution.py:356
  567.3 3.7 collective-permute-done.11
  576.2 2.8 collective-permute-done.9
  (344 shorter events, 112.3 us)
Async XLA Ops:
  7.2 90.0 %copy-start = (s32[4,2]{0,1:T(2,128)S(1)}, s32[4,2]{0,1:T(2,128)}, u32[]{:S(2)}) copy-start(s32[4,2]{0,1:T(2,128)} %param.21) | copy-start | bytes 100
  7.2 59.5 %all-gather.8.cloned.1.call-start = ((), (), s32[]{:S(2)}) async-start(), calls=%async_computation.2 | async-start | bytes 3829760 | tf_op jit(solution)/shard_map/all_gather | solution.py:416
  16.4 198.1 %all-gather.10.cloned.1.call-start = ((), (), s32[]{:S(2)}) async-start(), calls=%async_computation.4 | async-start | bytes 1253376 | tf_op jit(solution)/shard_map/all_gather | solution.py:406
  89.7 142.3 %all-gather.12.cloned.1.call-start = ((), (), s32[]{:S(2)}) async-start(), calls=%async_computation.5 | async-start | bytes 5013504 | tf_op jit(solution)/shard_map/all_gather | solution.py:406
  90.4 174.1 %all-gather.14.cloned.1.call-start = ((), (), s32[]{:S(2)}) async-start(), calls=%async_computation.6 | async-start | bytes 5013504 | tf_op jit(solution)/shard_map/all_gather | solution.py:406
  93.7 20.6 %collective-permute-start.1 = (bf16[1,512,768]{1,2,0:T(8,128)(2,1)}, bf16[1,512,768]{1,2,0:T(8,128)(2,1)S(1)}, u32[]{:S(2)}, u32[]{:S(2)}) collective-permute-start(bf16[1,512,768]{1,2,0:T(8,128)(2,1)} %copy.260), channel_id=1, source_target_pairs={{0,2},{2,0},{1,3},{3,1},{4,6},{6,4},{5,7},{7,5},{8,10},{10,8},{9,1... | collective-permute-start | bytes 2359304 | tf_op jit(solution)/shard_map/ppermute | solution.py:762
  96.4 189.3 %collective-permute-start = (bf16[1,512,768]{1,2,0:T(8,128)(2,1)}, bf16[1,512,768]{1,2,0:T(8,128)(2,1)}, u32[]{:S(2)}, u32[]{:S(2)}) collective-permute-start(bf16[1,512,768]{1,2,0:T(8,128)(2,1)} %copy.259), channel_id=1, source_target_pairs={{0,2},{2,0},{1,3},{3,1},{4,6},{6,4},{5,7},{7,5},{8,10},{10,8},{9,1... | collective-permute-start | bytes 2359304 | tf_op jit(solution)/shard_map/ppermute | solution.py:762
  97.2 27.4 %copy-start.25 = (bf16[1,512,768]{1,2,0:T(8,128)(2,1)}, bf16[1,512,768]{1,2,0:T(8,128)(2,1)S(1)}, u32[]{:S(2)}) copy-start(bf16[1,512,768]{1,2,0:T(8,128)(2,1)S(1)} %copy.196) | copy-start | bytes 2359300
  100.6 15.2 %slice-start.4 = ((bf16[8,2,112640]{2,1,0:T(2,128)(2,1)}), bf16[8,2,96]{2,1,0:T(2,128)(2,1)S(1)}, s32[]{:S(2)}) async-start(bf16[8,2,112640]{2,1,0:T(2,128)(2,1)} %reshape.1738), calls=%async_computation.12 | async-start | bytes 8192 | tf_op jit(solution)/shard_map/slice | solution.py:420
  101.8 13.7 %copy-start.33 = (bf16[8,2,112640]{2,1,0:T(2,128)(2,1)S(1)}, bf16[8,2,112640]{2,1,0:T(2,128)(2,1)}, u32[]{:S(2)}) copy-start(bf16[8,2,112640]{2,1,0:T(2,128)(2,1)} %reshape.1738) | copy-start | bytes 10813444
  114.3 16.9 %copy-start.29 = (bf16[1,512,768]{1,2,0:T(8,128)(2,1)}, bf16[1,512,768]{1,2,0:T(8,128)(2,1)S(1)}, u32[]{:S(2)}) copy-start(bf16[1,512,768]{1,2,0:T(8,128)(2,1)S(1)} %collective-permute-done.1) | copy-start | bytes 2359300
  114.8 16.4 %copy-start.52 = (f32[1024]{0:T(1024)}, f32[1024]{0:T(1024)S(1)}, u32[]{:S(2)}) copy-start(f32[1024]{0:T(1024)S(1)} %broadcast_multiply_fusion.11) | copy-start | bytes 12292
  115.5 15.8 %copy-start.54 = (f32[1024]{0:T(1024)}, f32[1024]{0:T(1024)S(1)}, u32[]{:S(2)}) copy-start(f32[1024]{0:T(1024)S(1)} %add_rsqrt_fusion.3) | copy-start | bytes 12292
  115.8 15.5 %copy-start.56 = (f32[768]{0:T(1024)}, f32[768]{0:T(1024)S(1)}, u32[]{:S(2)}) copy-start(f32[768]{0:T(1024)S(1)} %mul.279) | copy-start | bytes 9220
  124.4 358.9 %reduce-scatter.5.cloned.1.call-start = ((), (), s32[]{:S(2)}) async-start(), calls=%async_computation.3 | async-start | bytes 11943936 | tf_op jit(solution)/shard_map/reduce_scatter | solution.py:515
  134.0 14.8 %copy-start.5 = (bf16[1,512,768]{2,1,0:T(8,128)(2,1)}, bf16[1,512,768]{2,1,0:T(8,128)(2,1)S(1)}, u32[]{:S(2)}) copy-start(bf16[1,512,768]{2,1,0:T(8,128)(2,1)S(1)} %slice.282.k_ref) | copy-start | bytes 2359300
  136.8 12.1 %copy-start.7 = (bf16[1,512,768]{2,1,0:T(8,128)(2,1)}, bf16[1,512,768]{2,1,0:T(8,128)(2,1)S(1)}, u32[]{:S(2)}) copy-start(bf16[1,512,768]{2,1,0:T(8,128)(2,1)S(1)} %slice.285.v_ref) | copy-start | bytes 2359300
  148.8 29.3 %copy-start.9 = (bf16[1,512,768]{2,1,0:T(8,128)(2,1)}, bf16[1,512,768]{2,1,0:T(8,128)(2,1)S(1)}, u32[]{:S(2)}) copy-start(bf16[1,512,768]{2,1,0:T(8,128)(2,1)S(1)} %get-tuple-element.163.q_ref) | copy-start | bytes 2359300
  148.8 29.3 %copy-start.18 = (bf16[1,512,768]{2,1,0:T(8,128)(2,1)}, bf16[1,512,768]{2,1,0:T(8,128)(2,1)S(1)}, u32[]{:S(2)}) copy-start(bf16[1,512,768]{2,1,0:T(8,128)(2,1)S(1)} %get-tuple-element.164.q_ref) | copy-start | bytes 2359300
  150.0 28.1 %copy-start.3 = (bf16[1,1024,768]{2,1,0:T(8,128)(2,1)S(1)}, bf16[1,1024,768]{2,1,0:T(8,128)(2,1)}, u32[]{:S(2)}) copy-start(bf16[1,1024,768]{2,1,0:T(8,128)(2,1)} %copy-done.2) | copy-start | bytes 4718596
  150.0 28.1 %copy-start.11 = (bf16[1,1024,768]{2,1,0:T(8,128)(2,1)S(1)}, bf16[1,1024,768]{2,1,0:T(8,128)(2,1)}, u32[]{:S(2)}) copy-start(bf16[1,1024,768]{2,1,0:T(8,128)(2,1)} %slice.301.k_ref) | copy-start | bytes 4718596
  150.0 28.1 %copy-start.16 = (s32[12,8,1024]{2,1,0:T(8,128)S(1)}, s32[12,8,1024]{2,1,0:T(8,128)}, u32[]{:S(2)}) copy-start(s32[12,8,1024]{2,1,0:T(8,128)} %copy-done.15) | copy-start | bytes 1179652
  150.0 28.1 %copy-start.22 = (s32[1,512,8]{2,1,0:T(8,128)S(1)}, s32[1,512,8]{2,1,0:T(8,128)}, u32[]{:S(2)}) copy-start(s32[1,512,8]{2,1,0:T(8,128)} %get-tuple-element.172.pcq_ref) | copy-start | bytes 49156
  285.7 19.4 %slice-start = ((s8[12582912]{0:T(1024)(128)(4,1)}), s8[4194304]{0:T(1024)(128)(4,1)S(1)}, s32[]{:S(2)}) async-start(s8[12582912]{0:T(1024)(128)(4,1)} %bitcast.153), calls=%async_computation.8 | async-start | bytes 8388608
  285.7 19.4 %slice-start.1 = ((s8[12582912]{0:T(1024)(128)(4,1)}), s8[4194304]{0:T(1024)(128)(4,1)S(1)}, s32[]{:S(2)}) async-start(s8[12582912]{0:T(1024)(128)(4,1)} %bitcast.153), calls=%async_computation.9 | async-start | bytes 8388608
  285.7 19.4 %slice-start.2 = ((s8[12582912]{0:T(1024)(128)(4,1)}), s8[4194304]{0:T(1024)(128)(4,1)S(1)}, s32[]{:S(2)}) async-start(s8[12582912]{0:T(1024)(128)(4,1)} %bitcast.153), calls=%async_computation.10 | async-start | bytes 8388608
  305.1 17.0 %copy-start.37 = (f32[1024,768]{0,1:T(8,128)S(1)}, f32[1024,768]{0,1:T(8,128)}, u32[]{:S(2)}) copy-start(f32[1024,768]{0,1:T(8,128)} %copy-done.35) | copy-start | bytes 9437188
  322.1 23.4 %copy-start.41 = (bf16[1024,3072]{1,0:T(8,128)(2,1)}, bf16[1024,3072]{1,0:T(8,128)(2,1)S(1)}, u32[]{:S(2)}) copy-start(bf16[1024,3072]{1,0:T(8,128)(2,1)S(1)} %get-tuple-element.145) | copy-start | bytes 18874372
  361.2 203.5 %reduce-scatter.7.cloned.1.call-start = ((), (), s32[]{:S(2)}) async-start(), calls=%async_computation.7 | async-start | bytes 4313088
  374.2 9.7 %copy-start.8 = (bf16[1,512,768]{2,1,0:T(8,128)(2,1)S(1)}, bf16[1,512,768]{2,1,0:T(8,128)(2,1)}, u32[]{:S(2)}) copy-start(bf16[1,512,768]{2,1,0:T(8,128)(2,1)} %copy-done.7) | copy-start | bytes 2359300
  374.2 9.7 %copy-start.10 = (bf16[1,512,768]{2,1,0:T(8,128)(2,1)S(1)}, bf16[1,512,768]{2,1,0:T(8,128)(2,1)}, u32[]{:S(2)}) copy-start(bf16[1,512,768]{2,1,0:T(8,128)(2,1)} %copy-done.9) | copy-start | bytes 2359300
  374.2 9.7 %copy-start.21 = (s32[12,8,512]{2,1,0:T(8,128)S(1)}, s32[12,8,512]{2,1,0:T(8,128)}, u32[]{:S(2)}) copy-start(s32[12,8,512]{2,1,0:T(8,128)} %slice.299.patk_ref) | copy-start | bytes 589828
  376.7 100.7 %collective-permute-start.2 = (bf16[1,512,768]{2,1,0:T(8,128)(2,1)}, bf16[1,512,768]{2,1,0:T(8,128)(2,1)}, u32[]{:S(2)}, u32[]{:S(2)}) collective-permute-start(bf16[1,512,768]{2,1,0:T(8,128)(2,1)} %bitcast.200), channel_id=1, source_target_pairs={{0,2},{2,0},{1,3},{3,1},{4,6},{6,4},{5,7},{7,5},{8,10},{10,8},{9,1... | collective-permute-start | bytes 2359304 | tf_op jit(solution)/shard_map/ppermute | solution.py:355
  377.8 101.4 %collective-permute-start.4 = (bf16[1,512,768]{2,1,0:T(8,128)(2,1)}, bf16[1,512,768]{2,1,0:T(8,128)(2,1)}, u32[]{:S(2)}, u32[]{:S(2)}) collective-permute-start(bf16[1,512,768]{2,1,0:T(8,128)(2,1)} %bitcast.201), channel_id=1, source_target_pairs={{0,3},{3,0},{1,2},{2,1},{4,7},{7,4},{5,6},{6,5},{8,11},{11,8},{9,1... | collective-permute-start | bytes 2359304 | tf_op jit(solution)/shard_map/ppermute | solution.py:357
  380.2 98.9 %collective-permute-start.3 = (bf16[1,512,768]{2,1,0:T(8,128)(2,1)}, bf16[1,512,768]{2,1,0:T(8,128)(2,1)}, u32[]{:S(2)}, u32[]{:S(2)}) collective-permute-start(bf16[1,512,768]{2,1,0:T(8,128)(2,1)} %bitcast.192), channel_id=1, source_target_pairs={{0,1},{1,0},{2,3},{3,2},{4,5},{5,4},{6,7},{7,6},{8,9},{9,8},{10,11... | collective-permute-start | bytes 2359304 | tf_op jit(solution)/shard_map/ppermute | solution.py:356
  384.0 32.6 %copy-start.4 = (bf16[1,1024,768]{2,1,0:T(8,128)(2,1)S(1)}, bf16[1,1024,768]{2,1,0:T(8,128)(2,1)}, u32[]{:S(2)}) copy-start(bf16[1,1024,768]{2,1,0:T(8,128)(2,1)} %copy-done.2) | copy-start | bytes 4718596
  384.0 32.6 %copy-start.12 = (bf16[1,1024,768]{2,1,0:T(8,128)(2,1)S(1)}, bf16[1,1024,768]{2,1,0:T(8,128)(2,1)}, u32[]{:S(2)}) copy-start(bf16[1,1024,768]{2,1,0:T(8,128)(2,1)} %slice.301.k_ref) | copy-start | bytes 4718596
  384.0 32.6 %copy-start.17 = (s32[12,8,1024]{2,1,0:T(8,128)S(1)}, s32[12,8,1024]{2,1,0:T(8,128)}, u32[]{:S(2)}) copy-start(s32[12,8,1024]{2,1,0:T(8,128)} %copy-done.15) | copy-start | bytes 1179652
  384.0 32.6 %copy-start.19 = (bf16[1,512,768]{2,1,0:T(8,128)(2,1)S(1)}, bf16[1,512,768]{2,1,0:T(8,128)(2,1)}, u32[]{:S(2)}) copy-start(bf16[1,512,768]{2,1,0:T(8,128)(2,1)} %copy-done.18) | copy-start | bytes 2359300
  384.0 32.6 %copy-start.23 = (s32[1,512,8]{2,1,0:T(8,128)S(1)}, s32[1,512,8]{2,1,0:T(8,128)}, u32[]{:S(2)}) copy-start(s32[1,512,8]{2,1,0:T(8,128)} %get-tuple-element.172.pcq_ref) | copy-start | bytes 49156
  513.4 16.7 %collective-permute-start.10 = (bf16[96,1,3456]{2,0,1:T(8,128)(2,1)}, bf16[96,1,3456]{2,0,1:T(8,128)(2,1)}, u32[]{:S(2)}, u32[]{:S(2)}) collective-permute-start(bf16[96,1,3456]{2,0,1:T(8,128)(2,1)} %constant_dynamic-slice_fusion), channel_id=1, source_target_pairs={{0,1},{1,0},{2,3},{3,2},{4,5},{5,4},{6,7},{7,6},{8,9},{9,8},{10,11... | collective-permute-start | bytes 1990664 | tf_op jit(solution)/shard_map/ppermute | solution.py:445
  522.3 20.7 %collective-permute-start.5 = (bf16[1,512,768]{2,1,0:T(8,128)(2,1)}, bf16[1,512,768]{2,1,0:T(8,128)(2,1)}, u32[]{:S(2)}, u32[]{:S(2)}) collective-permute-start(bf16[1,512,768]{2,1,0:T(8,128)(2,1)} %bitcast.202), channel_id=1, source_target_pairs={{0,2},{2,0},{1,3},{3,1},{4,6},{6,4},{5,7},{7,5},{8,10},{10,8},{9,1... | collective-permute-start | bytes 2359304 | tf_op jit(solution)/shard_map/ppermute | solution.py:355
  523.6 37.6 %collective-permute-start.7 = (bf16[1,512,768]{2,1,0:T(8,128)(2,1)}, bf16[1,512,768]{2,1,0:T(8,128)(2,1)}, u32[]{:S(2)}, u32[]{:S(2)}) collective-permute-start(bf16[1,512,768]{2,1,0:T(8,128)(2,1)} %bitcast.203), channel_id=1, source_target_pairs={{0,3},{3,0},{1,2},{2,1},{4,7},{7,4},{5,6},{6,5},{8,11},{11,8},{9,1... | collective-permute-start | bytes 2359304 | tf_op jit(solution)/shard_map/ppermute | solution.py:357
  525.9 35.3 %collective-permute-start.6 = (bf16[1,512,768]{2,1,0:T(8,128)(2,1)S(1)}, bf16[1,512,768]{2,1,0:T(8,128)(2,1)S(1)}, u32[]{:S(2)}, u32[]{:S(2)}) collective-permute-start(bf16[1,512,768]{2,1,0:T(8,128)(2,1)S(1)} %bitcast.194), channel_id=1, source_target_pairs={{0,1},{1,0},{2,3},{3,2},{4,5},{5,4},{6,7},{7,6},{8,9},{9,8},{10,11... | collective-permute-start | bytes 2359304 | tf_op jit(solution)/shard_map/ppermute | solution.py:356
  531.3 39.7 %collective-permute-start.11 = (bf16[96,1,3456]{2,0,1:T(8,128)(2,1)S(1)}, bf16[96,1,3456]{2,0,1:T(8,128)(2,1)S(1)}, u32[]{:S(2)}, u32[]{:S(2)}) collective-permute-start(bf16[96,1,3456]{2,0,1:T(8,128)(2,1)S(1)} %add_convert_fusion.3), channel_id=1, source_target_pairs={{0,2},{2,0},{1,3},{3,1},{4,6},{6,4},{5,7},{7,5},{8,10},{10,8},{9,1... | collective-permute-start | bytes 1990664 | tf_op jit(solution)/shard_map/ppermute | solution.py:452
  566.6 6.2 %collective-permute-start.8 = (bf16[104,3,384]{2,0,1:T(8,128)(2,1)S(1)}, bf16[104,3,384]{2,0,1:T(8,128)(2,1)S(1)}, u32[]{:S(2)}, u32[]{:S(2)}) collective-permute-start(bf16[104,3,384]{2,0,1:T(8,128)(2,1)S(1)} %copy.268), channel_id=1, source_target_pairs={{0,1},{1,0},{2,3},{3,2},{4,5},{5,4},{6,7},{7,6},{8,9},{9,8},{10,11... | collective-permute-start | bytes 718856 | tf_op jit(solution)/shard_map/ppermute | solution.py:445
  572.8 11.0 %copy-start.1 = (s32[4,2]{0,1:T(2,128)S(1)}, s32[4,2]{0,1:T(2,128)}, u32[]{:S(2)}) copy-start(s32[4,2]{0,1:T(2,128)} %param.21) | copy-start | bytes 100
  572.9 6.2 %collective-permute-start.9 = (bf16[104,3,384]{2,0,1:T(8,128)(2,1)S(1)}, bf16[104,3,384]{2,0,1:T(8,128)(2,1)S(1)}, u32[]{:S(2)}, u32[]{:S(2)}) collective-permute-start(bf16[104,3,384]{2,0,1:T(8,128)(2,1)S(1)} %add_convert_fusion.4), channel_id=1, source_target_pairs={{0,2},{2,0},{1,3},{3,1},{4,6},{6,4},{5,7},{7,5},{8,10},{10,8},{9,1... | collective-permute-start | bytes 718856 | tf_op jit(solution)/shard_map/ppermute | solution.py:452
  (33 other events, 117.9 us)
Sparse Core Ops, SparseCore 0:
  16.5 50.1 all-gather.7
  89.8 35.7 all-gather.9
  127.9 52.3 all-gather.11
  182.6 51.4 all-gather.13
  361.3 109.2 reduce-scatter.4
  511.3 45.0 reduce-scatter.6

commit v13 on v12

--- a/solution.py
+++ b/solution.py
@@ -697,6 +697,8 @@
     ).reshape(ns * (block_rows + extra_rows), planes, model_width)
     widened, attn_in_grad = lax.optimization_barrier((widened, attn_in_grad))
     qkv_share = shard_stage(widened, 0)
+    early_total = finish_stage(early_share, 1).reshape(early_share.shape[0], -1)
+    early_total, attn_in_grad = lax.optimization_barrier((early_total, attn_in_grad))
     input_part = norm_back(first_normed, first_inv, norm_gains[0], attn_in_grad)[0]
     input_low = (middle_grad + input_part).astype(jnp.bfloat16)
     qkv_total = finish_stage(qkv_share, 2)
@@ -714,7 +716,6 @@
             count *= size
         small_pieces.append(small_total[offset : offset + count].reshape(local_shape))
         offset += count
-    early_total = finish_stage(early_share, 1).reshape(early_share.shape[0], -1)
     down_width = early_widths[0] // nt
     up_width = early_widths[1] // nt
     grad_shares = (

time: 602 us -> 626 us (1.040)
  waiting for transfers between devices: 99.9 us -> 122 us
    ppermute x2, waiting for transfers between devices: 5.59 us -> 13.4 us  [pair_reduce(): received = lax.ppermute(sent, axis_name, perm=[(0, 1), (1, 0)])]
    ppermute x2, waiting for transfers between devices: 6.55 us -> 14.3 us  [pair_sum(): received = lax.ppermute(share, axis_name, perm=[(0, 1), (1, 0)])]
  transfers between devices with their start and end apart: 18 -> 18, of which waited for: 8 -> 10; matrix products, arithmetic and copies ran while one was open for 27% -> 26% of each run, Pallas kernels for 25% -> 24%
where the time goes in v13:
time: 626 us; the launch traced here: 615 us
  Pallas kernels  145 us (23%)
  local copies, waits for them, and re-layouts  143 us (23%)
  waiting for transfers between devices  122 us (19%)
  matrix products  89.4 us (14%)
  other arithmetic  82.8 us (13%)
  between operations  17.2 us (3%)
  starting transfers between devices  15.7 us (3%)
    pallas_call x2, Pallas kernels, attention_backward(): pl.pallas_call(attention_bwd_kernel, grid=grid, in_specs=[query_spec, key...  81.2 us
    pallas_call x2, Pallas kernels, attention_forward(): pl.pallas_call(attention_fwd_kernel, grid=grid, in_specs=[query_spec, key...  63.6 us
    all_gather x1, waiting for transfers between devices, gather_packed(): lax.all_gather(flat, ('shard', 'tensor'), axis=0, tiled=False)  50.3 us
    unnamed x139, local copies, waits for them, and re-layouts  38.5 us
    reshape x5, local copies, waits for them, and re-layouts, gather_weight(): stacked.reshape((ns, nt) + local_block.shape)  38.2 us
    dot_general x3, matrix products, back_dot(): lax.dot_general(left_rows, weight_rows, (((1,), (1,)), ((), ())), preferr...  31.1 us
    ppermute x2, waiting for transfers between devices, spread_sequence(): from_tensor = lax.ppermute(kept, 'tensor', perm=swap)  22 us
    reduce_sum x1, other arithmetic, backward_pass(): unit_bias_grad = jnp.sum(hidden_low, 0, dtype=jnp.float32)  17 us
  transfers between devices with their start and end apart: 18, of which 10 were waited for; matrix products, arithmetic and copies ran while one was open for 26% of the time, Pallas kernels for 24%

profile of v13, /device:TPU:0, one launch (start us, length us, event | category | flops | bytes accessed | tf_op | source)
XLA Modules:
  0.0 615.2 jit_solution(4751627065688709556)
XLA Ops:
  16.4 50.3 %all-gather.8.cloned.1.call-done = bf16[16,880,128]{2,1,0:T(8,128)(2,1)} async-done(((bf16[1,880,128]{2,1,0:T(8,128)(2,1)}), bf16[16,880,128]{2,1,0:T(8,128)(2,1)}) %all-gather.8.cloned.1.call-update) | async-done | bytes 3604496 | tf_op jit(solution)/shard_map/all_gather | solution.py:416
  66.7 6.7 %reshape.1738 = bf16[8,2,112640]{2,1,0:T(2,128)(2,1)} reshape(bf16[16,880,128]{2,1,0:T(8,128)(2,1)} %all-gather.8.cloned.1.call-done) | data formatting | bytes 7208960 | tf_op jit(solution)/shard_map/reshape | solution.py:416
  75.4 4.8 reshape.1782
  80.2 5.5 copy.202
  85.7 4.0 reshape.1740
  104.3 10.0 %collective-permute-done.1 = bf16[1,512,768]{1,2,0:T(8,128)(2,1)S(1)} collective-permute-done((bf16[1,512,768]{1,2,0:T(8,128)(2,1)}, bf16[1,512,768]{1,2,0:T(8,128)(2,1)S(1)}, u32[]{:S(2)}, u32[]{:S(2)}) %collective-permute-start.1) | collective-permute-done | bytes 786464 | tf_op jit(solution)/shard_map/ppermute | solution.py:763
  124.7 6.5 %fusion.81 = (bf16[3,1024,768]{2,1,0:T(8,128)(2,1)S(1)}, f32[3,1024,768]{2,1,0:T(8,128)S(1)}) fusion(bf16[3,768,768]{2,1,0:T(8,128)(2,1)} %reshape.1740, f32[768]{0:T(1024)S(1)} %mul.279, f32[1024]{0:T(1024)S(1)} %add_rsqrt_fusion.3, f32[1024]{0:T(1024)S(1)} %broadcast_multiply_fusion.11, bf16[512,768]{0,1:T(8,128)(2,1)S(1)} %bitcast.157, ...), kind=kOutput, calls=%fused_computation.287 | convolution fusion | flops 3637248000 | bytes 19278848 | tf_op jit(solution)/shard_map/rd,jde->jre/dot_general | solution.py:530
  150.0 28.0 %shard_map.256 = f32[1,512,768]{2,1,0:T(8,128)S(1)} custom-call(bf16[1,512,768]{2,1,0:T(8,128)(2,1)S(1)} %get-tuple-element.167.q_ref, bf16[1,512,768]{2,1,0:T(8,128)(2,1)S(1)} %slice.282.k_ref, bf16[1,512,768]{2,1,0:T(8,128)(2,1)S(1)} %slice.285.v_ref, s32[12,512,8]{2,1,0:T(8,128)} %copy.262.patq_ref, s32[12,8,512]{2,1,0:T(8,128)S(1)} %copy-done.20, ...), custom_call_target="tpu_custom_call" | custom-call | flops 1610612736 | bytes 5505024 | tf_op jit(solution)/shard_map/pallas_call | solution.py:217
  178.1 35.6 %shard_map.257 = f32[1,512,768]{2,1,0:T(8,128)S(1)} custom-call(bf16[1,512,768]{2,1,0:T(8,128)(2,1)S(1)} %get-tuple-element.168.q_ref, bf16[1,1024,768]{2,1,0:T(8,128)(2,1)S(1)} %copy-done.11, bf16[1,1024,768]{2,1,0:T(8,128)(2,1)S(1)} %copy-done.3, s32[12,512,8]{2,1,0:T(8,128)} %copy.263.patq_ref, s32[12,8,1024]{2,1,0:T(8,128)S(1)} %copy-done.16, ...), custom_call_target="tpu_custom_call" | custom-call | flops 3221225472 | bytes 8650752 | tf_op jit(solution)/shard_map/pallas_call | solution.py:217
  214.5 11.3 %reshape.1743 = bf16[8,2,384,96]{2,1,0,3:T(2,128)(2,1)} reshape(bf16[6144,96]{0,1:T(8,128)(2,1)} %all-gather.10.cloned.1.call-done) | data formatting | bytes 2359296 | tf_op jit(solution)/shard_map/reshape | solution.py:407
  232.1 9.4 %copy.214 = bf16[8,2,96,1536]{3,1,2,0:T(2,128)(2,1)} copy(bf16[8,2,96,1536]{3,2,1,0:T(8,128)(2,1)} %bitcast.179) | data formatting | bytes 9437184 | tf_op jit(solution)/shard_map/reshape | solution.py:407
  241.5 3.7 copy.274
  245.2 9.2 %fusion.71 = (f32[1024]{0:T(1024)S(1)}, f32[1024,3072]{1,0:T(8,128)S(1)}) fusion(f32[3072]{0:T(1024)S(1)} %reshape.1767, bf16[768,3072]{1,0:T(8,128)(2,1)S(1)} %bitcast.182, f32[1024,768]{0,1:T(8,128)S(1)} %copy-done.36, f32[768]{0:T(1024)S(1)} %mul.294, f32[1024]{0:T(1024)S(1)} %add_rsqrt_fusion.1, f32[1024]{0:T(1024)S(1)} %broadcast_multiply_fusion.9), kind=kOutput, calls=%fused_computation.278 | convolution fusion | flops 4866440192 | bytes 20474880 | tf_op jit(solution)/shard_map/dot_general | solution.py:551
  254.5 4.5 copy-done.24
  259.0 5.6 multiply_reduce_fusion.2
  264.6 7.7 %reshape.1748 = bf16[8,2,1536,96]{2,1,0,3:T(2,128)(2,1)} reshape(bf16[24576,96]{0,1:T(8,128)(2,1)} %all-gather.14.cloned.1.call-done) | data formatting | bytes 9437184 | tf_op jit(solution)/shard_map/reshape | solution.py:407
  272.2 7.7 %copy.219 = bf16[8,2,1536,96]{2,1,3,0:T(2,128)(2,1)} copy(bf16[8,2,1536,96]{2,1,0,3:T(2,128)(2,1)} %reshape.1748) | data formatting | bytes 9437184 | tf_op jit(solution)/shard_map/reshape | solution.py:407
  279.9 5.8 copy.275
  285.7 19.4 %multiply_reduce_fusion = (bf16[3072]{0:T(1024)(128)(2,1)S(1)}, f32[1024]{0:T(1024)S(1)}, f32[1024]{0:T(1024)S(1)}, f32[1024,3072]{1,0:T(8,128)}) fusion(f32[1024]{0:T(1024)S(1)} %add_rsqrt_fusion, f32[1024]{0:T(1024)S(1)} %broadcast_multiply_fusion.2, f32[1024,3072]{1,0:T(8,128)} %copy-done.24, f32[3072]{0:T(1024)S(1)} %reshape.1767, ...), kind=kOutput, calls=%fused_computation.9 | convolution fusion | flops 4892388352 | bytes 31504384 | tf_op jit(solution)/shard_map/dot_general | solution.py:65
  305.2 17.0 %convert_reduce_fusion = (bf16[3072]{0:T(1024)(128)(2,1)S(1)}, bf16[1024,3072]{1,0:T(8,128)(2,1)S(1)}, bf16[1024,3072]{1,0:T(8,128)(2,1)S(1)}) fusion(f32[1024]{0:T(1024)S(1)} %broadcast_multiply_fusion, f32[1024]{0:T(1024)S(1)} %broadcast_multiply_fusion.2, f32[1024,3072]{1,0:T(8,128)S(1)} %bitcast.154, f32[3072]{0:T(1024)S(1)} %reshape.1767, ...), kind=kLoop, calls=%fused_computation.10 | loop fusion | flops 103805952 | bytes 37795840 | tf_op jit(solution)/shard_map/reduce_sum | solution.py:613
  322.2 9.4 %multiply_reduce_fusion.5 = (bf16[768]{0:T(1024)(128)(2,1)S(1)}, f32[1024]{0:T(1024)S(1)}, f32[1024]{0:T(1024)S(1)}, f32[1024,768]{0,1:T(8,128)S(1)}) fusion(f32[1024,768]{0,1:T(8,128)S(1)} %copy-done.37, f32[1024]{0:T(1024)S(1)} %add_rsqrt_fusion.1, f32[1024]{0:T(1024)S(1)} %broadcast_multiply_fusion.9, f32[768]{0:T(1024)S(1)} %mul.294, ...), kind=kOutput, calls=%fused_computation.61 | convolution fusion | flops 4838126592 | bytes 17322496 | tf_op jit(solution)/shard_map/dot_general | solution.py:65
  331.6 3.6 convert_reduce_fusion.5
  335.2 2.3 multiply_reduce_fusion.4
  337.6 2.7 fusion.36
  340.3 5.4 convolution_convert_fusion
  345.7 6.8 %convolution_convert_fusion.1 = bf16[768,3072]{1,0:T(8,128)(2,1)S(1)} fusion(bf16[1024,3072]{1,0:T(8,128)(2,1)S(1)} %get-tuple-element.149, bf16[512,768]{0,1:T(8,128)(2,1)} %bitcast.1, bf16[512,768]{0,1:T(8,128)(2,1)S(1)} %bitcast.191, pred[]{:T(512)S(6)} %eq.182), kind=kOutput, calls=%fused_computation.20 | convolution fusion | flops 4841275392 | bytes 12582913 | tf_op jit(solution)/shard_map/dot_general | solution.py:59
  352.5 2.4 multiply_convert_fusion.1
  356.6 4.7 pad_maximum_fusion
  363.2 9.8 %add_convert_fusion = bf16[1024,768]{0,1:T(8,128)(2,1)S(1)} fusion(f32[1024,768]{0,1:T(8,128)S(1)} %copy-done.38, bf16[1024,3072]{1,0:T(8,128)(2,1)} %copy-done.41, bf16[3072,768]{0,1:T(8,128)(2,1)} %bitcast.181, f32[768]{0:T(1024)S(1)} %add.737), kind=kOutput, calls=%fused_computation.62 | convolution fusion | flops 4834197504 | bytes 15731712 | tf_op jit(solution)/shard_map/dot_general | solution.py:556
  374.4 2.5 copy.227
  379.6 31.3 %shard_map.258 = (bf16[1,512,768]{2,1,0:T(8,128)(2,1)S(1)}, f32[1,512,768]{2,1,0:T(8,128)S(1)}, f32[1,512,768]{2,1,0:T(8,128)}) custom-call(bf16[1,512,768]{2,1,0:T(8,128)(2,1)S(1)} %copy-done.10, bf16[1,512,768]{2,1,0:T(8,128)(2,1)S(1)} %copy-done.6, bf16[1,512,768]{2,1,0:T(8,128)(2,1)S(1)} %copy-done.8, ...), custom_call_target="tpu_custom_call" | custom-call | flops 4026531840 | bytes 11010048 | tf_op jit(solution)/shard_map/pallas_call | solution.py:244
  412.2 49.9 %shard_map.259 = (bf16[1,512,768]{2,1,0:T(8,128)(2,1)S(1)}, f32[1,1024,768]{2,1,0:T(8,128)}, f32[1,1024,768]{2,1,0:T(8,128)}) custom-call(bf16[1,512,768]{2,1,0:T(8,128)(2,1)S(1)} %copy-done.19, bf16[1,1024,768]{2,1,0:T(8,128)(2,1)S(1)} %copy-done.12, bf16[1,1024,768]{2,1,0:T(8,128)(2,1)S(1)} %copy-done.4, ...), custom_call_target="tpu_custom_call" | custom-call | flops 8053063680 | bytes 20447232 | tf_op jit(solution)/shard_map/pallas_call | solution.py:244
  462.5 4.1 convert_reduce_fusion.3
  467.2 2.3 copy.226
  472.6 2.4 add_convert_fusion.2
  474.9 2.7 pad_maximum_fusion.2
  479.3 8.1 %collective-permute-done.3 = bf16[1,512,768]{2,1,0:T(8,128)(2,1)} collective-permute-done((bf16[1,512,768]{2,1,0:T(8,128)(2,1)}, bf16[1,512,768]{2,1,0:T(8,128)(2,1)}, u32[]{:S(2)}, u32[]{:S(2)}) %collective-permute-start.3) | collective-permute-done | bytes 786464 | tf_op jit(solution)/shard_map/ppermute | solution.py:356
  491.5 8.2 %fusion.37 = bf16[768,3,768]{2,0,1:T(8,128)(2,1)} fusion(bf16[3,1024,768]{2,1,0:T(8,128)(2,1)} %pad_maximum_fusion.2, f32[768]{0:T(1024)S(1)} %copy-done.57, f32[1024]{0:T(1024)S(1)} %copy-done.55, f32[1024]{0:T(1024)S(1)} %copy-done.53, bf16[512,768]{0,1:T(8,128)(2,1)S(1)} %bitcast.168, bf16[512,768]{0,1:T(8,128)(2,1)S(1)} %bitcast.160, pred[]{:T(512)S(6)} %eq.182), kind=kOutput, calls=%fused_computation.97 | convolution fusion | flops 3634888704 | bytes 9841665 | tf_op jit(solution)/shard_map/rd,jre->dje/dot_general | solution.py:662
  499.7 7.9 %convolution_bitcast_fusion.1 = f32[1024,768]{1,0:T(8,128)} fusion(bf16[3,1024,768]{2,1,0:T(8,128)(2,1)} %pad_maximum_fusion.2, bf16[3,768,768]{2,1,0:T(8,128)(2,1)S(1)} %copy-done.45), kind=kOutput, calls=%fused_computation.77 | convolution fusion | flops 3623878656 | bytes 11403264 | tf_op jit(solution)/shard_map/jre,jde->rd/dot_general | solution.py:667
  507.6 3.6 copy.228
  511.2 2.6 fusion.14
  522.2 12.5 %collective-permute-done.5 = bf16[96,1,3456]{2,0,1:T(8,128)(2,1)S(1)} collective-permute-done((bf16[96,1,3456]{2,0,1:T(8,128)(2,1)S(1)}, bf16[96,1,3456]{2,0,1:T(8,128)(2,1)S(1)}, u32[]{:S(2)}, u32[]{:S(2)}) %collective-permute-start.5) | collective-permute-done | bytes 663584 | tf_op jit(solution)/shard_map/ppermute | solution.py:445
  536.4 11.6 %collective-permute-done.6 = bf16[96,1,3456]{2,0,1:T(8,128)(2,1)S(1)} collective-permute-done((bf16[96,1,3456]{2,0,1:T(8,128)(2,1)S(1)}, bf16[96,1,3456]{2,0,1:T(8,128)(2,1)S(1)}, u32[]{:S(2)}, u32[]{:S(2)}) %collective-permute-start.6) | collective-permute-done | bytes 663584 | tf_op jit(solution)/shard_map/ppermute | solution.py:452
  549.3 2.4 copy.237
  551.7 3.0 multiply_reduce_fusion.10
  569.4 9.4 %collective-permute-done.7 = bf16[1,512,768]{2,1,0:T(8,128)(2,1)} collective-permute-done((bf16[1,512,768]{2,1,0:T(8,128)(2,1)}, bf16[1,512,768]{2,1,0:T(8,128)(2,1)}, u32[]{:S(2)}, u32[]{:S(2)}) %collective-permute-start.7) | collective-permute-done | bytes 786464 | tf_op jit(solution)/shard_map/ppermute | solution.py:355
  580.6 14.0 %collective-permute-done.8 = bf16[1,512,768]{2,1,0:T(8,128)(2,1)S(1)} collective-permute-done((bf16[1,512,768]{2,1,0:T(8,128)(2,1)S(1)}, bf16[1,512,768]{2,1,0:T(8,128)(2,1)S(1)}, u32[]{:S(2)}, u32[]{:S(2)}) %collective-permute-start.8) | collective-permute-done | bytes 786464 | tf_op jit(solution)/shard_map/ppermute | solution.py:356
  600.7 2.7 collective-permute-done.11
  (344 shorter events, 117.3 us)
Async XLA Ops:
  7.2 90.0 %copy-start = (s32[4,2]{0,1:T(2,128)S(1)}, s32[4,2]{0,1:T(2,128)}, u32[]{:S(2)}) copy-start(s32[4,2]{0,1:T(2,128)} %param.21) | copy-start | bytes 100
  7.2 59.5 %all-gather.8.cloned.1.call-start = ((), (), s32[]{:S(2)}) async-start(), calls=%async_computation.2 | async-start | bytes 3829760 | tf_op jit(solution)/shard_map/all_gather | solution.py:416
  16.4 198.1 %all-gather.10.cloned.1.call-start = ((), (), s32[]{:S(2)}) async-start(), calls=%async_computation.4 | async-start | bytes 1253376 | tf_op jit(solution)/shard_map/all_gather | solution.py:406
  89.7 142.3 %all-gather.12.cloned.1.call-start = ((), (), s32[]{:S(2)}) async-start(), calls=%async_computation.5 | async-start | bytes 5013504 | tf_op jit(solution)/shard_map/all_gather | solution.py:406
  90.4 174.1 %all-gather.14.cloned.1.call-start = ((), (), s32[]{:S(2)}) async-start(), calls=%async_computation.6 | async-start | bytes 5013504 | tf_op jit(solution)/shard_map/all_gather | solution.py:406
  93.7 20.6 %collective-permute-start.1 = (bf16[1,512,768]{1,2,0:T(8,128)(2,1)}, bf16[1,512,768]{1,2,0:T(8,128)(2,1)S(1)}, u32[]{:S(2)}, u32[]{:S(2)}) collective-permute-start(bf16[1,512,768]{1,2,0:T(8,128)(2,1)} %copy.260), channel_id=1, source_target_pairs={{0,2},{2,0},{1,3},{3,1},{4,6},{6,4},{5,7},{7,5},{8,10},{10,8},{9,1... | collective-permute-start | bytes 2359304 | tf_op jit(solution)/shard_map/ppermute | solution.py:763
  96.4 189.3 %collective-permute-start = (bf16[1,512,768]{1,2,0:T(8,128)(2,1)}, bf16[1,512,768]{1,2,0:T(8,128)(2,1)}, u32[]{:S(2)}, u32[]{:S(2)}) collective-permute-start(bf16[1,512,768]{1,2,0:T(8,128)(2,1)} %copy.259), channel_id=1, source_target_pairs={{0,2},{2,0},{1,3},{3,1},{4,6},{6,4},{5,7},{7,5},{8,10},{10,8},{9,1... | collective-permute-start | bytes 2359304 | tf_op jit(solution)/shard_map/ppermute | solution.py:763
  97.2 27.4 %copy-start.25 = (bf16[1,512,768]{1,2,0:T(8,128)(2,1)}, bf16[1,512,768]{1,2,0:T(8,128)(2,1)S(1)}, u32[]{:S(2)}) copy-start(bf16[1,512,768]{1,2,0:T(8,128)(2,1)S(1)} %copy.196) | copy-start | bytes 2359300
  100.6 15.2 %slice-start.4 = ((bf16[8,2,112640]{2,1,0:T(2,128)(2,1)}), bf16[8,2,96]{2,1,0:T(2,128)(2,1)S(1)}, s32[]{:S(2)}) async-start(bf16[8,2,112640]{2,1,0:T(2,128)(2,1)} %reshape.1738), calls=%async_computation.12 | async-start | bytes 8192 | tf_op jit(solution)/shard_map/slice | solution.py:420
  101.8 13.7 %copy-start.33 = (bf16[8,2,112640]{2,1,0:T(2,128)(2,1)S(1)}, bf16[8,2,112640]{2,1,0:T(2,128)(2,1)}, u32[]{:S(2)}) copy-start(bf16[8,2,112640]{2,1,0:T(2,128)(2,1)} %reshape.1738) | copy-start | bytes 10813444
  114.3 16.9 %copy-start.29 = (bf16[1,512,768]{1,2,0:T(8,128)(2,1)}, bf16[1,512,768]{1,2,0:T(8,128)(2,1)S(1)}, u32[]{:S(2)}) copy-start(bf16[1,512,768]{1,2,0:T(8,128)(2,1)S(1)} %collective-permute-done.1) | copy-start | bytes 2359300
  114.8 16.4 %copy-start.52 = (f32[1024]{0:T(1024)}, f32[1024]{0:T(1024)S(1)}, u32[]{:S(2)}) copy-start(f32[1024]{0:T(1024)S(1)} %broadcast_multiply_fusion.11) | copy-start | bytes 12292
  115.5 15.8 %copy-start.54 = (f32[1024]{0:T(1024)}, f32[1024]{0:T(1024)S(1)}, u32[]{:S(2)}) copy-start(f32[1024]{0:T(1024)S(1)} %add_rsqrt_fusion.3) | copy-start | bytes 12292
  115.8 15.5 %copy-start.56 = (f32[768]{0:T(1024)}, f32[768]{0:T(1024)S(1)}, u32[]{:S(2)}) copy-start(f32[768]{0:T(1024)S(1)} %mul.279) | copy-start | bytes 9220
  124.4 367.1 %reduce-scatter.5.cloned.1.call-start = ((), (), s32[]{:S(2)}) async-start(), calls=%async_computation.3 | async-start | bytes 11943936 | tf_op jit(solution)/shard_map/reduce_scatter | solution.py:515
  134.0 14.8 %copy-start.5 = (bf16[1,512,768]{2,1,0:T(8,128)(2,1)}, bf16[1,512,768]{2,1,0:T(8,128)(2,1)S(1)}, u32[]{:S(2)}) copy-start(bf16[1,512,768]{2,1,0:T(8,128)(2,1)S(1)} %slice.282.k_ref) | copy-start | bytes 2359300
  136.8 12.1 %copy-start.7 = (bf16[1,512,768]{2,1,0:T(8,128)(2,1)}, bf16[1,512,768]{2,1,0:T(8,128)(2,1)S(1)}, u32[]{:S(2)}) copy-start(bf16[1,512,768]{2,1,0:T(8,128)(2,1)S(1)} %slice.285.v_ref) | copy-start | bytes 2359300
  148.8 29.3 %copy-start.9 = (bf16[1,512,768]{2,1,0:T(8,128)(2,1)}, bf16[1,512,768]{2,1,0:T(8,128)(2,1)S(1)}, u32[]{:S(2)}) copy-start(bf16[1,512,768]{2,1,0:T(8,128)(2,1)S(1)} %get-tuple-element.167.q_ref) | copy-start | bytes 2359300
  148.8 29.3 %copy-start.18 = (bf16[1,512,768]{2,1,0:T(8,128)(2,1)}, bf16[1,512,768]{2,1,0:T(8,128)(2,1)S(1)}, u32[]{:S(2)}) copy-start(bf16[1,512,768]{2,1,0:T(8,128)(2,1)S(1)} %get-tuple-element.168.q_ref) | copy-start | bytes 2359300
  150.0 28.1 %copy-start.3 = (bf16[1,1024,768]{2,1,0:T(8,128)(2,1)S(1)}, bf16[1,1024,768]{2,1,0:T(8,128)(2,1)}, u32[]{:S(2)}) copy-start(bf16[1,1024,768]{2,1,0:T(8,128)(2,1)} %copy-done.2) | copy-start | bytes 4718596
  150.0 28.1 %copy-start.11 = (bf16[1,1024,768]{2,1,0:T(8,128)(2,1)S(1)}, bf16[1,1024,768]{2,1,0:T(8,128)(2,1)}, u32[]{:S(2)}) copy-start(bf16[1,1024,768]{2,1,0:T(8,128)(2,1)} %slice.301.k_ref) | copy-start | bytes 4718596
  150.0 28.1 %copy-start.16 = (s32[12,8,1024]{2,1,0:T(8,128)S(1)}, s32[12,8,1024]{2,1,0:T(8,128)}, u32[]{:S(2)}) copy-start(s32[12,8,1024]{2,1,0:T(8,128)} %copy-done.15) | copy-start | bytes 1179652
  150.0 28.1 %copy-start.22 = (s32[1,512,8]{2,1,0:T(8,128)S(1)}, s32[1,512,8]{2,1,0:T(8,128)}, u32[]{:S(2)}) copy-start(s32[1,512,8]{2,1,0:T(8,128)} %get-tuple-element.176.pcq_ref) | copy-start | bytes 49156
  245.2 9.3 %copy-start.44 = (bf16[96,8,2,1536]{3,1,2,0:T(8,128)(2,1)}, bf16[96,8,2,1536]{3,1,2,0:T(8,128)(2,1)S(1)}, u32[]{:S(2)}) copy-start(bf16[96,8,2,1536]{3,1,2,0:T(8,128)(2,1)S(1)} %copy.274) | copy-start | bytes 14155780
  285.7 19.5 %slice-start = ((s8[12582912]{0:T(1024)(128)(4,1)}), s8[4194304]{0:T(1024)(128)(4,1)S(1)}, s32[]{:S(2)}) async-start(s8[12582912]{0:T(1024)(128)(4,1)} %bitcast.153), calls=%async_computation.8 | async-start | bytes 8388608
  285.7 19.5 %slice-start.1 = ((s8[12582912]{0:T(1024)(128)(4,1)}), s8[4194304]{0:T(1024)(128)(4,1)S(1)}, s32[]{:S(2)}) async-start(s8[12582912]{0:T(1024)(128)(4,1)} %bitcast.153), calls=%async_computation.9 | async-start | bytes 8388608
  285.7 19.5 %slice-start.2 = ((s8[12582912]{0:T(1024)(128)(4,1)}), s8[4194304]{0:T(1024)(128)(4,1)S(1)}, s32[]{:S(2)}) async-start(s8[12582912]{0:T(1024)(128)(4,1)} %bitcast.153), calls=%async_computation.10 | async-start | bytes 8388608
  305.2 17.0 %copy-start.37 = (f32[1024,768]{0,1:T(8,128)S(1)}, f32[1024,768]{0,1:T(8,128)}, u32[]{:S(2)}) copy-start(f32[1024,768]{0,1:T(8,128)} %copy-done.35) | copy-start | bytes 9437188
  322.2 23.5 %copy-start.41 = (bf16[1024,3072]{1,0:T(8,128)(2,1)}, bf16[1024,3072]{1,0:T(8,128)(2,1)S(1)}, u32[]{:S(2)}) copy-start(bf16[1024,3072]{1,0:T(8,128)(2,1)S(1)} %get-tuple-element.149) | copy-start | bytes 18874372
  361.4 204.6 %reduce-scatter.7.cloned.1.call-start = ((), (), s32[]{:S(2)}) async-start(), calls=%async_computation.7 | async-start | bytes 4313088
  376.8 100.8 %collective-permute-start.2 = (bf16[1,512,768]{2,1,0:T(8,128)(2,1)}, bf16[1,512,768]{2,1,0:T(8,128)(2,1)}, u32[]{:S(2)}, u32[]{:S(2)}) collective-permute-start(bf16[1,512,768]{2,1,0:T(8,128)(2,1)} %bitcast.200), channel_id=1, source_target_pairs={{0,2},{2,0},{1,3},{3,1},{4,6},{6,4},{5,7},{7,5},{8,10},{10,8},{9,1... | collective-permute-start | bytes 2359304 | tf_op jit(solution)/shard_map/ppermute | solution.py:355
  377.8 109.5 %collective-permute-start.4 = (bf16[1,512,768]{2,1,0:T(8,128)(2,1)}, bf16[1,512,768]{2,1,0:T(8,128)(2,1)}, u32[]{:S(2)}, u32[]{:S(2)}) collective-permute-start(bf16[1,512,768]{2,1,0:T(8,128)(2,1)} %bitcast.201), channel_id=1, source_target_pairs={{0,3},{3,0},{1,2},{2,1},{4,7},{7,4},{5,6},{6,5},{8,11},{11,8},{9,1... | collective-permute-start | bytes 2359304 | tf_op jit(solution)/shard_map/ppermute | solution.py:357
  379.6 32.6 %copy-start.4 = (bf16[1,1024,768]{2,1,0:T(8,128)(2,1)S(1)}, bf16[1,1024,768]{2,1,0:T(8,128)(2,1)}, u32[]{:S(2)}) copy-start(bf16[1,1024,768]{2,1,0:T(8,128)(2,1)} %copy-done.2) | copy-start | bytes 4718596
  379.6 32.6 %copy-start.12 = (bf16[1,1024,768]{2,1,0:T(8,128)(2,1)S(1)}, bf16[1,1024,768]{2,1,0:T(8,128)(2,1)}, u32[]{:S(2)}) copy-start(bf16[1,1024,768]{2,1,0:T(8,128)(2,1)} %slice.301.k_ref) | copy-start | bytes 4718596
  379.6 32.6 %copy-start.17 = (s32[12,8,1024]{2,1,0:T(8,128)S(1)}, s32[12,8,1024]{2,1,0:T(8,128)}, u32[]{:S(2)}) copy-start(s32[12,8,1024]{2,1,0:T(8,128)} %copy-done.15) | copy-start | bytes 1179652
  379.6 32.6 %copy-start.19 = (bf16[1,512,768]{2,1,0:T(8,128)(2,1)S(1)}, bf16[1,512,768]{2,1,0:T(8,128)(2,1)}, u32[]{:S(2)}) copy-start(bf16[1,512,768]{2,1,0:T(8,128)(2,1)} %copy-done.18) | copy-start | bytes 2359300
  379.6 32.6 %copy-start.23 = (s32[1,512,8]{2,1,0:T(8,128)S(1)}, s32[1,512,8]{2,1,0:T(8,128)}, u32[]{:S(2)}) copy-start(s32[1,512,8]{2,1,0:T(8,128)} %get-tuple-element.176.pcq_ref) | copy-start | bytes 49156
  462.5 10.0 %copy-start.14 = (f32[1,512,768]{2,1,0:T(8,128)S(1)}, f32[1,512,768]{2,1,0:T(8,128)}, u32[]{:S(2)}) copy-start(f32[1,512,768]{2,1,0:T(8,128)} %copy-done.13) | copy-start | bytes 4718596
  469.5 17.8 %collective-permute-start.3 = (bf16[1,512,768]{2,1,0:T(8,128)(2,1)}, bf16[1,512,768]{2,1,0:T(8,128)(2,1)}, u32[]{:S(2)}, u32[]{:S(2)}) collective-permute-start(bf16[1,512,768]{2,1,0:T(8,128)(2,1)} %bitcast.192), channel_id=1, source_target_pairs={{0,1},{1,0},{2,3},{3,2},{4,5},{5,4},{6,7},{7,6},{8,9},{9,8},{10,11... | collective-permute-start | bytes 2359304 | tf_op jit(solution)/shard_map/ppermute | solution.py:356
  491.5 8.3 %copy-start.45 = (bf16[3,768,768]{2,1,0:T(8,128)(2,1)S(1)}, bf16[3,768,768]{2,1,0:T(8,128)(2,1)}, u32[]{:S(2)}) copy-start(bf16[3,768,768]{2,1,0:T(8,128)(2,1)} %reshape.1740) | copy-start | bytes 10616836
  520.7 14.0 %collective-permute-start.5 = (bf16[96,1,3456]{2,0,1:T(8,128)(2,1)S(1)}, bf16[96,1,3456]{2,0,1:T(8,128)(2,1)S(1)}, u32[]{:S(2)}, u32[]{:S(2)}) collective-permute-start(bf16[96,1,3456]{2,0,1:T(8,128)(2,1)S(1)} %constant_dynamic-slice_fusion.4), channel_id=1, source_target_pairs={{0,1},{1,0},{2,3},{3,2},{4,5},{5,4},{6,7},{7,6},{8,9},{9,8},{10,11... | collective-permute-start | bytes 1990664 | tf_op jit(solution)/shard_map/ppermute | solution.py:445
  534.8 13.2 %collective-permute-start.6 = (bf16[96,1,3456]{2,0,1:T(8,128)(2,1)S(1)}, bf16[96,1,3456]{2,0,1:T(8,128)(2,1)S(1)}, u32[]{:S(2)}, u32[]{:S(2)}) collective-permute-start(bf16[96,1,3456]{2,0,1:T(8,128)(2,1)S(1)} %add_convert_fusion.3), channel_id=1, source_target_pairs={{0,2},{2,0},{1,3},{3,1},{4,6},{6,4},{5,7},{7,5},{8,10},{10,8},{9,1... | collective-permute-start | bytes 1990664 | tf_op jit(solution)/shard_map/ppermute | solution.py:452
  558.1 20.7 %collective-permute-start.7 = (bf16[1,512,768]{2,1,0:T(8,128)(2,1)}, bf16[1,512,768]{2,1,0:T(8,128)(2,1)}, u32[]{:S(2)}, u32[]{:S(2)}) collective-permute-start(bf16[1,512,768]{2,1,0:T(8,128)(2,1)} %bitcast.202), channel_id=1, source_target_pairs={{0,2},{2,0},{1,3},{3,1},{4,6},{6,4},{5,7},{7,5},{8,10},{10,8},{9,1... | collective-permute-start | bytes 2359304 | tf_op jit(solution)/shard_map/ppermute | solution.py:355
  559.7 34.8 %collective-permute-start.9 = (bf16[1,512,768]{2,1,0:T(8,128)(2,1)}, bf16[1,512,768]{2,1,0:T(8,128)(2,1)}, u32[]{:S(2)}, u32[]{:S(2)}) collective-permute-start(bf16[1,512,768]{2,1,0:T(8,128)(2,1)} %bitcast.203), channel_id=1, source_target_pairs={{0,3},{3,0},{1,2},{2,1},{4,7},{7,4},{5,6},{6,5},{8,11},{11,8},{9,1... | collective-permute-start | bytes 2359304 | tf_op jit(solution)/shard_map/ppermute | solution.py:357
  560.6 33.9 %collective-permute-start.8 = (bf16[1,512,768]{2,1,0:T(8,128)(2,1)S(1)}, bf16[1,512,768]{2,1,0:T(8,128)(2,1)S(1)}, u32[]{:S(2)}, u32[]{:S(2)}) collective-permute-start(bf16[1,512,768]{2,1,0:T(8,128)(2,1)S(1)} %bitcast.194), channel_id=1, source_target_pairs={{0,1},{1,0},{2,3},{3,2},{4,5},{5,4},{6,7},{7,6},{8,9},{9,8},{10,11... | collective-permute-start | bytes 2359304 | tf_op jit(solution)/shard_map/ppermute | solution.py:356
  567.9 29.2 %collective-permute-start.10 = (bf16[104,3,384]{2,0,1:T(8,128)(2,1)S(1)}, bf16[104,3,384]{2,0,1:T(8,128)(2,1)S(1)}, u32[]{:S(2)}, u32[]{:S(2)}) collective-permute-start(bf16[104,3,384]{2,0,1:T(8,128)(2,1)S(1)} %copy.268), channel_id=1, source_target_pairs={{0,1},{1,0},{2,3},{3,2},{4,5},{5,4},{6,7},{7,6},{8,9},{9,8},{10,11... | collective-permute-start | bytes 718856 | tf_op jit(solution)/shard_map/ppermute | solution.py:445
  597.2 6.2 %collective-permute-start.11 = (bf16[104,3,384]{2,0,1:T(8,128)(2,1)S(1)}, bf16[104,3,384]{2,0,1:T(8,128)(2,1)S(1)}, u32[]{:S(2)}, u32[]{:S(2)}) collective-permute-start(bf16[104,3,384]{2,0,1:T(8,128)(2,1)S(1)} %add_convert_fusion.4), channel_id=1, source_target_pairs={{0,2},{2,0},{1,3},{3,1},{4,6},{6,4},{5,7},{7,5},{8,10},{10,8},{9,1... | collective-permute-start | bytes 718856 | tf_op jit(solution)/shard_map/ppermute | solution.py:452
  598.8 9.4 %copy-start.1 = (s32[4,2]{0,1:T(2,128)S(1)}, s32[4,2]{0,1:T(2,128)}, u32[]{:S(2)}) copy-start(s32[4,2]{0,1:T(2,128)} %param.21) | copy-start | bytes 100
  (33 other events, 102.3 us)
Sparse Core Ops, SparseCore 0:
  16.5 50.1 all-gather.7
  89.8 35.7 all-gather.9
  127.9 52.3 all-gather.11
  182.6 51.4 all-gather.13
  361.5 109.2 reduce-scatter.4
  519.5 46.4 reduce-scatter.6

commit v14 on v11

--- a/solution.py
+++ b/solution.py
@@ -208,7 +208,7 @@
 def attention_forward(query, keys, values, codes):
     seq_count, local_len, width = query.shape
     seq_len = keys.shape[1]
-    block_q = min(256, local_len)
+    block_q = min(128, local_len)
     grid = (seq_count, width // (PAIR * HD), local_len // block_q)
     query_spec, key_spec, patq_spec, patk_spec, pcq_spec, pck_spec = attention_specs(
         seq_count, local_len, seq_len, block_q
@@ -235,7 +235,7 @@
 def attention_backward(query, keys, values, grad_out, codes):
     seq_count, local_len, width = query.shape
     seq_len = keys.shape[1]
-    block_q = min(256, local_len)
+    block_q = min(128, local_len)
     grid = (seq_count, width // (PAIR * HD), local_len // block_q)
     query_spec, key_spec, patq_spec, patk_spec, pcq_spec, pck_spec = attention_specs(
         seq_count, local_len, seq_len, block_q

time: 592 us -> 603 us (1.019)
  Pallas kernels: 144 us -> 154 us
    pallas_call x2, Pallas kernels: 80.3 us -> 91.4 us  [attention_backward(): pl.pallas_call(attention_bwd_kernel, grid=grid, in_specs=[query_spec, key...]
  transfers between devices with their start and end apart: 18 -> 18, of which waited for: 8 -> 8; matrix products, arithmetic and copies ran while one was open for 26% -> 25% of each run, Pallas kernels for 24% -> 26%
where the time goes in v14:
time: 603 us; the launch traced here: 598 us
  Pallas kernels  154 us (26%)
  local copies, waits for them, and re-layouts  129 us (21%)
  waiting for transfers between devices  109 us (18%)
  matrix products  94.9 us (16%)
  other arithmetic  78.2 us (13%)
  between operations  17.3 us (3%)
  starting transfers between devices  15.7 us (3%)
    pallas_call x2, Pallas kernels, attention_backward(): pl.pallas_call(attention_bwd_kernel, grid=grid, in_specs=[query_spec, key...  91.4 us
    pallas_call x2, Pallas kernels, attention_forward(): pl.pallas_call(attention_fwd_kernel, grid=grid, in_specs=[query_spec, key...  63 us
    all_gather x1, waiting for transfers between devices, gather_packed(): lax.all_gather(flat, ('shard', 'tensor'), axis=0, tiled=False)  50.3 us
    unnamed x150, local copies, waits for them, and re-layouts  40.5 us
    dot_general x3, matrix products, back_dot(): lax.dot_general(left_rows, weight_rows, (((1,), (1,)), ((), ())), preferr...  31.4 us
    reshape x5, local copies, waits for them, and re-layouts, gather_weight(): stacked.reshape((ns, nt) + local_block.shape)  29.4 us
    ppermute x2, waiting for transfers between devices, pair_reduce(): received = lax.ppermute(sent, axis_name, perm=[(0, 1), (1, 0)])  29.3 us
    reduce_sum x1, other arithmetic, backward_pass(): unit_bias_grad = jnp.sum(hidden_low, 0, dtype=jnp.float32)  16.6 us
  transfers between devices with their start and end apart: 18, of which 8 were waited for; matrix products, arithmetic and copies ran while one was open for 25% of the time, Pallas kernels for 26%

profile of v14, /device:TPU:0, one launch (start us, length us, event | category | flops | bytes accessed | tf_op | source)
XLA Modules:
  0.0 597.9 jit_solution(4189838131198268778)
XLA Ops:
  16.4 50.3 %all-gather.8.cloned.1.call-done = bf16[16,880,128]{2,1,0:T(8,128)(2,1)} async-done(((bf16[1,880,128]{2,1,0:T(8,128)(2,1)}), bf16[16,880,128]{2,1,0:T(8,128)(2,1)}) %all-gather.8.cloned.1.call-update) | async-done | bytes 3604496 | tf_op jit(solution)/shard_map/all_gather | solution.py:416
  66.7 6.6 %reshape.1748 = bf16[8,2,112640]{2,1,0:T(2,128)(2,1)} reshape(bf16[16,880,128]{2,1,0:T(8,128)(2,1)} %all-gather.8.cloned.1.call-done) | data formatting | bytes 7208960 | tf_op jit(solution)/shard_map/reshape | solution.py:416
  75.4 4.8 reshape.1791
  80.1 5.5 copy.194
  85.6 4.0 reshape.1750
  90.8 2.9 constant_dynamic-slice_fusion.8
  96.3 2.3 copy.249
  107.1 8.4 %collective-permute-done.1 = bf16[1,512,768]{1,2,0:T(8,128)(2,1)S(1)} collective-permute-done((bf16[1,512,768]{1,2,0:T(8,128)(2,1)}, bf16[1,512,768]{1,2,0:T(8,128)(2,1)S(1)}, u32[]{:S(2)}, u32[]{:S(2)}) %collective-permute-start.1) | collective-permute-done | bytes 786464 | tf_op jit(solution)/shard_map/ppermute | solution.py:760
  117.0 9.5 %fusion.86 = (bf16[3,1024,768]{2,1,0:T(8,128)(2,1)S(1)}, f32[3,1024,768]{2,1,0:T(8,128)}) fusion(bf16[3,768,768]{2,1,0:T(8,128)(2,1)} %reshape.1750, f32[768]{0:T(1024)S(1)} %mul.279, f32[1024]{0:T(1024)S(1)} %add_rsqrt_fusion.3, f32[1024]{0:T(1024)S(1)} %broadcast_multiply_fusion.11, bf16[512,768]{0,1:T(8,128)(2,1)S(1)} %bitcast.167, ...), kind=kOutput, calls=%fused_computation.285 | convolution fusion | flops 3637248000 | bytes 19278848 | tf_op jit(solution)/shard_map/rd,jde->jre/dot_general | solution.py:530
  140.3 2.2 copy.252.patq_ref
  142.4 2.2 copy.253.patq_ref
  144.6 3.4 fusion.21
  148.3 26.8 %shard_map.256 = f32[1,512,768]{2,1,0:T(8,128)S(1)} custom-call(bf16[1,512,768]{2,1,0:T(8,128)(2,1)S(1)} %get-tuple-element.160.q_ref, bf16[1,512,768]{2,1,0:T(8,128)(2,1)S(1)} %slice.282.k_ref, bf16[1,512,768]{2,1,0:T(8,128)(2,1)S(1)} %slice.285.v_ref, s32[12,512,8]{2,1,0:T(8,128)} %copy.252.patq_ref, s32[12,8,512]{2,1,0:T(8,128)S(1)} %slice.299.patk_ref, ...), custom_call_target="tpu_custom_call" | custom-call | flops 1610612736 | bytes 8650752 | tf_op jit(solution)/shard_map/pallas_call | solution.py:217
  175.1 36.2 %shard_map.257 = f32[1,512,768]{2,1,0:T(8,128)S(1)} custom-call(bf16[1,512,768]{2,1,0:T(8,128)(2,1)S(1)} %get-tuple-element.161.q_ref, bf16[1,1024,768]{2,1,0:T(8,128)(2,1)S(1)} %copy-done.12, bf16[1,1024,768]{2,1,0:T(8,128)(2,1)S(1)} %get-tuple-element.143.v_ref, s32[12,512,8]{2,1,0:T(8,128)} %copy.253.patq_ref, s32[12,8,1024]{2,1,0:T(8,128)S(1)} %stack.57.patk_ref, ...), custom_call_target="tpu_custom_call" | custom-call | flops 3221225472 | bytes 14942208 | tf_op jit(solution)/shard_map/pallas_call | solution.py:217
  212.1 2.9 reshape.1753
  215.1 2.2 copy.205
  221.4 9.3 %copy.206 = bf16[8,2,96,1536]{3,1,2,0:T(2,128)(2,1)} copy(bf16[8,2,96,1536]{3,2,1,0:T(8,128)(2,1)} %bitcast.180) | data formatting | bytes 9437184 | tf_op jit(solution)/shard_map/reshape | solution.py:407
  230.7 3.8 copy.264
  234.6 12.2 %fusion.74 = (f32[1024]{0:T(1024)S(1)}, f32[1024,3072]{1,0:T(8,128)}) fusion(f32[3072]{0:T(1024)S(1)} %reshape.1776, bf16[768,3072]{1,0:T(8,128)(2,1)S(1)} %bitcast.183, f32[1024,768]{0,1:T(8,128)S(1)} %copy-done.37, f32[768]{0:T(1024)S(1)} %copy-done.62, f32[1024]{0:T(1024)S(1)} %add_rsqrt_fusion.1, f32[1024]{0:T(1024)S(1)} %broadcast_multiply_fusion.9), kind=kOutput, calls=%fused_computation.274 | convolution fusion | flops 4866440192 | bytes 20474880 | tf_op jit(solution)/shard_map/dot_general | solution.py:551
  246.8 8.1 %multiply_reduce_fusion.2 = f32[1024]{0:T(1024)S(1)} fusion(f32[1024]{0:T(1024)S(1)} %broadcast_multiply_fusion.2, f32[1024,3072]{1,0:T(8,128)} %get-tuple-element.185, f32[3072]{0:T(1024)S(1)} %reshape.1776), kind=kLoop, calls=%fused_computation.12 | loop fusion | flops 37747712 | bytes 12603392 | tf_op jit(solution)/shard_map/reduce_sum | solution.py:73
  254.9 7.3 %reshape.1758 = bf16[8,2,1536,96]{2,1,0,3:T(2,128)(2,1)} reshape(bf16[24576,96]{0,1:T(8,128)(2,1)} %all-gather.14.cloned.1.call-done) | data formatting | bytes 9437184 | tf_op jit(solution)/shard_map/reshape | solution.py:407
  262.2 7.7 %copy.211 = bf16[8,2,1536,96]{2,1,3,0:T(2,128)(2,1)} copy(bf16[8,2,1536,96]{2,1,0,3:T(2,128)(2,1)} %reshape.1758) | data formatting | bytes 9437184 | tf_op jit(solution)/shard_map/reshape | solution.py:407
  269.9 3.6 copy.265
  273.5 21.3 %multiply_reduce_fusion = (bf16[3072]{0:T(1024)(128)(2,1)S(1)}, f32[1024]{0:T(1024)S(1)}, f32[1024]{0:T(1024)S(1)}, bf16[1024,3072]{1,0:T(8,128)(2,1)}, f32[1024,3072]{1,0:T(8,128)}) fusion(f32[1024]{0:T(1024)S(1)} %add_rsqrt_fusion, f32[1024]{0:T(1024)S(1)} %broadcast_multiply_fusion.2, f32[1024,3072]{1,0:T(8,128)} %get-tuple-element.185, ...), kind=kOutput, calls=%fused_computation.9 | convolution fusion | flops 4898679808 | bytes 37795840 | tf_op jit(solution)/shard_map/dot_general | solution.py:65
  294.9 16.6 %fusion.75 = (bf16[3072]{0:T(1024)(128)(2,1)S(1)}, bf16[1024,3072]{1,0:T(8,128)(2,1)S(1)}) fusion(f32[1024]{0:T(1024)S(1)} %broadcast_multiply_fusion, f32[1024]{0:T(1024)S(1)} %broadcast_multiply_fusion.2, f32[1024,3072]{1,0:T(8,128)} %get-tuple-element.185, f32[3072]{0:T(1024)S(1)} %reshape.1776, f32[1024]{0:T(1024)S(1)} %broadcast_multiply_fusion.1, ...), kind=kLoop, calls=%fused_computation.275 | loop fusion | flops 94368768 | bytes 31504384 | tf_op jit(solution)/shard_map/reduce_sum | solution.py:613
  311.5 7.8 %multiply_reduce_fusion.5 = (bf16[768]{0:T(1024)(128)(2,1)S(1)}, f32[1024]{0:T(1024)S(1)}, f32[1024]{0:T(1024)S(1)}, f32[1024,768]{0,1:T(8,128)S(1)}) fusion(f32[1024,768]{0,1:T(8,128)S(1)} %copy-done.38, f32[1024]{0:T(1024)S(1)} %add_rsqrt_fusion.1, f32[1024]{0:T(1024)S(1)} %broadcast_multiply_fusion.9, f32[768]{0:T(1024)S(1)} %copy-done.62, ...), kind=kOutput, calls=%fused_computation.58 | convolution fusion | flops 4838126592 | bytes 17322496 | tf_op jit(solution)/shard_map/dot_general | solution.py:65
  319.3 5.4 convolution_convert_fusion
  324.7 3.4 convert_reduce_fusion.2
  330.3 2.3 multiply_reduce_fusion.4
  332.7 6.8 %convolution_convert_fusion.1 = bf16[768,3072]{1,0:T(8,128)(2,1)S(1)} fusion(bf16[1024,3072]{1,0:T(8,128)(2,1)S(1)} %bitcast.213, bf16[512,768]{0,1:T(8,128)(2,1)} %bitcast.1, bf16[512,768]{0,1:T(8,128)(2,1)S(1)} %bitcast.192, pred[]{:T(512)S(6)} %eq.182), kind=kOutput, calls=%fused_computation.18 | convolution fusion | flops 4841275392 | bytes 12582913 | tf_op jit(solution)/shard_map/dot_general | solution.py:59
  339.5 2.4 multiply_convert_fusion.1
  342.7 4.7 pad_maximum_fusion
  349.3 9.4 %add_convert_fusion = bf16[1024,768]{0,1:T(8,128)(2,1)S(1)} fusion(f32[1024,768]{0,1:T(8,128)S(1)} %copy-done.39, bf16[1024,3072]{1,0:T(8,128)(2,1)} %get-tuple-element.142, bf16[3072,768]{0,1:T(8,128)(2,1)} %bitcast.182, f32[768]{0:T(1024)S(1)} %add.737), kind=kOutput, calls=%fused_computation.59 | convolution fusion | flops 4834197504 | bytes 15731712 | tf_op jit(solution)/shard_map/dot_general | solution.py:556
  360.0 2.4 copy.219
  369.5 53.7 %shard_map.259 = (bf16[1,512,768]{2,1,0:T(8,128)(2,1)S(1)}, f32[1,1024,768]{2,1,0:T(8,128)}, f32[1,1024,768]{2,1,0:T(8,128)}) custom-call(bf16[1,512,768]{2,1,0:T(8,128)(2,1)S(1)} %copy-done.21, bf16[1,1024,768]{2,1,0:T(8,128)(2,1)S(1)} %copy-done.13, bf16[1,1024,768]{2,1,0:T(8,128)(2,1)S(1)} %copy-done.3, ...), custom_call_target="tpu_custom_call" | custom-call | flops 8053063680 | bytes 26738688 | tf_op jit(solution)/shard_map/pallas_call | solution.py:244
  428.6 37.7 %shard_map.258 = (bf16[1,512,768]{2,1,0:T(8,128)(2,1)S(1)}, f32[1,512,768]{2,1,0:T(8,128)S(1)}, f32[1,512,768]{2,1,0:T(8,128)}) custom-call(bf16[1,512,768]{2,1,0:T(8,128)(2,1)S(1)} %copy-done.9, bf16[1,512,768]{2,1,0:T(8,128)(2,1)S(1)} %copy-done.5, bf16[1,512,768]{2,1,0:T(8,128)(2,1)S(1)} %copy-done.7, bf16[1,512,768]{2,1,0:T(8,128)(2,1)S(1)} %copy-done.22, ...), custom_call_target="tpu_custom_call" | custom-call | flops 4026531840 | bytes 14155776 | tf_op jit(solution)/shard_map/pallas_call | solution.py:244
  467.7 4.0 fusion.77
  476.4 2.3 add_convert_fusion.2
  479.0 2.5 pad_maximum_fusion.1
  483.2 8.5 %collective-permute-done.3 = bf16[1,512,768]{2,1,0:T(8,128)(2,1)S(1)} collective-permute-done((bf16[1,512,768]{2,1,0:T(8,128)(2,1)}, bf16[1,512,768]{2,1,0:T(8,128)(2,1)S(1)}, u32[]{:S(2)}, u32[]{:S(2)}) %collective-permute-start.3) | collective-permute-done | bytes 786464 | tf_op jit(solution)/shard_map/ppermute | solution.py:356
  495.4 8.5 %fusion.38 = bf16[768,3,768]{2,0,1:T(8,128)(2,1)} fusion(bf16[3,1024,768]{2,1,0:T(8,128)(2,1)} %pad_maximum_fusion.1, f32[768]{0:T(1024)S(1)} %copy-done.61, f32[1024]{0:T(1024)S(1)} %copy-done.59, f32[1024]{0:T(1024)S(1)} %copy-done.57, bf16[512,768]{0,1:T(8,128)(2,1)S(1)} %bitcast.176, bf16[512,768]{0,1:T(8,128)(2,1)S(1)} %bitcast.169, pred[]{:T(512)S(6)} %eq.182), kind=kOutput, calls=%fused_computation.93 | convolution fusion | flops 3634888704 | bytes 9841665 | tf_op jit(solution)/shard_map/rd,jre->dje/dot_general | solution.py:662
  503.8 8.4 %fusion.19 = (bf16[768]{0:T(1024)(128)(2,1)S(1)}, f32[1024]{0:T(1024)S(1)}, f32[1024]{0:T(1024)S(1)}, f32[1024,768,1]{0,1,2:T(8,128)}) fusion(f32[1024]{0:T(1024)S(1)} %copy-done.59, f32[1024]{0:T(1024)S(1)} %copy-done.57, bf16[512,768]{0,1:T(8,128)(2,1)S(1)} %bitcast.170, bf16[512,768]{0,1:T(8,128)(2,1)S(1)} %bitcast.177, pred[]{:T(512)S(6)} %eq.182, ...), kind=kOutput, calls=%fused_computation.41 | convolution fusion | flops 3638031616 | bytes 12997121 | tf_op jit(solution)/shard_map/jre,jde->rd/dot_general | solution.py:667
  513.5 2.3 pad_maximum_fusion.2
  521.5 4.0 fusion.18
  530.7 24.3 %collective-permute-done.10 = bf16[96,1,3456]{2,0,1:T(8,128)(2,1)} collective-permute-done((bf16[96,1,3456]{2,0,1:T(8,128)(2,1)}, bf16[96,1,3456]{2,0,1:T(8,128)(2,1)}, u32[]{:S(2)}, u32[]{:S(2)}) %collective-permute-start.10) | collective-permute-done | bytes 663584 | tf_op jit(solution)/shard_map/ppermute | solution.py:445
  557.7 6.3 %collective-permute-done.5 = bf16[1,512,768]{2,1,0:T(8,128)(2,1)} collective-permute-done((bf16[1,512,768]{2,1,0:T(8,128)(2,1)}, bf16[1,512,768]{2,1,0:T(8,128)(2,1)}, u32[]{:S(2)}, u32[]{:S(2)}) %collective-permute-start.5) | collective-permute-done | bytes 786464 | tf_op jit(solution)/shard_map/ppermute | solution.py:355
  574.6 5.0 collective-permute-done.8
  583.0 2.9 collective-permute-done.9
  (352 shorter events, 105.7 us)
Async XLA Ops:
  7.2 92.0 %copy-start = (s32[4,2]{0,1:T(2,128)S(1)}, s32[4,2]{0,1:T(2,128)}, u32[]{:S(2)}) copy-start(s32[4,2]{0,1:T(2,128)} %param.21) | copy-start | bytes 100
  7.2 59.5 %all-gather.8.cloned.1.call-start = ((), (), s32[]{:S(2)}) async-start(), calls=%async_computation.2 | async-start | bytes 3829760 | tf_op jit(solution)/shard_map/all_gather | solution.py:416
  16.4 195.7 %all-gather.10.cloned.1.call-start = ((), (), s32[]{:S(2)}) async-start(), calls=%async_computation.4 | async-start | bytes 1253376 | tf_op jit(solution)/shard_map/all_gather | solution.py:406
  89.7 131.7 %all-gather.12.cloned.1.call-start = ((), (), s32[]{:S(2)}) async-start(), calls=%async_computation.5 | async-start | bytes 5013504 | tf_op jit(solution)/shard_map/all_gather | solution.py:406
  90.4 164.5 %all-gather.14.cloned.1.call-start = ((), (), s32[]{:S(2)}) async-start(), calls=%async_computation.6 | async-start | bytes 5013504 | tf_op jit(solution)/shard_map/all_gather | solution.py:406
  94.9 20.6 %collective-permute-start.1 = (bf16[1,512,768]{1,2,0:T(8,128)(2,1)}, bf16[1,512,768]{1,2,0:T(8,128)(2,1)S(1)}, u32[]{:S(2)}, u32[]{:S(2)}) collective-permute-start(bf16[1,512,768]{1,2,0:T(8,128)(2,1)} %copy.250), channel_id=1, source_target_pairs={{0,2},{2,0},{1,3},{3,1},{4,6},{6,4},{5,7},{7,5},{8,10},{10,8},{9,1... | collective-permute-start | bytes 2359304 | tf_op jit(solution)/shard_map/ppermute | solution.py:760
  98.6 174.9 %collective-permute-start = (bf16[1,512,768]{1,2,0:T(8,128)(2,1)}, bf16[1,512,768]{1,2,0:T(8,128)(2,1)}, u32[]{:S(2)}, u32[]{:S(2)}) collective-permute-start(bf16[1,512,768]{1,2,0:T(8,128)(2,1)} %copy.249), channel_id=1, source_target_pairs={{0,2},{2,0},{1,3},{3,1},{4,6},{6,4},{5,7},{7,5},{8,10},{10,8},{9,1... | collective-permute-start | bytes 2359304 | tf_op jit(solution)/shard_map/ppermute | solution.py:760
  103.3 13.7 %copy-start.33 = (bf16[1,512,768]{1,2,0:T(8,128)(2,1)}, bf16[1,512,768]{1,2,0:T(8,128)(2,1)S(1)}, u32[]{:S(2)}) copy-start(bf16[1,512,768]{1,2,0:T(8,128)(2,1)S(1)} %copy.188) | copy-start | bytes 2359300
  104.5 12.1 %copy-start.31 = (bf16[8,2,112640]{2,1,0:T(2,128)(2,1)S(1)}, bf16[8,2,112640]{2,1,0:T(2,128)(2,1)}, u32[]{:S(2)}) copy-start(bf16[8,2,112640]{2,1,0:T(2,128)(2,1)} %reshape.1748) | copy-start | bytes 10813444
  104.5 43.7 %copy-start.27 = (s32[1,8,512]{2,1,0:T(8,128)}, s32[1,8,512]{2,1,0:T(8,128)S(1)}, u32[]{:S(2)}) copy-start(s32[1,8,512]{2,1,0:T(8,128)S(1)} %pad_slice_fusion.2.pck_ref) | copy-start | bytes 49156
  107.1 41.1 %copy-start.16 = (s32[1,512,8]{2,1,0:T(8,128)}, s32[1,512,8]{2,1,0:T(8,128)S(1)}, u32[]{:S(2)}) copy-start(s32[1,512,8]{2,1,0:T(8,128)S(1)} %get-tuple-element.168.pcq_ref) | copy-start | bytes 49156
  115.5 11.1 %copy-start.41 = (bf16[1,512,768]{1,2,0:T(8,128)(2,1)}, bf16[1,512,768]{1,2,0:T(8,128)(2,1)S(1)}, u32[]{:S(2)}) copy-start(bf16[1,512,768]{1,2,0:T(8,128)(2,1)S(1)} %collective-permute-done.1) | copy-start | bytes 2359300
  116.6 9.9 %copy-start.58 = (f32[1024]{0:T(1024)}, f32[1024]{0:T(1024)S(1)}, u32[]{:S(2)}) copy-start(f32[1024]{0:T(1024)S(1)} %add_rsqrt_fusion.3) | copy-start | bytes 12292
  117.0 9.5 %copy-start.60 = (f32[768]{0:T(1024)}, f32[768]{0:T(1024)S(1)}, u32[]{:S(2)}) copy-start(f32[768]{0:T(1024)S(1)} %mul.279) | copy-start | bytes 9220
  126.6 21.6 %copy-start.4 = (bf16[1,512,768]{2,1,0:T(8,128)(2,1)}, bf16[1,512,768]{2,1,0:T(8,128)(2,1)S(1)}, u32[]{:S(2)}) copy-start(bf16[1,512,768]{2,1,0:T(8,128)(2,1)S(1)} %slice.282.k_ref) | copy-start | bytes 2359300
  136.8 38.3 %copy-start.18 = (s32[12,8,1024]{2,1,0:T(8,128)}, s32[12,8,1024]{2,1,0:T(8,128)S(1)}, u32[]{:S(2)}) copy-start(s32[12,8,1024]{2,1,0:T(8,128)S(1)} %stack.57.patk_ref) | copy-start | bytes 1179652
  136.8 11.4 %copy-start.23 = (s32[12,8,512]{2,1,0:T(8,128)}, s32[12,8,512]{2,1,0:T(8,128)S(1)}, u32[]{:S(2)}) copy-start(s32[12,8,512]{2,1,0:T(8,128)S(1)} %slice.299.patk_ref) | copy-start | bytes 589828
  136.8 358.5 %reduce-scatter.5.cloned.1.call-start = ((), (), s32[]{:S(2)}) async-start(), calls=%async_computation.3 | async-start | bytes 11943936 | tf_op jit(solution)/shard_map/reduce_scatter | solution.py:515
  148.0 27.1 %copy-start.2 = (bf16[1,1024,768]{2,1,0:T(8,128)(2,1)}, bf16[1,1024,768]{2,1,0:T(8,128)(2,1)S(1)}, u32[]{:S(2)}) copy-start(bf16[1,1024,768]{2,1,0:T(8,128)(2,1)S(1)} %get-tuple-element.143.v_ref) | copy-start | bytes 4718596
  148.1 27.0 %copy-start.6 = (bf16[1,512,768]{2,1,0:T(8,128)(2,1)}, bf16[1,512,768]{2,1,0:T(8,128)(2,1)S(1)}, u32[]{:S(2)}) copy-start(bf16[1,512,768]{2,1,0:T(8,128)(2,1)S(1)} %slice.285.v_ref) | copy-start | bytes 2359300
  148.2 26.9 %copy-start.8 = (bf16[1,512,768]{2,1,0:T(8,128)(2,1)}, bf16[1,512,768]{2,1,0:T(8,128)(2,1)S(1)}, u32[]{:S(2)}) copy-start(bf16[1,512,768]{2,1,0:T(8,128)(2,1)S(1)} %get-tuple-element.160.q_ref) | copy-start | bytes 2359300
  148.2 26.9 %copy-start.20 = (bf16[1,512,768]{2,1,0:T(8,128)(2,1)}, bf16[1,512,768]{2,1,0:T(8,128)(2,1)S(1)}, u32[]{:S(2)}) copy-start(bf16[1,512,768]{2,1,0:T(8,128)(2,1)S(1)} %get-tuple-element.161.q_ref) | copy-start | bytes 2359300
  148.2 26.8 %copy-start.12 = (bf16[1,1024,768]{2,1,0:T(8,128)(2,1)S(1)}, bf16[1,1024,768]{2,1,0:T(8,128)(2,1)}, u32[]{:S(2)}) copy-start(bf16[1,1024,768]{2,1,0:T(8,128)(2,1)} %slice.301.k_ref) | copy-start | bytes 4718596
  148.3 26.8 %copy-start.25 = (s32[1,512,8]{2,1,0:T(8,128)S(1)}, s32[1,512,8]{2,1,0:T(8,128)}, u32[]{:S(2)}) copy-start(s32[1,512,8]{2,1,0:T(8,128)} %get-tuple-element.169.pcq_ref) | copy-start | bytes 49156
  148.3 26.8 %copy-start.29 = (s32[1,8,1024]{2,1,0:T(8,128)S(1)}, s32[1,8,1024]{2,1,0:T(8,128)}, u32[]{:S(2)}) copy-start(s32[1,8,1024]{2,1,0:T(8,128)} %pad.26.pck_ref) | copy-start | bytes 98308
  212.1 5.4 copy-start.64
  234.6 12.3 %copy-start.47 = (bf16[96,8,2,1536]{3,1,2,0:T(8,128)(2,1)}, bf16[96,8,2,1536]{3,1,2,0:T(8,128)(2,1)S(1)}, u32[]{:S(2)}) copy-start(bf16[96,8,2,1536]{3,1,2,0:T(8,128)(2,1)S(1)} %copy.264) | copy-start | bytes 14155780
  273.5 21.4 %copy-start.46 = (bf16[96,8,2,1536]{3,1,2,0:T(8,128)(2,1)}, bf16[96,8,2,1536]{3,1,2,0:T(8,128)(2,1)S(1)}, u32[]{:S(2)}) copy-start(bf16[96,8,2,1536]{3,1,2,0:T(8,128)(2,1)S(1)} %copy.265) | copy-start | bytes 14155780
  294.9 16.6 %copy-start.38 = (f32[1024,768]{0,1:T(8,128)S(1)}, f32[1024,768]{0,1:T(8,128)}, u32[]{:S(2)}) copy-start(f32[1024,768]{0,1:T(8,128)} %copy-done.36) | copy-start | bytes 9437188
  347.4 224.1 %reduce-scatter.7.cloned.1.call-start = ((), (), s32[]{:S(2)}) async-start(), calls=%async_computation.7 | async-start | bytes 4313088
  358.7 5.3 copy-start.44
  362.4 120.8 %collective-permute-start.4 = (bf16[1,512,768]{2,1,0:T(8,128)(2,1)}, bf16[1,512,768]{2,1,0:T(8,128)(2,1)}, u32[]{:S(2)}, u32[]{:S(2)}) collective-permute-start(bf16[1,512,768]{2,1,0:T(8,128)(2,1)} %bitcast.201), channel_id=1, source_target_pairs={{0,3},{3,0},{1,2},{2,1},{4,7},{7,4},{5,6},{6,5},{8,11},{11,8},{9,1... | collective-permute-start | bytes 2359304 | tf_op jit(solution)/shard_map/ppermute | solution.py:357
  363.2 118.3 %collective-permute-start.2 = (bf16[1,512,768]{2,1,0:T(8,128)(2,1)}, bf16[1,512,768]{2,1,0:T(8,128)(2,1)}, u32[]{:S(2)}, u32[]{:S(2)}) collective-permute-start(bf16[1,512,768]{2,1,0:T(8,128)(2,1)} %bitcast.202), channel_id=1, source_target_pairs={{0,2},{2,0},{1,3},{3,1},{4,6},{6,4},{5,7},{7,5},{8,10},{10,8},{9,1... | collective-permute-start | bytes 2359304 | tf_op jit(solution)/shard_map/ppermute | solution.py:355
  369.5 55.9 %copy-start.5 = (bf16[1,512,768]{2,1,0:T(8,128)(2,1)S(1)}, bf16[1,512,768]{2,1,0:T(8,128)(2,1)}, u32[]{:S(2)}) copy-start(bf16[1,512,768]{2,1,0:T(8,128)(2,1)} %copy-done.4) | copy-start | bytes 2359300
  369.5 55.9 %copy-start.7 = (bf16[1,512,768]{2,1,0:T(8,128)(2,1)S(1)}, bf16[1,512,768]{2,1,0:T(8,128)(2,1)}, u32[]{:S(2)}) copy-start(bf16[1,512,768]{2,1,0:T(8,128)(2,1)} %copy-done.6) | copy-start | bytes 2359300
  369.5 55.9 %copy-start.17 = (s32[1,512,8]{2,1,0:T(8,128)S(1)}, s32[1,512,8]{2,1,0:T(8,128)}, u32[]{:S(2)}) copy-start(s32[1,512,8]{2,1,0:T(8,128)} %copy-done.16) | copy-start | bytes 49156
  369.5 55.9 %copy-start.28 = (s32[1,8,512]{2,1,0:T(8,128)S(1)}, s32[1,8,512]{2,1,0:T(8,128)}, u32[]{:S(2)}) copy-start(s32[1,8,512]{2,1,0:T(8,128)} %copy-done.27) | copy-start | bytes 49156
  467.7 8.7 %copy-start.15 = (f32[1,512,768]{2,1,0:T(8,128)S(1)}, f32[1,512,768]{2,1,0:T(8,128)}, u32[]{:S(2)}) copy-start(f32[1,512,768]{2,1,0:T(8,128)} %copy-done.14) | copy-start | bytes 4718596
  473.9 17.8 %collective-permute-start.3 = (bf16[1,512,768]{2,1,0:T(8,128)(2,1)}, bf16[1,512,768]{2,1,0:T(8,128)(2,1)S(1)}, u32[]{:S(2)}, u32[]{:S(2)}) collective-permute-start(bf16[1,512,768]{2,1,0:T(8,128)(2,1)} %bitcast.193), channel_id=1, source_target_pairs={{0,1},{1,0},{2,3},{3,2},{4,5},{5,4},{6,7},{7,6},{8,9},{9,8},{10,11... | collective-permute-start | bytes 2359304 | tf_op jit(solution)/shard_map/ppermute | solution.py:356
  495.3 8.5 %copy-start.48 = (bf16[3,768,768]{2,1,0:T(8,128)(2,1)S(1)}, bf16[3,768,768]{2,1,0:T(8,128)(2,1)}, u32[]{:S(2)}) copy-start(bf16[3,768,768]{2,1,0:T(8,128)(2,1)} %reshape.1750) | copy-start | bytes 10616836
  520.0 35.0 %collective-permute-start.10 = (bf16[96,1,3456]{2,0,1:T(8,128)(2,1)}, bf16[96,1,3456]{2,0,1:T(8,128)(2,1)}, u32[]{:S(2)}, u32[]{:S(2)}) collective-permute-start(bf16[96,1,3456]{2,0,1:T(8,128)(2,1)} %constant_dynamic-slice_fusion), channel_id=1, source_target_pairs={{0,1},{1,0},{2,3},{3,2},{4,5},{5,4},{6,7},{7,6},{8,9},{9,8},{10,11... | collective-permute-start | bytes 1990664 | tf_op jit(solution)/shard_map/ppermute | solution.py:445
  526.8 38.9 %collective-permute-start.7 = (bf16[1,512,768]{2,1,0:T(8,128)(2,1)}, bf16[1,512,768]{2,1,0:T(8,128)(2,1)}, u32[]{:S(2)}, u32[]{:S(2)}) collective-permute-start(bf16[1,512,768]{2,1,0:T(8,128)(2,1)} %bitcast.203), channel_id=1, source_target_pairs={{0,3},{3,0},{1,2},{2,1},{4,7},{7,4},{5,6},{6,5},{8,11},{11,8},{9,1... | collective-permute-start | bytes 2359304 | tf_op jit(solution)/shard_map/ppermute | solution.py:357
  527.9 36.2 %collective-permute-start.5 = (bf16[1,512,768]{2,1,0:T(8,128)(2,1)}, bf16[1,512,768]{2,1,0:T(8,128)(2,1)}, u32[]{:S(2)}, u32[]{:S(2)}) collective-permute-start(bf16[1,512,768]{2,1,0:T(8,128)(2,1)} %bitcast.204), channel_id=1, source_target_pairs={{0,2},{2,0},{1,3},{3,1},{4,6},{6,4},{5,7},{7,5},{8,10},{10,8},{9,1... | collective-permute-start | bytes 2359304 | tf_op jit(solution)/shard_map/ppermute | solution.py:355
  528.8 39.2 %collective-permute-start.6 = (bf16[1,512,768]{2,1,0:T(8,128)(2,1)S(1)}, bf16[1,512,768]{2,1,0:T(8,128)(2,1)S(1)}, u32[]{:S(2)}, u32[]{:S(2)}) collective-permute-start(bf16[1,512,768]{2,1,0:T(8,128)(2,1)S(1)} %bitcast.195), channel_id=1, source_target_pairs={{0,1},{1,0},{2,3},{3,2},{4,5},{5,4},{6,7},{7,6},{8,9},{9,8},{10,11... | collective-permute-start | bytes 2359304 | tf_op jit(solution)/shard_map/ppermute | solution.py:356
  556.2 18.2 %collective-permute-start.11 = (bf16[96,1,3456]{2,0,1:T(8,128)(2,1)S(1)}, bf16[96,1,3456]{2,0,1:T(8,128)(2,1)S(1)}, u32[]{:S(2)}, u32[]{:S(2)}) collective-permute-start(bf16[96,1,3456]{2,0,1:T(8,128)(2,1)S(1)} %add_convert_fusion.3), channel_id=1, source_target_pairs={{0,2},{2,0},{1,3},{3,1},{4,6},{6,4},{5,7},{7,5},{8,10},{10,8},{9,1... | collective-permute-start | bytes 1990664 | tf_op jit(solution)/shard_map/ppermute | solution.py:452
  573.4 6.2 %collective-permute-start.8 = (bf16[104,3,384]{2,0,1:T(8,128)(2,1)S(1)}, bf16[104,3,384]{2,0,1:T(8,128)(2,1)S(1)}, u32[]{:S(2)}, u32[]{:S(2)}) collective-permute-start(bf16[104,3,384]{2,0,1:T(8,128)(2,1)S(1)} %copy.258), channel_id=1, source_target_pairs={{0,1},{1,0},{2,3},{3,2},{4,5},{5,4},{6,7},{7,6},{8,9},{9,8},{10,11... | collective-permute-start | bytes 718856 | tf_op jit(solution)/shard_map/ppermute | solution.py:445
  579.6 11.0 %copy-start.1 = (s32[4,2]{0,1:T(2,128)S(1)}, s32[4,2]{0,1:T(2,128)}, u32[]{:S(2)}) copy-start(s32[4,2]{0,1:T(2,128)} %param.21) | copy-start | bytes 100
  579.6 6.2 %collective-permute-start.9 = (bf16[104,3,384]{2,0,1:T(8,128)(2,1)S(1)}, bf16[104,3,384]{2,0,1:T(8,128)(2,1)S(1)}, u32[]{:S(2)}, u32[]{:S(2)}) collective-permute-start(bf16[104,3,384]{2,0,1:T(8,128)(2,1)S(1)} %add_convert_fusion.4), channel_id=1, source_target_pairs={{0,2},{2,0},{1,3},{3,1},{4,6},{6,4},{5,7},{7,5},{8,10},{10,8},{9,1... | collective-permute-start | bytes 718856 | tf_op jit(solution)/shard_map/ppermute | solution.py:452
  (39 other events, 90.4 us)
Sparse Core Ops, SparseCore 0:
  16.5 50.1 all-gather.7
  89.8 35.6 all-gather.9
  127.8 52.5 all-gather.11
  182.6 51.6 all-gather.13
  347.5 109.1 reduce-scatter.4
  518.0 46.2 reduce-scatter.6
